TPU v7x, 8 devices: a whole 2x2x1 slice. The times are simulated.
8 devices in a mesh: rep: 2 (over y, z), dp: 4 (over x, core).
Axes of the slice: x: 2, y: 2, z: 1, core: 2. Of those that a mesh axis runs over, the one named last changes fastest.
Arguments:
- g_w_gate: bfloat16 [8, 2, 1280, 4480], P(('rep', 'dp')), parts along dimension 0
- g_w_up: bfloat16 [8, 2, 1280, 4480], P(('rep', 'dp')), parts along dimension 0
- g_w_down: bfloat16 [8, 2, 4480, 1280], P(('rep', 'dp')), parts along dimension 0
- w_gate: bfloat16 [2, 1280, 4480], replicated
- w_up: bfloat16 [2, 1280, 4480], replicated
- w_down: bfloat16 [2, 4480, 1280], replicated
- m_w_gate: float32 [2, 1280, 4480], P(None, 'dp')
- m_w_up: float32 [2, 1280, 4480], P(None, 'dp')
- m_w_down: float32 [2, 4480, 1280], P(None, 'dp')
- v_w_gate: float32 [2, 1280, 4480], P(None, 'dp')
- v_w_up: float32 [2, 1280, 4480], P(None, 'dp')
- v_w_down: float32 [2, 4480, 1280], P(None, 'dp')
Outputs:
- output 1: bfloat16 [4, 1280, 4480], P('rep'), parts along dimension 0
- output 2: bfloat16 [4, 1280, 4480], P('rep'), parts along dimension 0
- output 3: bfloat16 [4, 4480, 1280], P('rep'), parts along dimension 0
- output 4: float32 [4, 1280, 4480], P('rep', 'dp'), parts along dimension 0
- output 5: float32 [4, 1280, 4480], P('rep', 'dp'), parts along dimension 0
- output 6: float32 [4, 4480, 1280], P('rep', 'dp'), parts along dimension 0
- output 7: float32 [4, 1280, 4480], P('rep', 'dp'), parts along dimension 0
- output 8: float32 [4, 1280, 4480], P('rep', 'dp'), parts along dimension 0
- output 9: float32 [4, 4480, 1280], P('rep', 'dp'), parts along dimension 0
There are 2 independent parts. A program takes and returns all parts, laid end to end along the dimension named above; an argument that names none is the same for every part.
All inputs are finite; a program needn't handle non-finite values.
Results may differ from a plain program's by a relative error of at most 0.022.
Values are sent between devices in bfloat16 or wider.
A program may use at most 2 GiB of HBM per device.

v0:
```python
import jax
import jax.numpy as jnp
from jax import lax
from jax.sharding import PartitionSpec as P


def adamw(w, m, v, g):
    m = 0.9 * m + 0.1 * g
    v = 0.95 * v + 0.05 * g * g
    step = m * lax.rsqrt(v + 1e-8) + 0.1 * w
    return (w - 0.02 * step).astype(jnp.bfloat16), m, v


def solution(mesh):
    def step(*arrays):
        terms, weights, m, v = (arrays[i : i + 3] for i in (0, 3, 6, 9))
        gradients = [lax.psum_scatter(t[0], "dp", scatter_dimension=1, tiled=True).astype(jnp.float32) for t in terms]
        me = lax.axis_index("dp")
        own = [lax.dynamic_slice_in_dim(w, me * one.shape[1], one.shape[1], 1).astype(jnp.float32) for w, one in zip(weights, m, strict=True)]
        new = [adamw(w, m, v, g) for w, m, v, g in zip(own, m, v, gradients, strict=True)]
        whole = [lax.all_gather(one[0], "dp", axis=1, tiled=True) for one in new]
        return (*whole, *(one[1] for one in new), *(one[2] for one in new))

    all_of, cut = P(None, None, None), P(None, "dp", None)
    return jax.shard_map(
        step,
        mesh=mesh,
        in_specs=(P(("rep", "dp"), None, None, None),) * 3 + (all_of,) * 3 + (cut,) * 6,
        out_specs=(P("rep", None, None),) * 3 + (P("rep", "dp", None),) * 6,
        check_vma=False,
    )
```

profile of v0, /device:TPU:0, one launch (start us, length us, event | category | flops | bytes accessed | tf_op | source)
XLA Modules:
  0.0 960.5 jit_solution(14840540007730883997)
XLA Ops:
  7.2 0.0 reduce-scatter.8.cloned.1.call-start
  7.2 0.7 reduce-scatter.8.cloned.1.call-update
  7.9 0.0 reduce-scatter.6.cloned.1.call-start
  8.0 0.7 reduce-scatter.6.cloned.1.call-update
  8.7 0.0 reduce-scatter.4.cloned.1.call-start
  8.7 0.7 reduce-scatter.4.cloned.1.call-update
  9.4 0.0 all-gather.8.cloned.1.call-start
  9.4 159.6 %reduce-scatter.8.cloned.1.call-done = bf16[2,1120,1280]{2,1,0:T(8,128)(2,1)} async-done(((bf16[2,4480,1280]{2,1,0:T(8,128)(2,1)}), bf16[2,1120,1280]{2,1,0:T(8,128)(2,1)}) %reduce-scatter.8.cloned.1.call-update) | async-done | bytes 5734416 | tf_op jit(solution)/shard_map/reduce_scatter | solution.py:17
  169.1 23.6 %fusion.10 = (bf16[2,1120,1280]{2,1,0:T(8,128)(2,1)}, f32[2,1120,1280]{2,1,0:T(8,128)}, f32[2,1120,1280]{2,1,0:T(8,128)}) fusion(bf16[2,4480,1280]{2,1,0:T(8,128)(2,1)} %param.17, s32[]{:T(128)S(6)} %select_n.8, bf16[2,1120,1280]{2,1,0:T(8,128)(2,1)} %reduce-scatter.8.cloned.1.call-done, f32[2,1120,1280]{2,1,0:T(8,128)} %param.23, f32[2,1120,1280]{2,1,0:T(8,128)} %param.20), kind=kLoop, calls=%fused_computation.22 | loop fusion | flops 45875200 | bytes 63078404 | tf_op jit(solution)/shard_map/convert_element_type | solution.py:11
  192.6 0.0 all-gather.8.cloned.1.call-update
  192.7 0.0 all-gather.6.cloned.1.call-start
  192.7 134.7 %reduce-scatter.6.cloned.1.call-done = bf16[2,320,4480]{2,1,0:T(8,128)(2,1)} async-done(((bf16[2,1280,4480]{2,1,0:T(8,128)(2,1)}), bf16[2,320,4480]{2,1,0:T(8,128)(2,1)}) %reduce-scatter.6.cloned.1.call-update) | async-done | bytes 5734416 | tf_op jit(solution)/shard_map/reduce_scatter | solution.py:17
  327.4 21.9 %fusion.6 = (bf16[2,320,4480]{2,1,0:T(8,128)(2,1)}, f32[2,320,4480]{2,1,0:T(8,128)}, f32[2,320,4480]{2,1,0:T(8,128)}) fusion(bf16[2,1280,4480]{2,1,0:T(8,128)(2,1)} %param.16, s32[]{:T(128)S(6)} %select_n.7, bf16[2,320,4480]{2,1,0:T(8,128)(2,1)} %reduce-scatter.6.cloned.1.call-done, f32[2,320,4480]{2,1,0:T(8,128)} %param.22, f32[2,320,4480]{2,1,0:T(8,128)} %param.19), kind=kLoop, calls=%fused_computation.18 | loop fusion | flops 45875200 | bytes 63078404 | tf_op jit(solution)/shard_map/convert_element_type | solution.py:11
  349.3 0.0 all-gather.6.cloned.1.call-update
  349.3 0.0 all-gather.4.cloned.1.call-start
  349.4 136.3 %reduce-scatter.4.cloned.1.call-done = bf16[2,320,4480]{2,1,0:T(8,128)(2,1)} async-done(((bf16[2,1280,4480]{2,1,0:T(8,128)(2,1)}), bf16[2,320,4480]{2,1,0:T(8,128)(2,1)}) %reduce-scatter.4.cloned.1.call-update) | async-done | bytes 5734416 | tf_op jit(solution)/shard_map/reduce_scatter | solution.py:17
  485.7 21.9 %fusion.2 = (bf16[2,320,4480]{2,1,0:T(8,128)(2,1)}, f32[2,320,4480]{2,1,0:T(8,128)}, f32[2,320,4480]{2,1,0:T(8,128)}) fusion(bf16[2,1280,4480]{2,1,0:T(8,128)(2,1)} %param.15, s32[]{:T(128)S(6)} %select_n.7, bf16[2,320,4480]{2,1,0:T(8,128)(2,1)} %reduce-scatter.4.cloned.1.call-done, f32[2,320,4480]{2,1,0:T(8,128)} %param.21, f32[2,320,4480]{2,1,0:T(8,128)} %param.18), kind=kLoop, calls=%fused_computation.14 | loop fusion | flops 45875200 | bytes 63078404 | tf_op jit(solution)/shard_map/convert_element_type | solution.py:11
  507.6 0.0 all-gather.4.cloned.1.call-update
  507.6 118.7 %all-gather.8.cloned.1.call-done = bf16[2,4480,1280]{2,1,0:T(8,128)(2,1)} async-done(((bf16[2,1120,1280]{2,1,0:T(8,128)(2,1)}), bf16[2,4480,1280]{2,1,0:T(8,128)(2,1)}) %all-gather.8.cloned.1.call-update) | async-done | bytes 22937616 | tf_op jit(solution)/shard_map/all_gather | solution.py:21
  626.4 140.7 %all-gather.6.cloned.1.call-done = bf16[2,1280,4480]{2,1,0:T(8,128)(2,1)} async-done(((bf16[2,320,4480]{2,1,0:T(8,128)(2,1)}), bf16[2,1280,4480]{2,1,0:T(8,128)(2,1)}) %all-gather.6.cloned.1.call-update) | async-done | bytes 22937616 | tf_op jit(solution)/shard_map/all_gather | solution.py:21
  767.0 140.7 %all-gather.4.cloned.1.call-done = bf16[2,1280,4480]{2,1,0:T(8,128)(2,1)} async-done(((bf16[2,320,4480]{2,1,0:T(8,128)(2,1)}), bf16[2,1280,4480]{2,1,0:T(8,128)(2,1)}) %all-gather.4.cloned.1.call-update) | async-done | bytes 22937616 | tf_op jit(solution)/shard_map/all_gather | solution.py:21
  907.7 0.0 slice-start
  907.7 0.0 slice-start.1
  907.7 0.0 slice-start.2
  907.7 19.0 %copy.24 = bf16[2,1280,4480]{2,1,0:T(8,128)(2,1)} copy(bf16[2,1280,4480]{2,1,0:T(8,128)(2,1)} %all-gather.4.cloned.1.call-done) | data formatting | bytes 45875200
  926.7 0.0 slice-start.3
  926.7 0.0 slice-start.4
  926.7 0.0 slice-start.5
  926.7 18.7 %copy.25 = bf16[2,1280,4480]{2,1,0:T(8,128)(2,1)} copy(bf16[2,1280,4480]{2,1,0:T(8,128)(2,1)} %all-gather.6.cloned.1.call-done) | data formatting | bytes 45875200
  945.4 0.0 slice-done
  945.4 0.0 slice-done.1
  945.4 0.0 slice-done.2
  945.4 0.0 slice-done.3
  945.4 0.0 slice-done.4
  945.4 0.0 slice-done.5
  945.5 8.2 copy.26
  (1 shorter events, 0.0 us)
Async XLA Ops:
  7.2 161.9 %reduce-scatter.8.cloned.1.call-start = ((), (), s32[]{:S(2)}) async-start(), calls=%async_computation.7 | async-start | bytes 28672000 | tf_op jit(solution)/shard_map/reduce_scatter | solution.py:17
  7.9 319.5 %reduce-scatter.6.cloned.1.call-start = ((), (), s32[]{:S(2)}) async-start(), calls=%async_computation.5 | async-start | bytes 28672000 | tf_op jit(solution)/shard_map/reduce_scatter | solution.py:17
  8.7 477.0 %reduce-scatter.4.cloned.1.call-start = ((), (), s32[]{:S(2)}) async-start(), calls=%async_computation.3 | async-start | bytes 28672000 | tf_op jit(solution)/shard_map/reduce_scatter | solution.py:17
  9.4 617.0 %all-gather.8.cloned.1.call-start = ((), (), s32[]{:S(2)}) async-start(), calls=%async_computation.8 | async-start | bytes 28672000 | tf_op jit(solution)/shard_map/all_gather | solution.py:21
  192.7 574.4 %all-gather.6.cloned.1.call-start = ((), (), s32[]{:S(2)}) async-start(), calls=%async_computation.6 | async-start | bytes 28672000 | tf_op jit(solution)/shard_map/all_gather | solution.py:21
  349.3 558.4 %all-gather.4.cloned.1.call-start = ((), (), s32[]{:S(2)}) async-start(), calls=%async_computation.4 | async-start | bytes 28672000 | tf_op jit(solution)/shard_map/all_gather | solution.py:21
  907.7 37.7 %slice-start = ((s8[22937600]{0:T(1024)(128)(4,1)}), s8[4194304]{0:T(1024)(128)(4,1)S(1)}, s32[]{:S(2)}) async-start(s8[22937600]{0:T(1024)(128)(4,1)} %bitcast.6), calls=%async_computation.9 | async-start | bytes 8388608
  907.7 37.7 %slice-start.1 = ((s8[22937600]{0:T(1024)(128)(4,1)}), s8[4194304]{0:T(1024)(128)(4,1)S(1)}, s32[]{:S(2)}) async-start(s8[22937600]{0:T(1024)(128)(4,1)} %bitcast.6), calls=%async_computation.10 | async-start | bytes 8388608
  907.7 37.7 %slice-start.2 = ((s8[22937600]{0:T(1024)(128)(4,1)}), s8[4194304]{0:T(1024)(128)(4,1)S(1)}, s32[]{:S(2)}) async-start(s8[22937600]{0:T(1024)(128)(4,1)} %bitcast.6), calls=%async_computation.11 | async-start | bytes 8388608
  926.7 18.7 %slice-start.3 = ((s8[22937600]{0:T(1024)(128)(4,1)}), s8[4194304]{0:T(1024)(128)(4,1)S(1)}, s32[]{:S(2)}) async-start(s8[22937600]{0:T(1024)(128)(4,1)} %bitcast.6), calls=%async_computation.12 | async-start | bytes 8388608
  926.7 18.7 %slice-start.4 = ((s8[22937600]{0:T(1024)(128)(4,1)}), s8[4194304]{0:T(1024)(128)(4,1)S(1)}, s32[]{:S(2)}) async-start(s8[22937600]{0:T(1024)(128)(4,1)} %bitcast.6), calls=%async_computation.13 | async-start | bytes 8388608
  926.7 18.7 %slice-start.5 = ((s8[22937600]{0:T(1024)(128)(4,1)}), s8[1966080]{0:T(1024)(128)(4,1)S(1)}, s32[]{:S(2)}) async-start(s8[22937600]{0:T(1024)(128)(4,1)} %bitcast.6), calls=%async_computation.14 | async-start | bytes 3932160
Sparse Core Ops, SparseCore 0:
  10.6 158.4 reduce-scatter.7
  171.7 155.6 reduce-scatter.5
  330.0 155.6 reduce-scatter.3
  487.6 138.6 all-gather.7
  628.3 138.6 all-gather.5
  769.0 138.6 all-gather.3
where the time goes:
time: 961 us; the launch traced here: 960 us
  waiting for transfers between devices  833 us (87%)
  other arithmetic  67.4 us (7%)
  local copies, waits for them, and re-layouts  45.9 us (5%)
  between operations  14.2 us (1%)
    reduce_scatter x3, waiting for transfers between devices, step(): lax.psum_scatter(t[0], 'dp', scatter_dimension=1, tiled=True)  431 us
    all_gather x3, waiting for transfers between devices, step(): whole = [lax.all_gather(one[0], 'dp', axis=1, tiled=True) for one in new]  400 us
    convert_element_type x3, other arithmetic, adamw(): return ((w - 0.02 * step).astype(jnp.bfloat16), m, v)  67.4 us
    unnamed x15, local copies, waits for them, and re-layouts  45.9 us
  transfers between devices with their start and end apart: 6, of which 6 were waited for; matrix products, arithmetic and copies ran while one was open for 7% of the time, Pallas kernels for 0%

commit v1 on v0

v1 whole, which is shorter than its diff:
```python
import jax
import jax.numpy as jnp
from jax import lax
from jax.experimental import pallas as pl
from jax.experimental.pallas import tpu as pltpu
from jax.sharding import PartitionSpec as P


FAR = [(0, 2), (2, 0), (1, 3), (3, 1)]
MATE = [(0, 1), (1, 0), (2, 3), (3, 2)]
UNITS = 5

CHUNKS = [(0, 0, 0, 1), (0, 0, 1, 4), (0, 1, 0, 5), (1, 0, 0, 5), (1, 1, 0, 5), (2, 0, 0, 5), (2, 1, 0, 4), (2, 1, 4, 1)]

ANY = pl.BlockSpec(memory_space=pl.ANY)


def adamw(w, m, v, g):
    m = 0.9 * m + 0.1 * g
    v = 0.95 * v + 0.05 * g * g
    step = m * lax.rsqrt(v + 1e-8) + 0.1 * w
    return (w - 0.02 * step).astype(jnp.bfloat16), m, v


def far_of(d):
    return lax.rem(d + 2, 4)


def mate_of(d):
    return 3 - far_of(d)


def far_mate_of(d):
    return 3 - d


def me():
    return lax.axis_index("dp")


def in_hbm(x):
    return pltpu.with_memory_space_constraint(x, pltpu.HBM)


def solution(mesh):
    def work(*arrays):
        terms, weights, m, v = (arrays[i : i + 3] for i in (0, 3, 6, 9))
        rows = [one.shape[1] // UNITS for one in m]
        cols = [one.shape[2] for one in m]
        new_w, new_m, new_v = [None] * 3, [None] * 3, [None] * 3

        def run(body, grid, ins, in_specs, outs, out_specs, aliases):
            bytes_ = sum(o.size * o.dtype.itemsize for o in outs)
            return pl.pallas_call(
                body,
                out_shape=outs,
                grid=grid,
                in_specs=in_specs,
                out_specs=out_specs,
                input_output_aliases=aliases,
                compiler_params=pltpu.CompilerParams(vmem_limit_bytes=67043328),
                cost_estimate=pl.CostEstimate(flops=bytes_, bytes_accessed=bytes_, transcendentals=0),
            )(*ins)

        def send(x, pairs):
            return in_hbm(lax.ppermute(in_hbm(x), "dp", pairs))

        def term_spec(w, layer, u0, of):
            return pl.BlockSpec((1, 1, rows[w], cols[w]), lambda i: (0, layer, of(me()) * UNITS + u0 + i, 0))

        def full_spec(w, layer, u0, of):
            return pl.BlockSpec((1, rows[w], cols[w]), lambda i: (layer, of(me()) * UNITS + u0 + i, 0))

        def piece_spec(w):
            return pl.BlockSpec((rows[w], cols[w]), lambda i: (i, 0))

        def piece(w, n):
            return jax.ShapeDtypeStruct((n * rows[w], cols[w]), jnp.bfloat16)

        def cut(k, of):
            w, layer, u0, n = CHUNKS[k]

            def body(t, o):
                o[...] = t[0, 0]

            (one,) = run(body, (n,), [terms[w]], [term_spec(w, layer, u0, of)], [piece(w, n)], [piece_spec(w)], {})
            return send(one, MATE)

        def chip_sum(k, got):
            w, layer, u0, n = CHUNKS[k]

            def body(t, r, o):
                o[...] = (t[0, 0].astype(jnp.float32) + r[...].astype(jnp.float32)).astype(jnp.bfloat16)

            (one,) = run(
                body, (n,), [terms[w], got], [term_spec(w, layer, u0, far_of), piece_spec(w)], [piece(w, n)], [piece_spec(w)], {}
            )
            return send(one, FAR)

        def update(k, mate_term, far_sum):
            w, layer, u0, n = CHUNKS[k]

            def body(*refs):
                t, r, f, wt, mm, vv = refs[:6]
                o, full, mo, vo = refs[-4:]
                g = t[0, 0].astype(jnp.float32) + r[...].astype(jnp.float32) + f[...].astype(jnp.float32)
                g = g.astype(jnp.bfloat16).astype(jnp.float32)
                a, b, c = adamw(wt[0].astype(jnp.float32), mm[0], vv[0], g)
                o[...] = a
                full[0] = a
                mo[0] = b
                vo[0] = c

            moment = pl.BlockSpec((1, rows[w], cols[w]), lambda i: (layer, u0 + i, 0))
            mine = full_spec(w, layer, u0, lambda d: d)
            ins = [terms[w], mate_term, far_sum, weights[w], m[w], v[w]]
            specs = [term_spec(w, layer, u0, lambda d: d), piece_spec(w), piece_spec(w), mine, moment, moment]
            aliases = {}
            if new_w[w] is not None:
                ins += [new_w[w], new_m[w], new_v[w]]
                specs += [ANY] * 3
                aliases = {6: 1, 7: 2, 8: 3}
            like = lambda a: jax.ShapeDtypeStruct(a.shape, a.dtype)
            out, new_w[w], new_m[w], new_v[w] = run(
                body,
                (n,),
                ins,
                specs,
                [piece(w, n), like(weights[w]), like(m[w]), like(v[w])],
                [piece_spec(w), mine, moment, moment],
                aliases,
            )
            return send(out, FAR), send(out, MATE)

        def place(k, far, mate, far_mate):
            w, layer, u0, n = CHUNKS[k]

            def body(a, b, c, _, full):
                for j, one in enumerate((a, b, c)):

                    @pl.when(pl.program_id(1) == j)
                    def _():
                        full[0] = one[...]

            def where(i, j):
                d = me()
                owner = jnp.where(j == 0, far_of(d), jnp.where(j == 1, mate_of(d), far_mate_of(d)))
                return layer, owner * UNITS + u0 + i, 0

            spec = pl.BlockSpec((rows[w], cols[w]), lambda i, j: (i, 0))
            (new_w[w],) = run(
                body,
                (n, 3),
                [far, mate, far_mate, new_w[w]],
                [spec] * 3 + [ANY],
                [jax.ShapeDtypeStruct(weights[w].shape, jnp.bfloat16)],
                [pl.BlockSpec((1, rows[w], cols[w]), where)],
                {3: 0},
            )

        count = len(CHUNKS)
        got = [None] * (count + 1)
        far_sum, mate_term, out = [None] * count, [None] * count, [None] * count
        got[0] = cut(0, far_mate_of)
        for k in range(count):
            if k + 1 < count:
                got[k + 1] = cut(k + 1, far_mate_of)
            far_sum[k] = chip_sum(k, got[k])
        for k in range(count):
            mate_term[k] = cut(k, mate_of)
        forward = [None] * count

        for k in range(count):
            out[k] = update(k, mate_term[k], far_sum[k])
        for k in range(count):
            forward[k] = send(out[k][0], MATE)
            if k:
                place(k - 1, *out[k - 1], forward[k - 1])
        place(k, *out[k], forward[k])
        return (*new_w, *new_m, *new_v)

    all_of, cut_of = P(None, None, None), P(None, "dp", None)
    whole = jax.shard_map(
        work,
        mesh=mesh,
        in_specs=(P(("rep", "dp"), None, None, None),) * 3 + (all_of,) * 3 + (cut_of,) * 6,
        out_specs=(P("rep", None, None),) * 3 + (P("rep", "dp", None),) * 6,
        check_vma=False,
    )
    shapes = [(2, 1280, 4480), (2, 1280, 4480), (2, 4480, 1280)]
    jax.eval_shape(
        whole,
        *(jax.ShapeDtypeStruct((8, *s), jnp.bfloat16) for s in shapes),
        *(jax.ShapeDtypeStruct(s, jnp.bfloat16) for s in shapes),
        *(jax.ShapeDtypeStruct(s, jnp.float32) for s in shapes + shapes),
    )
    return whole
```

time: 961 us -> 897 us (0.933)
  Pallas kernels: 0 us -> 279 us
  waiting for transfers between devices: 833 us -> 583 us
  other arithmetic: 67.4 us -> 0 us
  local copies, waits for them, and re-layouts: 45.9 us -> 1.42 us
  starting transfers between devices: 0.24 us -> 30.2 us
  between operations: 14.2 us -> 0.76 us
    ppermute x0 -> x48, waiting for transfers between devices: none -> 583 us  [send(): return in_hbm(lax.ppermute(in_hbm(x), 'dp', pairs))]
    reduce_scatter x3 -> x0, waiting for transfers between devices: 431 us -> none  [step(): lax.psum_scatter(t[0], 'dp', scatter_dimension=1, tiled=True)]
    all_gather x3 -> x0, waiting for transfers between devices: 400 us -> none  [step(): whole = [lax.all_gather(one[0], 'dp', axis=1, tiled=True) for one in new]]
    pallas_call x0 -> x40, Pallas kernels: none -> 279 us  [run(): pl.pallas_call(body, out_shape=outs, grid=grid, in_specs=in_specs, out_sp...]
    convert_element_type x3 -> x0, other arithmetic: 67.4 us -> none  [adamw(): return ((w - 0.02 * step).astype(jnp.bfloat16), m, v)]
    unnamed x15 -> x18, local copies, waits for them, and re-layouts: 45.9 us -> 1.42 us
    ppermute x0 -> x48, starting transfers between devices: none -> 30.2 us  [send(): return in_hbm(lax.ppermute(in_hbm(x), 'dp', pairs))]
  transfers between devices with their start and end apart: 6 -> 48, of which waited for: 6 -> 15; matrix products, arithmetic and copies ran while one was open for 7% -> 0% of each run, Pallas kernels for 0% -> 31%
where the time goes in v1:
time: 897 us; the launch traced here: 894 us
  waiting for transfers between devices  583 us (65%)
  Pallas kernels  279 us (31%)
  starting transfers between devices  30.2 us (3%)
    ppermute x48, waiting for transfers between devices, send(): return in_hbm(lax.ppermute(in_hbm(x), 'dp', pairs))  583 us
    pallas_call x40, Pallas kernels, run(): pl.pallas_call(body, out_shape=outs, grid=grid, in_specs=in_specs, out_sp...  279 us
    ppermute x48, starting transfers between devices, send(): return in_hbm(lax.ppermute(in_hbm(x), 'dp', pairs))  30.2 us
  transfers between devices with their start and end apart: 48, of which 15 were waited for; matrix products, arithmetic and copies ran while one was open for 0% of the time, Pallas kernels for 31%

profile of v1, /device:TPU:0, one launch (start us, length us, event | category | flops | bytes accessed | tf_op | source)
XLA Modules:
  0.0 893.9 jit_solution(11491636146724033087)
XLA Ops:
  3.4 3.9 shard_map.190
  7.2 3.9 shard_map.191
  25.2 9.5 %collective-permute-done.8.refs_2_ = bf16[64,4480]{1,0:T(8,128)(2,1)} collective-permute-done((bf16[64,4480]{1,0:T(8,128)(2,1)}, bf16[64,4480]{1,0:T(8,128)(2,1)}, u32[]{:S(2)}, u32[]{:S(2)}) %collective-permute-start.8) | collective-permute-done | bytes 573472 | tf_op jit(solution)/shard_map/ppermute | solution.py:66
  34.7 4.9 shard_map.196
  41.6 3.9 shard_map.215
  47.0 4.8 shard_map.187
  51.9 7.3 collective-permute-done.15.a
  59.6 4.8 shard_map.188
  64.5 3.9 shard_map.216
  68.9 4.8 shard_map.202
  73.8 4.8 shard_map.203
  79.1 4.8 shard_map.219
  84.0 4.8 shard_map.205
  89.3 4.8 shard_map.206
  94.2 4.8 shard_map.218
  99.5 4.5 shard_map.192
  105.7 4.5 shard_map.217
  110.5 5.9 shard_map.220
  118.2 5.9 shard_map.189
  124.3 5.9 shard_map.204
  132.0 5.9 shard_map.207
  137.8 19.1 %collective-permute-done.5.refs_2_ = bf16[256,4480]{1,0:T(8,128)(2,1)} collective-permute-done((bf16[256,4480]{1,0:T(8,128)(2,1)}, bf16[256,4480]{1,0:T(8,128)(2,1)}, u32[]{:S(2)}, u32[]{:S(2)}) %collective-permute-start.5) | collective-permute-done | bytes 2293792 | tf_op jit(solution)/shard_map/ppermute | solution.py:66
  158.7 12.2 %shard_map.197 = (bf16[256,4480]{1,0:T(8,128)(2,1)}, bf16[2,1280,4480]{2,1,0:T(8,128)(2,1)}, f32[2,320,4480]{2,1,0:T(8,128)}, f32[2,320,4480]{2,1,0:T(8,128)}) custom-call(bf16[1,2,1280,4480]{3,2,1,0:T(8,128)(2,1)} %refs_0_.10, bf16[256,4480]{1,0:T(8,128)(2,1)} %collective-permute-done.3.refs_1_, ...), custom_call_target="tpu_custom_call", output_to_operand_aliasing={{1}: (6, {}), {2}: (7, {}), {3}: (8, {})} | custom-call | flops 48168960 | bytes 48168960 | tf_op jit(solution)/shard_map/pallas_call | solution.py:54
  170.9 35.3 %collective-permute-done.35.refs_2_ = bf16[896,1280]{1,0:T(8,128)(2,1)} collective-permute-done((bf16[896,1280]{1,0:T(8,128)(2,1)}, bf16[896,1280]{1,0:T(8,128)(2,1)}, u32[]{:S(2)}, u32[]{:S(2)}) %collective-permute-start.35) | collective-permute-done | bytes 2293792 | tf_op jit(solution)/shard_map/ppermute | solution.py:66
  207.9 59.7 %collective-permute-done.38.refs_2_ = bf16[1120,1280]{1,0:T(8,128)(2,1)} collective-permute-done((bf16[1120,1280]{1,0:T(8,128)(2,1)}, bf16[1120,1280]{1,0:T(8,128)(2,1)}, u32[]{:S(2)}, u32[]{:S(2)}) %collective-permute-start.38) | collective-permute-done | bytes 2867232 | tf_op jit(solution)/shard_map/ppermute | solution.py:66
  267.6 16.6 %shard_map.221 = (bf16[1120,1280]{1,0:T(8,128)(2,1)}, bf16[2,4480,1280]{2,1,0:T(8,128)(2,1)}, f32[2,1120,1280]{2,1,0:T(8,128)}, f32[2,1120,1280]{2,1,0:T(8,128)}) custom-call(bf16[1,2,4480,1280]{3,2,1,0:T(8,128)(2,1)} %refs_0_.15, bf16[1120,1280]{1,0:T(8,128)(2,1)} %collective-permute-done.36.refs_1_, bf16[1120,1280]{1,0:T(8,128)(2,1)} %collective-permute-done.38.refs_2_, ...), custom_call_target="tpu_custom_call" | custom-call | flops 48742400 | bytes 48742400 | tf_op jit(solution)/shard_map/pallas_call | solution.py:54
  284.2 12.1 %shard_map.222 = (bf16[896,1280]{1,0:T(8,128)(2,1)}, bf16[2,4480,1280]{2,1,0:T(8,128)(2,1)}, f32[2,1120,1280]{2,1,0:T(8,128)}, f32[2,1120,1280]{2,1,0:T(8,128)}) custom-call(bf16[1,2,4480,1280]{3,2,1,0:T(8,128)(2,1)} %refs_0_.15, bf16[896,1280]{1,0:T(8,128)(2,1)} %collective-permute-done.33.refs_1_, ...), custom_call_target="tpu_custom_call", output_to_operand_aliasing={{1}: (6, {}), {2}: (7, {}), {3}: (8, {})} | custom-call | flops 48168960 | bytes 48168960 | tf_op jit(solution)/shard_map/pallas_call | solution.py:54
  296.3 32.7 %collective-permute-done.2.refs_2_ = bf16[320,4480]{1,0:T(8,128)(2,1)} collective-permute-done((bf16[320,4480]{1,0:T(8,128)(2,1)}, bf16[320,4480]{1,0:T(8,128)(2,1)}, u32[]{:S(2)}, u32[]{:S(2)}) %collective-permute-start.2) | collective-permute-done | bytes 2867232 | tf_op jit(solution)/shard_map/ppermute | solution.py:66
  330.8 4.9 shard_map.223
  335.6 54.8 %collective-permute-done.20.refs_2_ = bf16[320,4480]{1,0:T(8,128)(2,1)} collective-permute-done((bf16[320,4480]{1,0:T(8,128)(2,1)}, bf16[320,4480]{1,0:T(8,128)(2,1)}, u32[]{:S(2)}, u32[]{:S(2)}) %collective-permute-start.20) | collective-permute-done | bytes 2867232 | tf_op jit(solution)/shard_map/ppermute | solution.py:66
  392.2 16.6 %shard_map.198 = (bf16[320,4480]{1,0:T(8,128)(2,1)}, bf16[2,1280,4480]{2,1,0:T(8,128)(2,1)}, f32[2,320,4480]{2,1,0:T(8,128)}, f32[2,320,4480]{2,1,0:T(8,128)}) custom-call(bf16[1,2,1280,4480]{3,2,1,0:T(8,128)(2,1)} %refs_0_.10, bf16[320,4480]{1,0:T(8,128)(2,1)} %collective-permute-done.refs_1_, ...), custom_call_target="tpu_custom_call", output_to_operand_aliasing={{1}: (6, {}), {2}: (7, {}), {3}: (8, {})} | custom-call | flops 48742400 | bytes 48742400 | tf_op jit(solution)/shard_map/pallas_call | solution.py:54
  408.8 43.1 %collective-permute-done.23.refs_2_ = bf16[320,4480]{1,0:T(8,128)(2,1)} collective-permute-done((bf16[320,4480]{1,0:T(8,128)(2,1)}, bf16[320,4480]{1,0:T(8,128)(2,1)}, u32[]{:S(2)}, u32[]{:S(2)}) %collective-permute-start.23) | collective-permute-done | bytes 2867232 | tf_op jit(solution)/shard_map/ppermute | solution.py:66
  453.7 108.8 %collective-permute-done.39.a = bf16[224,1280]{1,0:T(8,128)(2,1)} collective-permute-done((bf16[224,1280]{1,0:T(8,128)(2,1)}, bf16[224,1280]{1,0:T(8,128)(2,1)}, u32[]{:S(2)}, u32[]{:S(2)}) %collective-permute-start.39) | collective-permute-done | bytes 573472 | tf_op jit(solution)/shard_map/ppermute | solution.py:66
  562.5 16.5 %shard_map.208 = (bf16[320,4480]{1,0:T(8,128)(2,1)}, bf16[2,1280,4480]{2,1,0:T(8,128)(2,1)}, f32[2,320,4480]{2,1,0:T(8,128)}, f32[2,320,4480]{2,1,0:T(8,128)}) custom-call(bf16[1,2,1280,4480]{3,2,1,0:T(8,128)(2,1)} %refs_0_.12, bf16[320,4480]{1,0:T(8,128)(2,1)} %collective-permute-done.21.refs_1_, bf16[320,4480]{1,0:T(8,128)(2,1)} %collective-permute-done.23.refs_2_, ...), custom_call_target="tpu_custom_call" | custom-call | flops 48742400 | bytes 48742400 | tf_op jit(solution)/shard_map/pallas_call | solution.py:54
  579.1 16.8 %shard_map.209 = (bf16[320,4480]{1,0:T(8,128)(2,1)}, bf16[2,1280,4480]{2,1,0:T(8,128)(2,1)}, f32[2,320,4480]{2,1,0:T(8,128)}, f32[2,320,4480]{2,1,0:T(8,128)}) custom-call(bf16[1,2,1280,4480]{3,2,1,0:T(8,128)(2,1)} %refs_0_.12, bf16[320,4480]{1,0:T(8,128)(2,1)} %collective-permute-done.18.refs_1_, ...), custom_call_target="tpu_custom_call", output_to_operand_aliasing={{1}: (6, {}), {2}: (7, {}), {3}: (8, {})} | custom-call | flops 48742400 | bytes 48742400 | tf_op jit(solution)/shard_map/pallas_call | solution.py:54
  598.1 25.8 %collective-permute-done.9.a = bf16[320,4480]{1,0:T(8,128)(2,1)} collective-permute-done((bf16[320,4480]{1,0:T(8,128)(2,1)}, bf16[320,4480]{1,0:T(8,128)(2,1)}, u32[]{:S(2)}, u32[]{:S(2)}) %collective-permute-start.9) | collective-permute-done | bytes 2867232 | tf_op jit(solution)/shard_map/ppermute | solution.py:66
  625.7 59.6 %collective-permute-done.24.a = bf16[320,4480]{1,0:T(8,128)(2,1)S(1)} collective-permute-done((bf16[320,4480]{1,0:T(8,128)(2,1)}, bf16[320,4480]{1,0:T(8,128)(2,1)S(1)}, u32[]{:S(2)}, u32[]{:S(2)}) %collective-permute-start.24) | collective-permute-done | bytes 2867232 | tf_op jit(solution)/shard_map/ppermute | solution.py:66
  685.8 60.9 %collective-permute-done.27.a = bf16[320,4480]{1,0:T(8,128)(2,1)S(1)} collective-permute-done((bf16[320,4480]{1,0:T(8,128)(2,1)}, bf16[320,4480]{1,0:T(8,128)(2,1)S(1)}, u32[]{:S(2)}, u32[]{:S(2)}) %collective-permute-start.27) | collective-permute-done | bytes 2867232 | tf_op jit(solution)/shard_map/ppermute | solution.py:66
  747.3 60.1 %collective-permute-done.45.a = bf16[1120,1280]{1,0:T(8,128)(2,1)} collective-permute-done((bf16[1120,1280]{1,0:T(8,128)(2,1)}, bf16[1120,1280]{1,0:T(8,128)(2,1)}, u32[]{:S(2)}, u32[]{:S(2)}) %collective-permute-start.45) | collective-permute-done | bytes 2867232 | tf_op jit(solution)/shard_map/ppermute | solution.py:66
  808.5 4.2 collective-permute-done.29.c
  814.2 3.1 shard_map.199._
  817.3 10.6 %shard_map.200._ = bf16[2,1280,4480]{2,1,0:T(8,128)(2,1)} custom-call(bf16[256,4480]{1,0:T(8,128)(2,1)} %collective-permute-done.12.a, bf16[256,4480]{1,0:T(8,128)(2,1)} %collective-permute-done.13.b, bf16[256,4480]{1,0:T(8,128)(2,1)} %copy-done.8, bf16[2,1280,4480]{2,1,0:T(8,128)(2,1)} %shard_map.199._), custom_call_target="tpu_custom_call", output_to_operand_aliasing={{}: (3, {})} | custom-call | flops 22937600 | bytes 22937600 | tf_op jit(solution)/shard_map/pallas_call | solution.py:54
  827.9 13.0 %shard_map.201 = bf16[2,1280,4480]{2,1,0:T(8,128)(2,1)} custom-call(bf16[320,4480]{1,0:T(8,128)(2,1)} %collective-permute-done.9.a, bf16[320,4480]{1,0:T(8,128)(2,1)} %collective-permute-done.10.b, bf16[320,4480]{1,0:T(8,128)(2,1)} %copy-done.5, bf16[2,1280,4480]{2,1,0:T(8,128)(2,1)} %shard_map.200._), custom_call_target="tpu_custom_call", output_to_operand_aliasing={{}: (3, {})} | custom-call | flops 22937600 | bytes 22937600 | tf_op jit(solution)/shard_map/pallas_call | solution.py:54
  840.9 13.0 %shard_map.210._ = bf16[2,1280,4480]{2,1,0:T(8,128)(2,1)} custom-call(bf16[320,4480]{1,0:T(8,128)(2,1)} %copy-done.2, bf16[320,4480]{1,0:T(8,128)(2,1)} %copy-done.3, bf16[320,4480]{1,0:T(8,128)(2,1)} %copy-done.7, bf16[2,1280,4480]{2,1,0:T(8,128)(2,1)} %get-tuple-element.56._), custom_call_target="tpu_custom_call", output_to_operand_aliasing={{}: (3, {})} | custom-call | flops 22937600 | bytes 22937600 | tf_op jit(solution)/shard_map/pallas_call | solution.py:54
  854.0 13.0 %shard_map.211 = bf16[2,1280,4480]{2,1,0:T(8,128)(2,1)} custom-call(bf16[320,4480]{1,0:T(8,128)(2,1)} %copy-done, bf16[320,4480]{1,0:T(8,128)(2,1)} %copy-done.1, bf16[320,4480]{1,0:T(8,128)(2,1)} %copy-done.6, bf16[2,1280,4480]{2,1,0:T(8,128)(2,1)} %shard_map.210._), custom_call_target="tpu_custom_call", output_to_operand_aliasing={{}: (3, {})} | custom-call | flops 22937600 | bytes 22937600 | tf_op jit(solution)/shard_map/pallas_call | solution.py:54
  867.0 13.1 %shard_map.224._ = bf16[2,4480,1280]{2,1,0:T(8,128)(2,1)} custom-call(bf16[1120,1280]{1,0:T(8,128)(2,1)} %collective-permute-done.45.a, bf16[1120,1280]{1,0:T(8,128)(2,1)} %copy-done.4, bf16[1120,1280]{1,0:T(8,128)(2,1)} %collective-permute-done.47.c, bf16[2,4480,1280]{2,1,0:T(8,128)(2,1)} %get-tuple-element.66._), custom_call_target="tpu_custom_call", output_to_operand_aliasing={{}: (3, {})} | custom-call | flops 22937600 | bytes 22937600 | tf_op jit(solution)/shard_map/pallas_call | solution.py:54
  880.1 10.6 %shard_map.225._ = bf16[2,4480,1280]{2,1,0:T(8,128)(2,1)} custom-call(bf16[896,1280]{1,0:T(8,128)(2,1)} %collective-permute-done.42.a, bf16[896,1280]{1,0:T(8,128)(2,1)} %collective-permute-done.43.b, bf16[896,1280]{1,0:T(8,128)(2,1)} %collective-permute-done.44.c, bf16[2,4480,1280]{2,1,0:T(8,128)(2,1)} %shard_map.224._), custom_call_target="tpu_custom_call", output_to_operand_aliasing={{}: (3, {})} | custom-call | flops 22937600 | bytes 22937600 | tf_op jit(solution)/shard_map/pallas_call | solution.py:54
  890.7 3.2 shard_map.226
  (106 shorter events, 45.3 us)
Async XLA Ops:
  2.6 13.4 %collective-permute-start.7 = (bf16[64,4480]{1,0:T(8,128)(2,1)}, bf16[64,4480]{1,0:T(8,128)(2,1)}, u32[]{:S(2)}, u32[]{:S(2)}) collective-permute-start(bf16[64,4480]{1,0:T(8,128)(2,1)} %shard_map.194), channel_id=1, source_target_pairs={{0,1},{1,0},{2,3},{3,2},{4,5},{5,4},{6,7},{7,6}} | collective-permute-start | bytes 1720328 | tf_op jit(solution)/shard_map/ppermute | solution.py:66
  7.2 57.2 %collective-permute-start.3 = (bf16[256,4480]{1,0:T(8,128)(2,1)}, bf16[256,4480]{1,0:T(8,128)(2,1)}, u32[]{:S(2)}, u32[]{:S(2)}) collective-permute-start(bf16[256,4480]{1,0:T(8,128)(2,1)} %shard_map.190), channel_id=1, source_target_pairs={{0,1},{1,0},{2,3},{3,2},{4,5},{5,4},{6,7},{7,6}} | collective-permute-start | bytes 6881288 | tf_op jit(solution)/shard_map/ppermute | solution.py:66
  11.1 57.3 %collective-permute-start.4 = (bf16[256,4480]{1,0:T(8,128)(2,1)}, bf16[256,4480]{1,0:T(8,128)(2,1)}, u32[]{:S(2)}, u32[]{:S(2)}) collective-permute-start(bf16[256,4480]{1,0:T(8,128)(2,1)} %shard_map.191), channel_id=1, source_target_pairs={{0,1},{1,0},{2,3},{3,2},{4,5},{5,4},{6,7},{7,6}} | collective-permute-start | bytes 6881288 | tf_op jit(solution)/shard_map/ppermute | solution.py:66
  13.5 9.0 %collective-permute-start.31 = (bf16[224,1280]{1,0:T(8,128)(2,1)}, bf16[224,1280]{1,0:T(8,128)(2,1)}, u32[]{:S(2)}, u32[]{:S(2)}) collective-permute-start(bf16[224,1280]{1,0:T(8,128)(2,1)} %shard_map.213), channel_id=1, source_target_pairs={{0,1},{1,0},{2,3},{3,2},{4,5},{5,4},{6,7},{7,6}} | collective-permute-start | bytes 1720328 | tf_op jit(solution)/shard_map/ppermute | solution.py:66
  15.4 9.5 %collective-permute-start.6 = (bf16[64,4480]{1,0:T(8,128)(2,1)}, bf16[64,4480]{1,0:T(8,128)(2,1)}, u32[]{:S(2)}, u32[]{:S(2)}) collective-permute-start(bf16[64,4480]{1,0:T(8,128)(2,1)} %shard_map.193), channel_id=1, source_target_pairs={{0,1},{1,0},{2,3},{3,2},{4,5},{5,4},{6,7},{7,6}} | collective-permute-start | bytes 1720328 | tf_op jit(solution)/shard_map/ppermute | solution.py:66
  18.1 16.6 %collective-permute-start.8 = (bf16[64,4480]{1,0:T(8,128)(2,1)}, bf16[64,4480]{1,0:T(8,128)(2,1)}, u32[]{:S(2)}, u32[]{:S(2)}) collective-permute-start(bf16[64,4480]{1,0:T(8,128)(2,1)} %shard_map.195), channel_id=1, source_target_pairs={{0,2},{2,0},{1,3},{3,1},{4,6},{6,4},{5,7},{7,5}} | collective-permute-start | bytes 1720328 | tf_op jit(solution)/shard_map/ppermute | solution.py:66
  22.5 23.0 %collective-permute-start.30 = (bf16[224,1280]{1,0:T(8,128)(2,1)}, bf16[224,1280]{1,0:T(8,128)(2,1)}, u32[]{:S(2)}, u32[]{:S(2)}) collective-permute-start(bf16[224,1280]{1,0:T(8,128)(2,1)} %shard_map.212), channel_id=1, source_target_pairs={{0,1},{1,0},{2,3},{3,2},{4,5},{5,4},{6,7},{7,6}} | collective-permute-start | bytes 1720328 | tf_op jit(solution)/shard_map/ppermute | solution.py:66
  24.9 22.1 %collective-permute-start.32 = (bf16[224,1280]{1,0:T(8,128)(2,1)}, bf16[224,1280]{1,0:T(8,128)(2,1)}, u32[]{:S(2)}, u32[]{:S(2)}) collective-permute-start(bf16[224,1280]{1,0:T(8,128)(2,1)} %shard_map.214), channel_id=1, source_target_pairs={{0,2},{2,0},{1,3},{3,1},{4,6},{6,4},{5,7},{7,5}} | collective-permute-start | bytes 1720328 | tf_op jit(solution)/shard_map/ppermute | solution.py:66
  39.6 19.5 %collective-permute-start.15 = (bf16[64,4480]{1,0:T(8,128)(2,1)}, bf16[64,4480]{1,0:T(8,128)(2,1)}, u32[]{:S(2)}, u32[]{:S(2)}) collective-permute-start(bf16[64,4480]{1,0:T(8,128)(2,1)} %get-tuple-element.49), channel_id=1, source_target_pairs={{0,2},{2,0},{1,3},{3,1},{4,6},{6,4},{5,7},{7,5}} | collective-permute-start | bytes 1720328 | tf_op jit(solution)/shard_map/ppermute | solution.py:66
  45.5 33.1 %collective-permute-start.33 = (bf16[896,1280]{1,0:T(8,128)(2,1)}, bf16[896,1280]{1,0:T(8,128)(2,1)}, u32[]{:S(2)}, u32[]{:S(2)}) collective-permute-start(bf16[896,1280]{1,0:T(8,128)(2,1)} %shard_map.215), channel_id=1, source_target_pairs={{0,1},{1,0},{2,3},{3,2},{4,5},{5,4},{6,7},{7,6}} | collective-permute-start | bytes 6881288 | tf_op jit(solution)/shard_map/ppermute | solution.py:66
  47.0 12.1 %collective-permute-start.16 = (bf16[64,4480]{1,0:T(8,128)(2,1)}, bf16[64,4480]{1,0:T(8,128)(2,1)}, u32[]{:S(2)}, u32[]{:S(2)}) collective-permute-start(bf16[64,4480]{1,0:T(8,128)(2,1)} %get-tuple-element.49), channel_id=1, source_target_pairs={{0,1},{1,0},{2,3},{3,2},{4,5},{5,4},{6,7},{7,6}} | collective-permute-start | bytes 1720328 | tf_op jit(solution)/shard_map/ppermute | solution.py:66
  59.1 29.7 %collective-permute-start = (bf16[320,4480]{1,0:T(8,128)(2,1)}, bf16[320,4480]{1,0:T(8,128)(2,1)}, u32[]{:S(2)}, u32[]{:S(2)}) collective-permute-start(bf16[320,4480]{1,0:T(8,128)(2,1)} %shard_map.187), channel_id=1, source_target_pairs={{0,1},{1,0},{2,3},{3,2},{4,5},{5,4},{6,7},{7,6}} | collective-permute-start | bytes 8601608 | tf_op jit(solution)/shard_map/ppermute | solution.py:66
  59.1 14.6 %collective-permute-start.17 = (bf16[64,4480]{1,0:T(8,128)(2,1)}, bf16[64,4480]{1,0:T(8,128)(2,1)}, u32[]{:S(2)}, u32[]{:S(2)}) collective-permute-start(bf16[64,4480]{1,0:T(8,128)(2,1)} %collective-permute-done.15.a), channel_id=1, source_target_pairs={{0,1},{1,0},{2,3},{3,2},{4,5},{5,4},{6,7},{7,6}} | collective-permute-start | bytes 1720328 | tf_op jit(solution)/shard_map/ppermute | solution.py:66
  64.5 29.6 %collective-permute-start.1 = (bf16[320,4480]{1,0:T(8,128)(2,1)}, bf16[320,4480]{1,0:T(8,128)(2,1)}, u32[]{:S(2)}, u32[]{:S(2)}) collective-permute-start(bf16[320,4480]{1,0:T(8,128)(2,1)} %shard_map.188), channel_id=1, source_target_pairs={{0,1},{1,0},{2,3},{3,2},{4,5},{5,4},{6,7},{7,6}} | collective-permute-start | bytes 8601608 | tf_op jit(solution)/shard_map/ppermute | solution.py:66
  68.4 15.5 %collective-permute-start.34 = (bf16[896,1280]{1,0:T(8,128)(2,1)}, bf16[896,1280]{1,0:T(8,128)(2,1)}, u32[]{:S(2)}, u32[]{:S(2)}) collective-permute-start(bf16[896,1280]{1,0:T(8,128)(2,1)} %shard_map.216), channel_id=1, source_target_pairs={{0,1},{1,0},{2,3},{3,2},{4,5},{5,4},{6,7},{7,6}} | collective-permute-start | bytes 6881288 | tf_op jit(solution)/shard_map/ppermute | solution.py:66
  73.8 25.2 %collective-permute-start.18 = (bf16[320,4480]{1,0:T(8,128)(2,1)}, bf16[320,4480]{1,0:T(8,128)(2,1)}, u32[]{:S(2)}, u32[]{:S(2)}) collective-permute-start(bf16[320,4480]{1,0:T(8,128)(2,1)} %shard_map.202), channel_id=1, source_target_pairs={{0,1},{1,0},{2,3},{3,2},{4,5},{5,4},{6,7},{7,6}} | collective-permute-start | bytes 8601608 | tf_op jit(solution)/shard_map/ppermute | solution.py:66
  78.6 25.3 %collective-permute-start.19 = (bf16[320,4480]{1,0:T(8,128)(2,1)}, bf16[320,4480]{1,0:T(8,128)(2,1)}, u32[]{:S(2)}, u32[]{:S(2)}) collective-permute-start(bf16[320,4480]{1,0:T(8,128)(2,1)} %shard_map.203), channel_id=1, source_target_pairs={{0,1},{1,0},{2,3},{3,2},{4,5},{5,4},{6,7},{7,6}} | collective-permute-start | bytes 8601608 | tf_op jit(solution)/shard_map/ppermute | solution.py:66
  83.9 26.3 %collective-permute-start.37 = (bf16[1120,1280]{1,0:T(8,128)(2,1)}, bf16[1120,1280]{1,0:T(8,128)(2,1)}, u32[]{:S(2)}, u32[]{:S(2)}) collective-permute-start(bf16[1120,1280]{1,0:T(8,128)(2,1)} %shard_map.219), channel_id=1, source_target_pairs={{0,1},{1,0},{2,3},{3,2},{4,5},{5,4},{6,7},{7,6}} | collective-permute-start | bytes 8601608 | tf_op jit(solution)/shard_map/ppermute | solution.py:66
  88.8 27.6 %collective-permute-start.21 = (bf16[320,4480]{1,0:T(8,128)(2,1)}, bf16[320,4480]{1,0:T(8,128)(2,1)}, u32[]{:S(2)}, u32[]{:S(2)}) collective-permute-start(bf16[320,4480]{1,0:T(8,128)(2,1)} %shard_map.205), channel_id=1, source_target_pairs={{0,1},{1,0},{2,3},{3,2},{4,5},{5,4},{6,7},{7,6}} | collective-permute-start | bytes 8601608 | tf_op jit(solution)/shard_map/ppermute | solution.py:66
  94.1 29.9 %collective-permute-start.22 = (bf16[320,4480]{1,0:T(8,128)(2,1)}, bf16[320,4480]{1,0:T(8,128)(2,1)}, u32[]{:S(2)}, u32[]{:S(2)}) collective-permute-start(bf16[320,4480]{1,0:T(8,128)(2,1)} %shard_map.206), channel_id=1, source_target_pairs={{0,1},{1,0},{2,3},{3,2},{4,5},{5,4},{6,7},{7,6}} | collective-permute-start | bytes 8601608 | tf_op jit(solution)/shard_map/ppermute | solution.py:66
  99.0 31.2 %collective-permute-start.36 = (bf16[1120,1280]{1,0:T(8,128)(2,1)}, bf16[1120,1280]{1,0:T(8,128)(2,1)}, u32[]{:S(2)}, u32[]{:S(2)}) collective-permute-start(bf16[1120,1280]{1,0:T(8,128)(2,1)} %shard_map.218), channel_id=1, source_target_pairs={{0,1},{1,0},{2,3},{3,2},{4,5},{5,4},{6,7},{7,6}} | collective-permute-start | bytes 8601608 | tf_op jit(solution)/shard_map/ppermute | solution.py:66
  103.9 53.0 %collective-permute-start.5 = (bf16[256,4480]{1,0:T(8,128)(2,1)}, bf16[256,4480]{1,0:T(8,128)(2,1)}, u32[]{:S(2)}, u32[]{:S(2)}) collective-permute-start(bf16[256,4480]{1,0:T(8,128)(2,1)} %shard_map.192), channel_id=1, source_target_pairs={{0,2},{2,0},{1,3},{3,1},{4,6},{6,4},{5,7},{7,5}} | collective-permute-start | bytes 6881288 | tf_op jit(solution)/shard_map/ppermute | solution.py:66
  110.2 95.9 %collective-permute-start.35 = (bf16[896,1280]{1,0:T(8,128)(2,1)}, bf16[896,1280]{1,0:T(8,128)(2,1)}, u32[]{:S(2)}, u32[]{:S(2)}) collective-permute-start(bf16[896,1280]{1,0:T(8,128)(2,1)} %shard_map.217), channel_id=1, source_target_pairs={{0,2},{2,0},{1,3},{3,1},{4,6},{6,4},{5,7},{7,5}} | collective-permute-start | bytes 6881288 | tf_op jit(solution)/shard_map/ppermute | solution.py:66
  116.4 151.2 %collective-permute-start.38 = (bf16[1120,1280]{1,0:T(8,128)(2,1)}, bf16[1120,1280]{1,0:T(8,128)(2,1)}, u32[]{:S(2)}, u32[]{:S(2)}) collective-permute-start(bf16[1120,1280]{1,0:T(8,128)(2,1)} %shard_map.220), channel_id=1, source_target_pairs={{0,2},{2,0},{1,3},{3,1},{4,6},{6,4},{5,7},{7,5}} | collective-permute-start | bytes 8601608 | tf_op jit(solution)/shard_map/ppermute | solution.py:66
  124.0 205.0 %collective-permute-start.2 = (bf16[320,4480]{1,0:T(8,128)(2,1)}, bf16[320,4480]{1,0:T(8,128)(2,1)}, u32[]{:S(2)}, u32[]{:S(2)}) collective-permute-start(bf16[320,4480]{1,0:T(8,128)(2,1)} %shard_map.189), channel_id=1, source_target_pairs={{0,2},{2,0},{1,3},{3,1},{4,6},{6,4},{5,7},{7,5}} | collective-permute-start | bytes 8601608 | tf_op jit(solution)/shard_map/ppermute | solution.py:66
  130.2 260.3 %collective-permute-start.20 = (bf16[320,4480]{1,0:T(8,128)(2,1)}, bf16[320,4480]{1,0:T(8,128)(2,1)}, u32[]{:S(2)}, u32[]{:S(2)}) collective-permute-start(bf16[320,4480]{1,0:T(8,128)(2,1)} %shard_map.204), channel_id=1, source_target_pairs={{0,2},{2,0},{1,3},{3,1},{4,6},{6,4},{5,7},{7,5}} | collective-permute-start | bytes 8601608 | tf_op jit(solution)/shard_map/ppermute | solution.py:66
  157.0 294.9 %collective-permute-start.23 = (bf16[320,4480]{1,0:T(8,128)(2,1)}, bf16[320,4480]{1,0:T(8,128)(2,1)}, u32[]{:S(2)}, u32[]{:S(2)}) collective-permute-start(bf16[320,4480]{1,0:T(8,128)(2,1)} %shard_map.207), channel_id=1, source_target_pairs={{0,2},{2,0},{1,3},{3,1},{4,6},{6,4},{5,7},{7,5}} | collective-permute-start | bytes 8601608 | tf_op jit(solution)/shard_map/ppermute | solution.py:66
  206.1 389.7 %collective-permute-start.12 = (bf16[256,4480]{1,0:T(8,128)(2,1)}, bf16[256,4480]{1,0:T(8,128)(2,1)}, u32[]{:S(2)}, u32[]{:S(2)}) collective-permute-start(bf16[256,4480]{1,0:T(8,128)(2,1)} %get-tuple-element.48), channel_id=1, source_target_pairs={{0,2},{2,0},{1,3},{3,1},{4,6},{6,4},{5,7},{7,5}} | collective-permute-start | bytes 6881288 | tf_op jit(solution)/shard_map/ppermute | solution.py:66
  267.6 330.0 %collective-permute-start.13 = (bf16[256,4480]{1,0:T(8,128)(2,1)}, bf16[256,4480]{1,0:T(8,128)(2,1)}, u32[]{:S(2)}, u32[]{:S(2)}) collective-permute-start(bf16[256,4480]{1,0:T(8,128)(2,1)} %get-tuple-element.48), channel_id=1, source_target_pairs={{0,1},{1,0},{2,3},{3,2},{4,5},{5,4},{6,7},{7,6}} | collective-permute-start | bytes 6881288 | tf_op jit(solution)/shard_map/ppermute | solution.py:66
  329.0 268.8 %collective-permute-start.42 = (bf16[896,1280]{1,0:T(8,128)(2,1)}, bf16[896,1280]{1,0:T(8,128)(2,1)}, u32[]{:S(2)}, u32[]{:S(2)}) collective-permute-start(bf16[896,1280]{1,0:T(8,128)(2,1)} %get-tuple-element.64), channel_id=1, source_target_pairs={{0,2},{2,0},{1,3},{3,1},{4,6},{6,4},{5,7},{7,5}} | collective-permute-start | bytes 6881288 | tf_op jit(solution)/shard_map/ppermute | solution.py:66
  390.5 172.0 %collective-permute-start.39 = (bf16[224,1280]{1,0:T(8,128)(2,1)}, bf16[224,1280]{1,0:T(8,128)(2,1)}, u32[]{:S(2)}, u32[]{:S(2)}) collective-permute-start(bf16[224,1280]{1,0:T(8,128)(2,1)} %get-tuple-element.63), channel_id=1, source_target_pairs={{0,2},{2,0},{1,3},{3,1},{4,6},{6,4},{5,7},{7,5}} | collective-permute-start | bytes 1720328 | tf_op jit(solution)/shard_map/ppermute | solution.py:66
  451.9 172.0 %collective-permute-start.9 = (bf16[320,4480]{1,0:T(8,128)(2,1)}, bf16[320,4480]{1,0:T(8,128)(2,1)}, u32[]{:S(2)}, u32[]{:S(2)}) collective-permute-start(bf16[320,4480]{1,0:T(8,128)(2,1)} %get-tuple-element.47), channel_id=1, source_target_pairs={{0,2},{2,0},{1,3},{3,1},{4,6},{6,4},{5,7},{7,5}} | collective-permute-start | bytes 8601608 | tf_op jit(solution)/shard_map/ppermute | solution.py:66
  562.5 61.4 %collective-permute-start.10 = (bf16[320,4480]{1,0:T(8,128)(2,1)}, bf16[320,4480]{1,0:T(8,128)(2,1)}, u32[]{:S(2)}, u32[]{:S(2)}) collective-permute-start(bf16[320,4480]{1,0:T(8,128)(2,1)} %get-tuple-element.47), channel_id=1, source_target_pairs={{0,1},{1,0},{2,3},{3,2},{4,5},{5,4},{6,7},{7,6}} | collective-permute-start | bytes 8601608 | tf_op jit(solution)/shard_map/ppermute | solution.py:66
  595.8 89.4 %collective-permute-start.24 = (bf16[320,4480]{1,0:T(8,128)(2,1)}, bf16[320,4480]{1,0:T(8,128)(2,1)S(1)}, u32[]{:S(2)}, u32[]{:S(2)}) collective-permute-start(bf16[320,4480]{1,0:T(8,128)(2,1)} %get-tuple-element.54), channel_id=1, source_target_pairs={{0,2},{2,0},{1,3},{3,1},{4,6},{6,4},{5,7},{7,5}} | collective-permute-start | bytes 8601608 | tf_op jit(solution)/shard_map/ppermute | solution.py:66
  597.6 87.7 %collective-permute-start.25 = (bf16[320,4480]{1,0:T(8,128)(2,1)}, bf16[320,4480]{1,0:T(8,128)(2,1)S(1)}, u32[]{:S(2)}, u32[]{:S(2)}) collective-permute-start(bf16[320,4480]{1,0:T(8,128)(2,1)} %get-tuple-element.54), channel_id=1, source_target_pairs={{0,1},{1,0},{2,3},{3,2},{4,5},{5,4},{6,7},{7,6}} | collective-permute-start | bytes 8601608 | tf_op jit(solution)/shard_map/ppermute | solution.py:66
  597.8 148.9 %collective-permute-start.27 = (bf16[320,4480]{1,0:T(8,128)(2,1)}, bf16[320,4480]{1,0:T(8,128)(2,1)S(1)}, u32[]{:S(2)}, u32[]{:S(2)}) collective-permute-start(bf16[320,4480]{1,0:T(8,128)(2,1)} %get-tuple-element.55), channel_id=1, source_target_pairs={{0,2},{2,0},{1,3},{3,1},{4,6},{6,4},{5,7},{7,5}} | collective-permute-start | bytes 8601608 | tf_op jit(solution)/shard_map/ppermute | solution.py:66
  623.9 122.8 %collective-permute-start.28 = (bf16[320,4480]{1,0:T(8,128)(2,1)}, bf16[320,4480]{1,0:T(8,128)(2,1)S(1)}, u32[]{:S(2)}, u32[]{:S(2)}) collective-permute-start(bf16[320,4480]{1,0:T(8,128)(2,1)} %get-tuple-element.55), channel_id=1, source_target_pairs={{0,1},{1,0},{2,3},{3,2},{4,5},{5,4},{6,7},{7,6}} | collective-permute-start | bytes 8601608 | tf_op jit(solution)/shard_map/ppermute | solution.py:66
  624.0 183.4 %collective-permute-start.45 = (bf16[1120,1280]{1,0:T(8,128)(2,1)}, bf16[1120,1280]{1,0:T(8,128)(2,1)}, u32[]{:S(2)}, u32[]{:S(2)}) collective-permute-start(bf16[1120,1280]{1,0:T(8,128)(2,1)} %get-tuple-element.65), channel_id=1, source_target_pairs={{0,2},{2,0},{1,3},{3,1},{4,6},{6,4},{5,7},{7,5}} | collective-permute-start | bytes 8601608 | tf_op jit(solution)/shard_map/ppermute | solution.py:66
  685.3 122.1 %collective-permute-start.46 = (bf16[1120,1280]{1,0:T(8,128)(2,1)}, bf16[1120,1280]{1,0:T(8,128)(2,1)S(1)}, u32[]{:S(2)}, u32[]{:S(2)}) collective-permute-start(bf16[1120,1280]{1,0:T(8,128)(2,1)} %get-tuple-element.65), channel_id=1, source_target_pairs={{0,1},{1,0},{2,3},{3,2},{4,5},{5,4},{6,7},{7,6}} | collective-permute-start | bytes 8601608 | tf_op jit(solution)/shard_map/ppermute | solution.py:66
  685.3 122.6 %collective-permute-start.11 = (bf16[320,4480]{1,0:T(8,128)(2,1)}, bf16[320,4480]{1,0:T(8,128)(2,1)S(1)}, u32[]{:S(2)}, u32[]{:S(2)}) collective-permute-start(bf16[320,4480]{1,0:T(8,128)(2,1)} %collective-permute-done.9.a), channel_id=1, source_target_pairs={{0,1},{1,0},{2,3},{3,2},{4,5},{5,4},{6,7},{7,6}} | collective-permute-start | bytes 8601608 | tf_op jit(solution)/shard_map/ppermute | solution.py:66
  746.7 61.1 %collective-permute-start.14 = (bf16[256,4480]{1,0:T(8,128)(2,1)}, bf16[256,4480]{1,0:T(8,128)(2,1)S(1)}, u32[]{:S(2)}, u32[]{:S(2)}) collective-permute-start(bf16[256,4480]{1,0:T(8,128)(2,1)} %collective-permute-done.12.a), channel_id=1, source_target_pairs={{0,1},{1,0},{2,3},{3,2},{4,5},{5,4},{6,7},{7,6}} | collective-permute-start | bytes 6881288 | tf_op jit(solution)/shard_map/ppermute | solution.py:66
  746.8 61.6 %collective-permute-start.26 = (bf16[320,4480]{1,0:T(8,128)(2,1)S(1)}, bf16[320,4480]{1,0:T(8,128)(2,1)S(1)}, u32[]{:S(2)}, u32[]{:S(2)}) collective-permute-start(bf16[320,4480]{1,0:T(8,128)(2,1)S(1)} %collective-permute-done.24.a), channel_id=1, source_target_pairs={{0,1},{1,0},{2,3},{3,2},{4,5},{5,4},{6,7},{7,6}} | collective-permute-start | bytes 8601608 | tf_op jit(solution)/shard_map/ppermute | solution.py:66
  807.4 5.3 collective-permute-start.29
  807.4 59.7 %collective-permute-start.47 = (bf16[1120,1280]{1,0:T(8,128)(2,1)}, bf16[1120,1280]{1,0:T(8,128)(2,1)}, u32[]{:S(2)}, u32[]{:S(2)}) collective-permute-start(bf16[1120,1280]{1,0:T(8,128)(2,1)} %collective-permute-done.45.a), channel_id=1, source_target_pairs={{0,1},{1,0},{2,3},{3,2},{4,5},{5,4},{6,7},{7,6}} | collective-permute-start | bytes 8601608 | tf_op jit(solution)/shard_map/ppermute | solution.py:66
  807.9 72.2 %collective-permute-start.43 = (bf16[896,1280]{1,0:T(8,128)(2,1)}, bf16[896,1280]{1,0:T(8,128)(2,1)}, u32[]{:S(2)}, u32[]{:S(2)}) collective-permute-start(bf16[896,1280]{1,0:T(8,128)(2,1)} %get-tuple-element.64), channel_id=1, source_target_pairs={{0,1},{1,0},{2,3},{3,2},{4,5},{5,4},{6,7},{7,6}} | collective-permute-start | bytes 6881288 | tf_op jit(solution)/shard_map/ppermute | solution.py:66
  807.9 72.2 %collective-permute-start.44 = (bf16[896,1280]{1,0:T(8,128)(2,1)}, bf16[896,1280]{1,0:T(8,128)(2,1)}, u32[]{:S(2)}, u32[]{:S(2)}) collective-permute-start(bf16[896,1280]{1,0:T(8,128)(2,1)} %collective-permute-done.42.a), channel_id=1, source_target_pairs={{0,1},{1,0},{2,3},{3,2},{4,5},{5,4},{6,7},{7,6}} | collective-permute-start | bytes 6881288 | tf_op jit(solution)/shard_map/ppermute | solution.py:66
  808.4 82.3 %collective-permute-start.40 = (bf16[224,1280]{1,0:T(8,128)(2,1)}, bf16[224,1280]{1,0:T(8,128)(2,1)}, u32[]{:S(2)}, u32[]{:S(2)}) collective-permute-start(bf16[224,1280]{1,0:T(8,128)(2,1)} %get-tuple-element.63), channel_id=1, source_target_pairs={{0,1},{1,0},{2,3},{3,2},{4,5},{5,4},{6,7},{7,6}} | collective-permute-start | bytes 1720328 | tf_op jit(solution)/shard_map/ppermute | solution.py:66
  812.6 78.1 %collective-permute-start.41 = (bf16[224,1280]{1,0:T(8,128)(2,1)}, bf16[224,1280]{1,0:T(8,128)(2,1)}, u32[]{:S(2)}, u32[]{:S(2)}) collective-permute-start(bf16[224,1280]{1,0:T(8,128)(2,1)} %collective-permute-done.39.a), channel_id=1, source_target_pairs={{0,1},{1,0},{2,3},{3,2},{4,5},{5,4},{6,7},{7,6}} | collective-permute-start | bytes 1720328 | tf_op jit(solution)/shard_map/ppermute | solution.py:66
  (9 other events, 333.2 us)

commit v2 on v1

v2 whole, which is shorter than its diff:
```python
import jax
import jax.numpy as jnp
from jax import lax
from jax.experimental import pallas as pl
from jax.experimental.pallas import tpu as pltpu
from jax.sharding import PartitionSpec as P


FAR = [(0, 2), (2, 0), (1, 3), (3, 1)]
MATE = [(0, 1), (1, 0), (2, 3), (3, 2)]
UNITS = 10

CHUNKS = [
    (0, 0, 0, 1, 1),
    (0, 0, 1, 2, 1),
    (0, 0, 3, 3, 1),
    (0, 0, 6, 4, 2),
    (0, 1, 0, 10, 2),
    (1, 0, 0, 10, 2),
    (1, 1, 0, 10, 2),
    (2, 0, 0, 10, 2),
    (2, 1, 0, 6, 2),
    (2, 1, 6, 3, 1),
    (2, 1, 9, 1, 1),
]

ANY = pl.BlockSpec(memory_space=pl.ANY)


def adamw(w, m, v, g):
    m = 0.9 * m + 0.1 * g
    v = 0.95 * v + 0.05 * g * g
    step = m * lax.rsqrt(v + 1e-8) + 0.1 * w
    return (w - 0.02 * step).astype(jnp.bfloat16), m, v


def far_of(d):
    return lax.rem(d + 2, 4)


def mate_of(d):
    return 3 - far_of(d)


def far_mate_of(d):
    return 3 - d


def me():
    return lax.axis_index("dp")


def in_hbm(x):
    return pltpu.with_memory_space_constraint(x, pltpu.HBM)


def solution(mesh):
    def work(*arrays):
        terms, weights, m, v = (arrays[i : i + 3] for i in (0, 3, 6, 9))
        rows = [one.shape[1] // UNITS for one in m]
        cols = [one.shape[2] for one in m]
        new_w, new_m, new_v = [None] * 3, [None] * 3, [None] * 3

        def run(body, grid, ins, in_specs, outs, out_specs, aliases, scratch=()):
            bytes_ = sum(o.size * o.dtype.itemsize for o in outs)
            return pl.pallas_call(
                body,
                out_shape=outs,
                grid=grid,
                in_specs=in_specs,
                out_specs=out_specs,
                input_output_aliases=aliases,
                scratch_shapes=scratch,
                compiler_params=pltpu.CompilerParams(vmem_limit_bytes=67043328),
                cost_estimate=pl.CostEstimate(flops=bytes_, bytes_accessed=bytes_, transcendentals=0),
            )(*ins)

        def move(copies, held, in_sem, out_sem):
            into = [pltpu.make_async_copy(a, held.at[j], in_sem.at[j]) for j, (a, _) in enumerate(copies)]
            out = [pltpu.make_async_copy(held.at[j], b, out_sem.at[j]) for j, (_, b) in enumerate(copies)]
            for one in into:
                one.start()
            for one, then in zip(into, out):
                one.wait()
                then.start()
            for one in out:
                one.wait()

        def move_scratch(w, n):
            return [pltpu.VMEM((n, rows[w], cols[w]), jnp.bfloat16), pltpu.SemaphoreType.DMA((n,)), pltpu.SemaphoreType.DMA((n,))]

        def at(w, unit):
            return pl.ds(pl.multiple_of(unit * rows[w], rows[w]), rows[w])

        def send(x, pairs):
            return in_hbm(lax.ppermute(in_hbm(x), "dp", pairs))

        def term_spec(w, layer, u0, b, of):
            return pl.BlockSpec((1, 1, b * rows[w], cols[w]), lambda i: (0, layer, of(me()) * (UNITS // b) + u0 // b + i, 0))

        def full_spec(w, layer, u0, b, of):
            return pl.BlockSpec((1, b * rows[w], cols[w]), lambda i: (layer, of(me()) * (UNITS // b) + u0 // b + i, 0))

        def piece_spec(w, b):
            return pl.BlockSpec((b * rows[w], cols[w]), lambda i: (i, 0))

        def piece(w, n):
            return jax.ShapeDtypeStruct((n * rows[w], cols[w]), jnp.bfloat16)

        def cut(k, of):
            w, layer, u0, n, _ = CHUNKS[k]

            def body(t, o, *scratch):
                first = of(me()) * UNITS + u0
                move([(t.at[0, layer, at(w, first + i)], o.at[at(w, i)]) for i in range(n)], *scratch)

            (one,) = run(body, (), [terms[w]], [ANY], [piece(w, n)], [ANY], {}, move_scratch(w, n))
            return send(one, MATE)

        def chip_sum(k, got):
            w, layer, u0, n, b = CHUNKS[k]

            def body(t, r, o):
                o[...] = (t[0, 0].astype(jnp.float32) + r[...].astype(jnp.float32)).astype(jnp.bfloat16)

            (one,) = run(
                body, (n // b,), [terms[w], got], [term_spec(w, layer, u0, b, far_of), piece_spec(w, b)], [piece(w, n)], [piece_spec(w, b)], {}
            )
            return send(one, FAR)

        def update(k, mate_term, far_sum):
            w, layer, u0, n, b = CHUNKS[k]

            def body(*refs):
                t, r, f, wt, mm, vv = refs[:6]
                o, full, mo, vo = refs[-4:]
                g = t[0, 0].astype(jnp.float32) + r[...].astype(jnp.float32) + f[...].astype(jnp.float32)
                g = g.astype(jnp.bfloat16).astype(jnp.float32)
                new, mo[0], vo[0] = adamw(wt[0].astype(jnp.float32), mm[0], vv[0], g)
                o[...] = new
                full[0] = new

            moment = pl.BlockSpec((1, b * rows[w], cols[w]), lambda i: (layer, u0 // b + i, 0))
            mine = full_spec(w, layer, u0, b, lambda d: d)
            ins = [terms[w], mate_term, far_sum, weights[w], m[w], v[w]]
            specs = [term_spec(w, layer, u0, b, lambda d: d), piece_spec(w, b), piece_spec(w, b), mine, moment, moment]
            aliases = {}
            if new_w[w] is not None:
                ins += [new_w[w], new_m[w], new_v[w]]
                specs += [ANY] * 3
                aliases = {6: 1, 7: 2, 8: 3}
            like = lambda a: jax.ShapeDtypeStruct(a.shape, a.dtype)
            out, new_w[w], new_m[w], new_v[w] = run(
                body,
                (n // b,),
                ins,
                specs,
                [piece(w, n), like(weights[w]), like(m[w]), like(v[w])],
                [piece_spec(w, b), mine, moment, moment],
                aliases,
            )
            return send(out, FAR), send(out, MATE)

        def place(k, far, mate, far_mate):
            w, layer, u0, n, _ = CHUNKS[k]

            def body(a, b, c, _, full, *scratch):
                d = me()
                owners = ((a, far_of(d)), (b, mate_of(d)), (c, far_mate_of(d)))
                move(
                    [(one.at[at(w, i)], full.at[layer, at(w, of * UNITS + u0 + i)]) for i in range(n) for one, of in owners],
                    *scratch,
                )

            (new_w[w],) = run(
                body,
                (),
                [far, mate, far_mate, new_w[w]],
                [ANY] * 4,
                [jax.ShapeDtypeStruct(weights[w].shape, jnp.bfloat16)],
                [ANY],
                {3: 0},
                move_scratch(w, 3 * n),
            )

        count = len(CHUNKS)
        got = [None] * (count + 1)
        far_sum, mate_term, out = [None] * count, [None] * count, [None] * count
        got[0] = cut(0, far_mate_of)
        for k in range(count):
            if k + 1 < count:
                got[k + 1] = cut(k + 1, far_mate_of)
            far_sum[k] = chip_sum(k, got[k])
        for k in range(count):
            mate_term[k] = cut(k, mate_of)
        forward = [None] * count

        for k in range(count):
            out[k] = update(k, mate_term[k], far_sum[k])
        for k in range(count):
            forward[k] = send(out[k][0], MATE)
            place(k, *out[k], forward[k])
        return (*new_w, *new_m, *new_v)

    all_of, cut_of = P(None, None, None), P(None, "dp", None)
    whole = jax.shard_map(
        work,
        mesh=mesh,
        in_specs=(P(("rep", "dp"), None, None, None),) * 3 + (all_of,) * 3 + (cut_of,) * 6,
        out_specs=(P("rep", None, None),) * 3 + (P("rep", "dp", None),) * 6,
        check_vma=False,
    )
    shapes = [(2, 1280, 4480), (2, 1280, 4480), (2, 4480, 1280)]
    jax.eval_shape(
        whole,
        *(jax.ShapeDtypeStruct((8, *s), jnp.bfloat16) for s in shapes),
        *(jax.ShapeDtypeStruct(s, jnp.bfloat16) for s in shapes),
        *(jax.ShapeDtypeStruct(s, jnp.float32) for s in shapes + shapes),
    )
    return whole
```

time: 897 us -> 851 us (0.949)
  Pallas kernels: 279 us -> 246 us
  waiting for transfers between devices: 583 us -> 564 us
    pallas_call x40 -> x55, Pallas kernels: 279 us -> 246 us  [run(): pl.pallas_call(body, out_shape=outs, grid=grid, in_specs=in_specs, out_sp...]
    ppermute x48 -> x66, waiting for transfers between devices: 583 us -> 564 us  [send(): return in_hbm(lax.ppermute(in_hbm(x), 'dp', pairs))]
    ppermute x48 -> x66, starting transfers between devices: 30.2 us -> 36 us  [send(): return in_hbm(lax.ppermute(in_hbm(x), 'dp', pairs))]
  transfers between devices with their start and end apart: 48 -> 66, of which waited for: 15 -> 17; matrix products, arithmetic and copies ran while one was open for 0% -> 0% of each run, Pallas kernels for 31% -> 28%
where the time goes in v2:
time: 851 us; the launch traced here: 849 us
  waiting for transfers between devices  564 us (66%)
  Pallas kernels  246 us (29%)
  starting transfers between devices  36 us (4%)
    ppermute x66, waiting for transfers between devices, send(): return in_hbm(lax.ppermute(in_hbm(x), 'dp', pairs))  564 us
    pallas_call x55, Pallas kernels, run(): pl.pallas_call(body, out_shape=outs, grid=grid, in_specs=in_specs, out_sp...  246 us
    ppermute x66, starting transfers between devices, send(): return in_hbm(lax.ppermute(in_hbm(x), 'dp', pairs))  36 us
  transfers between devices with their start and end apart: 66, of which 17 were waited for; matrix products, arithmetic and copies ran while one was open for 0% of the time, Pallas kernels for 28%

profile of v2, /device:TPU:0, one launch (start us, length us, event | category | flops | bytes accessed | tf_op | source)
XLA Modules:
  0.0 848.9 jit_solution(14325155985393411110)
XLA Ops:
  19.3 3.0 collective-permute-start.14
  26.0 4.2 collective-permute-done.14.refs_2_
  30.2 3.2 shard_map.202
  47.0 3.2 shard_map.195
  52.7 8.7 %collective-permute-done.11.refs_2_ = bf16[64,4480]{1,0:T(8,128)(2,1)} collective-permute-done((bf16[64,4480]{1,0:T(8,128)(2,1)}, bf16[64,4480]{1,0:T(8,128)(2,1)}, u32[]{:S(2)}, u32[]{:S(2)}) %collective-permute-start.11) | collective-permute-done | bytes 573472 | tf_op jit(solution)/shard_map/ppermute | solution.py:96
  61.4 4.0 shard_map.203
  70.0 3.2 shard_map.227
  73.5 6.4 collective-permute-done.8.refs_2_
  79.9 2.7 shard_map.187
  82.6 9.6 %collective-permute-done.24.a = bf16[64,4480]{1,0:T(8,128)(2,1)} collective-permute-done((bf16[64,4480]{1,0:T(8,128)(2,1)}, bf16[64,4480]{1,0:T(8,128)(2,1)}, u32[]{:S(2)}, u32[]{:S(2)}) %collective-permute-start.24) | collective-permute-done | bytes 573472 | tf_op jit(solution)/shard_map/ppermute | solution.py:96
  96.4 2.7 shard_map.188
  99.1 11.4 %collective-permute-done.47.refs_2_ = bf16[336,1280]{1,0:T(8,128)(2,1)} collective-permute-done((bf16[336,1280]{1,0:T(8,128)(2,1)}, bf16[336,1280]{1,0:T(8,128)(2,1)}, u32[]{:S(2)}, u32[]{:S(2)}) %collective-permute-start.47) | collective-permute-done | bytes 860192 | tf_op jit(solution)/shard_map/ppermute | solution.py:96
  110.6 2.7 shard_map.212
  113.9 6.6 shard_map.204
  120.5 14.2 %collective-permute-done.5.refs_2_ = bf16[128,4480]{1,0:T(8,128)(2,1)} collective-permute-done((bf16[128,4480]{1,0:T(8,128)(2,1)}, bf16[128,4480]{1,0:T(8,128)(2,1)}, u32[]{:S(2)}, u32[]{:S(2)}) %collective-permute-start.5) | collective-permute-done | bytes 1146912 | tf_op jit(solution)/shard_map/ppermute | solution.py:96
  136.5 2.7 shard_map.213
  139.2 16.5 %collective-permute-done.21.a = bf16[96,4480]{1,0:T(8,128)(2,1)} collective-permute-done((bf16[96,4480]{1,0:T(8,128)(2,1)}, bf16[96,4480]{1,0:T(8,128)(2,1)}, u32[]{:S(2)}, u32[]{:S(2)}) %collective-permute-start.21) | collective-permute-done | bytes 860192 | tf_op jit(solution)/shard_map/ppermute | solution.py:96
  155.7 2.7 shard_map.215
  158.9 2.7 shard_map.232
  161.7 2.7 shard_map.216
  165.0 2.7 shard_map.231
  167.7 5.9 shard_map.189
  175.4 6.4 shard_map.205
  182.1 5.9 shard_map.233
  189.9 5.9 shard_map.214
  195.8 67.7 %collective-permute-done.18.a = bf16[128,4480]{1,0:T(8,128)(2,1)} collective-permute-done((bf16[128,4480]{1,0:T(8,128)(2,1)}, bf16[128,4480]{1,0:T(8,128)(2,1)}, u32[]{:S(2)}, u32[]{:S(2)}) %collective-permute-start.18) | collective-permute-done | bytes 1146912 | tf_op jit(solution)/shard_map/ppermute | solution.py:96
  265.3 5.9 shard_map.217
  271.4 4.0 shard_map.230
  277.2 16.6 %shard_map.206 = (bf16[320,4480]{1,0:T(8,128)(2,1)}, bf16[2,1280,4480]{2,1,0:T(8,128)(2,1)}, f32[2,320,4480]{2,1,0:T(8,128)}, f32[2,320,4480]{2,1,0:T(8,128)}) custom-call(bf16[1,2,1280,4480]{3,2,1,0:T(8,128)(2,1)} %refs_0_.15, bf16[320,4480]{1,0:T(8,128)(2,1)} %collective-permute-done.refs_1_, ...), custom_call_target="tpu_custom_call", output_to_operand_aliasing={{1}: (6, {}), {2}: (7, {}), {3}: (8, {})} | custom-call | flops 48742400 | bytes 48742400 | tf_op jit(solution)/shard_map/pallas_call | solution.py:66
  293.7 190.5 %collective-permute-done.50.refs_2_ = bf16[672,1280]{1,0:T(8,128)(2,1)} collective-permute-done((bf16[672,1280]{1,0:T(8,128)(2,1)}, bf16[672,1280]{1,0:T(8,128)(2,1)}, u32[]{:S(2)}, u32[]{:S(2)}) %collective-permute-start.50) | collective-permute-done | bytes 1720352 | tf_op jit(solution)/shard_map/ppermute | solution.py:96
  486.0 16.6 %shard_map.234 = (bf16[1120,1280]{1,0:T(8,128)(2,1)}, bf16[2,4480,1280]{2,1,0:T(8,128)(2,1)}, f32[2,1120,1280]{2,1,0:T(8,128)}, f32[2,1120,1280]{2,1,0:T(8,128)}) custom-call(bf16[1,2,4480,1280]{3,2,1,0:T(8,128)(2,1)} %refs_0_.21, bf16[1120,1280]{1,0:T(8,128)(2,1)} %collective-permute-done.51.refs_1_, bf16[1120,1280]{1,0:T(8,128)(2,1)} %collective-permute-done.53.refs_2_, ...), custom_call_target="tpu_custom_call" | custom-call | flops 48742400 | bytes 48742400 | tf_op jit(solution)/shard_map/pallas_call | solution.py:66
  502.6 10.9 %shard_map.235 = (bf16[672,1280]{1,0:T(8,128)(2,1)}, bf16[2,4480,1280]{2,1,0:T(8,128)(2,1)}, f32[2,1120,1280]{2,1,0:T(8,128)}, f32[2,1120,1280]{2,1,0:T(8,128)}) custom-call(bf16[1,2,4480,1280]{3,2,1,0:T(8,128)(2,1)} %refs_0_.21, bf16[672,1280]{1,0:T(8,128)(2,1)} %collective-permute-done.48.refs_1_, ...), custom_call_target="tpu_custom_call", output_to_operand_aliasing={{1}: (6, {}), {2}: (7, {}), {3}: (8, {})} | custom-call | flops 47595520 | bytes 47595520 | tf_op jit(solution)/shard_map/pallas_call | solution.py:66
  513.4 6.6 shard_map.236
  520.1 3.2 shard_map.237
  525.6 30.1 %collective-permute-done.54.a = bf16[112,1280]{1,0:T(8,128)(2,1)} collective-permute-done((bf16[112,1280]{1,0:T(8,128)(2,1)}, bf16[112,1280]{1,0:T(8,128)(2,1)}, u32[]{:S(2)}, u32[]{:S(2)}) %collective-permute-start.54) | collective-permute-done | bytes 286752 | tf_op jit(solution)/shard_map/ppermute | solution.py:96
  555.7 16.6 %shard_map.218 = (bf16[320,4480]{1,0:T(8,128)(2,1)}, bf16[2,1280,4480]{2,1,0:T(8,128)(2,1)}, f32[2,320,4480]{2,1,0:T(8,128)}, f32[2,320,4480]{2,1,0:T(8,128)}) custom-call(bf16[1,2,1280,4480]{3,2,1,0:T(8,128)(2,1)} %refs_0_.17, bf16[320,4480]{1,0:T(8,128)(2,1)} %collective-permute-done.33.refs_1_, bf16[320,4480]{1,0:T(8,128)(2,1)} %collective-permute-done.35.refs_2_, ...), custom_call_target="tpu_custom_call" | custom-call | flops 48742400 | bytes 48742400 | tf_op jit(solution)/shard_map/pallas_call | solution.py:66
  572.2 16.7 %shard_map.219 = (bf16[320,4480]{1,0:T(8,128)(2,1)}, bf16[2,1280,4480]{2,1,0:T(8,128)(2,1)}, f32[2,320,4480]{2,1,0:T(8,128)}, f32[2,320,4480]{2,1,0:T(8,128)}) custom-call(bf16[1,2,1280,4480]{3,2,1,0:T(8,128)(2,1)} %refs_0_.17, bf16[320,4480]{1,0:T(8,128)(2,1)} %collective-permute-done.30.refs_1_, ...), custom_call_target="tpu_custom_call", output_to_operand_aliasing={{1}: (6, {}), {2}: (7, {}), {3}: (8, {})} | custom-call | flops 48742400 | bytes 48742400 | tf_op jit(solution)/shard_map/pallas_call | solution.py:66
  590.8 20.2 %collective-permute-done.60.a = bf16[672,1280]{1,0:T(8,128)(2,1)} collective-permute-done((bf16[672,1280]{1,0:T(8,128)(2,1)}, bf16[672,1280]{1,0:T(8,128)(2,1)}, u32[]{:S(2)}, u32[]{:S(2)}) %collective-permute-start.60) | collective-permute-done | bytes 1720352 | tf_op jit(solution)/shard_map/ppermute | solution.py:96
  613.3 59.0 %collective-permute-done.36.a = bf16[320,4480]{1,0:T(8,128)(2,1)S(1)} collective-permute-done((bf16[320,4480]{1,0:T(8,128)(2,1)}, bf16[320,4480]{1,0:T(8,128)(2,1)S(1)}, u32[]{:S(2)}, u32[]{:S(2)}) %collective-permute-start.36) | collective-permute-done | bytes 2867232 | tf_op jit(solution)/shard_map/ppermute | solution.py:96
  672.8 60.9 %collective-permute-done.39.a = bf16[320,4480]{1,0:T(8,128)(2,1)S(1)} collective-permute-done((bf16[320,4480]{1,0:T(8,128)(2,1)}, bf16[320,4480]{1,0:T(8,128)(2,1)S(1)}, u32[]{:S(2)}, u32[]{:S(2)}) %collective-permute-start.39) | collective-permute-done | bytes 2867232 | tf_op jit(solution)/shard_map/ppermute | solution.py:96
  734.3 59.6 %collective-permute-done.63.a = bf16[1120,1280]{1,0:T(8,128)(2,1)S(1)} collective-permute-done((bf16[1120,1280]{1,0:T(8,128)(2,1)}, bf16[1120,1280]{1,0:T(8,128)(2,1)S(1)}, u32[]{:S(2)}, u32[]{:S(2)}) %collective-permute-start.63) | collective-permute-done | bytes 2867232 | tf_op jit(solution)/shard_map/ppermute | solution.py:96
  795.4 3.7 collective-permute-done.65.c
  807.5 3.0 shard_map.210._
  810.5 7.2 shard_map.211
  817.7 7.2 shard_map.220._
  824.9 7.2 shard_map.221
  832.1 7.2 shard_map.238._
  839.3 4.9 shard_map.239._
  (159 shorter events, 82.3 us)
Async XLA Ops:
  10.9 26.9 %collective-permute-start.6 = (bf16[96,4480]{1,0:T(8,128)(2,1)}, bf16[96,4480]{1,0:T(8,128)(2,1)}, u32[]{:S(2)}, u32[]{:S(2)}) collective-permute-start(bf16[96,4480]{1,0:T(8,128)(2,1)} %shard_map.193), channel_id=1, source_target_pairs={{0,1},{1,0},{2,3},{3,2},{4,5},{5,4},{6,7},{7,6}} | collective-permute-start | bytes 2580488 | tf_op jit(solution)/shard_map/ppermute | solution.py:96
  15.1 25.2 %collective-permute-start.7 = (bf16[96,4480]{1,0:T(8,128)(2,1)}, bf16[96,4480]{1,0:T(8,128)(2,1)}, u32[]{:S(2)}, u32[]{:S(2)}) collective-permute-start(bf16[96,4480]{1,0:T(8,128)(2,1)} %shard_map.194), channel_id=1, source_target_pairs={{0,1},{1,0},{2,3},{3,2},{4,5},{5,4},{6,7},{7,6}} | collective-permute-start | bytes 2580488 | tf_op jit(solution)/shard_map/ppermute | solution.py:96
  37.8 29.5 %collective-permute-start.3 = (bf16[128,4480]{1,0:T(8,128)(2,1)}, bf16[128,4480]{1,0:T(8,128)(2,1)}, u32[]{:S(2)}, u32[]{:S(2)}) collective-permute-start(bf16[128,4480]{1,0:T(8,128)(2,1)} %shard_map.190), channel_id=1, source_target_pairs={{0,1},{1,0},{2,3},{3,2},{4,5},{5,4},{6,7},{7,6}} | collective-permute-start | bytes 3440648 | tf_op jit(solution)/shard_map/ppermute | solution.py:96
  40.3 29.4 %collective-permute-start.4 = (bf16[128,4480]{1,0:T(8,128)(2,1)}, bf16[128,4480]{1,0:T(8,128)(2,1)}, u32[]{:S(2)}, u32[]{:S(2)}) collective-permute-start(bf16[128,4480]{1,0:T(8,128)(2,1)} %shard_map.191), channel_id=1, source_target_pairs={{0,1},{1,0},{2,3},{3,2},{4,5},{5,4},{6,7},{7,6}} | collective-permute-start | bytes 3440648 | tf_op jit(solution)/shard_map/ppermute | solution.py:96
  43.3 22.2 %collective-permute-start.46 = (bf16[336,1280]{1,0:T(8,128)(2,1)}, bf16[336,1280]{1,0:T(8,128)(2,1)}, u32[]{:S(2)}, u32[]{:S(2)}) collective-permute-start(bf16[336,1280]{1,0:T(8,128)(2,1)} %shard_map.226), channel_id=1, source_target_pairs={{0,1},{1,0},{2,3},{3,2},{4,5},{5,4},{6,7},{7,6}} | collective-permute-start | bytes 2580488 | tf_op jit(solution)/shard_map/ppermute | solution.py:96
  50.2 29.7 %collective-permute-start.8 = (bf16[96,4480]{1,0:T(8,128)(2,1)}, bf16[96,4480]{1,0:T(8,128)(2,1)}, u32[]{:S(2)}, u32[]{:S(2)}) collective-permute-start(bf16[96,4480]{1,0:T(8,128)(2,1)} %shard_map.195), channel_id=1, source_target_pairs={{0,2},{2,0},{1,3},{3,1},{4,6},{6,4},{5,7},{7,5}} | collective-permute-start | bytes 2580488 | tf_op jit(solution)/shard_map/ppermute | solution.py:96
  61.4 51.9 %collective-permute-start.48 = (bf16[672,1280]{1,0:T(8,128)(2,1)}, bf16[672,1280]{1,0:T(8,128)(2,1)}, u32[]{:S(2)}, u32[]{:S(2)}) collective-permute-start(bf16[672,1280]{1,0:T(8,128)(2,1)} %shard_map.228), channel_id=1, source_target_pairs={{0,1},{1,0},{2,3},{3,2},{4,5},{5,4},{6,7},{7,6}} | collective-permute-start | bytes 5160968 | tf_op jit(solution)/shard_map/ppermute | solution.py:96
  65.5 26.7 %collective-permute-start.24 = (bf16[64,4480]{1,0:T(8,128)(2,1)}, bf16[64,4480]{1,0:T(8,128)(2,1)}, u32[]{:S(2)}, u32[]{:S(2)}) collective-permute-start(bf16[64,4480]{1,0:T(8,128)(2,1)} %get-tuple-element.68), channel_id=1, source_target_pairs={{0,2},{2,0},{1,3},{3,1},{4,6},{6,4},{5,7},{7,5}} | collective-permute-start | bytes 1720328 | tf_op jit(solution)/shard_map/ppermute | solution.py:96
  69.7 44.2 %collective-permute-start.49 = (bf16[672,1280]{1,0:T(8,128)(2,1)}, bf16[672,1280]{1,0:T(8,128)(2,1)}, u32[]{:S(2)}, u32[]{:S(2)}) collective-permute-start(bf16[672,1280]{1,0:T(8,128)(2,1)} %shard_map.229), channel_id=1, source_target_pairs={{0,1},{1,0},{2,3},{3,2},{4,5},{5,4},{6,7},{7,6}} | collective-permute-start | bytes 5160968 | tf_op jit(solution)/shard_map/ppermute | solution.py:96
  73.2 37.4 %collective-permute-start.47 = (bf16[336,1280]{1,0:T(8,128)(2,1)}, bf16[336,1280]{1,0:T(8,128)(2,1)}, u32[]{:S(2)}, u32[]{:S(2)}) collective-permute-start(bf16[336,1280]{1,0:T(8,128)(2,1)} %shard_map.227), channel_id=1, source_target_pairs={{0,2},{2,0},{1,3},{3,1},{4,6},{6,4},{5,7},{7,5}} | collective-permute-start | bytes 2580488 | tf_op jit(solution)/shard_map/ppermute | solution.py:96
  92.2 69.5 %collective-permute-start = (bf16[320,4480]{1,0:T(8,128)(2,1)}, bf16[320,4480]{1,0:T(8,128)(2,1)}, u32[]{:S(2)}, u32[]{:S(2)}) collective-permute-start(bf16[320,4480]{1,0:T(8,128)(2,1)} %shard_map.187), channel_id=1, source_target_pairs={{0,1},{1,0},{2,3},{3,2},{4,5},{5,4},{6,7},{7,6}} | collective-permute-start | bytes 8601608 | tf_op jit(solution)/shard_map/ppermute | solution.py:96
  94.7 40.0 %collective-permute-start.5 = (bf16[128,4480]{1,0:T(8,128)(2,1)}, bf16[128,4480]{1,0:T(8,128)(2,1)}, u32[]{:S(2)}, u32[]{:S(2)}) collective-permute-start(bf16[128,4480]{1,0:T(8,128)(2,1)} %shard_map.192), channel_id=1, source_target_pairs={{0,2},{2,0},{1,3},{3,1},{4,6},{6,4},{5,7},{7,5}} | collective-permute-start | bytes 3440648 | tf_op jit(solution)/shard_map/ppermute | solution.py:96
  110.6 53.8 %collective-permute-start.1 = (bf16[320,4480]{1,0:T(8,128)(2,1)}, bf16[320,4480]{1,0:T(8,128)(2,1)}, u32[]{:S(2)}, u32[]{:S(2)}) collective-permute-start(bf16[320,4480]{1,0:T(8,128)(2,1)} %shard_map.188), channel_id=1, source_target_pairs={{0,1},{1,0},{2,3},{3,2},{4,5},{5,4},{6,7},{7,6}} | collective-permute-start | bytes 8601608 | tf_op jit(solution)/shard_map/ppermute | solution.py:96
  113.3 54.3 %collective-permute-start.30 = (bf16[320,4480]{1,0:T(8,128)(2,1)}, bf16[320,4480]{1,0:T(8,128)(2,1)}, u32[]{:S(2)}, u32[]{:S(2)}) collective-permute-start(bf16[320,4480]{1,0:T(8,128)(2,1)} %shard_map.212), channel_id=1, source_target_pairs={{0,1},{1,0},{2,3},{3,2},{4,5},{5,4},{6,7},{7,6}} | collective-permute-start | bytes 8601608 | tf_op jit(solution)/shard_map/ppermute | solution.py:96
  113.8 22.6 %collective-permute-start.26 = (bf16[64,4480]{1,0:T(8,128)(2,1)}, bf16[64,4480]{1,0:T(8,128)(2,1)}, u32[]{:S(2)}, u32[]{:S(2)}) collective-permute-start(bf16[64,4480]{1,0:T(8,128)(2,1)} %collective-permute-done.24.a), channel_id=1, source_target_pairs={{0,1},{1,0},{2,3},{3,2},{4,5},{5,4},{6,7},{7,6}} | collective-permute-start | bytes 1720328 | tf_op jit(solution)/shard_map/ppermute | solution.py:96
  136.5 21.9 %collective-permute-start.22 = (bf16[96,4480]{1,0:T(8,128)(2,1)}, bf16[96,4480]{1,0:T(8,128)(2,1)}, u32[]{:S(2)}, u32[]{:S(2)}) collective-permute-start(bf16[96,4480]{1,0:T(8,128)(2,1)} %get-tuple-element.67), channel_id=1, source_target_pairs={{0,1},{1,0},{2,3},{3,2},{4,5},{5,4},{6,7},{7,6}} | collective-permute-start | bytes 2580488 | tf_op jit(solution)/shard_map/ppermute | solution.py:96
  158.4 23.3 %collective-permute-start.33 = (bf16[320,4480]{1,0:T(8,128)(2,1)}, bf16[320,4480]{1,0:T(8,128)(2,1)}, u32[]{:S(2)}, u32[]{:S(2)}) collective-permute-start(bf16[320,4480]{1,0:T(8,128)(2,1)} %shard_map.215), channel_id=1, source_target_pairs={{0,1},{1,0},{2,3},{3,2},{4,5},{5,4},{6,7},{7,6}} | collective-permute-start | bytes 8601608 | tf_op jit(solution)/shard_map/ppermute | solution.py:96
  164.4 23.5 %collective-permute-start.34 = (bf16[320,4480]{1,0:T(8,128)(2,1)}, bf16[320,4480]{1,0:T(8,128)(2,1)}, u32[]{:S(2)}, u32[]{:S(2)}) collective-permute-start(bf16[320,4480]{1,0:T(8,128)(2,1)} %shard_map.216), channel_id=1, source_target_pairs={{0,1},{1,0},{2,3},{3,2},{4,5},{5,4},{6,7},{7,6}} | collective-permute-start | bytes 8601608 | tf_op jit(solution)/shard_map/ppermute | solution.py:96
  167.7 22.1 %collective-permute-start.51 = (bf16[1120,1280]{1,0:T(8,128)(2,1)}, bf16[1120,1280]{1,0:T(8,128)(2,1)}, u32[]{:S(2)}, u32[]{:S(2)}) collective-permute-start(bf16[1120,1280]{1,0:T(8,128)(2,1)} %shard_map.231), channel_id=1, source_target_pairs={{0,1},{1,0},{2,3},{3,2},{4,5},{5,4},{6,7},{7,6}} | collective-permute-start | bytes 8601608 | tf_op jit(solution)/shard_map/ppermute | solution.py:96
  173.6 103.6 %collective-permute-start.2 = (bf16[320,4480]{1,0:T(8,128)(2,1)}, bf16[320,4480]{1,0:T(8,128)(2,1)}, u32[]{:S(2)}, u32[]{:S(2)}) collective-permute-start(bf16[320,4480]{1,0:T(8,128)(2,1)} %shard_map.189), channel_id=1, source_target_pairs={{0,2},{2,0},{1,3},{3,1},{4,6},{6,4},{5,7},{7,5}} | collective-permute-start | bytes 8601608 | tf_op jit(solution)/shard_map/ppermute | solution.py:96
  181.8 81.8 %collective-permute-start.18 = (bf16[128,4480]{1,0:T(8,128)(2,1)}, bf16[128,4480]{1,0:T(8,128)(2,1)}, u32[]{:S(2)}, u32[]{:S(2)}) collective-permute-start(bf16[128,4480]{1,0:T(8,128)(2,1)} %get-tuple-element.66), channel_id=1, source_target_pairs={{0,2},{2,0},{1,3},{3,1},{4,6},{6,4},{5,7},{7,5}} | collective-permute-start | bytes 3440648 | tf_op jit(solution)/shard_map/ppermute | solution.py:96
  182.1 89.1 %collective-permute-start.19 = (bf16[128,4480]{1,0:T(8,128)(2,1)}, bf16[128,4480]{1,0:T(8,128)(2,1)}, u32[]{:S(2)}, u32[]{:S(2)}) collective-permute-start(bf16[128,4480]{1,0:T(8,128)(2,1)} %get-tuple-element.66), channel_id=1, source_target_pairs={{0,1},{1,0},{2,3},{3,2},{4,5},{5,4},{6,7},{7,6}} | collective-permute-start | bytes 3440648 | tf_op jit(solution)/shard_map/ppermute | solution.py:96
  188.0 298.0 %collective-permute-start.53 = (bf16[1120,1280]{1,0:T(8,128)(2,1)}, bf16[1120,1280]{1,0:T(8,128)(2,1)}, u32[]{:S(2)}, u32[]{:S(2)}) collective-permute-start(bf16[1120,1280]{1,0:T(8,128)(2,1)} %shard_map.233), channel_id=1, source_target_pairs={{0,2},{2,0},{1,3},{3,1},{4,6},{6,4},{5,7},{7,5}} | collective-permute-start | bytes 8601608 | tf_op jit(solution)/shard_map/ppermute | solution.py:96
  189.7 85.7 %collective-permute-start.23 = (bf16[96,4480]{1,0:T(8,128)(2,1)}, bf16[96,4480]{1,0:T(8,128)(2,1)}, u32[]{:S(2)}, u32[]{:S(2)}) collective-permute-start(bf16[96,4480]{1,0:T(8,128)(2,1)} %collective-permute-done.21.a), channel_id=1, source_target_pairs={{0,1},{1,0},{2,3},{3,2},{4,5},{5,4},{6,7},{7,6}} | collective-permute-start | bytes 2580488 | tf_op jit(solution)/shard_map/ppermute | solution.py:96
  263.5 260.1 %collective-permute-start.32 = (bf16[320,4480]{1,0:T(8,128)(2,1)}, bf16[320,4480]{1,0:T(8,128)(2,1)}, u32[]{:S(2)}, u32[]{:S(2)}) collective-permute-start(bf16[320,4480]{1,0:T(8,128)(2,1)} %shard_map.214), channel_id=1, source_target_pairs={{0,2},{2,0},{1,3},{3,1},{4,6},{6,4},{5,7},{7,5}} | collective-permute-start | bytes 8601608 | tf_op jit(solution)/shard_map/ppermute | solution.py:96
  271.1 254.2 %collective-permute-start.35 = (bf16[320,4480]{1,0:T(8,128)(2,1)}, bf16[320,4480]{1,0:T(8,128)(2,1)}, u32[]{:S(2)}, u32[]{:S(2)}) collective-permute-start(bf16[320,4480]{1,0:T(8,128)(2,1)} %shard_map.217), channel_id=1, source_target_pairs={{0,2},{2,0},{1,3},{3,1},{4,6},{6,4},{5,7},{7,5}} | collective-permute-start | bytes 8601608 | tf_op jit(solution)/shard_map/ppermute | solution.py:96
  275.4 208.8 %collective-permute-start.50 = (bf16[672,1280]{1,0:T(8,128)(2,1)}, bf16[672,1280]{1,0:T(8,128)(2,1)}, u32[]{:S(2)}, u32[]{:S(2)}) collective-permute-start(bf16[672,1280]{1,0:T(8,128)(2,1)} %shard_map.230), channel_id=1, source_target_pairs={{0,2},{2,0},{1,3},{3,1},{4,6},{6,4},{5,7},{7,5}} | collective-permute-start | bytes 5160968 | tf_op jit(solution)/shard_map/ppermute | solution.py:96
  277.2 246.1 %collective-permute-start.20 = (bf16[128,4480]{1,0:T(8,128)(2,1)}, bf16[128,4480]{1,0:T(8,128)(2,1)}, u32[]{:S(2)}, u32[]{:S(2)}) collective-permute-start(bf16[128,4480]{1,0:T(8,128)(2,1)} %collective-permute-done.18.a), channel_id=1, source_target_pairs={{0,1},{1,0},{2,3},{3,2},{4,5},{5,4},{6,7},{7,6}} | collective-permute-start | bytes 3440648 | tf_op jit(solution)/shard_map/ppermute | solution.py:96
  484.2 128.5 %collective-permute-start.15 = (bf16[320,4480]{1,0:T(8,128)(2,1)}, bf16[320,4480]{1,0:T(8,128)(2,1)}, u32[]{:S(2)}, u32[]{:S(2)}) collective-permute-start(bf16[320,4480]{1,0:T(8,128)(2,1)} %get-tuple-element.65), channel_id=1, source_target_pairs={{0,2},{2,0},{1,3},{3,1},{4,6},{6,4},{5,7},{7,5}} | collective-permute-start | bytes 8601608 | tf_op jit(solution)/shard_map/ppermute | solution.py:96
  485.9 127.0 %collective-permute-start.16 = (bf16[320,4480]{1,0:T(8,128)(2,1)}, bf16[320,4480]{1,0:T(8,128)(2,1)}, u32[]{:S(2)}, u32[]{:S(2)}) collective-permute-start(bf16[320,4480]{1,0:T(8,128)(2,1)} %get-tuple-element.65), channel_id=1, source_target_pairs={{0,1},{1,0},{2,3},{3,2},{4,5},{5,4},{6,7},{7,6}} | collective-permute-start | bytes 8601608 | tf_op jit(solution)/shard_map/ppermute | solution.py:96
  523.3 32.4 %collective-permute-start.54 = (bf16[112,1280]{1,0:T(8,128)(2,1)}, bf16[112,1280]{1,0:T(8,128)(2,1)}, u32[]{:S(2)}, u32[]{:S(2)}) collective-permute-start(bf16[112,1280]{1,0:T(8,128)(2,1)} %get-tuple-element.86), channel_id=1, source_target_pairs={{0,2},{2,0},{1,3},{3,1},{4,6},{6,4},{5,7},{7,5}} | collective-permute-start | bytes 860168 | tf_op jit(solution)/shard_map/ppermute | solution.py:96
  523.6 65.4 %collective-permute-start.57 = (bf16[336,1280]{1,0:T(8,128)(2,1)}, bf16[336,1280]{1,0:T(8,128)(2,1)}, u32[]{:S(2)}, u32[]{:S(2)}) collective-permute-start(bf16[336,1280]{1,0:T(8,128)(2,1)} %get-tuple-element.87), channel_id=1, source_target_pairs={{0,2},{2,0},{1,3},{3,1},{4,6},{6,4},{5,7},{7,5}} | collective-permute-start | bytes 2580488 | tf_op jit(solution)/shard_map/ppermute | solution.py:96
  525.3 85.7 %collective-permute-start.60 = (bf16[672,1280]{1,0:T(8,128)(2,1)}, bf16[672,1280]{1,0:T(8,128)(2,1)}, u32[]{:S(2)}, u32[]{:S(2)}) collective-permute-start(bf16[672,1280]{1,0:T(8,128)(2,1)} %get-tuple-element.88), channel_id=1, source_target_pairs={{0,2},{2,0},{1,3},{3,1},{4,6},{6,4},{5,7},{7,5}} | collective-permute-start | bytes 5160968 | tf_op jit(solution)/shard_map/ppermute | solution.py:96
  555.7 55.3 %collective-permute-start.61 = (bf16[672,1280]{1,0:T(8,128)(2,1)}, bf16[672,1280]{1,0:T(8,128)(2,1)}, u32[]{:S(2)}, u32[]{:S(2)}) collective-permute-start(bf16[672,1280]{1,0:T(8,128)(2,1)} %get-tuple-element.88), channel_id=1, source_target_pairs={{0,1},{1,0},{2,3},{3,2},{4,5},{5,4},{6,7},{7,6}} | collective-permute-start | bytes 5160968 | tf_op jit(solution)/shard_map/ppermute | solution.py:96
  589.0 83.3 %collective-permute-start.36 = (bf16[320,4480]{1,0:T(8,128)(2,1)}, bf16[320,4480]{1,0:T(8,128)(2,1)S(1)}, u32[]{:S(2)}, u32[]{:S(2)}) collective-permute-start(bf16[320,4480]{1,0:T(8,128)(2,1)} %get-tuple-element.74), channel_id=1, source_target_pairs={{0,2},{2,0},{1,3},{3,1},{4,6},{6,4},{5,7},{7,5}} | collective-permute-start | bytes 8601608 | tf_op jit(solution)/shard_map/ppermute | solution.py:96
  611.0 61.3 %collective-permute-start.37 = (bf16[320,4480]{1,0:T(8,128)(2,1)}, bf16[320,4480]{1,0:T(8,128)(2,1)S(1)}, u32[]{:S(2)}, u32[]{:S(2)}) collective-permute-start(bf16[320,4480]{1,0:T(8,128)(2,1)} %get-tuple-element.74), channel_id=1, source_target_pairs={{0,1},{1,0},{2,3},{3,2},{4,5},{5,4},{6,7},{7,6}} | collective-permute-start | bytes 8601608 | tf_op jit(solution)/shard_map/ppermute | solution.py:96
  611.0 122.8 %collective-permute-start.39 = (bf16[320,4480]{1,0:T(8,128)(2,1)}, bf16[320,4480]{1,0:T(8,128)(2,1)S(1)}, u32[]{:S(2)}, u32[]{:S(2)}) collective-permute-start(bf16[320,4480]{1,0:T(8,128)(2,1)} %get-tuple-element.75), channel_id=1, source_target_pairs={{0,2},{2,0},{1,3},{3,1},{4,6},{6,4},{5,7},{7,5}} | collective-permute-start | bytes 8601608 | tf_op jit(solution)/shard_map/ppermute | solution.py:96
  612.7 121.0 %collective-permute-start.40 = (bf16[320,4480]{1,0:T(8,128)(2,1)}, bf16[320,4480]{1,0:T(8,128)(2,1)S(1)}, u32[]{:S(2)}, u32[]{:S(2)}) collective-permute-start(bf16[320,4480]{1,0:T(8,128)(2,1)} %get-tuple-element.75), channel_id=1, source_target_pairs={{0,1},{1,0},{2,3},{3,2},{4,5},{5,4},{6,7},{7,6}} | collective-permute-start | bytes 8601608 | tf_op jit(solution)/shard_map/ppermute | solution.py:96
  612.9 180.9 %collective-permute-start.63 = (bf16[1120,1280]{1,0:T(8,128)(2,1)}, bf16[1120,1280]{1,0:T(8,128)(2,1)S(1)}, u32[]{:S(2)}, u32[]{:S(2)}) collective-permute-start(bf16[1120,1280]{1,0:T(8,128)(2,1)} %get-tuple-element.89), channel_id=1, source_target_pairs={{0,2},{2,0},{1,3},{3,1},{4,6},{6,4},{5,7},{7,5}} | collective-permute-start | bytes 8601608 | tf_op jit(solution)/shard_map/ppermute | solution.py:96
  672.3 121.5 %collective-permute-start.64 = (bf16[1120,1280]{1,0:T(8,128)(2,1)}, bf16[1120,1280]{1,0:T(8,128)(2,1)S(1)}, u32[]{:S(2)}, u32[]{:S(2)}) collective-permute-start(bf16[1120,1280]{1,0:T(8,128)(2,1)} %get-tuple-element.89), channel_id=1, source_target_pairs={{0,1},{1,0},{2,3},{3,2},{4,5},{5,4},{6,7},{7,6}} | collective-permute-start | bytes 8601608 | tf_op jit(solution)/shard_map/ppermute | solution.py:96
  672.3 122.0 %collective-permute-start.17 = (bf16[320,4480]{1,0:T(8,128)(2,1)}, bf16[320,4480]{1,0:T(8,128)(2,1)S(1)}, u32[]{:S(2)}, u32[]{:S(2)}) collective-permute-start(bf16[320,4480]{1,0:T(8,128)(2,1)} %collective-permute-done.15.a), channel_id=1, source_target_pairs={{0,1},{1,0},{2,3},{3,2},{4,5},{5,4},{6,7},{7,6}} | collective-permute-start | bytes 8601608 | tf_op jit(solution)/shard_map/ppermute | solution.py:96
  733.8 60.6 %collective-permute-start.38 = (bf16[320,4480]{1,0:T(8,128)(2,1)S(1)}, bf16[320,4480]{1,0:T(8,128)(2,1)S(1)}, u32[]{:S(2)}, u32[]{:S(2)}) collective-permute-start(bf16[320,4480]{1,0:T(8,128)(2,1)S(1)} %collective-permute-done.36.a), channel_id=1, source_target_pairs={{0,1},{1,0},{2,3},{3,2},{4,5},{5,4},{6,7},{7,6}} | collective-permute-start | bytes 8601608 | tf_op jit(solution)/shard_map/ppermute | solution.py:96
  733.8 61.1 %collective-permute-start.41 = (bf16[320,4480]{1,0:T(8,128)(2,1)S(1)}, bf16[320,4480]{1,0:T(8,128)(2,1)S(1)}, u32[]{:S(2)}, u32[]{:S(2)}) collective-permute-start(bf16[320,4480]{1,0:T(8,128)(2,1)S(1)} %collective-permute-done.39.a), channel_id=1, source_target_pairs={{0,1},{1,0},{2,3},{3,2},{4,5},{5,4},{6,7},{7,6}} | collective-permute-start | bytes 8601608 | tf_op jit(solution)/shard_map/ppermute | solution.py:96
  793.9 45.4 %collective-permute-start.62 = (bf16[672,1280]{1,0:T(8,128)(2,1)}, bf16[672,1280]{1,0:T(8,128)(2,1)}, u32[]{:S(2)}, u32[]{:S(2)}) collective-permute-start(bf16[672,1280]{1,0:T(8,128)(2,1)} %collective-permute-done.60.a), channel_id=1, source_target_pairs={{0,1},{1,0},{2,3},{3,2},{4,5},{5,4},{6,7},{7,6}} | collective-permute-start | bytes 5160968 | tf_op jit(solution)/shard_map/ppermute | solution.py:96
  794.4 49.8 %collective-permute-start.58 = (bf16[336,1280]{1,0:T(8,128)(2,1)}, bf16[336,1280]{1,0:T(8,128)(2,1)}, u32[]{:S(2)}, u32[]{:S(2)}) collective-permute-start(bf16[336,1280]{1,0:T(8,128)(2,1)} %get-tuple-element.87), channel_id=1, source_target_pairs={{0,1},{1,0},{2,3},{3,2},{4,5},{5,4},{6,7},{7,6}} | collective-permute-start | bytes 2580488 | tf_op jit(solution)/shard_map/ppermute | solution.py:96
  794.4 49.8 %collective-permute-start.59 = (bf16[336,1280]{1,0:T(8,128)(2,1)}, bf16[336,1280]{1,0:T(8,128)(2,1)}, u32[]{:S(2)}, u32[]{:S(2)}) collective-permute-start(bf16[336,1280]{1,0:T(8,128)(2,1)} %collective-permute-done.57.a), channel_id=1, source_target_pairs={{0,1},{1,0},{2,3},{3,2},{4,5},{5,4},{6,7},{7,6}} | collective-permute-start | bytes 2580488 | tf_op jit(solution)/shard_map/ppermute | solution.py:96
  794.9 51.9 %collective-permute-start.55 = (bf16[112,1280]{1,0:T(8,128)(2,1)}, bf16[112,1280]{1,0:T(8,128)(2,1)}, u32[]{:S(2)}, u32[]{:S(2)}) collective-permute-start(bf16[112,1280]{1,0:T(8,128)(2,1)} %get-tuple-element.86), channel_id=1, source_target_pairs={{0,1},{1,0},{2,3},{3,2},{4,5},{5,4},{6,7},{7,6}} | collective-permute-start | bytes 860168 | tf_op jit(solution)/shard_map/ppermute | solution.py:96
  799.1 47.7 %collective-permute-start.56 = (bf16[112,1280]{1,0:T(8,128)(2,1)}, bf16[112,1280]{1,0:T(8,128)(2,1)}, u32[]{:S(2)}, u32[]{:S(2)}) collective-permute-start(bf16[112,1280]{1,0:T(8,128)(2,1)} %collective-permute-done.54.a), channel_id=1, source_target_pairs={{0,1},{1,0},{2,3},{3,2},{4,5},{5,4},{6,7},{7,6}} | collective-permute-start | bytes 860168 | tf_op jit(solution)/shard_map/ppermute | solution.py:96
  (28 other events, 560.8 us)

commit v3 on v2

v3 whole, which is shorter than its diff:
```python
import math

import jax
import jax.numpy as jnp
from jax import lax
from jax.experimental import pallas as pl
from jax.experimental.pallas import tpu as pltpu
from jax.sharding import PartitionSpec as P


FAR = [(0, 2), (2, 0), (1, 3), (3, 1)]
MATE = [(0, 1), (1, 0), (2, 3), (3, 2)]
UNITS = 20

CHUNKS = [
    (0, 0, 0, 1, 1),
    (0, 0, 1, 3, 1),
    (0, 0, 4, 6, 2),
    (0, 0, 10, 10, 2),
    (0, 1, 0, 20, 4),
    (2, 0, 0, 20, 4),
    (2, 1, 0, 20, 4),
    (1, 0, 0, 20, 4),
    (1, 1, 0, 10, 2),
    (1, 1, 10, 5, 1),
    (1, 1, 15, 3, 1),
    (1, 1, 18, 2, 2),
]
EARLY = 2
LAST = len(CHUNKS) - 1

FULL = 67043328
SPARE = {"cut_early": 4 << 20, "sum_0": 4 << 20, "sum_1": 4 << 20, "cutf_2": 160 << 10, "cutf_3": 160 << 10, "place_far": 1 << 20, "place_to": 1 << 20}

ANY = pl.BlockSpec(memory_space=pl.ANY)
WHOLE = pl.BlockSpec(memory_space=pltpu.VMEM)
DMA = pltpu.SemaphoreType.DMA


def adamw(w, m, v, g):
    m = 0.9 * m + 0.1 * g
    v = 0.95 * v + 0.05 * g * g
    step = m * lax.rsqrt(v + 1e-8) + 0.1 * w
    return (w - 0.02 * step).astype(jnp.bfloat16), m, v


def me_of(d):
    return d


def far_of(d):
    return lax.rem(d + 2, 4)


def mate_of(d):
    return 3 - far_of(d)


def far_mate_of(d):
    return 3 - d


def me():
    return lax.axis_index("dp")


def in_space(x, space):
    return pltpu.with_memory_space_constraint(x, space)


def add(a, b):
    return (a.astype(jnp.float32) + b.astype(jnp.float32)).astype(jnp.bfloat16)


def move(copies, held, in_sem, out_sem):
    into = [pltpu.make_async_copy(a, held.at[j], in_sem.at[j]) for j, (a, _) in enumerate(copies)]
    out = [pltpu.make_async_copy(held.at[j], b, out_sem.at[j]) for j, (_, b) in enumerate(copies)]
    for one in into:
        one.start()
    for one, then in zip(into, out):
        one.wait()
        then.start()
    for one in out:
        one.wait()


def solution(mesh):
    def work(*arrays):
        terms, weights, m, v = (arrays[i : i + 3] for i in (0, 3, 6, 9))
        rows = [one.shape[1] // UNITS for one in m]
        cols = [one.shape[2] for one in m]
        new_w, new_m, new_v = [None] * 3, [None] * 3, [None] * 3

        def run(name, body, grid, ins, in_specs, outs, out_specs, aliases, scratch=()):
            size = sum(2 * math.prod(o.shape) for o in outs)
            return pl.pallas_call(
                body,
                out_shape=outs,
                grid=grid,
                in_specs=in_specs,
                out_specs=out_specs,
                input_output_aliases=aliases,
                scratch_shapes=scratch,
                compiler_params=pltpu.CompilerParams(vmem_limit_bytes=FULL - SPARE.get(name, 0)),
                cost_estimate=pl.CostEstimate(flops=size, bytes_accessed=size, transcendentals=0),
            )(*ins)

        def send(x, pairs, space=pltpu.HBM):
            return in_space(lax.ppermute(x, "dp", pairs), space)

        def at(w, unit, n):
            return pl.ds(pl.multiple_of(unit * rows[w], rows[w]), n * rows[w])

        def shape(w, n, kind=jax.ShapeDtypeStruct):
            return kind((n * rows[w], cols[w]), jnp.bfloat16)

        def move_scratch(w, copies, b):
            return [pltpu.VMEM((copies, b * rows[w], cols[w]), jnp.bfloat16), DMA((copies,)), DMA((copies,))]

        def term_spec(w, layer, u0, b, of):
            return pl.BlockSpec((1, 1, b * rows[w], cols[w]), lambda i: (0, layer, of(me()) * (UNITS // b) + u0 // b + i, 0))

        def full_spec(w, layer, u0, b, of):
            return pl.BlockSpec((1, b * rows[w], cols[w]), lambda i: (layer, of(me()) * (UNITS // b) + u0 // b + i, 0))

        def piece_spec(w, b):
            return pl.BlockSpec((b * rows[w], cols[w]), lambda i: (i, 0))

        def cut(k, of, tag):
            w, layer, u0, n, b = CHUNKS[k]

            def body(t, o, *scratch):
                first = of(me()) * UNITS + u0
                move([(t.at[0, layer, at(w, first + i, b)], o.at[at(w, i, b)]) for i in range(0, n, b)], *scratch)

            (one,) = run(
                f"cut{tag}_{k}", body, (), [in_space(terms[w], pltpu.HBM)], [ANY], [shape(w, n)], [ANY], {}, move_scratch(w, n // b, b)
            )
            return send(one, MATE)

        def cut_early():
            w, layer = CHUNKS[0][:2]
            pieces = [(u0, n, of) for _, _, u0, n, _ in CHUNKS[:EARLY] for of in (far_mate_of, far_of)]

            def body(t, *refs):
                sem = refs[-1]
                copies = [
                    pltpu.make_async_copy(t.at[0, layer, at(w, of(me()) * UNITS + u0, n)], to, sem.at[j])
                    for j, ((u0, n, of), to) in enumerate(zip(pieces, refs))
                ]
                for one in copies:
                    one.start()
                for one in copies:
                    one.wait()

            out = run(
                "cut_early",
                body,
                (),
                [in_space(terms[w], pltpu.HBM)],
                [ANY],
                [shape(w, n, pltpu.VMEM) for _, n, _ in pieces],
                [WHOLE] * len(pieces),
                {},
                [DMA((len(pieces),))],
            )
            return [send(out[2 * k], MATE, pltpu.VMEM) for k in range(EARLY)], out[1::2]

        def sum_early(k, got, own):
            w, _, _, n, _ = CHUNKS[k]

            def body(t, r, o):
                o[...] = add(t[...], r[...])

            grid, outs, specs = ((1,), [shape(w, n)], [piece_spec(w, n)]) if k else ((), [shape(w, n, pltpu.VMEM)], [WHOLE])
            (one,) = run(f"sum_{k}", body, grid, [in_space(own, pltpu.VMEM), got], [WHOLE] * 2, outs, specs, {})
            return send(one, FAR)

        def chip_sum(k, got):
            w, layer, u0, n, b = CHUNKS[k]

            def body(t, r, o):
                o[...] = add(t[0, 0], r[...])

            (one,) = run(
                f"sum_{k}",
                body,
                (n // b,),
                [terms[w], got],
                [term_spec(w, layer, u0, b, far_of), piece_spec(w, b)],
                [shape(w, n)],
                [piece_spec(w, b)],
                {},
            )
            return send(one, FAR)

        def update(k, mate_term, far_sum):
            w, layer, u0, n, b = CHUNKS[k]

            def body(*refs):
                t, r, f, wt, mm, vv = refs[:6]
                o, full, mo, vo = refs[-4:]
                g = t[0, 0].astype(jnp.float32) + r[...].astype(jnp.float32) + f[...].astype(jnp.float32)
                g = g.astype(jnp.bfloat16).astype(jnp.float32)
                new, mo[0], vo[0] = adamw(wt[0].astype(jnp.float32), mm[0], vv[0], g)
                o[...] = new
                full[0] = new

            moment = pl.BlockSpec((1, b * rows[w], cols[w]), lambda i: (layer, u0 // b + i, 0))
            mine = full_spec(w, layer, u0, b, me_of)
            ins = [terms[w], mate_term, far_sum, weights[w], m[w], v[w]]
            specs = [term_spec(w, layer, u0, b, me_of), piece_spec(w, b), piece_spec(w, b), mine, moment, moment]
            aliases = {}
            if new_w[w] is not None:
                ins += [new_w[w], new_m[w], new_v[w]]
                specs += [ANY] * 3
                aliases = {6: 1, 7: 2, 8: 3}
            outs = [shape(w, n), *(jax.ShapeDtypeStruct(a.shape, a.dtype) for a in (weights[w], m[w], v[w]))]
            out, new_w[w], new_m[w], new_v[w] = run(
                f"adam_{k}", body, (n // b,), ins, specs, outs, [piece_spec(w, b), mine, moment, moment], aliases
            )
            return send(out, FAR), send(out, MATE)

        def place(k, name, pieces, owners):
            w, layer, u0, n, b = CHUNKS[k]

            def body(*refs):
                count = len(pieces)
                full, d = refs[count + 1], me()
                copies = [
                    (one.at[at(w, i, b)], full.at[layer, at(w, of(d) * UNITS + u0 + i, b)])
                    for i in range(0, n, b)
                    for one, of in zip(refs[:count], owners)
                ]
                move(copies, *refs[count + 2 :])

            (new_w[w],) = run(
                name,
                body,
                (),
                [*pieces, new_w[w]],
                [ANY] * (len(pieces) + 1),
                [jax.ShapeDtypeStruct(weights[w].shape, jnp.bfloat16)],
                [ANY],
                {len(pieces): 0},
                move_scratch(w, n // b * len(pieces), b),
            )

        def place_last(piece):
            w, layer, u0, n, _ = CHUNKS[LAST]

            def body(one, _, full, sem):
                copy = pltpu.make_async_copy(one, full.at[layer, at(w, far_mate_of(me()) * UNITS + u0, n)], sem)
                copy.start()
                copy.wait()

            like = jax.ShapeDtypeStruct(weights[w].shape, jnp.bfloat16)
            (new_w[w],) = run("place_to", body, (), [piece, new_w[w]], [WHOLE, ANY], [like], [ANY], {1: 0}, [DMA])

        count = len(CHUNKS)
        got, far_sum, mate_term, out = ([None] * count for _ in range(4))
        got[:EARLY], own = cut_early()
        for k in range(EARLY):
            far_sum[k] = sum_early(k, got[k], own[k])
        got[EARLY] = cut(EARLY, far_mate_of, "f")
        for k in range(EARLY, count):
            if k + 1 < count:
                got[k + 1] = cut(k + 1, far_mate_of, "f")
            far_sum[k] = chip_sum(k, got[k])
        for k in range(count):
            mate_term[k] = cut(k, mate_of, "m")
        for k in range(count):
            out[k] = update(k, mate_term[k], far_sum[k])
        place(LAST, "place_own", out[LAST][1:], [mate_of])
        for k in range(LAST):
            forward = send(out[k][0], MATE)
            place(k, f"place_{k}", [*out[k], forward], [far_of, mate_of, far_mate_of])
        forward = send(out[LAST][0], MATE, pltpu.VMEM)
        place(LAST, "place_far", out[LAST][:1], [far_of])
        place_last(forward)
        return (*new_w, *new_m, *new_v)

    all_of, cut_of = P(None, None, None), P(None, "dp", None)
    whole = jax.shard_map(
        work,
        mesh=mesh,
        in_specs=(P(("rep", "dp"), None, None, None),) * 3 + (all_of,) * 3 + (cut_of,) * 6,
        out_specs=(P("rep", None, None),) * 3 + (P("rep", "dp", None),) * 6,
        check_vma=False,
    )
    shapes = [(2, 1280, 4480), (2, 1280, 4480), (2, 4480, 1280)]
    jax.eval_shape(
        whole,
        *(jax.ShapeDtypeStruct((8, *s), jnp.bfloat16) for s in shapes),
        *(jax.ShapeDtypeStruct(s, jnp.bfloat16) for s in shapes),
        *(jax.ShapeDtypeStruct(s, jnp.float32) for s in shapes + shapes),
    )
    return whole
```

time: 851 us -> 883 us (1.038)
  Pallas kernels: 246 us -> 263 us
  waiting for transfers between devices: 564 us -> 581 us
    pallas_call x55 -> x61, Pallas kernels: 246 us -> 263 us  [run(): pl.pallas_call(body, out_shape=outs, grid=grid, in_specs=in_specs, out_sp...]
    ppermute x66 -> x72, waiting for transfers between devices: 564 us -> 581 us  [send(): return in_space(lax.ppermute(x, 'dp', pairs), space)]
    ppermute x66 -> x72, starting transfers between devices: 36 us -> 30.6 us  [send(): return in_space(lax.ppermute(x, 'dp', pairs), space)]
  transfers between devices with their start and end apart: 66 -> 72, of which waited for: 17 -> 22; matrix products, arithmetic and copies ran while one was open for 0% -> 0% of each run, Pallas kernels for 28% -> 29%
where the time goes in v3:
time: 883 us; the launch traced here: 881 us
  waiting for transfers between devices  581 us (66%)
  Pallas kernels  263 us (30%)
  starting transfers between devices  30.6 us (3%)
    ppermute x72, waiting for transfers between devices, send(): return in_space(lax.ppermute(x, 'dp', pairs), space)  581 us
    pallas_call x61, Pallas kernels, run(): pl.pallas_call(body, out_shape=outs, grid=grid, in_specs=in_specs, out_sp...  263 us
    ppermute x72, starting transfers between devices, send(): return in_space(lax.ppermute(x, 'dp', pairs), space)  30.6 us
  transfers between devices with their start and end apart: 72, of which 22 were waited for; matrix products, arithmetic and copies ran while one was open for 0% of the time, Pallas kernels for 29%

profile of v3, /device:TPU:0, one launch (start us, length us, event | category | flops | bytes accessed | tf_op | source)
XLA Modules:
  0.0 880.7 jit_solution(10401529462263316829)
XLA Ops:
  20.2 2.9 collective-permute-start.14
  50.5 2.8 shard_map.216
  56.1 4.6 shard_map.202
  60.7 5.3 collective-permute-done.35.refs_2_
  66.3 4.0 shard_map.219
  74.7 4.4 collective-permute-done.24.refs_0_
  87.2 3.2 shard_map.195
  93.4 2.7 shard_map.188
  96.2 17.0 %collective-permute-done.8.refs_2_ = bf16[96,4480]{1,0:T(8,128)(2,1)} collective-permute-done((bf16[96,4480]{1,0:T(8,128)(2,1)}, bf16[96,4480]{1,0:T(8,128)(2,1)}, u32[]{:S(2)}, u32[]{:S(2)}) %collective-permute-start.8) | collective-permute-done | bytes 860192 | tf_op jit(solution)/shard_map/ppermute | solution.py:109
  113.2 6.6 shard_map.203
  120.4 4.5 shard_map.222
  124.8 16.8 %collective-permute-done.21.refs_0_ = bf16[96,4480]{1,0:T(8,128)(2,1)} collective-permute-done((bf16[96,4480]{1,0:T(8,128)(2,1)}, bf16[96,4480]{1,0:T(8,128)(2,1)}, u32[]{:S(2)}, u32[]{:S(2)}) %collective-permute-start.21) | collective-permute-done | bytes 860192 | tf_op jit(solution)/shard_map/ppermute | solution.py:109
  142.0 4.5 shard_map.192
  151.0 2.7 shard_map.242
  156.9 19.4 %collective-permute-done.41.refs_2_ = bf16[160,4480]{1,0:T(8,128)(2,1)} collective-permute-done((bf16[160,4480]{1,0:T(8,128)(2,1)}, bf16[160,4480]{1,0:T(8,128)(2,1)}, u32[]{:S(2)}, u32[]{:S(2)}) %collective-permute-start.41) | collective-permute-done | bytes 1433632 | tf_op jit(solution)/shard_map/ppermute | solution.py:109
  176.3 2.7 shard_map.239
  179.0 26.7 %collective-permute-done.5.refs_2_ = bf16[160,4480]{1,0:T(8,128)(2,1)} collective-permute-done((bf16[160,4480]{1,0:T(8,128)(2,1)}, bf16[160,4480]{1,0:T(8,128)(2,1)}, u32[]{:S(2)}, u32[]{:S(2)}) %collective-permute-start.5) | collective-permute-done | bytes 1433632 | tf_op jit(solution)/shard_map/ppermute | solution.py:109
  205.7 2.7 shard_map.238
  208.9 5.9 shard_map.225
  215.1 10.0 %shard_map.204 = (bf16[160,4480]{1,0:T(8,128)(2,1)}, bf16[2,1280,4480]{2,1,0:T(8,128)(2,1)}, f32[2,320,4480]{2,1,0:T(8,128)}, f32[2,320,4480]{2,1,0:T(8,128)}) custom-call(bf16[1,2,1280,4480]{3,2,1,0:T(8,128)(2,1)} %refs_0_.16, bf16[160,4480]{1,0:T(8,128)(2,1)} %collective-permute-done.3.refs_1_, ...), custom_call_target="tpu_custom_call", output_to_operand_aliasing={{1}: (6, {}), {2}: (7, {}), {3}: (8, {})} | custom-call | flops 35840000 | bytes 35840000 | tf_op jit(solution)/shard_map/pallas_call | solution.py:96
  226.9 5.9 shard_map.189
  233.1 5.9 shard_map.243
  240.7 5.9 shard_map.240
  246.8 64.0 %collective-permute-done.18.refs_0_ = bf16[160,4480]{1,0:T(8,128)(2,1)} collective-permute-done((bf16[160,4480]{1,0:T(8,128)(2,1)}, bf16[160,4480]{1,0:T(8,128)(2,1)}, u32[]{:S(2)}, u32[]{:S(2)}) %collective-permute-start.18) | collective-permute-done | bytes 1433632 | tf_op jit(solution)/shard_map/ppermute | solution.py:109
  311.4 16.5 %shard_map.226 = (bf16[320,4480]{1,0:T(8,128)(2,1)}, bf16[2,1280,4480]{2,1,0:T(8,128)(2,1)}, f32[2,320,4480]{2,1,0:T(8,128)}, f32[2,320,4480]{2,1,0:T(8,128)}) custom-call(bf16[1,2,1280,4480]{3,2,1,0:T(8,128)(2,1)} %refs_0_.21, bf16[320,4480]{1,0:T(8,128)(2,1)} %collective-permute-done.42.refs_1_, bf16[320,4480]{1,0:T(8,128)(2,1)} %collective-permute-done.44.refs_2_, ...), custom_call_target="tpu_custom_call" | custom-call | flops 37273600 | bytes 37273600 | tf_op jit(solution)/shard_map/pallas_call | solution.py:96
  327.9 10.0 %shard_map.227 = (bf16[160,4480]{1,0:T(8,128)(2,1)}, bf16[2,1280,4480]{2,1,0:T(8,128)(2,1)}, f32[2,320,4480]{2,1,0:T(8,128)}, f32[2,320,4480]{2,1,0:T(8,128)}) custom-call(bf16[1,2,1280,4480]{3,2,1,0:T(8,128)(2,1)} %refs_0_.21, bf16[160,4480]{1,0:T(8,128)(2,1)} %collective-permute-done.39.refs_1_, ...), custom_call_target="tpu_custom_call", output_to_operand_aliasing={{1}: (6, {}), {2}: (7, {}), {3}: (8, {})} | custom-call | flops 35840000 | bytes 35840000 | tf_op jit(solution)/shard_map/pallas_call | solution.py:96
  337.9 6.7 shard_map.228
  344.6 4.6 shard_map.229
  349.3 3.2 shard_map.230
  352.5 19.8 %collective-permute-done.2.refs_2_ = bf16[320,4480]{1,0:T(8,128)(2,1)} collective-permute-done((bf16[320,4480]{1,0:T(8,128)(2,1)}, bf16[320,4480]{1,0:T(8,128)(2,1)}, u32[]{:S(2)}, u32[]{:S(2)}) %collective-permute-start.2) | collective-permute-done | bytes 2867232 | tf_op jit(solution)/shard_map/ppermute | solution.py:109
  374.3 59.4 %collective-permute-done.65.refs_2_ = bf16[1120,1280]{1,0:T(8,128)(2,1)} collective-permute-done((bf16[1120,1280]{1,0:T(8,128)(2,1)}, bf16[1120,1280]{1,0:T(8,128)(2,1)}, u32[]{:S(2)}, u32[]{:S(2)}) %collective-permute-start.65) | collective-permute-done | bytes 2867232 | tf_op jit(solution)/shard_map/ppermute | solution.py:109
  434.0 61.1 %collective-permute-done.62.refs_2_ = bf16[1120,1280]{1,0:T(8,128)(2,1)} collective-permute-done((bf16[1120,1280]{1,0:T(8,128)(2,1)}, bf16[1120,1280]{1,0:T(8,128)(2,1)}, u32[]{:S(2)}, u32[]{:S(2)}) %collective-permute-start.62) | collective-permute-done | bytes 2867232 | tf_op jit(solution)/shard_map/ppermute | solution.py:109
  495.5 5.7 collective-permute-done.45.refs_0_
  501.2 100.5 %collective-permute-done.47.refs_0_ = bf16[48,4480]{1,0:T(8,128)(2,1)S(1)} collective-permute-done((bf16[48,4480]{1,0:T(8,128)(2,1)}, bf16[48,4480]{1,0:T(8,128)(2,1)S(1)}, u32[]{:S(2)}, u32[]{:S(2)}) %collective-permute-start.47) | collective-permute-done | bytes 430112 | tf_op jit(solution)/shard_map/ppermute | solution.py:109
  604.4 14.7 %collective-permute-done.50.refs_0_ = bf16[80,4480]{1,0:T(8,128)(2,1)} collective-permute-done((bf16[80,4480]{1,0:T(8,128)(2,1)}, bf16[80,4480]{1,0:T(8,128)(2,1)}, u32[]{:S(2)}, u32[]{:S(2)}) %collective-permute-start.50) | collective-permute-done | bytes 716832 | tf_op jit(solution)/shard_map/ppermute | solution.py:109
  619.7 5.5 collective-permute-done.49.refs_2_
  626.0 16.5 %shard_map.205 = (bf16[320,4480]{1,0:T(8,128)(2,1)}, bf16[2,1280,4480]{2,1,0:T(8,128)(2,1)}, f32[2,320,4480]{2,1,0:T(8,128)}, f32[2,320,4480]{2,1,0:T(8,128)}) custom-call(bf16[1,2,1280,4480]{3,2,1,0:T(8,128)(2,1)} %refs_0_.16, bf16[320,4480]{1,0:T(8,128)(2,1)} %collective-permute-done.refs_1_, ...), custom_call_target="tpu_custom_call", output_to_operand_aliasing={{1}: (6, {}), {2}: (7, {}), {3}: (8, {})} | custom-call | flops 37273600 | bytes 37273600 | tf_op jit(solution)/shard_map/pallas_call | solution.py:96
  642.9 16.6 %shard_map.244 = (bf16[1120,1280]{1,0:T(8,128)(2,1)}, bf16[2,4480,1280]{2,1,0:T(8,128)(2,1)}, f32[2,1120,1280]{2,1,0:T(8,128)}, f32[2,1120,1280]{2,1,0:T(8,128)}) custom-call(bf16[1,2,4480,1280]{3,2,1,0:T(8,128)(2,1)} %refs_0_.23, bf16[1120,1280]{1,0:T(8,128)(2,1)} %collective-permute-done.63.refs_1_, bf16[1120,1280]{1,0:T(8,128)(2,1)} %collective-permute-done.65.refs_2_, ...), custom_call_target="tpu_custom_call" | custom-call | flops 37273600 | bytes 37273600 | tf_op jit(solution)/shard_map/pallas_call | solution.py:96
  661.3 16.6 %shard_map.245 = (bf16[1120,1280]{1,0:T(8,128)(2,1)}, bf16[2,4480,1280]{2,1,0:T(8,128)(2,1)}, f32[2,1120,1280]{2,1,0:T(8,128)}, f32[2,1120,1280]{2,1,0:T(8,128)}) custom-call(bf16[1,2,4480,1280]{3,2,1,0:T(8,128)(2,1)} %refs_0_.23, bf16[1120,1280]{1,0:T(8,128)(2,1)} %collective-permute-done.60.refs_1_, ...), custom_call_target="tpu_custom_call", output_to_operand_aliasing={{1}: (6, {}), {2}: (7, {}), {3}: (8, {})} | custom-call | flops 37273600 | bytes 37273600 | tf_op jit(solution)/shard_map/pallas_call | solution.py:96
  678.2 29.7 %collective-permute-done.15.refs_0_ = bf16[320,4480]{1,0:T(8,128)(2,1)} collective-permute-done((bf16[320,4480]{1,0:T(8,128)(2,1)}, bf16[320,4480]{1,0:T(8,128)(2,1)}, u32[]{:S(2)}, u32[]{:S(2)}) %collective-permute-start.15) | collective-permute-done | bytes 2867232 | tf_op jit(solution)/shard_map/ppermute | solution.py:109
  708.4 60.9 %collective-permute-done.69.refs_0_ = bf16[1120,1280]{1,0:T(8,128)(2,1)} collective-permute-done((bf16[1120,1280]{1,0:T(8,128)(2,1)}, bf16[1120,1280]{1,0:T(8,128)(2,1)}, u32[]{:S(2)}, u32[]{:S(2)}) %collective-permute-start.69) | collective-permute-done | bytes 2867232 | tf_op jit(solution)/shard_map/ppermute | solution.py:109
  769.3 60.6 %collective-permute-done.66.refs_0_ = bf16[1120,1280]{1,0:T(8,128)(2,1)} collective-permute-done((bf16[1120,1280]{1,0:T(8,128)(2,1)}, bf16[1120,1280]{1,0:T(8,128)(2,1)}, u32[]{:S(2)}, u32[]{:S(2)}) %collective-permute-start.66) | collective-permute-done | bytes 2867232 | tf_op jit(solution)/shard_map/ppermute | solution.py:109
  837.0 3.9 shard_map.209.refs_3_
  842.6 6.7 shard_map.232.refs_3_
  849.3 3.9 shard_map.233.refs_3_
  860.6 6.7 shard_map.210
  867.3 6.7 shard_map.246.refs_3_
  874.0 6.7 shard_map.247
  (181 shorter events, 105.0 us)
Async XLA Ops:
  6.7 22.6 %collective-permute-start.34 = (bf16[48,4480]{1,0:T(8,128)(2,1)}, bf16[48,4480]{1,0:T(8,128)(2,1)}, u32[]{:S(2)}, u32[]{:S(2)}) collective-permute-start(bf16[48,4480]{1,0:T(8,128)(2,1)} %shard_map.215), channel_id=1, source_target_pairs={{0,1},{1,0},{2,3},{3,2},{4,5},{5,4},{6,7},{7,6}} | collective-permute-start | bytes 1290248 | tf_op jit(solution)/shard_map/ppermute | solution.py:109
  27.4 23.1 %collective-permute-start.37 = (bf16[80,4480]{1,0:T(8,128)(2,1)}, bf16[80,4480]{1,0:T(8,128)(2,1)}, u32[]{:S(2)}, u32[]{:S(2)}) collective-permute-start(bf16[80,4480]{1,0:T(8,128)(2,1)} %shard_map.218), channel_id=1, source_target_pairs={{0,1},{1,0},{2,3},{3,2},{4,5},{5,4},{6,7},{7,6}} | collective-permute-start | bytes 2150408 | tf_op jit(solution)/shard_map/ppermute | solution.py:109
  29.3 24.1 %collective-permute-start.36 = (bf16[80,4480]{1,0:T(8,128)(2,1)}, bf16[80,4480]{1,0:T(8,128)(2,1)}, u32[]{:S(2)}, u32[]{:S(2)}) collective-permute-start(bf16[80,4480]{1,0:T(8,128)(2,1)} %shard_map.217), channel_id=1, source_target_pairs={{0,1},{1,0},{2,3},{3,2},{4,5},{5,4},{6,7},{7,6}} | collective-permute-start | bytes 2150408 | tf_op jit(solution)/shard_map/ppermute | solution.py:109
  38.3 28.0 %collective-permute-start.7 = (bf16[96,4480]{1,0:T(8,128)(2,1)}, bf16[96,4480]{1,0:T(8,128)(2,1)}, u32[]{:S(2)}, u32[]{:S(2)}) collective-permute-start(bf16[96,4480]{1,0:T(8,128)(2,1)} %shard_map.194), channel_id=1, source_target_pairs={{0,1},{1,0},{2,3},{3,2},{4,5},{5,4},{6,7},{7,6}} | collective-permute-start | bytes 2580488 | tf_op jit(solution)/shard_map/ppermute | solution.py:109
  48.0 35.9 %collective-permute-start.40 = (bf16[160,4480]{1,0:T(8,128)(2,1)}, bf16[160,4480]{1,0:T(8,128)(2,1)}, u32[]{:S(2)}, u32[]{:S(2)}) collective-permute-start(bf16[160,4480]{1,0:T(8,128)(2,1)} %shard_map.221), channel_id=1, source_target_pairs={{0,1},{1,0},{2,3},{3,2},{4,5},{5,4},{6,7},{7,6}} | collective-permute-start | bytes 4300808 | tf_op jit(solution)/shard_map/ppermute | solution.py:109
  55.9 30.8 %collective-permute-start.39 = (bf16[160,4480]{1,0:T(8,128)(2,1)}, bf16[160,4480]{1,0:T(8,128)(2,1)}, u32[]{:S(2)}, u32[]{:S(2)}) collective-permute-start(bf16[160,4480]{1,0:T(8,128)(2,1)} %shard_map.220), channel_id=1, source_target_pairs={{0,1},{1,0},{2,3},{3,2},{4,5},{5,4},{6,7},{7,6}} | collective-permute-start | bytes 4300808 | tf_op jit(solution)/shard_map/ppermute | solution.py:109
  70.3 22.8 %collective-permute-start.38 = (bf16[80,4480]{1,0:T(8,128)(2,1)}, bf16[80,4480]{1,0:T(8,128)(2,1)}, u32[]{:S(2)}, u32[]{:S(2)}) collective-permute-start(bf16[80,4480]{1,0:T(8,128)(2,1)} %shard_map.219), channel_id=1, source_target_pairs={{0,2},{2,0},{1,3},{3,1},{4,6},{6,4},{5,7},{7,5}} | collective-permute-start | bytes 2150408 | tf_op jit(solution)/shard_map/ppermute | solution.py:109
  79.1 71.8 %collective-permute-start.43 = (bf16[320,4480]{1,0:T(8,128)(2,1)}, bf16[320,4480]{1,0:T(8,128)(2,1)}, u32[]{:S(2)}, u32[]{:S(2)}) collective-permute-start(bf16[320,4480]{1,0:T(8,128)(2,1)} %shard_map.224), channel_id=1, source_target_pairs={{0,1},{1,0},{2,3},{3,2},{4,5},{5,4},{6,7},{7,6}} | collective-permute-start | bytes 8601608 | tf_op jit(solution)/shard_map/ppermute | solution.py:109
  83.9 35.9 %collective-permute-start.3 = (bf16[160,4480]{1,0:T(8,128)(2,1)}, bf16[160,4480]{1,0:T(8,128)(2,1)}, u32[]{:S(2)}, u32[]{:S(2)}) collective-permute-start(bf16[160,4480]{1,0:T(8,128)(2,1)} %shard_map.190), channel_id=1, source_target_pairs={{0,1},{1,0},{2,3},{3,2},{4,5},{5,4},{6,7},{7,6}} | collective-permute-start | bytes 4300808 | tf_op jit(solution)/shard_map/ppermute | solution.py:109
  86.7 67.0 %collective-permute-start.42 = (bf16[320,4480]{1,0:T(8,128)(2,1)}, bf16[320,4480]{1,0:T(8,128)(2,1)}, u32[]{:S(2)}, u32[]{:S(2)}) collective-permute-start(bf16[320,4480]{1,0:T(8,128)(2,1)} %shard_map.223), channel_id=1, source_target_pairs={{0,1},{1,0},{2,3},{3,2},{4,5},{5,4},{6,7},{7,6}} | collective-permute-start | bytes 8601608 | tf_op jit(solution)/shard_map/ppermute | solution.py:109
  96.1 112.3 %collective-permute-start.1 = (bf16[320,4480]{1,0:T(8,128)(2,1)}, bf16[320,4480]{1,0:T(8,128)(2,1)}, u32[]{:S(2)}, u32[]{:S(2)}) collective-permute-start(bf16[320,4480]{1,0:T(8,128)(2,1)} %shard_map.188), channel_id=1, source_target_pairs={{0,1},{1,0},{2,3},{3,2},{4,5},{5,4},{6,7},{7,6}} | collective-permute-start | bytes 8601608 | tf_op jit(solution)/shard_map/ppermute | solution.py:109
  119.8 21.8 %collective-permute-start.21 = (bf16[96,4480]{1,0:T(8,128)(2,1)}, bf16[96,4480]{1,0:T(8,128)(2,1)}, u32[]{:S(2)}, u32[]{:S(2)}) collective-permute-start(bf16[96,4480]{1,0:T(8,128)(2,1)} %get-tuple-element.79), channel_id=1, source_target_pairs={{0,2},{2,0},{1,3},{3,1},{4,6},{6,4},{5,7},{7,5}} | collective-permute-start | bytes 2580488 | tf_op jit(solution)/shard_map/ppermute | solution.py:109
  120.2 26.3 %collective-permute-start.22 = (bf16[96,4480]{1,0:T(8,128)(2,1)}, bf16[96,4480]{1,0:T(8,128)(2,1)}, u32[]{:S(2)}, u32[]{:S(2)}) collective-permute-start(bf16[96,4480]{1,0:T(8,128)(2,1)} %get-tuple-element.79), channel_id=1, source_target_pairs={{0,1},{1,0},{2,3},{3,2},{4,5},{5,4},{6,7},{7,6}} | collective-permute-start | bytes 2580488 | tf_op jit(solution)/shard_map/ppermute | solution.py:109
  141.7 34.6 %collective-permute-start.41 = (bf16[160,4480]{1,0:T(8,128)(2,1)}, bf16[160,4480]{1,0:T(8,128)(2,1)}, u32[]{:S(2)}, u32[]{:S(2)}) collective-permute-start(bf16[160,4480]{1,0:T(8,128)(2,1)} %shard_map.222), channel_id=1, source_target_pairs={{0,2},{2,0},{1,3},{3,1},{4,6},{6,4},{5,7},{7,5}} | collective-permute-start | bytes 4300808 | tf_op jit(solution)/shard_map/ppermute | solution.py:109
  146.5 59.2 %collective-permute-start.5 = (bf16[160,4480]{1,0:T(8,128)(2,1)}, bf16[160,4480]{1,0:T(8,128)(2,1)}, u32[]{:S(2)}, u32[]{:S(2)}) collective-permute-start(bf16[160,4480]{1,0:T(8,128)(2,1)} %shard_map.192), channel_id=1, source_target_pairs={{0,2},{2,0},{1,3},{3,1},{4,6},{6,4},{5,7},{7,5}} | collective-permute-start | bytes 4300808 | tf_op jit(solution)/shard_map/ppermute | solution.py:109
  150.9 63.9 %collective-permute-start = (bf16[320,4480]{1,0:T(8,128)(2,1)}, bf16[320,4480]{1,0:T(8,128)(2,1)}, u32[]{:S(2)}, u32[]{:S(2)}) collective-permute-start(bf16[320,4480]{1,0:T(8,128)(2,1)} %shard_map.187), channel_id=1, source_target_pairs={{0,1},{1,0},{2,3},{3,2},{4,5},{5,4},{6,7},{7,6}} | collective-permute-start | bytes 8601608 | tf_op jit(solution)/shard_map/ppermute | solution.py:109
  153.7 61.4 %collective-permute-start.64 = (bf16[1120,1280]{1,0:T(8,128)(2,1)}, bf16[1120,1280]{1,0:T(8,128)(2,1)}, u32[]{:S(2)}, u32[]{:S(2)}) collective-permute-start(bf16[1120,1280]{1,0:T(8,128)(2,1)} %shard_map.242), channel_id=1, source_target_pairs={{0,1},{1,0},{2,3},{3,2},{4,5},{5,4},{6,7},{7,6}} | collective-permute-start | bytes 8601608 | tf_op jit(solution)/shard_map/ppermute | solution.py:109
  176.3 48.8 %collective-permute-start.63 = (bf16[1120,1280]{1,0:T(8,128)(2,1)}, bf16[1120,1280]{1,0:T(8,128)(2,1)}, u32[]{:S(2)}, u32[]{:S(2)}) collective-permute-start(bf16[1120,1280]{1,0:T(8,128)(2,1)} %shard_map.241), channel_id=1, source_target_pairs={{0,1},{1,0},{2,3},{3,2},{4,5},{5,4},{6,7},{7,6}} | collective-permute-start | bytes 8601608 | tf_op jit(solution)/shard_map/ppermute | solution.py:109
  205.7 27.1 %collective-permute-start.61 = (bf16[1120,1280]{1,0:T(8,128)(2,1)}, bf16[1120,1280]{1,0:T(8,128)(2,1)}, u32[]{:S(2)}, u32[]{:S(2)}) collective-permute-start(bf16[1120,1280]{1,0:T(8,128)(2,1)} %shard_map.239), channel_id=1, source_target_pairs={{0,1},{1,0},{2,3},{3,2},{4,5},{5,4},{6,7},{7,6}} | collective-permute-start | bytes 8601608 | tf_op jit(solution)/shard_map/ppermute | solution.py:109
  208.4 30.6 %collective-permute-start.60 = (bf16[1120,1280]{1,0:T(8,128)(2,1)}, bf16[1120,1280]{1,0:T(8,128)(2,1)}, u32[]{:S(2)}, u32[]{:S(2)}) collective-permute-start(bf16[1120,1280]{1,0:T(8,128)(2,1)} %shard_map.238), channel_id=1, source_target_pairs={{0,1},{1,0},{2,3},{3,2},{4,5},{5,4},{6,7},{7,6}} | collective-permute-start | bytes 8601608 | tf_op jit(solution)/shard_map/ppermute | solution.py:109
  214.8 96.0 %collective-permute-start.44 = (bf16[320,4480]{1,0:T(8,128)(2,1)}, bf16[320,4480]{1,0:T(8,128)(2,1)}, u32[]{:S(2)}, u32[]{:S(2)}) collective-permute-start(bf16[320,4480]{1,0:T(8,128)(2,1)} %shard_map.225), channel_id=1, source_target_pairs={{0,2},{2,0},{1,3},{3,1},{4,6},{6,4},{5,7},{7,5}} | collective-permute-start | bytes 8601608 | tf_op jit(solution)/shard_map/ppermute | solution.py:109
  215.1 31.4 %collective-permute-start.23 = (bf16[96,4480]{1,0:T(8,128)(2,1)}, bf16[96,4480]{1,0:T(8,128)(2,1)}, u32[]{:S(2)}, u32[]{:S(2)}) collective-permute-start(bf16[96,4480]{1,0:T(8,128)(2,1)} %collective-permute-done.21.refs_0_), channel_id=1, source_target_pairs={{0,1},{1,0},{2,3},{3,2},{4,5},{5,4},{6,7},{7,6}} | collective-permute-start | bytes 2580488 | tf_op jit(solution)/shard_map/ppermute | solution.py:109
  225.1 85.7 %collective-permute-start.18 = (bf16[160,4480]{1,0:T(8,128)(2,1)}, bf16[160,4480]{1,0:T(8,128)(2,1)}, u32[]{:S(2)}, u32[]{:S(2)}) collective-permute-start(bf16[160,4480]{1,0:T(8,128)(2,1)} %get-tuple-element.78), channel_id=1, source_target_pairs={{0,2},{2,0},{1,3},{3,1},{4,6},{6,4},{5,7},{7,5}} | collective-permute-start | bytes 4300808 | tf_op jit(solution)/shard_map/ppermute | solution.py:109
  232.7 139.5 %collective-permute-start.2 = (bf16[320,4480]{1,0:T(8,128)(2,1)}, bf16[320,4480]{1,0:T(8,128)(2,1)}, u32[]{:S(2)}, u32[]{:S(2)}) collective-permute-start(bf16[320,4480]{1,0:T(8,128)(2,1)} %shard_map.189), channel_id=1, source_target_pairs={{0,2},{2,0},{1,3},{3,1},{4,6},{6,4},{5,7},{7,5}} | collective-permute-start | bytes 8601608 | tf_op jit(solution)/shard_map/ppermute | solution.py:109
  238.9 194.8 %collective-permute-start.65 = (bf16[1120,1280]{1,0:T(8,128)(2,1)}, bf16[1120,1280]{1,0:T(8,128)(2,1)}, u32[]{:S(2)}, u32[]{:S(2)}) collective-permute-start(bf16[1120,1280]{1,0:T(8,128)(2,1)} %shard_map.243), channel_id=1, source_target_pairs={{0,2},{2,0},{1,3},{3,1},{4,6},{6,4},{5,7},{7,5}} | collective-permute-start | bytes 8601608 | tf_op jit(solution)/shard_map/ppermute | solution.py:109
  246.5 248.6 %collective-permute-start.62 = (bf16[1120,1280]{1,0:T(8,128)(2,1)}, bf16[1120,1280]{1,0:T(8,128)(2,1)}, u32[]{:S(2)}, u32[]{:S(2)}) collective-permute-start(bf16[1120,1280]{1,0:T(8,128)(2,1)} %shard_map.240), channel_id=1, source_target_pairs={{0,2},{2,0},{1,3},{3,1},{4,6},{6,4},{5,7},{7,5}} | collective-permute-start | bytes 8601608 | tf_op jit(solution)/shard_map/ppermute | solution.py:109
  310.8 41.6 %collective-permute-start.19 = (bf16[160,4480]{1,0:T(8,128)(2,1)}, bf16[160,4480]{1,0:T(8,128)(2,1)}, u32[]{:S(2)}, u32[]{:S(2)}) collective-permute-start(bf16[160,4480]{1,0:T(8,128)(2,1)} %get-tuple-element.78), channel_id=1, source_target_pairs={{0,1},{1,0},{2,3},{3,2},{4,5},{5,4},{6,7},{7,6}} | collective-permute-start | bytes 4300808 | tf_op jit(solution)/shard_map/ppermute | solution.py:109
  310.8 61.7 %collective-permute-start.20 = (bf16[160,4480]{1,0:T(8,128)(2,1)}, bf16[160,4480]{1,0:T(8,128)(2,1)}, u32[]{:S(2)}, u32[]{:S(2)}) collective-permute-start(bf16[160,4480]{1,0:T(8,128)(2,1)} %collective-permute-done.18.refs_0_), channel_id=1, source_target_pairs={{0,1},{1,0},{2,3},{3,2},{4,5},{5,4},{6,7},{7,6}} | collective-permute-start | bytes 4300808 | tf_op jit(solution)/shard_map/ppermute | solution.py:109
  352.5 142.7 %collective-permute-start.59 = (bf16[32,4480]{1,0:T(8,128)(2,1)}, bf16[32,4480]{1,0:T(8,128)(2,1)S(1)}, u32[]{:S(2)}, u32[]{:S(2)}) collective-permute-start(bf16[32,4480]{1,0:T(8,128)(2,1)} %get-tuple-element.95), channel_id=1, source_target_pairs={{0,1},{1,0},{2,3},{3,2},{4,5},{5,4},{6,7},{7,6}} | collective-permute-start | bytes 860168 | tf_op jit(solution)/shard_map/ppermute | solution.py:109
  372.3 128.9 %collective-permute-start.45 = (bf16[32,4480]{1,0:T(8,128)(2,1)}, bf16[32,4480]{1,0:T(8,128)(2,1)S(1)}, u32[]{:S(2)}, u32[]{:S(2)}) collective-permute-start(bf16[32,4480]{1,0:T(8,128)(2,1)} %get-tuple-element.95), channel_id=1, source_target_pairs={{0,2},{2,0},{1,3},{3,1},{4,6},{6,4},{5,7},{7,5}} | collective-permute-start | bytes 860168 | tf_op jit(solution)/shard_map/ppermute | solution.py:109
  372.6 246.5 %collective-permute-start.53 = (bf16[160,4480]{1,0:T(8,128)(2,1)}, bf16[160,4480]{1,0:T(8,128)(2,1)}, u32[]{:S(2)}, u32[]{:S(2)}) collective-permute-start(bf16[160,4480]{1,0:T(8,128)(2,1)} %get-tuple-element.98), channel_id=1, source_target_pairs={{0,2},{2,0},{1,3},{3,1},{4,6},{6,4},{5,7},{7,5}} | collective-permute-start | bytes 4300808 | tf_op jit(solution)/shard_map/ppermute | solution.py:109
  433.7 244.1 %collective-permute-start.56 = (bf16[320,4480]{1,0:T(8,128)(2,1)}, bf16[320,4480]{1,0:T(8,128)(2,1)}, u32[]{:S(2)}, u32[]{:S(2)}) collective-permute-start(bf16[320,4480]{1,0:T(8,128)(2,1)} %get-tuple-element.99), channel_id=1, source_target_pairs={{0,2},{2,0},{1,3},{3,1},{4,6},{6,4},{5,7},{7,5}} | collective-permute-start | bytes 8601608 | tf_op jit(solution)/shard_map/ppermute | solution.py:109
  495.2 183.0 %collective-permute-start.57 = (bf16[320,4480]{1,0:T(8,128)(2,1)}, bf16[320,4480]{1,0:T(8,128)(2,1)}, u32[]{:S(2)}, u32[]{:S(2)}) collective-permute-start(bf16[320,4480]{1,0:T(8,128)(2,1)} %get-tuple-element.99), channel_id=1, source_target_pairs={{0,1},{1,0},{2,3},{3,2},{4,5},{5,4},{6,7},{7,6}} | collective-permute-start | bytes 8601608 | tf_op jit(solution)/shard_map/ppermute | solution.py:109
  495.2 106.5 %collective-permute-start.47 = (bf16[48,4480]{1,0:T(8,128)(2,1)}, bf16[48,4480]{1,0:T(8,128)(2,1)S(1)}, u32[]{:S(2)}, u32[]{:S(2)}) collective-permute-start(bf16[48,4480]{1,0:T(8,128)(2,1)} %get-tuple-element.96), channel_id=1, source_target_pairs={{0,2},{2,0},{1,3},{3,1},{4,6},{6,4},{5,7},{7,5}} | collective-permute-start | bytes 1290248 | tf_op jit(solution)/shard_map/ppermute | solution.py:109
  501.2 100.8 %collective-permute-start.48 = (bf16[48,4480]{1,0:T(8,128)(2,1)}, bf16[48,4480]{1,0:T(8,128)(2,1)S(1)}, u32[]{:S(2)}, u32[]{:S(2)}) collective-permute-start(bf16[48,4480]{1,0:T(8,128)(2,1)} %get-tuple-element.96), channel_id=1, source_target_pairs={{0,1},{1,0},{2,3},{3,2},{4,5},{5,4},{6,7},{7,6}} | collective-permute-start | bytes 1290248 | tf_op jit(solution)/shard_map/ppermute | solution.py:109
  619.1 23.4 %collective-permute-start.54 = (bf16[160,4480]{1,0:T(8,128)(2,1)}, bf16[160,4480]{1,0:T(8,128)(2,1)}, u32[]{:S(2)}, u32[]{:S(2)}) collective-permute-start(bf16[160,4480]{1,0:T(8,128)(2,1)} %get-tuple-element.98), channel_id=1, source_target_pairs={{0,1},{1,0},{2,3},{3,2},{4,5},{5,4},{6,7},{7,6}} | collective-permute-start | bytes 4300808 | tf_op jit(solution)/shard_map/ppermute | solution.py:109
  619.1 40.4 %collective-permute-start.55 = (bf16[160,4480]{1,0:T(8,128)(2,1)}, bf16[160,4480]{1,0:T(8,128)(2,1)}, u32[]{:S(2)}, u32[]{:S(2)}) collective-permute-start(bf16[160,4480]{1,0:T(8,128)(2,1)} %collective-permute-done.53.refs_0_), channel_id=1, source_target_pairs={{0,1},{1,0},{2,3},{3,2},{4,5},{5,4},{6,7},{7,6}} | collective-permute-start | bytes 4300808 | tf_op jit(solution)/shard_map/ppermute | solution.py:109
  625.2 34.2 %collective-permute-start.52 = (bf16[80,4480]{1,0:T(8,128)(2,1)}, bf16[80,4480]{1,0:T(8,128)(2,1)}, u32[]{:S(2)}, u32[]{:S(2)}) collective-permute-start(bf16[80,4480]{1,0:T(8,128)(2,1)} %collective-permute-done.50.refs_0_), channel_id=1, source_target_pairs={{0,1},{1,0},{2,3},{3,2},{4,5},{5,4},{6,7},{7,6}} | collective-permute-start | bytes 2150408 | tf_op jit(solution)/shard_map/ppermute | solution.py:109
  642.5 65.3 %collective-permute-start.15 = (bf16[320,4480]{1,0:T(8,128)(2,1)}, bf16[320,4480]{1,0:T(8,128)(2,1)}, u32[]{:S(2)}, u32[]{:S(2)}) collective-permute-start(bf16[320,4480]{1,0:T(8,128)(2,1)} %get-tuple-element.77), channel_id=1, source_target_pairs={{0,2},{2,0},{1,3},{3,1},{4,6},{6,4},{5,7},{7,5}} | collective-permute-start | bytes 8601608 | tf_op jit(solution)/shard_map/ppermute | solution.py:109
  659.5 48.4 %collective-permute-start.16 = (bf16[320,4480]{1,0:T(8,128)(2,1)}, bf16[320,4480]{1,0:T(8,128)(2,1)}, u32[]{:S(2)}, u32[]{:S(2)}) collective-permute-start(bf16[320,4480]{1,0:T(8,128)(2,1)} %get-tuple-element.77), channel_id=1, source_target_pairs={{0,1},{1,0},{2,3},{3,2},{4,5},{5,4},{6,7},{7,6}} | collective-permute-start | bytes 8601608 | tf_op jit(solution)/shard_map/ppermute | solution.py:109
  659.5 109.8 %collective-permute-start.69 = (bf16[1120,1280]{1,0:T(8,128)(2,1)}, bf16[1120,1280]{1,0:T(8,128)(2,1)}, u32[]{:S(2)}, u32[]{:S(2)}) collective-permute-start(bf16[1120,1280]{1,0:T(8,128)(2,1)} %get-tuple-element.105), channel_id=1, source_target_pairs={{0,2},{2,0},{1,3},{3,1},{4,6},{6,4},{5,7},{7,5}} | collective-permute-start | bytes 8601608 | tf_op jit(solution)/shard_map/ppermute | solution.py:109
  677.9 152.1 %collective-permute-start.66 = (bf16[1120,1280]{1,0:T(8,128)(2,1)}, bf16[1120,1280]{1,0:T(8,128)(2,1)}, u32[]{:S(2)}, u32[]{:S(2)}) collective-permute-start(bf16[1120,1280]{1,0:T(8,128)(2,1)} %get-tuple-element.104), channel_id=1, source_target_pairs={{0,2},{2,0},{1,3},{3,1},{4,6},{6,4},{5,7},{7,5}} | collective-permute-start | bytes 8601608 | tf_op jit(solution)/shard_map/ppermute | solution.py:109
  678.2 151.7 %collective-permute-start.58 = (bf16[320,4480]{1,0:T(8,128)(2,1)}, bf16[320,4480]{1,0:T(8,128)(2,1)}, u32[]{:S(2)}, u32[]{:S(2)}) collective-permute-start(bf16[320,4480]{1,0:T(8,128)(2,1)} %collective-permute-done.56.refs_0_), channel_id=1, source_target_pairs={{0,1},{1,0},{2,3},{3,2},{4,5},{5,4},{6,7},{7,6}} | collective-permute-start | bytes 8601608 | tf_op jit(solution)/shard_map/ppermute | solution.py:109
  707.9 152.7 %collective-permute-start.17 = (bf16[320,4480]{1,0:T(8,128)(2,1)}, bf16[320,4480]{1,0:T(8,128)(2,1)}, u32[]{:S(2)}, u32[]{:S(2)}) collective-permute-start(bf16[320,4480]{1,0:T(8,128)(2,1)} %collective-permute-done.15.refs_0_), channel_id=1, source_target_pairs={{0,1},{1,0},{2,3},{3,2},{4,5},{5,4},{6,7},{7,6}} | collective-permute-start | bytes 8601608 | tf_op jit(solution)/shard_map/ppermute | solution.py:109
  707.9 159.4 %collective-permute-start.70 = (bf16[1120,1280]{1,0:T(8,128)(2,1)}, bf16[1120,1280]{1,0:T(8,128)(2,1)}, u32[]{:S(2)}, u32[]{:S(2)}) collective-permute-start(bf16[1120,1280]{1,0:T(8,128)(2,1)} %get-tuple-element.105), channel_id=1, source_target_pairs={{0,1},{1,0},{2,3},{3,2},{4,5},{5,4},{6,7},{7,6}} | collective-permute-start | bytes 8601608 | tf_op jit(solution)/shard_map/ppermute | solution.py:109
  769.3 98.0 %collective-permute-start.71 = (bf16[1120,1280]{1,0:T(8,128)(2,1)}, bf16[1120,1280]{1,0:T(8,128)(2,1)}, u32[]{:S(2)}, u32[]{:S(2)}) collective-permute-start(bf16[1120,1280]{1,0:T(8,128)(2,1)} %collective-permute-done.69.refs_0_), channel_id=1, source_target_pairs={{0,1},{1,0},{2,3},{3,2},{4,5},{5,4},{6,7},{7,6}} | collective-permute-start | bytes 8601608 | tf_op jit(solution)/shard_map/ppermute | solution.py:109
  829.9 44.1 %collective-permute-start.67 = (bf16[1120,1280]{1,0:T(8,128)(2,1)}, bf16[1120,1280]{1,0:T(8,128)(2,1)}, u32[]{:S(2)}, u32[]{:S(2)}) collective-permute-start(bf16[1120,1280]{1,0:T(8,128)(2,1)} %get-tuple-element.104), channel_id=1, source_target_pairs={{0,1},{1,0},{2,3},{3,2},{4,5},{5,4},{6,7},{7,6}} | collective-permute-start | bytes 8601608 | tf_op jit(solution)/shard_map/ppermute | solution.py:109
  829.9 44.1 %collective-permute-start.68 = (bf16[1120,1280]{1,0:T(8,128)(2,1)}, bf16[1120,1280]{1,0:T(8,128)(2,1)}, u32[]{:S(2)}, u32[]{:S(2)}) collective-permute-start(bf16[1120,1280]{1,0:T(8,128)(2,1)} %collective-permute-done.66.refs_0_), channel_id=1, source_target_pairs={{0,1},{1,0},{2,3},{3,2},{4,5},{5,4},{6,7},{7,6}} | collective-permute-start | bytes 8601608 | tf_op jit(solution)/shard_map/ppermute | solution.py:109
  (36 other events, 554.1 us)

commit v4 on v3

--- a/solution.py
+++ b/solution.py
@@ -13,24 +13,25 @@
 UNITS = 20
 
 CHUNKS = [
-    (0, 0, 0, 1, 1),
-    (0, 0, 1, 3, 1),
-    (0, 0, 4, 6, 2),
-    (0, 0, 10, 10, 2),
-    (0, 1, 0, 20, 4),
-    (2, 0, 0, 20, 4),
-    (2, 1, 0, 20, 4),
-    (1, 0, 0, 20, 4),
-    (1, 1, 0, 10, 2),
-    (1, 1, 10, 5, 1),
-    (1, 1, 15, 3, 1),
-    (1, 1, 18, 2, 2),
+    (0, 0, 0, 1, 1, 1, 1),
+    (0, 0, 1, 3, 1, 3, 1),
+    (0, 0, 4, 6, 2, 2, 2),
+    (0, 0, 10, 10, 2, 10, 10),
+    (0, 1, 0, 20, 4, 20, 10),
+    (2, 0, 0, 20, 4, 20, 10),
+    (2, 1, 0, 20, 4, 20, 10),
+    (1, 0, 0, 20, 4, 20, 10),
+    (1, 1, 0, 10, 2, 10, 10),
+    (1, 1, 10, 5, 1, 5, 5),
+    (1, 1, 15, 3, 1, 1, 1),
+    (1, 1, 18, 2, 2, 2, 2),
 ]
 EARLY = 2
 LAST = len(CHUNKS) - 1
 
 FULL = 67043328
-SPARE = {"cut_early": 4 << 20, "sum_0": 4 << 20, "sum_1": 4 << 20, "cutf_2": 160 << 10, "cutf_3": 160 << 10, "place_far": 1 << 20, "place_to": 1 << 20}
+SPARE = {"cutf_0": 4 << 20, "cutf_1": 4 << 20, "sum_0": 4 << 20, "sum_1": 4 << 20, "cutf_2": 160 << 10, "cutf_3": 160 << 10}
+SPARE |= {"place_10": 320 << 10, "place_last": 1 << 20}
 
 ANY = pl.BlockSpec(memory_space=pl.ANY)
 WHOLE = pl.BlockSpec(memory_space=pltpu.VMEM)
@@ -127,7 +128,7 @@
             return pl.BlockSpec((b * rows[w], cols[w]), lambda i: (i, 0))
 
         def cut(k, of, tag):
-            w, layer, u0, n, b = CHUNKS[k]
+            w, layer, u0, n, b = CHUNKS[k][:5]
 
             def body(t, o, *scratch):
                 first = of(me()) * UNITS + u0
@@ -138,36 +139,25 @@
             )
             return send(one, MATE)
 
-        def cut_early():
-            w, layer = CHUNKS[0][:2]
-            pieces = [(u0, n, of) for _, _, u0, n, _ in CHUNKS[:EARLY] for of in (far_mate_of, far_of)]
+        def cut_early(k):
+            w, layer, u0, n = CHUNKS[k][:4]
 
             def body(t, *refs):
-                sem = refs[-1]
                 copies = [
-                    pltpu.make_async_copy(t.at[0, layer, at(w, of(me()) * UNITS + u0, n)], to, sem.at[j])
-                    for j, ((u0, n, of), to) in enumerate(zip(pieces, refs))
+                    pltpu.make_async_copy(t.at[0, layer, at(w, of(me()) * UNITS + u0, n)], to, refs[-1].at[j])
+                    for j, (of, to) in enumerate(((far_mate_of, refs[0]), (far_of, refs[1])))
                 ]
                 for one in copies:
                     one.start()
                 for one in copies:
                     one.wait()
 
-            out = run(
-                "cut_early",
-                body,
-                (),
-                [in_space(terms[w], pltpu.HBM)],
-                [ANY],
-                [shape(w, n, pltpu.VMEM) for _, n, _ in pieces],
-                [WHOLE] * len(pieces),
-                {},
-                [DMA((len(pieces),))],
-            )
-            return [send(out[2 * k], MATE, pltpu.VMEM) for k in range(EARLY)], out[1::2]
+            outs = [shape(w, n, pltpu.VMEM)] * 2
+            mine, own = run(f"cutf_{k}", body, (), [in_space(terms[w], pltpu.HBM)], [ANY], outs, [WHOLE] * 2, {}, [DMA((2,))])
+            return send(mine, MATE, pltpu.VMEM), own
 
         def sum_early(k, got, own):
-            w, _, _, n, _ = CHUNKS[k]
+            w, _, _, n = CHUNKS[k][:4]
 
             def body(t, r, o):
                 o[...] = add(t[...], r[...])
@@ -177,7 +167,7 @@
             return send(one, FAR)
 
         def chip_sum(k, got):
-            w, layer, u0, n, b = CHUNKS[k]
+            w, layer, u0, n, _, b, _ = CHUNKS[k]
 
             def body(t, r, o):
                 o[...] = add(t[0, 0], r[...])
@@ -195,7 +185,7 @@
             return send(one, FAR)
 
         def update(k, mate_term, far_sum):
-            w, layer, u0, n, b = CHUNKS[k]
+            w, layer, u0, n, _, _, b = CHUNKS[k]
 
             def body(*refs):
                 t, r, f, wt, mm, vv = refs[:6]
@@ -219,10 +209,13 @@
             out, new_w[w], new_m[w], new_v[w] = run(
                 f"adam_{k}", body, (n // b,), ins, specs, outs, [piece_spec(w, b), mine, moment, moment], aliases
             )
-            return send(out, FAR), send(out, MATE)
+            if k < LAST:
+                return send(out, FAR), send(out, MATE)
+            place(k, "place_own", [send(out, MATE)], [mate_of])
+            return out
 
         def place(k, name, pieces, owners):
-            w, layer, u0, n, b = CHUNKS[k]
+            w, layer, u0, n, b = CHUNKS[k][:5]
 
             def body(*refs):
                 count = len(pieces)
@@ -246,22 +239,27 @@
                 move_scratch(w, n // b * len(pieces), b),
             )
 
-        def place_last(piece):
-            w, layer, u0, n, _ = CHUNKS[LAST]
-
-            def body(one, _, full, sem):
-                copy = pltpu.make_async_copy(one, full.at[layer, at(w, far_mate_of(me()) * UNITS + u0, n)], sem)
-                copy.start()
-                copy.wait()
+        def place_last(far, far_mate):
+            w, layer, u0, n = CHUNKS[LAST][:4]
+
+            def body(far, far_mate, _, full, sem):
+                copies = [
+                    pltpu.make_async_copy(one, full.at[layer, at(w, of(me()) * UNITS + u0, n)], sem.at[j])
+                    for j, (one, of) in enumerate(((far, far_of), (far_mate, far_mate_of)))
+                ]
+                for one in copies:
+                    one.start()
+                for one in copies:
+                    one.wait()
 
             like = jax.ShapeDtypeStruct(weights[w].shape, jnp.bfloat16)
-            (new_w[w],) = run("place_to", body, (), [piece, new_w[w]], [WHOLE, ANY], [like], [ANY], {1: 0}, [DMA])
+            (new_w[w],) = run("place_last", body, (), [far, far_mate, new_w[w]], [WHOLE, WHOLE, ANY], [like], [ANY], {2: 0}, [DMA((2,))])
 
         count = len(CHUNKS)
         got, far_sum, mate_term, out = ([None] * count for _ in range(4))
-        got[:EARLY], own = cut_early()
+        early = [cut_early(k) for k in range(EARLY)]
         for k in range(EARLY):
-            far_sum[k] = sum_early(k, got[k], own[k])
+            far_sum[k] = sum_early(k, *early[k])
         got[EARLY] = cut(EARLY, far_mate_of, "f")
         for k in range(EARLY, count):
             if k + 1 < count:
@@ -271,13 +269,13 @@
             mate_term[k] = cut(k, mate_of, "m")
         for k in range(count):
             out[k] = update(k, mate_term[k], far_sum[k])
-        place(LAST, "place_own", out[LAST][1:], [mate_of])
         for k in range(LAST):
+            if k == LAST - 1:
+                last = send(out[LAST], FAR, pltpu.VMEM)
             forward = send(out[k][0], MATE)
             place(k, f"place_{k}", [*out[k], forward], [far_of, mate_of, far_mate_of])
-        forward = send(out[LAST][0], MATE, pltpu.VMEM)
-        place(LAST, "place_far", out[LAST][:1], [far_of])
-        place_last(forward)
+        forward = send(last, MATE, pltpu.VMEM)
+        place_last(last, forward)
         return (*new_w, *new_m, *new_v)
 
     all_of, cut_of = P(None, None, None), P(None, "dp", None)

time: 883 us -> 878 us (level)
  Pallas kernels: 263 us -> 241 us
  waiting for transfers between devices: 581 us -> 597 us
    pallas_call x61, Pallas kernels: 263 us -> 241 us  [run(): pl.pallas_call(body, out_shape=outs, grid=grid, in_specs=in_specs, out_sp...]
    ppermute x72, waiting for transfers between devices: 581 us -> 597 us  [send(): return in_space(lax.ppermute(x, 'dp', pairs), space)]
  transfers between devices with their start and end apart: 72 -> 72, of which waited for: 22 -> 22; matrix products, arithmetic and copies ran while one was open for 0% -> 0% of each run, Pallas kernels for 29% -> 27%
where the time goes in v4:
time: 878 us; the launch traced here: 877 us
  waiting for transfers between devices  597 us (68%)
  Pallas kernels  241 us (27%)
  starting transfers between devices  31.6 us (4%)
    ppermute x72, waiting for transfers between devices, send(): return in_space(lax.ppermute(x, 'dp', pairs), space)  597 us
    pallas_call x61, Pallas kernels, run(): pl.pallas_call(body, out_shape=outs, grid=grid, in_specs=in_specs, out_sp...  241 us
    ppermute x72, starting transfers between devices, send(): return in_space(lax.ppermute(x, 'dp', pairs), space)  31.6 us
  transfers between devices with their start and end apart: 72, of which 22 were waited for; matrix products, arithmetic and copies ran while one was open for 0% of the time, Pallas kernels for 27%

profile of v4, /device:TPU:0, one launch (start us, length us, event | category | flops | bytes accessed | tf_op | source)
XLA Modules:
  0.0 876.9 jit_solution(5008610849886373088)
XLA Ops:
  21.0 3.0 collective-permute-start.14
  51.3 2.8 shard_map.217
  56.9 4.6 shard_map.203
  61.5 5.2 collective-permute-done.35.refs_2_
  71.2 2.7 shard_map.225
  73.9 5.9 collective-permute-done.24.refs_0_
  84.7 2.7 shard_map.224
  87.9 3.2 shard_map.195
  97.0 16.9 %collective-permute-done.8.refs_2_ = bf16[96,4480]{1,0:T(8,128)(2,1)} collective-permute-done((bf16[96,4480]{1,0:T(8,128)(2,1)}, bf16[96,4480]{1,0:T(8,128)(2,1)}, u32[]{:S(2)}, u32[]{:S(2)}) %collective-permute-start.8) | collective-permute-done | bytes 860192 | tf_op jit(solution)/shard_map/ppermute | solution.py:110
  113.9 6.6 shard_map.204
  121.2 3.2 shard_map.223
  124.4 18.0 %collective-permute-done.21.refs_0_ = bf16[96,4480]{1,0:T(8,128)(2,1)} collective-permute-done((bf16[96,4480]{1,0:T(8,128)(2,1)}, bf16[96,4480]{1,0:T(8,128)(2,1)}, u32[]{:S(2)}, u32[]{:S(2)}) %collective-permute-start.21) | collective-permute-done | bytes 860192 | tf_op jit(solution)/shard_map/ppermute | solution.py:110
  142.8 3.3 shard_map.192
  150.5 2.7 shard_map.242
  156.5 20.5 %collective-permute-done.41.refs_2_ = bf16[160,4480]{1,0:T(8,128)(2,1)} collective-permute-done((bf16[160,4480]{1,0:T(8,128)(2,1)}, bf16[160,4480]{1,0:T(8,128)(2,1)}, u32[]{:S(2)}, u32[]{:S(2)}) %collective-permute-start.41) | collective-permute-done | bytes 1433632 | tf_op jit(solution)/shard_map/ppermute | solution.py:110
  177.0 2.7 shard_map.239
  179.7 26.7 %collective-permute-done.5.refs_2_ = bf16[160,4480]{1,0:T(8,128)(2,1)} collective-permute-done((bf16[160,4480]{1,0:T(8,128)(2,1)}, bf16[160,4480]{1,0:T(8,128)(2,1)}, u32[]{:S(2)}, u32[]{:S(2)}) %collective-permute-start.5) | collective-permute-done | bytes 1433632 | tf_op jit(solution)/shard_map/ppermute | solution.py:110
  206.4 2.7 shard_map.238
  209.7 4.9 shard_map.226
  215.0 9.8 %shard_map.205 = (bf16[160,4480]{1,0:T(8,128)(2,1)}, bf16[2,1280,4480]{2,1,0:T(8,128)(2,1)}, f32[2,320,4480]{2,1,0:T(8,128)}, f32[2,320,4480]{2,1,0:T(8,128)}) custom-call(bf16[1,2,1280,4480]{3,2,1,0:T(8,128)(2,1)} %refs_0_.16, bf16[160,4480]{1,0:T(8,128)(2,1)} %collective-permute-done.3.refs_1_, ...), custom_call_target="tpu_custom_call", output_to_operand_aliasing={{1}: (6, {}), {2}: (7, {}), {3}: (8, {})} | custom-call | flops 35840000 | bytes 35840000 | tf_op jit(solution)/shard_map/pallas_call | solution.py:97
  226.5 4.9 shard_map.189
  231.7 4.9 shard_map.243
  238.3 4.9 shard_map.240
  243.5 67.1 %collective-permute-done.18.refs_0_ = bf16[160,4480]{1,0:T(8,128)(2,1)} collective-permute-done((bf16[160,4480]{1,0:T(8,128)(2,1)}, bf16[160,4480]{1,0:T(8,128)(2,1)}, u32[]{:S(2)}, u32[]{:S(2)}) %collective-permute-start.18) | collective-permute-done | bytes 1433632 | tf_op jit(solution)/shard_map/ppermute | solution.py:110
  311.1 13.4 %shard_map.227 = (bf16[320,4480]{1,0:T(8,128)(2,1)}, bf16[2,1280,4480]{2,1,0:T(8,128)(2,1)}, f32[2,320,4480]{2,1,0:T(8,128)}, f32[2,320,4480]{2,1,0:T(8,128)}) custom-call(bf16[1,2,1280,4480]{3,2,1,0:T(8,128)(2,1)} %refs_0_.21, bf16[320,4480]{1,0:T(8,128)(2,1)} %collective-permute-done.42.refs_1_, bf16[320,4480]{1,0:T(8,128)(2,1)} %collective-permute-done.44.refs_2_, ...), custom_call_target="tpu_custom_call" | custom-call | flops 37273600 | bytes 37273600 | tf_op jit(solution)/shard_map/pallas_call | solution.py:97
  324.5 9.8 %shard_map.228 = (bf16[160,4480]{1,0:T(8,128)(2,1)}, bf16[2,1280,4480]{2,1,0:T(8,128)(2,1)}, f32[2,320,4480]{2,1,0:T(8,128)}, f32[2,320,4480]{2,1,0:T(8,128)}) custom-call(bf16[1,2,1280,4480]{3,2,1,0:T(8,128)(2,1)} %refs_0_.21, bf16[160,4480]{1,0:T(8,128)(2,1)} %collective-permute-done.39.refs_1_, ...), custom_call_target="tpu_custom_call", output_to_operand_aliasing={{1}: (6, {}), {2}: (7, {}), {3}: (8, {})} | custom-call | flops 35840000 | bytes 35840000 | tf_op jit(solution)/shard_map/pallas_call | solution.py:97
  334.4 5.7 shard_map.229
  340.1 4.6 shard_map.230
  344.8 3.2 shard_map.231
  348.3 23.8 %collective-permute-done.2.refs_2_ = bf16[320,4480]{1,0:T(8,128)(2,1)} collective-permute-done((bf16[320,4480]{1,0:T(8,128)(2,1)}, bf16[320,4480]{1,0:T(8,128)(2,1)}, u32[]{:S(2)}, u32[]{:S(2)}) %collective-permute-start.2) | collective-permute-done | bytes 2867232 | tf_op jit(solution)/shard_map/ppermute | solution.py:110
  374.1 59.4 %collective-permute-done.65.refs_2_ = bf16[1120,1280]{1,0:T(8,128)(2,1)} collective-permute-done((bf16[1120,1280]{1,0:T(8,128)(2,1)}, bf16[1120,1280]{1,0:T(8,128)(2,1)}, u32[]{:S(2)}, u32[]{:S(2)}) %collective-permute-start.65) | collective-permute-done | bytes 2867232 | tf_op jit(solution)/shard_map/ppermute | solution.py:110
  433.9 61.1 %collective-permute-done.62.refs_2_ = bf16[1120,1280]{1,0:T(8,128)(2,1)} collective-permute-done((bf16[1120,1280]{1,0:T(8,128)(2,1)}, bf16[1120,1280]{1,0:T(8,128)(2,1)}, u32[]{:S(2)}, u32[]{:S(2)}) %collective-permute-start.62) | collective-permute-done | bytes 2867232 | tf_op jit(solution)/shard_map/ppermute | solution.py:110
  495.4 5.6 collective-permute-done.45.far
  501.0 100.4 %collective-permute-done.47.refs_0_ = bf16[48,4480]{1,0:T(8,128)(2,1)S(1)} collective-permute-done((bf16[48,4480]{1,0:T(8,128)(2,1)}, bf16[48,4480]{1,0:T(8,128)(2,1)S(1)}, u32[]{:S(2)}, u32[]{:S(2)}) %collective-permute-start.47) | collective-permute-done | bytes 430112 | tf_op jit(solution)/shard_map/ppermute | solution.py:110
  604.3 14.6 %collective-permute-done.50.refs_0_ = bf16[80,4480]{1,0:T(8,128)(2,1)} collective-permute-done((bf16[80,4480]{1,0:T(8,128)(2,1)}, bf16[80,4480]{1,0:T(8,128)(2,1)}, u32[]{:S(2)}, u32[]{:S(2)}) %collective-permute-start.50) | collective-permute-done | bytes 716832 | tf_op jit(solution)/shard_map/ppermute | solution.py:110
  619.4 5.5 collective-permute-done.49.refs_2_
  625.7 13.4 %shard_map.206 = (bf16[320,4480]{1,0:T(8,128)(2,1)}, bf16[2,1280,4480]{2,1,0:T(8,128)(2,1)}, f32[2,320,4480]{2,1,0:T(8,128)}, f32[2,320,4480]{2,1,0:T(8,128)}) custom-call(bf16[1,2,1280,4480]{3,2,1,0:T(8,128)(2,1)} %refs_0_.16, bf16[320,4480]{1,0:T(8,128)(2,1)} %collective-permute-done.refs_1_, ...), custom_call_target="tpu_custom_call", output_to_operand_aliasing={{1}: (6, {}), {2}: (7, {}), {3}: (8, {})} | custom-call | flops 37273600 | bytes 37273600 | tf_op jit(solution)/shard_map/pallas_call | solution.py:97
  639.5 13.5 %shard_map.244 = (bf16[1120,1280]{1,0:T(8,128)(2,1)}, bf16[2,4480,1280]{2,1,0:T(8,128)(2,1)}, f32[2,1120,1280]{2,1,0:T(8,128)}, f32[2,1120,1280]{2,1,0:T(8,128)}) custom-call(bf16[1,2,4480,1280]{3,2,1,0:T(8,128)(2,1)} %refs_0_.23, bf16[1120,1280]{1,0:T(8,128)(2,1)} %collective-permute-done.63.refs_1_, bf16[1120,1280]{1,0:T(8,128)(2,1)} %collective-permute-done.65.refs_2_, ...), custom_call_target="tpu_custom_call" | custom-call | flops 37273600 | bytes 37273600 | tf_op jit(solution)/shard_map/pallas_call | solution.py:97
  654.8 13.5 %shard_map.245 = (bf16[1120,1280]{1,0:T(8,128)(2,1)}, bf16[2,4480,1280]{2,1,0:T(8,128)(2,1)}, f32[2,1120,1280]{2,1,0:T(8,128)}, f32[2,1120,1280]{2,1,0:T(8,128)}) custom-call(bf16[1,2,4480,1280]{3,2,1,0:T(8,128)(2,1)} %refs_0_.23, bf16[1120,1280]{1,0:T(8,128)(2,1)} %collective-permute-done.60.refs_1_, ...), custom_call_target="tpu_custom_call", output_to_operand_aliasing={{1}: (6, {}), {2}: (7, {}), {3}: (8, {})} | custom-call | flops 37273600 | bytes 37273600 | tf_op jit(solution)/shard_map/pallas_call | solution.py:97
  668.8 35.7 %collective-permute-done.15.refs_0_ = bf16[320,4480]{1,0:T(8,128)(2,1)} collective-permute-done((bf16[320,4480]{1,0:T(8,128)(2,1)}, bf16[320,4480]{1,0:T(8,128)(2,1)}, u32[]{:S(2)}, u32[]{:S(2)}) %collective-permute-start.15) | collective-permute-done | bytes 2867232 | tf_op jit(solution)/shard_map/ppermute | solution.py:110
  705.0 60.9 %collective-permute-done.69.refs_0_ = bf16[1120,1280]{1,0:T(8,128)(2,1)} collective-permute-done((bf16[1120,1280]{1,0:T(8,128)(2,1)}, bf16[1120,1280]{1,0:T(8,128)(2,1)}, u32[]{:S(2)}, u32[]{:S(2)}) %collective-permute-start.69) | collective-permute-done | bytes 2867232 | tf_op jit(solution)/shard_map/ppermute | solution.py:110
  765.9 60.6 %collective-permute-done.66.refs_0_ = bf16[1120,1280]{1,0:T(8,128)(2,1)} collective-permute-done((bf16[1120,1280]{1,0:T(8,128)(2,1)}, bf16[1120,1280]{1,0:T(8,128)(2,1)}, u32[]{:S(2)}, u32[]{:S(2)}) %collective-permute-start.66) | collective-permute-done | bytes 2867232 | tf_op jit(solution)/shard_map/ppermute | solution.py:110
  833.6 3.9 shard_map.210.refs_3_
  839.2 6.7 shard_map.233.refs_3_
  845.9 3.9 shard_map.234.refs_3_
  856.5 6.7 shard_map.211
  863.3 6.7 shard_map.246.refs_3_
  870.0 6.7 shard_map.247
  (181 shorter events, 105.8 us)
Async XLA Ops:
  6.7 23.5 %collective-permute-start.34 = (bf16[48,4480]{1,0:T(8,128)(2,1)}, bf16[48,4480]{1,0:T(8,128)(2,1)}, u32[]{:S(2)}, u32[]{:S(2)}) collective-permute-start(bf16[48,4480]{1,0:T(8,128)(2,1)} %shard_map.216), channel_id=1, source_target_pairs={{0,1},{1,0},{2,3},{3,2},{4,5},{5,4},{6,7},{7,6}} | collective-permute-start | bytes 1290248 | tf_op jit(solution)/shard_map/ppermute | solution.py:110
  28.2 23.0 %collective-permute-start.37 = (bf16[80,4480]{1,0:T(8,128)(2,1)}, bf16[80,4480]{1,0:T(8,128)(2,1)}, u32[]{:S(2)}, u32[]{:S(2)}) collective-permute-start(bf16[80,4480]{1,0:T(8,128)(2,1)} %shard_map.219), channel_id=1, source_target_pairs={{0,1},{1,0},{2,3},{3,2},{4,5},{5,4},{6,7},{7,6}} | collective-permute-start | bytes 2150408 | tf_op jit(solution)/shard_map/ppermute | solution.py:110
  30.2 24.0 %collective-permute-start.36 = (bf16[80,4480]{1,0:T(8,128)(2,1)}, bf16[80,4480]{1,0:T(8,128)(2,1)}, u32[]{:S(2)}, u32[]{:S(2)}) collective-permute-start(bf16[80,4480]{1,0:T(8,128)(2,1)} %shard_map.218), channel_id=1, source_target_pairs={{0,1},{1,0},{2,3},{3,2},{4,5},{5,4},{6,7},{7,6}} | collective-permute-start | bytes 2150408 | tf_op jit(solution)/shard_map/ppermute | solution.py:110
  39.1 28.0 %collective-permute-start.7 = (bf16[96,4480]{1,0:T(8,128)(2,1)}, bf16[96,4480]{1,0:T(8,128)(2,1)}, u32[]{:S(2)}, u32[]{:S(2)}) collective-permute-start(bf16[96,4480]{1,0:T(8,128)(2,1)} %shard_map.194), channel_id=1, source_target_pairs={{0,1},{1,0},{2,3},{3,2},{4,5},{5,4},{6,7},{7,6}} | collective-permute-start | bytes 2580488 | tf_op jit(solution)/shard_map/ppermute | solution.py:110
  48.8 35.9 %collective-permute-start.40 = (bf16[160,4480]{1,0:T(8,128)(2,1)}, bf16[160,4480]{1,0:T(8,128)(2,1)}, u32[]{:S(2)}, u32[]{:S(2)}) collective-permute-start(bf16[160,4480]{1,0:T(8,128)(2,1)} %shard_map.222), channel_id=1, source_target_pairs={{0,1},{1,0},{2,3},{3,2},{4,5},{5,4},{6,7},{7,6}} | collective-permute-start | bytes 4300808 | tf_op jit(solution)/shard_map/ppermute | solution.py:110
  56.7 30.7 %collective-permute-start.39 = (bf16[160,4480]{1,0:T(8,128)(2,1)}, bf16[160,4480]{1,0:T(8,128)(2,1)}, u32[]{:S(2)}, u32[]{:S(2)}) collective-permute-start(bf16[160,4480]{1,0:T(8,128)(2,1)} %shard_map.221), channel_id=1, source_target_pairs={{0,1},{1,0},{2,3},{3,2},{4,5},{5,4},{6,7},{7,6}} | collective-permute-start | bytes 4300808 | tf_op jit(solution)/shard_map/ppermute | solution.py:110
  69.5 24.3 %collective-permute-start.38 = (bf16[80,4480]{1,0:T(8,128)(2,1)}, bf16[80,4480]{1,0:T(8,128)(2,1)}, u32[]{:S(2)}, u32[]{:S(2)}) collective-permute-start(bf16[80,4480]{1,0:T(8,128)(2,1)} %shard_map.220), channel_id=1, source_target_pairs={{0,2},{2,0},{1,3},{3,1},{4,6},{6,4},{5,7},{7,5}} | collective-permute-start | bytes 2150408 | tf_op jit(solution)/shard_map/ppermute | solution.py:110
  79.8 70.7 %collective-permute-start.43 = (bf16[320,4480]{1,0:T(8,128)(2,1)}, bf16[320,4480]{1,0:T(8,128)(2,1)}, u32[]{:S(2)}, u32[]{:S(2)}) collective-permute-start(bf16[320,4480]{1,0:T(8,128)(2,1)} %shard_map.225), channel_id=1, source_target_pairs={{0,1},{1,0},{2,3},{3,2},{4,5},{5,4},{6,7},{7,6}} | collective-permute-start | bytes 8601608 | tf_op jit(solution)/shard_map/ppermute | solution.py:110
  84.7 35.9 %collective-permute-start.3 = (bf16[160,4480]{1,0:T(8,128)(2,1)}, bf16[160,4480]{1,0:T(8,128)(2,1)}, u32[]{:S(2)}, u32[]{:S(2)}) collective-permute-start(bf16[160,4480]{1,0:T(8,128)(2,1)} %shard_map.190), channel_id=1, source_target_pairs={{0,1},{1,0},{2,3},{3,2},{4,5},{5,4},{6,7},{7,6}} | collective-permute-start | bytes 4300808 | tf_op jit(solution)/shard_map/ppermute | solution.py:110
  87.4 65.8 %collective-permute-start.42 = (bf16[320,4480]{1,0:T(8,128)(2,1)}, bf16[320,4480]{1,0:T(8,128)(2,1)}, u32[]{:S(2)}, u32[]{:S(2)}) collective-permute-start(bf16[320,4480]{1,0:T(8,128)(2,1)} %shard_map.224), channel_id=1, source_target_pairs={{0,1},{1,0},{2,3},{3,2},{4,5},{5,4},{6,7},{7,6}} | collective-permute-start | bytes 8601608 | tf_op jit(solution)/shard_map/ppermute | solution.py:110
  96.9 112.2 %collective-permute-start.1 = (bf16[320,4480]{1,0:T(8,128)(2,1)}, bf16[320,4480]{1,0:T(8,128)(2,1)}, u32[]{:S(2)}, u32[]{:S(2)}) collective-permute-start(bf16[320,4480]{1,0:T(8,128)(2,1)} %shard_map.188), channel_id=1, source_target_pairs={{0,1},{1,0},{2,3},{3,2},{4,5},{5,4},{6,7},{7,6}} | collective-permute-start | bytes 8601608 | tf_op jit(solution)/shard_map/ppermute | solution.py:110
  120.6 21.8 %collective-permute-start.21 = (bf16[96,4480]{1,0:T(8,128)(2,1)}, bf16[96,4480]{1,0:T(8,128)(2,1)}, u32[]{:S(2)}, u32[]{:S(2)}) collective-permute-start(bf16[96,4480]{1,0:T(8,128)(2,1)} %get-tuple-element.79), channel_id=1, source_target_pairs={{0,2},{2,0},{1,3},{3,1},{4,6},{6,4},{5,7},{7,5}} | collective-permute-start | bytes 2580488 | tf_op jit(solution)/shard_map/ppermute | solution.py:110
  121.0 25.1 %collective-permute-start.22 = (bf16[96,4480]{1,0:T(8,128)(2,1)}, bf16[96,4480]{1,0:T(8,128)(2,1)}, u32[]{:S(2)}, u32[]{:S(2)}) collective-permute-start(bf16[96,4480]{1,0:T(8,128)(2,1)} %get-tuple-element.79), channel_id=1, source_target_pairs={{0,1},{1,0},{2,3},{3,2},{4,5},{5,4},{6,7},{7,6}} | collective-permute-start | bytes 2580488 | tf_op jit(solution)/shard_map/ppermute | solution.py:110
  142.4 34.6 %collective-permute-start.41 = (bf16[160,4480]{1,0:T(8,128)(2,1)}, bf16[160,4480]{1,0:T(8,128)(2,1)}, u32[]{:S(2)}, u32[]{:S(2)}) collective-permute-start(bf16[160,4480]{1,0:T(8,128)(2,1)} %shard_map.223), channel_id=1, source_target_pairs={{0,2},{2,0},{1,3},{3,1},{4,6},{6,4},{5,7},{7,5}} | collective-permute-start | bytes 4300808 | tf_op jit(solution)/shard_map/ppermute | solution.py:110
  146.1 60.3 %collective-permute-start.5 = (bf16[160,4480]{1,0:T(8,128)(2,1)}, bf16[160,4480]{1,0:T(8,128)(2,1)}, u32[]{:S(2)}, u32[]{:S(2)}) collective-permute-start(bf16[160,4480]{1,0:T(8,128)(2,1)} %shard_map.192), channel_id=1, source_target_pairs={{0,2},{2,0},{1,3},{3,1},{4,6},{6,4},{5,7},{7,5}} | collective-permute-start | bytes 4300808 | tf_op jit(solution)/shard_map/ppermute | solution.py:110
  150.5 64.1 %collective-permute-start = (bf16[320,4480]{1,0:T(8,128)(2,1)}, bf16[320,4480]{1,0:T(8,128)(2,1)}, u32[]{:S(2)}, u32[]{:S(2)}) collective-permute-start(bf16[320,4480]{1,0:T(8,128)(2,1)} %shard_map.187), channel_id=1, source_target_pairs={{0,1},{1,0},{2,3},{3,2},{4,5},{5,4},{6,7},{7,6}} | collective-permute-start | bytes 8601608 | tf_op jit(solution)/shard_map/ppermute | solution.py:110
  153.3 61.7 %collective-permute-start.64 = (bf16[1120,1280]{1,0:T(8,128)(2,1)}, bf16[1120,1280]{1,0:T(8,128)(2,1)}, u32[]{:S(2)}, u32[]{:S(2)}) collective-permute-start(bf16[1120,1280]{1,0:T(8,128)(2,1)} %shard_map.242), channel_id=1, source_target_pairs={{0,1},{1,0},{2,3},{3,2},{4,5},{5,4},{6,7},{7,6}} | collective-permute-start | bytes 8601608 | tf_op jit(solution)/shard_map/ppermute | solution.py:110
  177.0 47.8 %collective-permute-start.63 = (bf16[1120,1280]{1,0:T(8,128)(2,1)}, bf16[1120,1280]{1,0:T(8,128)(2,1)}, u32[]{:S(2)}, u32[]{:S(2)}) collective-permute-start(bf16[1120,1280]{1,0:T(8,128)(2,1)} %shard_map.241), channel_id=1, source_target_pairs={{0,1},{1,0},{2,3},{3,2},{4,5},{5,4},{6,7},{7,6}} | collective-permute-start | bytes 8601608 | tf_op jit(solution)/shard_map/ppermute | solution.py:110
  206.4 24.9 %collective-permute-start.61 = (bf16[1120,1280]{1,0:T(8,128)(2,1)}, bf16[1120,1280]{1,0:T(8,128)(2,1)}, u32[]{:S(2)}, u32[]{:S(2)}) collective-permute-start(bf16[1120,1280]{1,0:T(8,128)(2,1)} %shard_map.239), channel_id=1, source_target_pairs={{0,1},{1,0},{2,3},{3,2},{4,5},{5,4},{6,7},{7,6}} | collective-permute-start | bytes 8601608 | tf_op jit(solution)/shard_map/ppermute | solution.py:110
  209.1 27.5 %collective-permute-start.60 = (bf16[1120,1280]{1,0:T(8,128)(2,1)}, bf16[1120,1280]{1,0:T(8,128)(2,1)}, u32[]{:S(2)}, u32[]{:S(2)}) collective-permute-start(bf16[1120,1280]{1,0:T(8,128)(2,1)} %shard_map.238), channel_id=1, source_target_pairs={{0,1},{1,0},{2,3},{3,2},{4,5},{5,4},{6,7},{7,6}} | collective-permute-start | bytes 8601608 | tf_op jit(solution)/shard_map/ppermute | solution.py:110
  214.6 96.0 %collective-permute-start.44 = (bf16[320,4480]{1,0:T(8,128)(2,1)}, bf16[320,4480]{1,0:T(8,128)(2,1)}, u32[]{:S(2)}, u32[]{:S(2)}) collective-permute-start(bf16[320,4480]{1,0:T(8,128)(2,1)} %shard_map.226), channel_id=1, source_target_pairs={{0,2},{2,0},{1,3},{3,1},{4,6},{6,4},{5,7},{7,5}} | collective-permute-start | bytes 8601608 | tf_op jit(solution)/shard_map/ppermute | solution.py:110
  215.0 28.2 %collective-permute-start.23 = (bf16[96,4480]{1,0:T(8,128)(2,1)}, bf16[96,4480]{1,0:T(8,128)(2,1)}, u32[]{:S(2)}, u32[]{:S(2)}) collective-permute-start(bf16[96,4480]{1,0:T(8,128)(2,1)} %collective-permute-done.21.refs_0_), channel_id=1, source_target_pairs={{0,1},{1,0},{2,3},{3,2},{4,5},{5,4},{6,7},{7,6}} | collective-permute-start | bytes 2580488 | tf_op jit(solution)/shard_map/ppermute | solution.py:110
  224.8 85.8 %collective-permute-start.18 = (bf16[160,4480]{1,0:T(8,128)(2,1)}, bf16[160,4480]{1,0:T(8,128)(2,1)}, u32[]{:S(2)}, u32[]{:S(2)}) collective-permute-start(bf16[160,4480]{1,0:T(8,128)(2,1)} %get-tuple-element.78), channel_id=1, source_target_pairs={{0,2},{2,0},{1,3},{3,1},{4,6},{6,4},{5,7},{7,5}} | collective-permute-start | bytes 4300808 | tf_op jit(solution)/shard_map/ppermute | solution.py:110
  231.4 140.7 %collective-permute-start.2 = (bf16[320,4480]{1,0:T(8,128)(2,1)}, bf16[320,4480]{1,0:T(8,128)(2,1)}, u32[]{:S(2)}, u32[]{:S(2)}) collective-permute-start(bf16[320,4480]{1,0:T(8,128)(2,1)} %shard_map.189), channel_id=1, source_target_pairs={{0,2},{2,0},{1,3},{3,1},{4,6},{6,4},{5,7},{7,5}} | collective-permute-start | bytes 8601608 | tf_op jit(solution)/shard_map/ppermute | solution.py:110
  236.6 196.9 %collective-permute-start.65 = (bf16[1120,1280]{1,0:T(8,128)(2,1)}, bf16[1120,1280]{1,0:T(8,128)(2,1)}, u32[]{:S(2)}, u32[]{:S(2)}) collective-permute-start(bf16[1120,1280]{1,0:T(8,128)(2,1)} %shard_map.243), channel_id=1, source_target_pairs={{0,2},{2,0},{1,3},{3,1},{4,6},{6,4},{5,7},{7,5}} | collective-permute-start | bytes 8601608 | tf_op jit(solution)/shard_map/ppermute | solution.py:110
  243.2 251.8 %collective-permute-start.62 = (bf16[1120,1280]{1,0:T(8,128)(2,1)}, bf16[1120,1280]{1,0:T(8,128)(2,1)}, u32[]{:S(2)}, u32[]{:S(2)}) collective-permute-start(bf16[1120,1280]{1,0:T(8,128)(2,1)} %shard_map.240), channel_id=1, source_target_pairs={{0,2},{2,0},{1,3},{3,1},{4,6},{6,4},{5,7},{7,5}} | collective-permute-start | bytes 8601608 | tf_op jit(solution)/shard_map/ppermute | solution.py:110
  310.6 37.3 %collective-permute-start.19 = (bf16[160,4480]{1,0:T(8,128)(2,1)}, bf16[160,4480]{1,0:T(8,128)(2,1)}, u32[]{:S(2)}, u32[]{:S(2)}) collective-permute-start(bf16[160,4480]{1,0:T(8,128)(2,1)} %get-tuple-element.78), channel_id=1, source_target_pairs={{0,1},{1,0},{2,3},{3,2},{4,5},{5,4},{6,7},{7,6}} | collective-permute-start | bytes 4300808 | tf_op jit(solution)/shard_map/ppermute | solution.py:110
  310.6 61.8 %collective-permute-start.20 = (bf16[160,4480]{1,0:T(8,128)(2,1)}, bf16[160,4480]{1,0:T(8,128)(2,1)}, u32[]{:S(2)}, u32[]{:S(2)}) collective-permute-start(bf16[160,4480]{1,0:T(8,128)(2,1)} %collective-permute-done.18.refs_0_), channel_id=1, source_target_pairs={{0,1},{1,0},{2,3},{3,2},{4,5},{5,4},{6,7},{7,6}} | collective-permute-start | bytes 4300808 | tf_op jit(solution)/shard_map/ppermute | solution.py:110
  348.0 147.0 %collective-permute-start.59 = (bf16[32,4480]{1,0:T(8,128)(2,1)}, bf16[32,4480]{1,0:T(8,128)(2,1)S(1)}, u32[]{:S(2)}, u32[]{:S(2)}) collective-permute-start(bf16[32,4480]{1,0:T(8,128)(2,1)} %get-tuple-element.95), channel_id=1, source_target_pairs={{0,1},{1,0},{2,3},{3,2},{4,5},{5,4},{6,7},{7,6}} | collective-permute-start | bytes 860168 | tf_op jit(solution)/shard_map/ppermute | solution.py:110
  372.1 128.9 %collective-permute-start.45 = (bf16[32,4480]{1,0:T(8,128)(2,1)}, bf16[32,4480]{1,0:T(8,128)(2,1)S(1)}, u32[]{:S(2)}, u32[]{:S(2)}) collective-permute-start(bf16[32,4480]{1,0:T(8,128)(2,1)} %get-tuple-element.95), channel_id=1, source_target_pairs={{0,2},{2,0},{1,3},{3,1},{4,6},{6,4},{5,7},{7,5}} | collective-permute-start | bytes 860168 | tf_op jit(solution)/shard_map/ppermute | solution.py:110
  372.4 246.4 %collective-permute-start.53 = (bf16[160,4480]{1,0:T(8,128)(2,1)}, bf16[160,4480]{1,0:T(8,128)(2,1)}, u32[]{:S(2)}, u32[]{:S(2)}) collective-permute-start(bf16[160,4480]{1,0:T(8,128)(2,1)} %get-tuple-element.98), channel_id=1, source_target_pairs={{0,2},{2,0},{1,3},{3,1},{4,6},{6,4},{5,7},{7,5}} | collective-permute-start | bytes 4300808 | tf_op jit(solution)/shard_map/ppermute | solution.py:110
  433.5 234.8 %collective-permute-start.56 = (bf16[320,4480]{1,0:T(8,128)(2,1)}, bf16[320,4480]{1,0:T(8,128)(2,1)}, u32[]{:S(2)}, u32[]{:S(2)}) collective-permute-start(bf16[320,4480]{1,0:T(8,128)(2,1)} %get-tuple-element.99), channel_id=1, source_target_pairs={{0,2},{2,0},{1,3},{3,1},{4,6},{6,4},{5,7},{7,5}} | collective-permute-start | bytes 8601608 | tf_op jit(solution)/shard_map/ppermute | solution.py:110
  494.9 173.8 %collective-permute-start.57 = (bf16[320,4480]{1,0:T(8,128)(2,1)}, bf16[320,4480]{1,0:T(8,128)(2,1)}, u32[]{:S(2)}, u32[]{:S(2)}) collective-permute-start(bf16[320,4480]{1,0:T(8,128)(2,1)} %get-tuple-element.99), channel_id=1, source_target_pairs={{0,1},{1,0},{2,3},{3,2},{4,5},{5,4},{6,7},{7,6}} | collective-permute-start | bytes 8601608 | tf_op jit(solution)/shard_map/ppermute | solution.py:110
  495.0 106.5 %collective-permute-start.47 = (bf16[48,4480]{1,0:T(8,128)(2,1)}, bf16[48,4480]{1,0:T(8,128)(2,1)S(1)}, u32[]{:S(2)}, u32[]{:S(2)}) collective-permute-start(bf16[48,4480]{1,0:T(8,128)(2,1)} %get-tuple-element.96), channel_id=1, source_target_pairs={{0,2},{2,0},{1,3},{3,1},{4,6},{6,4},{5,7},{7,5}} | collective-permute-start | bytes 1290248 | tf_op jit(solution)/shard_map/ppermute | solution.py:110
  501.0 100.8 %collective-permute-start.48 = (bf16[48,4480]{1,0:T(8,128)(2,1)}, bf16[48,4480]{1,0:T(8,128)(2,1)S(1)}, u32[]{:S(2)}, u32[]{:S(2)}) collective-permute-start(bf16[48,4480]{1,0:T(8,128)(2,1)} %get-tuple-element.96), channel_id=1, source_target_pairs={{0,1},{1,0},{2,3},{3,2},{4,5},{5,4},{6,7},{7,6}} | collective-permute-start | bytes 1290248 | tf_op jit(solution)/shard_map/ppermute | solution.py:110
  618.9 20.3 %collective-permute-start.54 = (bf16[160,4480]{1,0:T(8,128)(2,1)}, bf16[160,4480]{1,0:T(8,128)(2,1)}, u32[]{:S(2)}, u32[]{:S(2)}) collective-permute-start(bf16[160,4480]{1,0:T(8,128)(2,1)} %get-tuple-element.98), channel_id=1, source_target_pairs={{0,1},{1,0},{2,3},{3,2},{4,5},{5,4},{6,7},{7,6}} | collective-permute-start | bytes 4300808 | tf_op jit(solution)/shard_map/ppermute | solution.py:110
  618.9 34.2 %collective-permute-start.55 = (bf16[160,4480]{1,0:T(8,128)(2,1)}, bf16[160,4480]{1,0:T(8,128)(2,1)}, u32[]{:S(2)}, u32[]{:S(2)}) collective-permute-start(bf16[160,4480]{1,0:T(8,128)(2,1)} %collective-permute-done.53.refs_0_), channel_id=1, source_target_pairs={{0,1},{1,0},{2,3},{3,2},{4,5},{5,4},{6,7},{7,6}} | collective-permute-start | bytes 4300808 | tf_op jit(solution)/shard_map/ppermute | solution.py:110
  624.9 28.1 %collective-permute-start.52 = (bf16[80,4480]{1,0:T(8,128)(2,1)}, bf16[80,4480]{1,0:T(8,128)(2,1)}, u32[]{:S(2)}, u32[]{:S(2)}) collective-permute-start(bf16[80,4480]{1,0:T(8,128)(2,1)} %collective-permute-done.50.refs_0_), channel_id=1, source_target_pairs={{0,1},{1,0},{2,3},{3,2},{4,5},{5,4},{6,7},{7,6}} | collective-permute-start | bytes 2150408 | tf_op jit(solution)/shard_map/ppermute | solution.py:110
  639.1 65.3 %collective-permute-start.15 = (bf16[320,4480]{1,0:T(8,128)(2,1)}, bf16[320,4480]{1,0:T(8,128)(2,1)}, u32[]{:S(2)}, u32[]{:S(2)}) collective-permute-start(bf16[320,4480]{1,0:T(8,128)(2,1)} %get-tuple-element.77), channel_id=1, source_target_pairs={{0,2},{2,0},{1,3},{3,1},{4,6},{6,4},{5,7},{7,5}} | collective-permute-start | bytes 8601608 | tf_op jit(solution)/shard_map/ppermute | solution.py:110
  653.0 51.5 %collective-permute-start.16 = (bf16[320,4480]{1,0:T(8,128)(2,1)}, bf16[320,4480]{1,0:T(8,128)(2,1)}, u32[]{:S(2)}, u32[]{:S(2)}) collective-permute-start(bf16[320,4480]{1,0:T(8,128)(2,1)} %get-tuple-element.77), channel_id=1, source_target_pairs={{0,1},{1,0},{2,3},{3,2},{4,5},{5,4},{6,7},{7,6}} | collective-permute-start | bytes 8601608 | tf_op jit(solution)/shard_map/ppermute | solution.py:110
  653.1 112.8 %collective-permute-start.69 = (bf16[1120,1280]{1,0:T(8,128)(2,1)}, bf16[1120,1280]{1,0:T(8,128)(2,1)}, u32[]{:S(2)}, u32[]{:S(2)}) collective-permute-start(bf16[1120,1280]{1,0:T(8,128)(2,1)} %get-tuple-element.105), channel_id=1, source_target_pairs={{0,2},{2,0},{1,3},{3,1},{4,6},{6,4},{5,7},{7,5}} | collective-permute-start | bytes 8601608 | tf_op jit(solution)/shard_map/ppermute | solution.py:110
  668.3 158.2 %collective-permute-start.66 = (bf16[1120,1280]{1,0:T(8,128)(2,1)}, bf16[1120,1280]{1,0:T(8,128)(2,1)}, u32[]{:S(2)}, u32[]{:S(2)}) collective-permute-start(bf16[1120,1280]{1,0:T(8,128)(2,1)} %get-tuple-element.104), channel_id=1, source_target_pairs={{0,2},{2,0},{1,3},{3,1},{4,6},{6,4},{5,7},{7,5}} | collective-permute-start | bytes 8601608 | tf_op jit(solution)/shard_map/ppermute | solution.py:110
  668.8 157.7 %collective-permute-start.58 = (bf16[320,4480]{1,0:T(8,128)(2,1)}, bf16[320,4480]{1,0:T(8,128)(2,1)}, u32[]{:S(2)}, u32[]{:S(2)}) collective-permute-start(bf16[320,4480]{1,0:T(8,128)(2,1)} %collective-permute-done.56.refs_0_), channel_id=1, source_target_pairs={{0,1},{1,0},{2,3},{3,2},{4,5},{5,4},{6,7},{7,6}} | collective-permute-start | bytes 8601608 | tf_op jit(solution)/shard_map/ppermute | solution.py:110
  704.5 152.1 %collective-permute-start.17 = (bf16[320,4480]{1,0:T(8,128)(2,1)}, bf16[320,4480]{1,0:T(8,128)(2,1)}, u32[]{:S(2)}, u32[]{:S(2)}) collective-permute-start(bf16[320,4480]{1,0:T(8,128)(2,1)} %collective-permute-done.15.refs_0_), channel_id=1, source_target_pairs={{0,1},{1,0},{2,3},{3,2},{4,5},{5,4},{6,7},{7,6}} | collective-permute-start | bytes 8601608 | tf_op jit(solution)/shard_map/ppermute | solution.py:110
  704.5 158.8 %collective-permute-start.70 = (bf16[1120,1280]{1,0:T(8,128)(2,1)}, bf16[1120,1280]{1,0:T(8,128)(2,1)}, u32[]{:S(2)}, u32[]{:S(2)}) collective-permute-start(bf16[1120,1280]{1,0:T(8,128)(2,1)} %get-tuple-element.105), channel_id=1, source_target_pairs={{0,1},{1,0},{2,3},{3,2},{4,5},{5,4},{6,7},{7,6}} | collective-permute-start | bytes 8601608 | tf_op jit(solution)/shard_map/ppermute | solution.py:110
  765.9 97.3 %collective-permute-start.71 = (bf16[1120,1280]{1,0:T(8,128)(2,1)}, bf16[1120,1280]{1,0:T(8,128)(2,1)}, u32[]{:S(2)}, u32[]{:S(2)}) collective-permute-start(bf16[1120,1280]{1,0:T(8,128)(2,1)} %collective-permute-done.69.refs_0_), channel_id=1, source_target_pairs={{0,1},{1,0},{2,3},{3,2},{4,5},{5,4},{6,7},{7,6}} | collective-permute-start | bytes 8601608 | tf_op jit(solution)/shard_map/ppermute | solution.py:110
  826.5 43.4 %collective-permute-start.67 = (bf16[1120,1280]{1,0:T(8,128)(2,1)}, bf16[1120,1280]{1,0:T(8,128)(2,1)}, u32[]{:S(2)}, u32[]{:S(2)}) collective-permute-start(bf16[1120,1280]{1,0:T(8,128)(2,1)} %get-tuple-element.104), channel_id=1, source_target_pairs={{0,1},{1,0},{2,3},{3,2},{4,5},{5,4},{6,7},{7,6}} | collective-permute-start | bytes 8601608 | tf_op jit(solution)/shard_map/ppermute | solution.py:110
  826.5 43.4 %collective-permute-start.68 = (bf16[1120,1280]{1,0:T(8,128)(2,1)}, bf16[1120,1280]{1,0:T(8,128)(2,1)}, u32[]{:S(2)}, u32[]{:S(2)}) collective-permute-start(bf16[1120,1280]{1,0:T(8,128)(2,1)} %collective-permute-done.66.refs_0_), channel_id=1, source_target_pairs={{0,1},{1,0},{2,3},{3,2},{4,5},{5,4},{6,7},{7,6}} | collective-permute-start | bytes 8601608 | tf_op jit(solution)/shard_map/ppermute | solution.py:110
  (36 other events, 442.4 us)

commit v5 on v4

--- a/solution.py
+++ b/solution.py
@@ -12,28 +12,37 @@
 MATE = [(0, 1), (1, 0), (2, 3), (3, 2)]
 UNITS = 20
 
-CHUNKS = [
-    (0, 0, 0, 1, 1, 1, 1),
-    (0, 0, 1, 3, 1, 3, 1),
-    (0, 0, 4, 6, 2, 2, 2),
-    (0, 0, 10, 10, 2, 10, 10),
-    (0, 1, 0, 20, 4, 20, 10),
-    (2, 0, 0, 20, 4, 20, 10),
-    (2, 1, 0, 20, 4, 20, 10),
-    (1, 0, 0, 20, 4, 20, 10),
-    (1, 1, 0, 10, 2, 10, 10),
-    (1, 1, 10, 5, 1, 5, 5),
-    (1, 1, 15, 3, 1, 1, 1),
-    (1, 1, 18, 2, 2, 2, 2),
+SUMS = [
+    (0, 0, 0, 2, 2),
+    (0, 0, 2, 2, 2),
+    (0, 0, 4, 6, 2),
+    (0, 0, 10, 10, 10),
+    (0, 1, 0, 20, 20),
+    (2, 0, 0, 20, 20),
+    (2, 1, 0, 20, 20),
+    (1, 0, 0, 20, 20),
+    (1, 1, 0, 20, 20),
+]
+NEWS = [
+    (0, 0, 0, 20, 20),
+    (0, 1, 0, 20, 10),
+    (2, 0, 0, 20, 10),
+    (2, 1, 0, 20, 10),
+    (1, 0, 0, 20, 10),
+    (1, 1, 0, 10, 10),
+    (1, 1, 10, 4, 2),
+    (1, 1, 14, 4, 2),
+    (1, 1, 18, 2, 2),
 ]
 EARLY = 2
-LAST = len(CHUNKS) - 1
+LAST = len(NEWS) - 1
 
 FULL = 67043328
-SPARE = {"cutf_0": 4 << 20, "cutf_1": 4 << 20, "sum_0": 4 << 20, "sum_1": 4 << 20, "cutf_2": 160 << 10, "cutf_3": 160 << 10}
-SPARE |= {"place_10": 320 << 10, "place_last": 1 << 20}
-
-ANY = pl.BlockSpec(memory_space=pl.ANY)
+SPARE = {"cutf_0": 4 << 20, "cutf_1": 4 << 20, "sum_0": 4 << 20, "cutf_2": 2 << 20, "sum_1": 4 << 20}
+SPARE |= {name: 600 << 10 for name in ("cutf_3", "sum_2", "cutf_4")}
+SPARE |= {f"place_{LAST - 1}": 320 << 10, "place_last": 1 << 20}
+
+ANY = pl.BlockSpec(memory_space=pltpu.HBM)
 WHOLE = pl.BlockSpec(memory_space=pltpu.VMEM)
 DMA = pltpu.SemaphoreType.DMA
 
@@ -118,29 +127,31 @@
         def move_scratch(w, copies, b):
             return [pltpu.VMEM((copies, b * rows[w], cols[w]), jnp.bfloat16), DMA((copies,)), DMA((copies,))]
 
-        def term_spec(w, layer, u0, b, of):
-            return pl.BlockSpec((1, 1, b * rows[w], cols[w]), lambda i: (0, layer, of(me()) * (UNITS // b) + u0 // b + i, 0))
-
-        def full_spec(w, layer, u0, b, of):
-            return pl.BlockSpec((1, b * rows[w], cols[w]), lambda i: (layer, of(me()) * (UNITS // b) + u0 // b + i, 0))
-
-        def piece_spec(w, b):
-            return pl.BlockSpec((b * rows[w], cols[w]), lambda i: (i, 0))
-
-        def cut(k, of, tag):
-            w, layer, u0, n, b = CHUNKS[k][:5]
+        def pieces_of(n, most=4):
+            return n // next(c for c in range(most, 0, -1) if n % c == 0)
+
+        def term_spec(w, layer, u0, b, of, **mode):
+            return pl.BlockSpec((1, 1, b * rows[w], cols[w]), lambda i: (0, layer, of(me()) * (UNITS // b) + u0 // b + i, 0), **mode)
+
+        def full_spec(w, layer, u0, b, of, **mode):
+            return pl.BlockSpec((1, b * rows[w], cols[w]), lambda i: (layer, of(me()) * (UNITS // b) + u0 // b + i, 0), **mode)
+
+        def piece_spec(w, b, u0=0, **mode):
+            return pl.BlockSpec((b * rows[w], cols[w]), lambda i: (u0 // b + i, 0), **mode)
+
+        def cut(name, w, spans, of):
+            b = pieces_of(spans[0][2])
+            starts = [(layer, u0 + i) for layer, u0, n in spans for i in range(0, n, b)]
 
             def body(t, o, *scratch):
-                first = of(me()) * UNITS + u0
-                move([(t.at[0, layer, at(w, first + i, b)], o.at[at(w, i, b)]) for i in range(0, n, b)], *scratch)
-
-            (one,) = run(
-                f"cut{tag}_{k}", body, (), [in_space(terms[w], pltpu.HBM)], [ANY], [shape(w, n)], [ANY], {}, move_scratch(w, n // b, b)
-            )
-            return send(one, MATE)
+                first = of(me()) * UNITS
+                move([(t.at[0, layer, at(w, first + u, b)], o.at[at(w, i * b, b)]) for i, (layer, u) in enumerate(starts)], *scratch)
+
+            term, count = in_space(terms[w], pltpu.HBM), len(starts)
+            return run(name, body, (), [term], [ANY], [shape(w, count * b)], [ANY], {}, move_scratch(w, count, b))[0]
 
         def cut_early(k):
-            w, layer, u0, n = CHUNKS[k][:4]
+            w, layer, u0, n, _ = SUMS[k]
 
             def body(t, *refs):
                 copies = [
@@ -153,69 +164,65 @@
                     one.wait()
 
             outs = [shape(w, n, pltpu.VMEM)] * 2
-            mine, own = run(f"cutf_{k}", body, (), [in_space(terms[w], pltpu.HBM)], [ANY], outs, [WHOLE] * 2, {}, [DMA((2,))])
-            return send(mine, MATE, pltpu.VMEM), own
-
-        def sum_early(k, got, own):
-            w, _, _, n = CHUNKS[k][:4]
+            return run(f"cutf_{k}", body, (), [in_space(terms[w], pltpu.HBM)], [ANY], outs, [WHOLE] * 2, {}, [DMA((2,))])
+
+        def sum_early(k, own, got):
+            w, _, _, n, _ = SUMS[k]
 
             def body(t, r, o):
                 o[...] = add(t[...], r[...])
 
-            grid, outs, specs = ((1,), [shape(w, n)], [piece_spec(w, n)]) if k else ((), [shape(w, n, pltpu.VMEM)], [WHOLE])
-            (one,) = run(f"sum_{k}", body, grid, [in_space(own, pltpu.VMEM), got], [WHOLE] * 2, outs, specs, {})
+            (one,) = run(f"sum_{k}", body, (), [in_space(own, pltpu.VMEM), got], [WHOLE] * 2, [shape(w, n, pltpu.VMEM)], [WHOLE], {})
             return send(one, FAR)
 
         def chip_sum(k, got):
-            w, layer, u0, n, _, b, _ = CHUNKS[k]
+            w, layer, u0, n, b = SUMS[k]
 
             def body(t, r, o):
                 o[...] = add(t[0, 0], r[...])
 
-            (one,) = run(
-                f"sum_{k}",
-                body,
-                (n // b,),
-                [terms[w], got],
-                [term_spec(w, layer, u0, b, far_of), piece_spec(w, b)],
-                [shape(w, n)],
-                [piece_spec(w, b)],
-                {},
-            )
+            specs = [term_spec(w, layer, u0, b, far_of), piece_spec(w, b)]
+            (one,) = run(f"sum_{k}", body, (n // b,), [terms[w], got], specs, [shape(w, n)], [piece_spec(w, b)], {})
             return send(one, FAR)
 
-        def update(k, mate_term, far_sum):
-            w, layer, u0, n, _, _, b = CHUNKS[k]
-
-            def body(*refs):
-                t, r, f, wt, mm, vv = refs[:6]
+        def update(k, mate_term, far_sums):
+            w, layer, u0, n, b = NEWS[k]
+            many = len(far_sums) > 1
+            mode = {"pipeline_mode": pl.Buffered(1)} if n == b == UNITS else {}
+
+            def body(t, r, wt, mm, vv, *refs):
                 o, full, mo, vo = refs[-4:]
-                g = t[0, 0].astype(jnp.float32) + r[...].astype(jnp.float32) + f[...].astype(jnp.float32)
-                g = g.astype(jnp.bfloat16).astype(jnp.float32)
-                new, mo[0], vo[0] = adamw(wt[0].astype(jnp.float32), mm[0], vv[0], g)
-                o[...] = new
-                full[0] = new
-
-            moment = pl.BlockSpec((1, b * rows[w], cols[w]), lambda i: (layer, u0 // b + i, 0))
-            mine = full_spec(w, layer, u0, b, me_of)
-            ins = [terms[w], mate_term, far_sum, weights[w], m[w], v[w]]
-            specs = [term_spec(w, layer, u0, b, me_of), piece_spec(w, b), piece_spec(w, b), mine, moment, moment]
+                first = 0
+                for f in refs[: len(far_sums)]:
+                    at = pl.ds(first, f.shape[0])
+                    g = t[0, 0, at].astype(jnp.float32) + r[at].astype(jnp.float32) + f[...].astype(jnp.float32)
+                    g = g.astype(jnp.bfloat16).astype(jnp.float32)
+                    new, mo[0, at], vo[0, at] = adamw(wt[0, at].astype(jnp.float32), mm[0, at], vv[0, at], g)
+                    o[at] = new
+                    full[0, at] = new
+                    first += f.shape[0]
+
+            moment = pl.BlockSpec((1, b * rows[w], cols[w]), lambda i: (layer, u0 // b + i, 0), **mode)
+            mine = full_spec(w, layer, u0, b, me_of, **mode)
+            out = piece_spec(w, b, **mode)
+            ins = [terms[w], mate_term, weights[w], m[w], v[w], *far_sums]
+            specs = [term_spec(w, layer, u0, b, me_of, **mode), piece_spec(w, b, layer * UNITS + u0, **mode), mine, moment, moment]
+            specs += [pl.BlockSpec(f.shape, lambda i: (0, 0), **mode) if many else piece_spec(w, b, u0, **mode) for f in far_sums]
             aliases = {}
             if new_w[w] is not None:
+                aliases = {len(ins) + j: 1 + j for j in range(3)}
                 ins += [new_w[w], new_m[w], new_v[w]]
                 specs += [ANY] * 3
-                aliases = {6: 1, 7: 2, 8: 3}
             outs = [shape(w, n), *(jax.ShapeDtypeStruct(a.shape, a.dtype) for a in (weights[w], m[w], v[w]))]
-            out, new_w[w], new_m[w], new_v[w] = run(
-                f"adam_{k}", body, (n // b,), ins, specs, outs, [piece_spec(w, b), mine, moment, moment], aliases
-            )
+            new, new_w[w], new_m[w], new_v[w] = run(f"adam_{k}", body, (n // b,), ins, specs, outs, [out, mine, moment, moment], aliases)
             if k < LAST:
-                return send(out, FAR), send(out, MATE)
-            place(k, "place_own", [send(out, MATE)], [mate_of])
-            return out
+                return send(new, FAR), send(new, MATE)
+            place(k, "place_own", [send(new, MATE)], [mate_of])
+            return new
 
         def place(k, name, pieces, owners):
-            w, layer, u0, n, b = CHUNKS[k][:5]
+            w, layer, u0, n, _ = NEWS[k]
+            b = pieces_of(n)
 
             def body(*refs):
                 count = len(pieces)
@@ -240,7 +247,7 @@
             )
 
         def place_last(far, far_mate):
-            w, layer, u0, n = CHUNKS[LAST][:4]
+            w, layer, u0, n, _ = NEWS[LAST]
 
             def body(far, far_mate, _, full, sem):
                 copies = [
@@ -255,20 +262,26 @@
             like = jax.ShapeDtypeStruct(weights[w].shape, jnp.bfloat16)
             (new_w[w],) = run("place_last", body, (), [far, far_mate, new_w[w]], [WHOLE, WHOLE, ANY], [like], [ANY], {2: 0}, [DMA((2,))])
 
-        count = len(CHUNKS)
-        got, far_sum, mate_term, out = ([None] * count for _ in range(4))
-        early = [cut_early(k) for k in range(EARLY)]
-        for k in range(EARLY):
-            far_sum[k] = sum_early(k, *early[k])
-        got[EARLY] = cut(EARLY, far_mate_of, "f")
-        for k in range(EARLY, count):
-            if k + 1 < count:
-                got[k + 1] = cut(k + 1, far_mate_of, "f")
-            far_sum[k] = chip_sum(k, got[k])
-        for k in range(count):
-            mate_term[k] = cut(k, mate_of, "m")
-        for k in range(count):
-            out[k] = update(k, mate_term[k], far_sum[k])
+        def for_mate(k):
+            w, layer, u0, n, _ = SUMS[k]
+            return (cut(f"cutf_{k}", w, [(layer, u0, n)], far_mate_of),) if k >= EARLY else cut_early(k)
+
+        def to_mate(k, piece):
+            return send(piece, MATE, pltpu.VMEM if k < EARLY else pltpu.HBM)
+
+        cuts, got, far_sum = [for_mate(0)], [], []
+        for k in range(len(SUMS)):
+            got.append(to_mate(k, cuts[k][0]))
+            if k + 1 < len(SUMS):
+                cuts.append(for_mate(k + 1))
+            far_sum.append(chip_sum(k, got[k]) if k >= EARLY else sum_early(k, cuts[k][1], got[k]))
+        mate_term = {}
+        for w in (0, 2, 1):
+            piece = cut(f"cutm_{w}", w, [(layer, 0, UNITS) for layer in range(2)], mate_of)
+            mate_term[w] = send(piece, MATE)
+        out = []
+        for k, (w, layer, *_) in enumerate(NEWS):
+            out.append(update(k, mate_term[w], [f for f, of in zip(far_sum, SUMS) if of[:2] == (w, layer)]))
         for k in range(LAST):
             if k == LAST - 1:
                 last = send(out[LAST], FAR, pltpu.VMEM)

time: 878 us -> 860 us (0.979)
  Pallas kernels: 241 us -> 207 us
  waiting for transfers between devices: 597 us -> 617 us
    pallas_call x61 -> x40, Pallas kernels: 241 us -> 207 us  [run(): pl.pallas_call(body, out_shape=outs, grid=grid, in_specs=in_specs, out_sp...]
    ppermute x72 -> x48, waiting for transfers between devices: 597 us -> 617 us  [send(): return in_space(lax.ppermute(x, 'dp', pairs), space)]
    ppermute x72 -> x48, starting transfers between devices: 31.6 us -> 30.9 us  [send(): return in_space(lax.ppermute(x, 'dp', pairs), space)]
  transfers between devices with their start and end apart: 72 -> 48, of which waited for: 22 -> 16; matrix products, arithmetic and copies ran while one was open for 0% -> 0% of each run, Pallas kernels for 27% -> 23%
where the time goes in v5:
time: 860 us; the launch traced here: 859 us
  waiting for transfers between devices  617 us (72%)
  Pallas kernels  207 us (24%)
  starting transfers between devices  30.9 us (4%)
    ppermute x48, waiting for transfers between devices, send(): return in_space(lax.ppermute(x, 'dp', pairs), space)  617 us
    pallas_call x40, Pallas kernels, run(): pl.pallas_call(body, out_shape=outs, grid=grid, in_specs=in_specs, out_sp...  207 us
    ppermute x48, starting transfers between devices, send(): return in_space(lax.ppermute(x, 'dp', pairs), space)  30.9 us
  transfers between devices with their start and end apart: 48, of which 16 were waited for; matrix products, arithmetic and copies ran while one was open for 0% of the time, Pallas kernels for 23%

profile of v5, /device:TPU:0, one launch (start us, length us, event | category | flops | bytes accessed | tf_op | source)
XLA Modules:
  0.0 859.3 jit_solution(1365050380735281371)
XLA Ops:
  3.7 2.7 shard_map.203
  11.5 2.7 shard_map.205
  14.2 3.2 shard_map.197
  17.5 3.0 collective-permute-start.10
  24.5 3.2 shard_map.195
  30.5 28.7 %collective-permute-done.6.refs_1_ = bf16[32,4480]{1,0:T(8,128)(2,1)} collective-permute-done((bf16[32,4480]{1,0:T(8,128)(2,1)}, bf16[32,4480]{1,0:T(8,128)(2,1)}, u32[]{:S(2)}, u32[]{:S(2)}) %collective-permute-start.6) | collective-permute-done | bytes 286752 | tf_op jit(solution)/shard_map/ppermute | solution.py:119
  61.2 2.7 shard_map.188
  63.9 19.1 %collective-permute-done.4.refs_0_ = bf16[32,4480]{1,0:T(8,128)(2,1)} collective-permute-done((bf16[32,4480]{1,0:T(8,128)(2,1)}, bf16[32,4480]{1,0:T(8,128)(2,1)}, u32[]{:S(2)}, u32[]{:S(2)}) %collective-permute-start.4) | collective-permute-done | bytes 286752 | tf_op jit(solution)/shard_map/ppermute | solution.py:119
  83.1 5.1 shard_map.202
  88.7 2.7 shard_map.219
  91.5 2.7 shard_map.221
  94.8 4.9 shard_map.204
  101.4 4.9 shard_map.206
  106.6 5.1 shard_map.187
  111.7 5.1 shard_map.218
  117.4 4.9 shard_map.189
  122.3 42.7 %collective-permute-done.19.refs_0_ = bf16[320,4480]{1,0:T(8,128)(2,1)} collective-permute-done((bf16[320,4480]{1,0:T(8,128)(2,1)}, bf16[320,4480]{1,0:T(8,128)(2,1)}, u32[]{:S(2)}, u32[]{:S(2)}) %collective-permute-start.19) | collective-permute-done | bytes 2867232 | tf_op jit(solution)/shard_map/ppermute | solution.py:119
  166.7 4.9 shard_map.220
  171.6 54.8 %collective-permute-done.21.refs_0_ = bf16[320,4480]{1,0:T(8,128)(2,1)} collective-permute-done((bf16[320,4480]{1,0:T(8,128)(2,1)}, bf16[320,4480]{1,0:T(8,128)(2,1)}, u32[]{:S(2)}, u32[]{:S(2)}) %collective-permute-start.21) | collective-permute-done | bytes 2867232 | tf_op jit(solution)/shard_map/ppermute | solution.py:119
  228.2 4.9 shard_map.222
  233.4 13.5 %shard_map.207 = (bf16[320,4480]{1,0:T(8,128)(2,1)}, bf16[2,1280,4480]{2,1,0:T(8,128)(2,1)}, f32[2,320,4480]{2,1,0:T(8,128)}, f32[2,320,4480]{2,1,0:T(8,128)}) custom-call(bf16[1,2,1280,4480]{3,2,1,0:T(8,128)(2,1)} %t.48, bf16[640,4480]{1,0:T(8,128)(2,1)} %collective-permute-done.17.r, bf16[2,1280,4480]{2,1,0:T(8,128)(2,1)} %wt.15, f32[2,320,4480]{2,1,0:T(8,128)} %mm.15, ...), custom_call_target="tpu_custom_call" | custom-call | flops 37273600 | bytes 37273600 | tf_op jit(solution)/shard_map/pallas_call | solution.py:106
  246.8 9.8 %shard_map.208 = (bf16[160,4480]{1,0:T(8,128)(2,1)}, bf16[2,1280,4480]{2,1,0:T(8,128)(2,1)}, f32[2,320,4480]{2,1,0:T(8,128)}, f32[2,320,4480]{2,1,0:T(8,128)}) custom-call(bf16[1,2,1280,4480]{3,2,1,0:T(8,128)(2,1)} %t.48, bf16[640,4480]{1,0:T(8,128)(2,1)} %collective-permute-done.17.r, ...), custom_call_target="tpu_custom_call", output_to_operand_aliasing={{1}: (6, {}), {2}: (7, {}), {3}: (8, {})} | custom-call | flops 35840000 | bytes 35840000 | tf_op jit(solution)/shard_map/pallas_call | solution.py:106
  256.6 31.2 %collective-permute-done.2.refs_0_ = bf16[320,4480]{1,0:T(8,128)(2,1)} collective-permute-done((bf16[320,4480]{1,0:T(8,128)(2,1)}, bf16[320,4480]{1,0:T(8,128)(2,1)}, u32[]{:S(2)}, u32[]{:S(2)}) %collective-permute-start.2) | collective-permute-done | bytes 2867232 | tf_op jit(solution)/shard_map/ppermute | solution.py:119
  289.6 4.0 shard_map.209
  293.6 4.0 shard_map.210
  297.6 3.2 shard_map.211
  300.7 48.6 %collective-permute-done.39.refs_0_ = bf16[1120,1280]{1,0:T(8,128)(2,1)} collective-permute-done((bf16[1120,1280]{1,0:T(8,128)(2,1)}, bf16[1120,1280]{1,0:T(8,128)(2,1)}, u32[]{:S(2)}, u32[]{:S(2)}) %collective-permute-start.39) | collective-permute-done | bytes 2867232 | tf_op jit(solution)/shard_map/ppermute | solution.py:119
  351.1 59.7 %collective-permute-done.41.refs_0_ = bf16[1120,1280]{1,0:T(8,128)(2,1)} collective-permute-done((bf16[1120,1280]{1,0:T(8,128)(2,1)}, bf16[1120,1280]{1,0:T(8,128)(2,1)}, u32[]{:S(2)}, u32[]{:S(2)}) %collective-permute-start.41) | collective-permute-done | bytes 2867232 | tf_op jit(solution)/shard_map/ppermute | solution.py:119
  410.8 35.8 %collective-permute-done.22.far = bf16[32,4480]{1,0:T(8,128)(2,1)S(1)} collective-permute-done((bf16[32,4480]{1,0:T(8,128)(2,1)}, bf16[32,4480]{1,0:T(8,128)(2,1)S(1)}, u32[]{:S(2)}, u32[]{:S(2)}) %collective-permute-start.22) | collective-permute-done | bytes 286752 | tf_op jit(solution)/shard_map/ppermute | solution.py:119
  454.2 10.3 %collective-permute-done.24.refs_0_ = bf16[64,4480]{1,0:T(8,128)(2,1)} collective-permute-done((bf16[64,4480]{1,0:T(8,128)(2,1)}, bf16[64,4480]{1,0:T(8,128)(2,1)}, u32[]{:S(2)}, u32[]{:S(2)}) %collective-permute-start.24) | collective-permute-done | bytes 573472 | tf_op jit(solution)/shard_map/ppermute | solution.py:119
  464.5 11.4 %collective-permute-done.27.refs_0_ = bf16[64,4480]{1,0:T(8,128)(2,1)} collective-permute-done((bf16[64,4480]{1,0:T(8,128)(2,1)}, bf16[64,4480]{1,0:T(8,128)(2,1)}, u32[]{:S(2)}, u32[]{:S(2)}) %collective-permute-start.27) | collective-permute-done | bytes 573472 | tf_op jit(solution)/shard_map/ppermute | solution.py:119
  475.9 13.7 %shard_map.223 = (bf16[1120,1280]{1,0:T(8,128)(2,1)}, bf16[2,4480,1280]{2,1,0:T(8,128)(2,1)}, f32[2,1120,1280]{2,1,0:T(8,128)}, f32[2,1120,1280]{2,1,0:T(8,128)}) custom-call(bf16[1,2,4480,1280]{3,2,1,0:T(8,128)(2,1)} %t.55, bf16[2240,1280]{1,0:T(8,128)(2,1)} %collective-permute-done.37.r, bf16[2,4480,1280]{2,1,0:T(8,128)(2,1)} %wt.17, ...), custom_call_target="tpu_custom_call" | custom-call | flops 37273600 | bytes 37273600 | tf_op jit(solution)/shard_map/pallas_call | solution.py:106
  489.6 13.6 %shard_map.224 = (bf16[1120,1280]{1,0:T(8,128)(2,1)}, bf16[2,4480,1280]{2,1,0:T(8,128)(2,1)}, f32[2,1120,1280]{2,1,0:T(8,128)}, f32[2,1120,1280]{2,1,0:T(8,128)}) custom-call(bf16[1,2,4480,1280]{3,2,1,0:T(8,128)(2,1)} %t.55, bf16[2240,1280]{1,0:T(8,128)(2,1)} %collective-permute-done.37.r, ...), custom_call_target="tpu_custom_call", output_to_operand_aliasing={{1}: (6, {}), {2}: (7, {}), {3}: (8, {})} | custom-call | flops 37273600 | bytes 37273600 | tf_op jit(solution)/shard_map/pallas_call | solution.py:106
  507.2 17.8 %shard_map.198 = (bf16[320,4480]{1,0:T(8,128)(2,1)}, bf16[2,1280,4480]{2,1,0:T(8,128)(2,1)}, f32[2,320,4480]{2,1,0:T(8,128)}, f32[2,320,4480]{2,1,0:T(8,128)}) custom-call(bf16[1,2,1280,4480]{3,2,1,0:T(8,128)(2,1)} %t.38, bf16[640,4480]{1,0:T(8,128)(2,1)} %collective-permute-done.r, bf16[2,1280,4480]{2,1,0:T(8,128)(2,1)} %wt.10, f32[2,320,4480]{2,1,0:T(8,128)} %mm.10, ...), custom_call_target="tpu_custom_call" | custom-call | flops 37273600 | bytes 37273600 | tf_op jit(solution)/shard_map/pallas_call | solution.py:106
  525.1 13.8 %shard_map.199 = (bf16[320,4480]{1,0:T(8,128)(2,1)}, bf16[2,1280,4480]{2,1,0:T(8,128)(2,1)}, f32[2,320,4480]{2,1,0:T(8,128)}, f32[2,320,4480]{2,1,0:T(8,128)}) custom-call(bf16[1,2,1280,4480]{3,2,1,0:T(8,128)(2,1)} %t.38, bf16[640,4480]{1,0:T(8,128)(2,1)} %collective-permute-done.r, ...), custom_call_target="tpu_custom_call", output_to_operand_aliasing={{1}: (6, {}), {2}: (7, {}), {3}: (8, {})} | custom-call | flops 37273600 | bytes 37273600 | tf_op jit(solution)/shard_map/pallas_call | solution.py:106
  538.9 29.9 %collective-permute-done.42.refs_0_ = bf16[1120,1280]{1,0:T(8,128)(2,1)} collective-permute-done((bf16[1120,1280]{1,0:T(8,128)(2,1)}, bf16[1120,1280]{1,0:T(8,128)(2,1)}, u32[]{:S(2)}, u32[]{:S(2)}) %collective-permute-start.42) | collective-permute-done | bytes 2867232 | tf_op jit(solution)/shard_map/ppermute | solution.py:119
  570.8 59.4 %collective-permute-done.45.refs_0_ = bf16[1120,1280]{1,0:T(8,128)(2,1)} collective-permute-done((bf16[1120,1280]{1,0:T(8,128)(2,1)}, bf16[1120,1280]{1,0:T(8,128)(2,1)}, u32[]{:S(2)}, u32[]{:S(2)}) %collective-permute-start.45) | collective-permute-done | bytes 2867232 | tf_op jit(solution)/shard_map/ppermute | solution.py:119
  630.2 61.4 %collective-permute-done.33.refs_0_ = bf16[320,4480]{1,0:T(8,128)(2,1)} collective-permute-done((bf16[320,4480]{1,0:T(8,128)(2,1)}, bf16[320,4480]{1,0:T(8,128)(2,1)}, u32[]{:S(2)}, u32[]{:S(2)}) %collective-permute-start.33) | collective-permute-done | bytes 2867232 | tf_op jit(solution)/shard_map/ppermute | solution.py:119
  692.2 60.9 %collective-permute-done.11.refs_0_ = bf16[320,4480]{1,0:T(8,128)(2,1)} collective-permute-done((bf16[320,4480]{1,0:T(8,128)(2,1)}, bf16[320,4480]{1,0:T(8,128)(2,1)}, u32[]{:S(2)}, u32[]{:S(2)}) %collective-permute-start.11) | collective-permute-done | bytes 2867232 | tf_op jit(solution)/shard_map/ppermute | solution.py:119
  753.1 60.7 %collective-permute-done.14.refs_0_ = bf16[320,4480]{1,0:T(8,128)(2,1)} collective-permute-done((bf16[320,4480]{1,0:T(8,128)(2,1)}, bf16[320,4480]{1,0:T(8,128)(2,1)}, u32[]{:S(2)}, u32[]{:S(2)}) %collective-permute-start.14) | collective-permute-done | bytes 2867232 | tf_op jit(solution)/shard_map/ppermute | solution.py:119
  816.0 6.5 shard_map.213.refs_3_
  822.6 3.6 shard_map.214.refs_3_
  826.2 2.4 shard_map.215.refs_3_
  828.6 2.4 shard_map.216._
  832.8 6.6 shard_map.225.refs_3_
  839.4 6.6 shard_map.226
  846.0 6.5 shard_map.200.refs_3_
  852.6 6.5 shard_map.201
  (102 shorter events, 46.1 us)
Async XLA Ops:
  2.9 11.3 %collective-permute-start.9 = (bf16[160,4480]{1,0:T(8,128)(2,1)}, bf16[160,4480]{1,0:T(8,128)(2,1)}, u32[]{:S(2)}, u32[]{:S(2)}) collective-permute-start(bf16[160,4480]{1,0:T(8,128)(2,1)} %shard_map.196), channel_id=1, source_target_pairs={{0,1},{1,0},{2,3},{3,2},{4,5},{5,4},{6,7},{7,6}} | collective-permute-start | bytes 4300808 | tf_op jit(solution)/shard_map/ppermute | solution.py:119
  6.5 87.8 %collective-permute-start.18 = (bf16[320,4480]{1,0:T(8,128)(2,1)}, bf16[320,4480]{1,0:T(8,128)(2,1)}, u32[]{:S(2)}, u32[]{:S(2)}) collective-permute-start(bf16[320,4480]{1,0:T(8,128)(2,1)} %shard_map.203), channel_id=1, source_target_pairs={{0,1},{1,0},{2,3},{3,2},{4,5},{5,4},{6,7},{7,6}} | collective-permute-start | bytes 8601608 | tf_op jit(solution)/shard_map/ppermute | solution.py:119
  8.5 16.0 %collective-permute-start.7 = (bf16[96,4480]{1,0:T(8,128)(2,1)}, bf16[96,4480]{1,0:T(8,128)(2,1)}, u32[]{:S(2)}, u32[]{:S(2)}) collective-permute-start(bf16[96,4480]{1,0:T(8,128)(2,1)} %shard_map.194), channel_id=1, source_target_pairs={{0,1},{1,0},{2,3},{3,2},{4,5},{5,4},{6,7},{7,6}} | collective-permute-start | bytes 2580488 | tf_op jit(solution)/shard_map/ppermute | solution.py:119
  11.5 10.8 %collective-permute-start.5 = (bf16[32,4480]{1,0:T(8,128)(2,1)}, bf16[32,4480]{1,0:T(8,128)(2,1)}, u32[]{:S(2)}, u32[]{:S(2)}) collective-permute-start(bf16[32,4480]{1,0:T(8,128)(2,1)} %get-tuple-element.52), channel_id=1, source_target_pairs={{0,1},{1,0},{2,3},{3,2},{4,5},{5,4},{6,7},{7,6}} | collective-permute-start | bytes 860168 | tf_op jit(solution)/shard_map/ppermute | solution.py:119
  17.5 74.0 %collective-permute-start.10 = (bf16[160,4480]{1,0:T(8,128)(2,1)}, bf16[160,4480]{1,0:T(8,128)(2,1)}, u32[]{:S(2)}, u32[]{:S(2)}) collective-permute-start(bf16[160,4480]{1,0:T(8,128)(2,1)} %shard_map.197), channel_id=1, source_target_pairs={{0,2},{2,0},{1,3},{3,1},{4,6},{6,4},{5,7},{7,5}} | collective-permute-start | bytes 4300808 | tf_op jit(solution)/shard_map/ppermute | solution.py:119
  20.4 79.2 %collective-permute-start.20 = (bf16[320,4480]{1,0:T(8,128)(2,1)}, bf16[320,4480]{1,0:T(8,128)(2,1)}, u32[]{:S(2)}, u32[]{:S(2)}) collective-permute-start(bf16[320,4480]{1,0:T(8,128)(2,1)} %shard_map.205), channel_id=1, source_target_pairs={{0,1},{1,0},{2,3},{3,2},{4,5},{5,4},{6,7},{7,6}} | collective-permute-start | bytes 8601608 | tf_op jit(solution)/shard_map/ppermute | solution.py:119
  22.2 5.5 collective-permute-start.3
  24.5 34.7 %collective-permute-start.6 = (bf16[32,4480]{1,0:T(8,128)(2,1)}, bf16[32,4480]{1,0:T(8,128)(2,1)}, u32[]{:S(2)}, u32[]{:S(2)}) collective-permute-start(bf16[32,4480]{1,0:T(8,128)(2,1)} %shard_map.193), channel_id=1, source_target_pairs={{0,2},{2,0},{1,3},{3,1},{4,6},{6,4},{5,7},{7,5}} | collective-permute-start | bytes 860168 | tf_op jit(solution)/shard_map/ppermute | solution.py:119
  27.7 60.5 %collective-permute-start.8 = (bf16[96,4480]{1,0:T(8,128)(2,1)}, bf16[96,4480]{1,0:T(8,128)(2,1)}, u32[]{:S(2)}, u32[]{:S(2)}) collective-permute-start(bf16[96,4480]{1,0:T(8,128)(2,1)} %shard_map.195), channel_id=1, source_target_pairs={{0,2},{2,0},{1,3},{3,1},{4,6},{6,4},{5,7},{7,5}} | collective-permute-start | bytes 2580488 | tf_op jit(solution)/shard_map/ppermute | solution.py:119
  59.1 23.9 %collective-permute-start.4 = (bf16[32,4480]{1,0:T(8,128)(2,1)}, bf16[32,4480]{1,0:T(8,128)(2,1)}, u32[]{:S(2)}, u32[]{:S(2)}) collective-permute-start(bf16[32,4480]{1,0:T(8,128)(2,1)} %shard_map.191), channel_id=1, source_target_pairs={{0,2},{2,0},{1,3},{3,1},{4,6},{6,4},{5,7},{7,5}} | collective-permute-start | bytes 860168 | tf_op jit(solution)/shard_map/ppermute | solution.py:119
  83.1 23.3 %collective-permute-start.1 = (bf16[320,4480]{1,0:T(8,128)(2,1)}, bf16[320,4480]{1,0:T(8,128)(2,1)}, u32[]{:S(2)}, u32[]{:S(2)}) collective-permute-start(bf16[320,4480]{1,0:T(8,128)(2,1)} %shard_map.188), channel_id=1, source_target_pairs={{0,1},{1,0},{2,3},{3,2},{4,5},{5,4},{6,7},{7,6}} | collective-permute-start | bytes 8601608 | tf_op jit(solution)/shard_map/ppermute | solution.py:119
  88.2 144.9 %collective-permute-start.17 = (bf16[640,4480]{1,0:T(8,128)(2,1)}, bf16[640,4480]{1,0:T(8,128)(2,1)}, u32[]{:S(2)}, u32[]{:S(2)}) collective-permute-start(bf16[640,4480]{1,0:T(8,128)(2,1)} %shard_map.202), channel_id=1, source_target_pairs={{0,1},{1,0},{2,3},{3,2},{4,5},{5,4},{6,7},{7,6}} | collective-permute-start | bytes 17203208 | tf_op jit(solution)/shard_map/ppermute | solution.py:119
  91.5 20.2 %collective-permute-start.38 = (bf16[1120,1280]{1,0:T(8,128)(2,1)}, bf16[1120,1280]{1,0:T(8,128)(2,1)}, u32[]{:S(2)}, u32[]{:S(2)}) collective-permute-start(bf16[1120,1280]{1,0:T(8,128)(2,1)} %shard_map.219), channel_id=1, source_target_pairs={{0,1},{1,0},{2,3},{3,2},{4,5},{5,4},{6,7},{7,6}} | collective-permute-start | bytes 8601608 | tf_op jit(solution)/shard_map/ppermute | solution.py:119
  94.3 22.6 %collective-permute-start.40 = (bf16[1120,1280]{1,0:T(8,128)(2,1)}, bf16[1120,1280]{1,0:T(8,128)(2,1)}, u32[]{:S(2)}, u32[]{:S(2)}) collective-permute-start(bf16[1120,1280]{1,0:T(8,128)(2,1)} %shard_map.221), channel_id=1, source_target_pairs={{0,1},{1,0},{2,3},{3,2},{4,5},{5,4},{6,7},{7,6}} | collective-permute-start | bytes 8601608 | tf_op jit(solution)/shard_map/ppermute | solution.py:119
  99.7 65.3 %collective-permute-start.19 = (bf16[320,4480]{1,0:T(8,128)(2,1)}, bf16[320,4480]{1,0:T(8,128)(2,1)}, u32[]{:S(2)}, u32[]{:S(2)}) collective-permute-start(bf16[320,4480]{1,0:T(8,128)(2,1)} %shard_map.204), channel_id=1, source_target_pairs={{0,2},{2,0},{1,3},{3,1},{4,6},{6,4},{5,7},{7,5}} | collective-permute-start | bytes 8601608 | tf_op jit(solution)/shard_map/ppermute | solution.py:119
  106.3 120.1 %collective-permute-start.21 = (bf16[320,4480]{1,0:T(8,128)(2,1)}, bf16[320,4480]{1,0:T(8,128)(2,1)}, u32[]{:S(2)}, u32[]{:S(2)}) collective-permute-start(bf16[320,4480]{1,0:T(8,128)(2,1)} %shard_map.206), channel_id=1, source_target_pairs={{0,2},{2,0},{1,3},{3,1},{4,6},{6,4},{5,7},{7,5}} | collective-permute-start | bytes 8601608 | tf_op jit(solution)/shard_map/ppermute | solution.py:119
  111.7 335.6 %collective-permute-start = (bf16[640,4480]{1,0:T(8,128)(2,1)}, bf16[640,4480]{1,0:T(8,128)(2,1)}, u32[]{:S(2)}, u32[]{:S(2)}) collective-permute-start(bf16[640,4480]{1,0:T(8,128)(2,1)} %shard_map.187), channel_id=1, source_target_pairs={{0,1},{1,0},{2,3},{3,2},{4,5},{5,4},{6,7},{7,6}} | collective-permute-start | bytes 17203208 | tf_op jit(solution)/shard_map/ppermute | solution.py:119
  116.9 331.0 %collective-permute-start.37 = (bf16[2240,1280]{1,0:T(8,128)(2,1)}, bf16[2240,1280]{1,0:T(8,128)(2,1)}, u32[]{:S(2)}, u32[]{:S(2)}) collective-permute-start(bf16[2240,1280]{1,0:T(8,128)(2,1)} %shard_map.218), channel_id=1, source_target_pairs={{0,1},{1,0},{2,3},{3,2},{4,5},{5,4},{6,7},{7,6}} | collective-permute-start | bytes 17203208 | tf_op jit(solution)/shard_map/ppermute | solution.py:119
  165.0 122.9 %collective-permute-start.2 = (bf16[320,4480]{1,0:T(8,128)(2,1)}, bf16[320,4480]{1,0:T(8,128)(2,1)}, u32[]{:S(2)}, u32[]{:S(2)}) collective-permute-start(bf16[320,4480]{1,0:T(8,128)(2,1)} %shard_map.189), channel_id=1, source_target_pairs={{0,2},{2,0},{1,3},{3,1},{4,6},{6,4},{5,7},{7,5}} | collective-permute-start | bytes 8601608 | tf_op jit(solution)/shard_map/ppermute | solution.py:119
  226.4 122.9 %collective-permute-start.39 = (bf16[1120,1280]{1,0:T(8,128)(2,1)}, bf16[1120,1280]{1,0:T(8,128)(2,1)}, u32[]{:S(2)}, u32[]{:S(2)}) collective-permute-start(bf16[1120,1280]{1,0:T(8,128)(2,1)} %shard_map.220), channel_id=1, source_target_pairs={{0,2},{2,0},{1,3},{3,1},{4,6},{6,4},{5,7},{7,5}} | collective-permute-start | bytes 8601608 | tf_op jit(solution)/shard_map/ppermute | solution.py:119
  233.1 177.7 %collective-permute-start.41 = (bf16[1120,1280]{1,0:T(8,128)(2,1)}, bf16[1120,1280]{1,0:T(8,128)(2,1)}, u32[]{:S(2)}, u32[]{:S(2)}) collective-permute-start(bf16[1120,1280]{1,0:T(8,128)(2,1)} %shard_map.222), channel_id=1, source_target_pairs={{0,2},{2,0},{1,3},{3,1},{4,6},{6,4},{5,7},{7,5}} | collective-permute-start | bytes 8601608 | tf_op jit(solution)/shard_map/ppermute | solution.py:119
  287.9 159.9 %collective-permute-start.30 = (bf16[160,4480]{1,0:T(8,128)(2,1)}, bf16[160,4480]{1,0:T(8,128)(2,1)}, u32[]{:S(2)}, u32[]{:S(2)}) collective-permute-start(bf16[160,4480]{1,0:T(8,128)(2,1)} %get-tuple-element.74), channel_id=1, source_target_pairs={{0,2},{2,0},{1,3},{3,1},{4,6},{6,4},{5,7},{7,5}} | collective-permute-start | bytes 4300808 | tf_op jit(solution)/shard_map/ppermute | solution.py:119
  349.3 97.3 %collective-permute-start.22 = (bf16[32,4480]{1,0:T(8,128)(2,1)}, bf16[32,4480]{1,0:T(8,128)(2,1)S(1)}, u32[]{:S(2)}, u32[]{:S(2)}) collective-permute-start(bf16[32,4480]{1,0:T(8,128)(2,1)} %get-tuple-element.71), channel_id=1, source_target_pairs={{0,2},{2,0},{1,3},{3,1},{4,6},{6,4},{5,7},{7,5}} | collective-permute-start | bytes 860168 | tf_op jit(solution)/shard_map/ppermute | solution.py:119
  410.8 37.6 %collective-permute-start.36 = (bf16[32,4480]{1,0:T(8,128)(2,1)}, bf16[32,4480]{1,0:T(8,128)(2,1)S(1)}, u32[]{:S(2)}, u32[]{:S(2)}) collective-permute-start(bf16[32,4480]{1,0:T(8,128)(2,1)} %get-tuple-element.71), channel_id=1, source_target_pairs={{0,1},{1,0},{2,3},{3,2},{4,5},{5,4},{6,7},{7,6}} | collective-permute-start | bytes 860168 | tf_op jit(solution)/shard_map/ppermute | solution.py:119
  446.6 3.5 collective-permute-start.23
  447.3 57.9 %collective-permute-start.31 = (bf16[160,4480]{1,0:T(8,128)(2,1)}, bf16[160,4480]{1,0:T(8,128)(2,1)}, u32[]{:S(2)}, u32[]{:S(2)}) collective-permute-start(bf16[160,4480]{1,0:T(8,128)(2,1)} %get-tuple-element.74), channel_id=1, source_target_pairs={{0,1},{1,0},{2,3},{3,2},{4,5},{5,4},{6,7},{7,6}} | collective-permute-start | bytes 4300808 | tf_op jit(solution)/shard_map/ppermute | solution.py:119
  447.8 57.7 %collective-permute-start.32 = (bf16[160,4480]{1,0:T(8,128)(2,1)}, bf16[160,4480]{1,0:T(8,128)(2,1)}, u32[]{:S(2)}, u32[]{:S(2)}) collective-permute-start(bf16[160,4480]{1,0:T(8,128)(2,1)} %collective-permute-done.30.refs_0_), channel_id=1, source_target_pairs={{0,1},{1,0},{2,3},{3,2},{4,5},{5,4},{6,7},{7,6}} | collective-permute-start | bytes 4300808 | tf_op jit(solution)/shard_map/ppermute | solution.py:119
  447.8 6.0 collective-permute-start.25
  448.3 16.2 %collective-permute-start.24 = (bf16[64,4480]{1,0:T(8,128)(2,1)}, bf16[64,4480]{1,0:T(8,128)(2,1)}, u32[]{:S(2)}, u32[]{:S(2)}) collective-permute-start(bf16[64,4480]{1,0:T(8,128)(2,1)} %get-tuple-element.72), channel_id=1, source_target_pairs={{0,2},{2,0},{1,3},{3,1},{4,6},{6,4},{5,7},{7,5}} | collective-permute-start | bytes 1720328 | tf_op jit(solution)/shard_map/ppermute | solution.py:119
  450.8 25.1 %collective-permute-start.27 = (bf16[64,4480]{1,0:T(8,128)(2,1)}, bf16[64,4480]{1,0:T(8,128)(2,1)}, u32[]{:S(2)}, u32[]{:S(2)}) collective-permute-start(bf16[64,4480]{1,0:T(8,128)(2,1)} %get-tuple-element.73), channel_id=1, source_target_pairs={{0,2},{2,0},{1,3},{3,1},{4,6},{6,4},{5,7},{7,5}} | collective-permute-start | bytes 1720328 | tf_op jit(solution)/shard_map/ppermute | solution.py:119
  453.9 49.3 %collective-permute-start.28 = (bf16[64,4480]{1,0:T(8,128)(2,1)}, bf16[64,4480]{1,0:T(8,128)(2,1)}, u32[]{:S(2)}, u32[]{:S(2)}) collective-permute-start(bf16[64,4480]{1,0:T(8,128)(2,1)} %get-tuple-element.73), channel_id=1, source_target_pairs={{0,1},{1,0},{2,3},{3,2},{4,5},{5,4},{6,7},{7,6}} | collective-permute-start | bytes 1720328 | tf_op jit(solution)/shard_map/ppermute | solution.py:119
  464.5 39.0 %collective-permute-start.26 = (bf16[64,4480]{1,0:T(8,128)(2,1)}, bf16[64,4480]{1,0:T(8,128)(2,1)}, u32[]{:S(2)}, u32[]{:S(2)}) collective-permute-start(bf16[64,4480]{1,0:T(8,128)(2,1)} %collective-permute-done.24.refs_0_), channel_id=1, source_target_pairs={{0,1},{1,0},{2,3},{3,2},{4,5},{5,4},{6,7},{7,6}} | collective-permute-start | bytes 1720328 | tf_op jit(solution)/shard_map/ppermute | solution.py:119
  475.8 29.3 %collective-permute-start.29 = (bf16[64,4480]{1,0:T(8,128)(2,1)}, bf16[64,4480]{1,0:T(8,128)(2,1)}, u32[]{:S(2)}, u32[]{:S(2)}) collective-permute-start(bf16[64,4480]{1,0:T(8,128)(2,1)} %collective-permute-done.27.refs_0_), channel_id=1, source_target_pairs={{0,1},{1,0},{2,3},{3,2},{4,5},{5,4},{6,7},{7,6}} | collective-permute-start | bytes 1720328 | tf_op jit(solution)/shard_map/ppermute | solution.py:119
  503.2 21.9 %collective-permute-start.43 = (bf16[1120,1280]{1,0:T(8,128)(2,1)}, bf16[1120,1280]{1,0:T(8,128)(2,1)}, u32[]{:S(2)}, u32[]{:S(2)}) collective-permute-start(bf16[1120,1280]{1,0:T(8,128)(2,1)} %get-tuple-element.80), channel_id=1, source_target_pairs={{0,1},{1,0},{2,3},{3,2},{4,5},{5,4},{6,7},{7,6}} | collective-permute-start | bytes 8601608 | tf_op jit(solution)/shard_map/ppermute | solution.py:119
  503.4 65.3 %collective-permute-start.42 = (bf16[1120,1280]{1,0:T(8,128)(2,1)}, bf16[1120,1280]{1,0:T(8,128)(2,1)}, u32[]{:S(2)}, u32[]{:S(2)}) collective-permute-start(bf16[1120,1280]{1,0:T(8,128)(2,1)} %get-tuple-element.80), channel_id=1, source_target_pairs={{0,2},{2,0},{1,3},{3,1},{4,6},{6,4},{5,7},{7,5}} | collective-permute-start | bytes 8601608 | tf_op jit(solution)/shard_map/ppermute | solution.py:119
  505.2 65.3 %collective-permute-start.46 = (bf16[1120,1280]{1,0:T(8,128)(2,1)}, bf16[1120,1280]{1,0:T(8,128)(2,1)}, u32[]{:S(2)}, u32[]{:S(2)}) collective-permute-start(bf16[1120,1280]{1,0:T(8,128)(2,1)} %get-tuple-element.81), channel_id=1, source_target_pairs={{0,1},{1,0},{2,3},{3,2},{4,5},{5,4},{6,7},{7,6}} | collective-permute-start | bytes 8601608 | tf_op jit(solution)/shard_map/ppermute | solution.py:119
  505.2 125.0 %collective-permute-start.45 = (bf16[1120,1280]{1,0:T(8,128)(2,1)}, bf16[1120,1280]{1,0:T(8,128)(2,1)}, u32[]{:S(2)}, u32[]{:S(2)}) collective-permute-start(bf16[1120,1280]{1,0:T(8,128)(2,1)} %get-tuple-element.81), channel_id=1, source_target_pairs={{0,2},{2,0},{1,3},{3,1},{4,6},{6,4},{5,7},{7,5}} | collective-permute-start | bytes 8601608 | tf_op jit(solution)/shard_map/ppermute | solution.py:119
  505.5 186.1 %collective-permute-start.33 = (bf16[320,4480]{1,0:T(8,128)(2,1)}, bf16[320,4480]{1,0:T(8,128)(2,1)}, u32[]{:S(2)}, u32[]{:S(2)}) collective-permute-start(bf16[320,4480]{1,0:T(8,128)(2,1)} %get-tuple-element.75), channel_id=1, source_target_pairs={{0,2},{2,0},{1,3},{3,1},{4,6},{6,4},{5,7},{7,5}} | collective-permute-start | bytes 8601608 | tf_op jit(solution)/shard_map/ppermute | solution.py:119
  525.0 166.6 %collective-permute-start.34 = (bf16[320,4480]{1,0:T(8,128)(2,1)}, bf16[320,4480]{1,0:T(8,128)(2,1)}, u32[]{:S(2)}, u32[]{:S(2)}) collective-permute-start(bf16[320,4480]{1,0:T(8,128)(2,1)} %get-tuple-element.75), channel_id=1, source_target_pairs={{0,1},{1,0},{2,3},{3,2},{4,5},{5,4},{6,7},{7,6}} | collective-permute-start | bytes 8601608 | tf_op jit(solution)/shard_map/ppermute | solution.py:119
  568.8 184.3 %collective-permute-start.11 = (bf16[320,4480]{1,0:T(8,128)(2,1)}, bf16[320,4480]{1,0:T(8,128)(2,1)}, u32[]{:S(2)}, u32[]{:S(2)}) collective-permute-start(bf16[320,4480]{1,0:T(8,128)(2,1)} %get-tuple-element.56), channel_id=1, source_target_pairs={{0,2},{2,0},{1,3},{3,1},{4,6},{6,4},{5,7},{7,5}} | collective-permute-start | bytes 8601608 | tf_op jit(solution)/shard_map/ppermute | solution.py:119
  570.5 243.3 %collective-permute-start.14 = (bf16[320,4480]{1,0:T(8,128)(2,1)}, bf16[320,4480]{1,0:T(8,128)(2,1)}, u32[]{:S(2)}, u32[]{:S(2)}) collective-permute-start(bf16[320,4480]{1,0:T(8,128)(2,1)} %get-tuple-element.57), channel_id=1, source_target_pairs={{0,2},{2,0},{1,3},{3,1},{4,6},{6,4},{5,7},{7,5}} | collective-permute-start | bytes 8601608 | tf_op jit(solution)/shard_map/ppermute | solution.py:119
  630.2 183.6 %collective-permute-start.47 = (bf16[1120,1280]{1,0:T(8,128)(2,1)}, bf16[1120,1280]{1,0:T(8,128)(2,1)}, u32[]{:S(2)}, u32[]{:S(2)}) collective-permute-start(bf16[1120,1280]{1,0:T(8,128)(2,1)} %collective-permute-done.45.refs_0_), channel_id=1, source_target_pairs={{0,1},{1,0},{2,3},{3,2},{4,5},{5,4},{6,7},{7,6}} | collective-permute-start | bytes 8601608 | tf_op jit(solution)/shard_map/ppermute | solution.py:119
  691.7 122.7 %collective-permute-start.35 = (bf16[320,4480]{1,0:T(8,128)(2,1)}, bf16[320,4480]{1,0:T(8,128)(2,1)}, u32[]{:S(2)}, u32[]{:S(2)}) collective-permute-start(bf16[320,4480]{1,0:T(8,128)(2,1)} %collective-permute-done.33.refs_0_), channel_id=1, source_target_pairs={{0,1},{1,0},{2,3},{3,2},{4,5},{5,4},{6,7},{7,6}} | collective-permute-start | bytes 8601608 | tf_op jit(solution)/shard_map/ppermute | solution.py:119
  691.7 147.7 %collective-permute-start.44 = (bf16[1120,1280]{1,0:T(8,128)(2,1)}, bf16[1120,1280]{1,0:T(8,128)(2,1)}, u32[]{:S(2)}, u32[]{:S(2)}) collective-permute-start(bf16[1120,1280]{1,0:T(8,128)(2,1)} %collective-permute-done.42.refs_0_), channel_id=1, source_target_pairs={{0,1},{1,0},{2,3},{3,2},{4,5},{5,4},{6,7},{7,6}} | collective-permute-start | bytes 8601608 | tf_op jit(solution)/shard_map/ppermute | solution.py:119
  753.1 92.9 %collective-permute-start.15 = (bf16[320,4480]{1,0:T(8,128)(2,1)}, bf16[320,4480]{1,0:T(8,128)(2,1)}, u32[]{:S(2)}, u32[]{:S(2)}) collective-permute-start(bf16[320,4480]{1,0:T(8,128)(2,1)} %get-tuple-element.57), channel_id=1, source_target_pairs={{0,1},{1,0},{2,3},{3,2},{4,5},{5,4},{6,7},{7,6}} | collective-permute-start | bytes 8601608 | tf_op jit(solution)/shard_map/ppermute | solution.py:119
  813.8 32.2 %collective-permute-start.16 = (bf16[320,4480]{1,0:T(8,128)(2,1)}, bf16[320,4480]{1,0:T(8,128)(2,1)}, u32[]{:S(2)}, u32[]{:S(2)}) collective-permute-start(bf16[320,4480]{1,0:T(8,128)(2,1)} %collective-permute-done.14.refs_0_), channel_id=1, source_target_pairs={{0,1},{1,0},{2,3},{3,2},{4,5},{5,4},{6,7},{7,6}} | collective-permute-start | bytes 8601608 | tf_op jit(solution)/shard_map/ppermute | solution.py:119
  813.8 38.7 %collective-permute-start.12 = (bf16[320,4480]{1,0:T(8,128)(2,1)}, bf16[320,4480]{1,0:T(8,128)(2,1)}, u32[]{:S(2)}, u32[]{:S(2)}) collective-permute-start(bf16[320,4480]{1,0:T(8,128)(2,1)} %get-tuple-element.56), channel_id=1, source_target_pairs={{0,1},{1,0},{2,3},{3,2},{4,5},{5,4},{6,7},{7,6}} | collective-permute-start | bytes 8601608 | tf_op jit(solution)/shard_map/ppermute | solution.py:119
  814.3 38.2 %collective-permute-start.13 = (bf16[320,4480]{1,0:T(8,128)(2,1)}, bf16[320,4480]{1,0:T(8,128)(2,1)}, u32[]{:S(2)}, u32[]{:S(2)}) collective-permute-start(bf16[320,4480]{1,0:T(8,128)(2,1)} %collective-permute-done.11.refs_0_), channel_id=1, source_target_pairs={{0,1},{1,0},{2,3},{3,2},{4,5},{5,4},{6,7},{7,6}} | collective-permute-start | bytes 8601608 | tf_op jit(solution)/shard_map/ppermute | solution.py:119
  (7 other events, 12.6 us)

commit v6 on v5

--- a/solution.py
+++ b/solution.py
@@ -38,7 +38,7 @@
 LAST = len(NEWS) - 1
 
 FULL = 67043328
-SPARE = {"cutf_0": 4 << 20, "cutf_1": 4 << 20, "sum_0": 4 << 20, "cutf_2": 2 << 20, "sum_1": 4 << 20}
+SPARE = {"cutf_2": 2 << 20, "sum_1": 4 << 20}
 SPARE |= {name: 600 << 10 for name in ("cutf_3", "sum_2", "cutf_4")}
 SPARE |= {f"place_{LAST - 1}": 320 << 10, "place_last": 1 << 20}
 
@@ -150,21 +150,42 @@
             term, count = in_space(terms[w], pltpu.HBM), len(starts)
             return run(name, body, (), [term], [ANY], [shape(w, count * b)], [ANY], {}, move_scratch(w, count, b))[0]
 
-        def cut_early(k):
-            w, layer, u0, n, _ = SUMS[k]
-
-            def body(t, *refs):
-                copies = [
-                    pltpu.make_async_copy(t.at[0, layer, at(w, of(me()) * UNITS + u0, n)], to, refs[-1].at[j])
-                    for j, (of, to) in enumerate(((far_mate_of, refs[0]), (far_of, refs[1])))
+        def head():
+            w, layer, u0, n, _ = SUMS[0]
+            _, _, u1, n1, _ = SUMS[1]
+
+            def body(t, o, mine, own, kept, got, sem, send_sem, recv_sem):
+                d = me()
+                mate = {"dp": mate_of(d)}
+                barrier = pltpu.get_barrier_semaphore()
+                pl.semaphore_signal(barrier, inc=1, device_id=mate, device_id_type=pl.DeviceIdType.MESH)
+                loads = [
+                    pltpu.make_async_copy(t.at[0, layer, at(w, of(d) * UNITS + u, to.shape[0] // rows[w])], to, sem.at[j])
+                    for j, (u, of, to) in enumerate(
+                        ((u0, far_of, kept), (u1, far_mate_of, mine), (u1, far_of, own))
+                    )
                 ]
-                for one in copies:
+                pl.semaphore_wait(barrier, 1)
+                copy = pltpu.make_async_remote_copy(t.at[0, layer, at(w, far_mate_of(d) * UNITS + u0, n)], got, send_sem, recv_sem, device_id=mate, device_id_type=pl.DeviceIdType.MESH)
+                copy.start()
+                for one in loads:
                     one.start()
-                for one in copies:
+                for one in loads:
                     one.wait()
-
-            outs = [shape(w, n, pltpu.VMEM)] * 2
-            return run(f"cutf_{k}", body, (), [in_space(terms[w], pltpu.HBM)], [ANY], outs, [WHOLE] * 2, {}, [DMA((2,))])
+                copy.wait_recv()
+                o[...] = add(kept[...], got[...])
+                copy.wait_send()
+
+            return pl.pallas_call(
+                body,
+                out_shape=[shape(w, c, pltpu.VMEM) for c in (n, n1, n1)],
+                in_specs=[ANY],
+                out_specs=[WHOLE] * 3,
+                scratch_shapes=[*[shape(w, n, pltpu.VMEM)] * 2, DMA((3,)), DMA, DMA],
+                name="head",
+                compiler_params=pltpu.CompilerParams(vmem_limit_bytes=FULL - (4 << 20), collective_id=0, has_side_effects=True),
+                cost_estimate=pl.CostEstimate(flops=1 << 20, bytes_accessed=1 << 20, transcendentals=0),
+            )(in_space(terms[w], pltpu.HBM))
 
         def sum_early(k, own, got):
             w, _, _, n, _ = SUMS[k]
@@ -262,19 +283,14 @@
             like = jax.ShapeDtypeStruct(weights[w].shape, jnp.bfloat16)
             (new_w[w],) = run("place_last", body, (), [far, far_mate, new_w[w]], [WHOLE, WHOLE, ANY], [like], [ANY], {2: 0}, [DMA((2,))])
 
-        def for_mate(k):
-            w, layer, u0, n, _ = SUMS[k]
-            return (cut(f"cutf_{k}", w, [(layer, u0, n)], far_mate_of),) if k >= EARLY else cut_early(k)
-
-        def to_mate(k, piece):
-            return send(piece, MATE, pltpu.VMEM if k < EARLY else pltpu.HBM)
-
-        cuts, got, far_sum = [for_mate(0)], [], []
-        for k in range(len(SUMS)):
-            got.append(to_mate(k, cuts[k][0]))
+        first, piece, own = head()
+        far_sum = [send(first, FAR)]
+        for k in range(1, len(SUMS)):
+            got = send(piece, MATE, pltpu.VMEM if k < EARLY else pltpu.HBM)
             if k + 1 < len(SUMS):
-                cuts.append(for_mate(k + 1))
-            far_sum.append(chip_sum(k, got[k]) if k >= EARLY else sum_early(k, cuts[k][1], got[k]))
+                w, layer, u0, n, _ = SUMS[k + 1]
+                piece = cut(f"cutf_{k + 1}", w, [(layer, u0, n)], far_mate_of)
+            far_sum.append(chip_sum(k, got) if k >= EARLY else sum_early(k, own, got))
         mate_term = {}
         for w in (0, 2, 1):
             piece = cut(f"cutm_{w}", w, [(layer, 0, UNITS) for layer in range(2)], mate_of)

time: 860 us -> 858 us (level)
    pallas_call x40 -> x37, Pallas kernels: 207 us -> 202 us  [run(): pl.pallas_call(body, out_shape=outs, grid=grid, in_specs=in_specs, out_sp...]
    ppermute x48 -> x47, waiting for transfers between devices: 617 us -> 615 us  [send(): return in_space(lax.ppermute(x, 'dp', pairs), space)]
    ppermute x48 -> x47, starting transfers between devices: 30.9 us -> 30 us  [send(): return in_space(lax.ppermute(x, 'dp', pairs), space)]
  transfers between devices with their start and end apart: 48 -> 47, of which waited for: 16 -> 16; matrix products, arithmetic and copies ran while one was open for 0% -> 0% of each run, Pallas kernels for 23% -> 23%
where the time goes in v6:
time: 858 us; the launch traced here: 857 us
  waiting for transfers between devices  615 us (72%)
  Pallas kernels  209 us (24%)
  starting transfers between devices  30 us (3%)
    ppermute x47, waiting for transfers between devices, send(): return in_space(lax.ppermute(x, 'dp', pairs), space)  615 us
    pallas_call x37, Pallas kernels, run(): pl.pallas_call(body, out_shape=outs, grid=grid, in_specs=in_specs, out_sp...  202 us
    ppermute x47, starting transfers between devices, send(): return in_space(lax.ppermute(x, 'dp', pairs), space)  30 us
  transfers between devices with their start and end apart: 47, of which 16 were waited for; matrix products, arithmetic and copies ran while one was open for 0% of the time, Pallas kernels for 23%

profile of v6, /device:TPU:0, one launch (start us, length us, event | category | flops | bytes accessed | tf_op | source)
XLA Modules:
  0.0 857.2 jit_solution(8473372196439080760)
XLA Ops:
  3.7 2.7 shard_map.200
  9.0 2.7 shard_map.202
  11.7 3.2 shard_map.194
  14.9 2.5 collective-permute-start.9
  17.7 6.6 head.1
  24.8 3.2 shard_map.192
  30.5 25.6 %collective-permute-done.3.refs_0_ = bf16[32,4480]{1,0:T(8,128)(2,1)} collective-permute-done((bf16[32,4480]{1,0:T(8,128)(2,1)}, bf16[32,4480]{1,0:T(8,128)(2,1)}, u32[]{:S(2)}, u32[]{:S(2)}) %collective-permute-start.3) | collective-permute-done | bytes 286752 | tf_op jit(solution)/shard_map/ppermute | solution.py:119
  58.2 2.7 shard_map.188
  60.9 19.6 %collective-permute-done.5.refs_1_ = bf16[32,4480]{1,0:T(8,128)(2,1)} collective-permute-done((bf16[32,4480]{1,0:T(8,128)(2,1)}, bf16[32,4480]{1,0:T(8,128)(2,1)}, u32[]{:S(2)}, u32[]{:S(2)}) %collective-permute-start.5) | collective-permute-done | bytes 286752 | tf_op jit(solution)/shard_map/ppermute | solution.py:119
  80.5 5.1 shard_map.199
  86.2 2.7 shard_map.216
  89.0 2.7 shard_map.218
  92.2 4.9 shard_map.201
  98.9 4.9 shard_map.203
  104.1 5.1 shard_map.187
  109.2 5.1 shard_map.215
  114.8 4.9 shard_map.189
  119.7 42.7 %collective-permute-done.18.refs_0_ = bf16[320,4480]{1,0:T(8,128)(2,1)} collective-permute-done((bf16[320,4480]{1,0:T(8,128)(2,1)}, bf16[320,4480]{1,0:T(8,128)(2,1)}, u32[]{:S(2)}, u32[]{:S(2)}) %collective-permute-start.18) | collective-permute-done | bytes 2867232 | tf_op jit(solution)/shard_map/ppermute | solution.py:119
  164.2 4.9 shard_map.217
  169.1 54.8 %collective-permute-done.20.refs_0_ = bf16[320,4480]{1,0:T(8,128)(2,1)} collective-permute-done((bf16[320,4480]{1,0:T(8,128)(2,1)}, bf16[320,4480]{1,0:T(8,128)(2,1)}, u32[]{:S(2)}, u32[]{:S(2)}) %collective-permute-start.20) | collective-permute-done | bytes 2867232 | tf_op jit(solution)/shard_map/ppermute | solution.py:119
  225.7 4.9 shard_map.219
  230.8 13.5 %shard_map.204 = (bf16[320,4480]{1,0:T(8,128)(2,1)}, bf16[2,1280,4480]{2,1,0:T(8,128)(2,1)}, f32[2,320,4480]{2,1,0:T(8,128)}, f32[2,320,4480]{2,1,0:T(8,128)}) custom-call(bf16[1,2,1280,4480]{3,2,1,0:T(8,128)(2,1)} %t.46, bf16[640,4480]{1,0:T(8,128)(2,1)} %collective-permute-done.16.r, bf16[2,1280,4480]{2,1,0:T(8,128)(2,1)} %wt.15, f32[2,320,4480]{2,1,0:T(8,128)} %mm.15, ...), custom_call_target="tpu_custom_call" | custom-call | flops 37273600 | bytes 37273600 | tf_op jit(solution)/shard_map/pallas_call | solution.py:106
  244.3 9.8 %shard_map.205 = (bf16[160,4480]{1,0:T(8,128)(2,1)}, bf16[2,1280,4480]{2,1,0:T(8,128)(2,1)}, f32[2,320,4480]{2,1,0:T(8,128)}, f32[2,320,4480]{2,1,0:T(8,128)}) custom-call(bf16[1,2,1280,4480]{3,2,1,0:T(8,128)(2,1)} %t.46, bf16[640,4480]{1,0:T(8,128)(2,1)} %collective-permute-done.16.r, ...), custom_call_target="tpu_custom_call", output_to_operand_aliasing={{1}: (6, {}), {2}: (7, {}), {3}: (8, {})} | custom-call | flops 35840000 | bytes 35840000 | tf_op jit(solution)/shard_map/pallas_call | solution.py:106
  254.1 31.2 %collective-permute-done.2.refs_0_ = bf16[320,4480]{1,0:T(8,128)(2,1)} collective-permute-done((bf16[320,4480]{1,0:T(8,128)(2,1)}, bf16[320,4480]{1,0:T(8,128)(2,1)}, u32[]{:S(2)}, u32[]{:S(2)}) %collective-permute-start.2) | collective-permute-done | bytes 2867232 | tf_op jit(solution)/shard_map/ppermute | solution.py:119
  287.1 4.0 shard_map.206
  291.1 4.0 shard_map.207
  295.0 3.2 shard_map.208
  298.2 48.6 %collective-permute-done.38.refs_0_ = bf16[1120,1280]{1,0:T(8,128)(2,1)} collective-permute-done((bf16[1120,1280]{1,0:T(8,128)(2,1)}, bf16[1120,1280]{1,0:T(8,128)(2,1)}, u32[]{:S(2)}, u32[]{:S(2)}) %collective-permute-start.38) | collective-permute-done | bytes 2867232 | tf_op jit(solution)/shard_map/ppermute | solution.py:119
  348.5 59.7 %collective-permute-done.40.refs_0_ = bf16[1120,1280]{1,0:T(8,128)(2,1)} collective-permute-done((bf16[1120,1280]{1,0:T(8,128)(2,1)}, bf16[1120,1280]{1,0:T(8,128)(2,1)}, u32[]{:S(2)}, u32[]{:S(2)}) %collective-permute-start.40) | collective-permute-done | bytes 2867232 | tf_op jit(solution)/shard_map/ppermute | solution.py:119
  408.2 35.8 %collective-permute-done.21.far = bf16[32,4480]{1,0:T(8,128)(2,1)S(1)} collective-permute-done((bf16[32,4480]{1,0:T(8,128)(2,1)}, bf16[32,4480]{1,0:T(8,128)(2,1)S(1)}, u32[]{:S(2)}, u32[]{:S(2)}) %collective-permute-start.21) | collective-permute-done | bytes 286752 | tf_op jit(solution)/shard_map/ppermute | solution.py:119
  451.7 10.3 %collective-permute-done.23.refs_0_ = bf16[64,4480]{1,0:T(8,128)(2,1)} collective-permute-done((bf16[64,4480]{1,0:T(8,128)(2,1)}, bf16[64,4480]{1,0:T(8,128)(2,1)}, u32[]{:S(2)}, u32[]{:S(2)}) %collective-permute-start.23) | collective-permute-done | bytes 573472 | tf_op jit(solution)/shard_map/ppermute | solution.py:119
  462.0 11.4 %collective-permute-done.26.refs_0_ = bf16[64,4480]{1,0:T(8,128)(2,1)} collective-permute-done((bf16[64,4480]{1,0:T(8,128)(2,1)}, bf16[64,4480]{1,0:T(8,128)(2,1)}, u32[]{:S(2)}, u32[]{:S(2)}) %collective-permute-start.26) | collective-permute-done | bytes 573472 | tf_op jit(solution)/shard_map/ppermute | solution.py:119
  473.3 13.7 %shard_map.220 = (bf16[1120,1280]{1,0:T(8,128)(2,1)}, bf16[2,4480,1280]{2,1,0:T(8,128)(2,1)}, f32[2,1120,1280]{2,1,0:T(8,128)}, f32[2,1120,1280]{2,1,0:T(8,128)}) custom-call(bf16[1,2,4480,1280]{3,2,1,0:T(8,128)(2,1)} %t.53, bf16[2240,1280]{1,0:T(8,128)(2,1)} %collective-permute-done.36.r, bf16[2,4480,1280]{2,1,0:T(8,128)(2,1)} %wt.17, ...), custom_call_target="tpu_custom_call" | custom-call | flops 37273600 | bytes 37273600 | tf_op jit(solution)/shard_map/pallas_call | solution.py:106
  487.0 13.6 %shard_map.221 = (bf16[1120,1280]{1,0:T(8,128)(2,1)}, bf16[2,4480,1280]{2,1,0:T(8,128)(2,1)}, f32[2,1120,1280]{2,1,0:T(8,128)}, f32[2,1120,1280]{2,1,0:T(8,128)}) custom-call(bf16[1,2,4480,1280]{3,2,1,0:T(8,128)(2,1)} %t.53, bf16[2240,1280]{1,0:T(8,128)(2,1)} %collective-permute-done.36.r, ...), custom_call_target="tpu_custom_call", output_to_operand_aliasing={{1}: (6, {}), {2}: (7, {}), {3}: (8, {})} | custom-call | flops 37273600 | bytes 37273600 | tf_op jit(solution)/shard_map/pallas_call | solution.py:106
  504.7 17.8 %shard_map.195 = (bf16[320,4480]{1,0:T(8,128)(2,1)}, bf16[2,1280,4480]{2,1,0:T(8,128)(2,1)}, f32[2,320,4480]{2,1,0:T(8,128)}, f32[2,320,4480]{2,1,0:T(8,128)}) custom-call(bf16[1,2,1280,4480]{3,2,1,0:T(8,128)(2,1)} %t.36, bf16[640,4480]{1,0:T(8,128)(2,1)} %collective-permute-done.r, bf16[2,1280,4480]{2,1,0:T(8,128)(2,1)} %wt.10, f32[2,320,4480]{2,1,0:T(8,128)} %mm.10, ...), custom_call_target="tpu_custom_call" | custom-call | flops 37273600 | bytes 37273600 | tf_op jit(solution)/shard_map/pallas_call | solution.py:106
  522.5 14.0 %shard_map.196 = (bf16[320,4480]{1,0:T(8,128)(2,1)}, bf16[2,1280,4480]{2,1,0:T(8,128)(2,1)}, f32[2,320,4480]{2,1,0:T(8,128)}, f32[2,320,4480]{2,1,0:T(8,128)}) custom-call(bf16[1,2,1280,4480]{3,2,1,0:T(8,128)(2,1)} %t.36, bf16[640,4480]{1,0:T(8,128)(2,1)} %collective-permute-done.r, ...), custom_call_target="tpu_custom_call", output_to_operand_aliasing={{1}: (6, {}), {2}: (7, {}), {3}: (8, {})} | custom-call | flops 37273600 | bytes 37273600 | tf_op jit(solution)/shard_map/pallas_call | solution.py:106
  536.6 29.7 %collective-permute-done.41.refs_0_ = bf16[1120,1280]{1,0:T(8,128)(2,1)} collective-permute-done((bf16[1120,1280]{1,0:T(8,128)(2,1)}, bf16[1120,1280]{1,0:T(8,128)(2,1)}, u32[]{:S(2)}, u32[]{:S(2)}) %collective-permute-start.41) | collective-permute-done | bytes 2867232 | tf_op jit(solution)/shard_map/ppermute | solution.py:119
  568.0 59.7 %collective-permute-done.44.refs_0_ = bf16[1120,1280]{1,0:T(8,128)(2,1)} collective-permute-done((bf16[1120,1280]{1,0:T(8,128)(2,1)}, bf16[1120,1280]{1,0:T(8,128)(2,1)}, u32[]{:S(2)}, u32[]{:S(2)}) %collective-permute-start.44) | collective-permute-done | bytes 2867232 | tf_op jit(solution)/shard_map/ppermute | solution.py:119
  627.7 61.4 %collective-permute-done.32.refs_0_ = bf16[320,4480]{1,0:T(8,128)(2,1)} collective-permute-done((bf16[320,4480]{1,0:T(8,128)(2,1)}, bf16[320,4480]{1,0:T(8,128)(2,1)}, u32[]{:S(2)}, u32[]{:S(2)}) %collective-permute-start.32) | collective-permute-done | bytes 2867232 | tf_op jit(solution)/shard_map/ppermute | solution.py:119
  689.1 61.4 %collective-permute-done.10.refs_0_ = bf16[320,4480]{1,0:T(8,128)(2,1)} collective-permute-done((bf16[320,4480]{1,0:T(8,128)(2,1)}, bf16[320,4480]{1,0:T(8,128)(2,1)}, u32[]{:S(2)}, u32[]{:S(2)}) %collective-permute-start.10) | collective-permute-done | bytes 2867232 | tf_op jit(solution)/shard_map/ppermute | solution.py:119
  750.6 60.7 %collective-permute-done.13.refs_0_ = bf16[320,4480]{1,0:T(8,128)(2,1)} collective-permute-done((bf16[320,4480]{1,0:T(8,128)(2,1)}, bf16[320,4480]{1,0:T(8,128)(2,1)}, u32[]{:S(2)}, u32[]{:S(2)}) %collective-permute-start.13) | collective-permute-done | bytes 2867232 | tf_op jit(solution)/shard_map/ppermute | solution.py:119
  814.0 6.5 shard_map.210.refs_3_
  820.5 3.6 shard_map.211.refs_3_
  826.5 2.4 shard_map.213._
  830.8 6.6 shard_map.222.refs_3_
  837.3 6.6 shard_map.223
  843.9 6.5 shard_map.197.refs_3_
  850.5 6.5 shard_map.198
  (94 shorter events, 42.2 us)
Async XLA Ops:
  2.9 8.8 %collective-permute-start.8 = (bf16[160,4480]{1,0:T(8,128)(2,1)}, bf16[160,4480]{1,0:T(8,128)(2,1)}, u32[]{:S(2)}, u32[]{:S(2)}) collective-permute-start(bf16[160,4480]{1,0:T(8,128)(2,1)} %shard_map.193), channel_id=1, source_target_pairs={{0,1},{1,0},{2,3},{3,2},{4,5},{5,4},{6,7},{7,6}} | collective-permute-start | bytes 4300808 | tf_op jit(solution)/shard_map/ppermute | solution.py:119
  6.5 85.2 %collective-permute-start.17 = (bf16[320,4480]{1,0:T(8,128)(2,1)}, bf16[320,4480]{1,0:T(8,128)(2,1)}, u32[]{:S(2)}, u32[]{:S(2)}) collective-permute-start(bf16[320,4480]{1,0:T(8,128)(2,1)} %shard_map.200), channel_id=1, source_target_pairs={{0,1},{1,0},{2,3},{3,2},{4,5},{5,4},{6,7},{7,6}} | collective-permute-start | bytes 8601608 | tf_op jit(solution)/shard_map/ppermute | solution.py:119
  8.5 16.1 %collective-permute-start.6 = (bf16[96,4480]{1,0:T(8,128)(2,1)}, bf16[96,4480]{1,0:T(8,128)(2,1)}, u32[]{:S(2)}, u32[]{:S(2)}) collective-permute-start(bf16[96,4480]{1,0:T(8,128)(2,1)} %shard_map.191), channel_id=1, source_target_pairs={{0,1},{1,0},{2,3},{3,2},{4,5},{5,4},{6,7},{7,6}} | collective-permute-start | bytes 2580488 | tf_op jit(solution)/shard_map/ppermute | solution.py:119
  14.9 74.0 %collective-permute-start.9 = (bf16[160,4480]{1,0:T(8,128)(2,1)}, bf16[160,4480]{1,0:T(8,128)(2,1)}, u32[]{:S(2)}, u32[]{:S(2)}) collective-permute-start(bf16[160,4480]{1,0:T(8,128)(2,1)} %shard_map.194), channel_id=1, source_target_pairs={{0,2},{2,0},{1,3},{3,1},{4,6},{6,4},{5,7},{7,5}} | collective-permute-start | bytes 4300808 | tf_op jit(solution)/shard_map/ppermute | solution.py:119
  17.4 79.7 %collective-permute-start.19 = (bf16[320,4480]{1,0:T(8,128)(2,1)}, bf16[320,4480]{1,0:T(8,128)(2,1)}, u32[]{:S(2)}, u32[]{:S(2)}) collective-permute-start(bf16[320,4480]{1,0:T(8,128)(2,1)} %shard_map.202), channel_id=1, source_target_pairs={{0,1},{1,0},{2,3},{3,2},{4,5},{5,4},{6,7},{7,6}} | collective-permute-start | bytes 8601608 | tf_op jit(solution)/shard_map/ppermute | solution.py:119
  24.3 3.7 collective-permute-start.4
  24.5 31.6 %collective-permute-start.3 = (bf16[32,4480]{1,0:T(8,128)(2,1)}, bf16[32,4480]{1,0:T(8,128)(2,1)}, u32[]{:S(2)}, u32[]{:S(2)}) collective-permute-start(bf16[32,4480]{1,0:T(8,128)(2,1)} %get-tuple-element.48), channel_id=1, source_target_pairs={{0,2},{2,0},{1,3},{3,1},{4,6},{6,4},{5,7},{7,5}} | collective-permute-start | bytes 860168 | tf_op jit(solution)/shard_map/ppermute | solution.py:119
  28.0 57.6 %collective-permute-start.7 = (bf16[96,4480]{1,0:T(8,128)(2,1)}, bf16[96,4480]{1,0:T(8,128)(2,1)}, u32[]{:S(2)}, u32[]{:S(2)}) collective-permute-start(bf16[96,4480]{1,0:T(8,128)(2,1)} %shard_map.192), channel_id=1, source_target_pairs={{0,2},{2,0},{1,3},{3,1},{4,6},{6,4},{5,7},{7,5}} | collective-permute-start | bytes 2580488 | tf_op jit(solution)/shard_map/ppermute | solution.py:119
  56.2 24.4 %collective-permute-start.5 = (bf16[32,4480]{1,0:T(8,128)(2,1)}, bf16[32,4480]{1,0:T(8,128)(2,1)}, u32[]{:S(2)}, u32[]{:S(2)}) collective-permute-start(bf16[32,4480]{1,0:T(8,128)(2,1)} %shard_map.190), channel_id=1, source_target_pairs={{0,2},{2,0},{1,3},{3,1},{4,6},{6,4},{5,7},{7,5}} | collective-permute-start | bytes 860168 | tf_op jit(solution)/shard_map/ppermute | solution.py:119
  80.5 23.3 %collective-permute-start.1 = (bf16[320,4480]{1,0:T(8,128)(2,1)}, bf16[320,4480]{1,0:T(8,128)(2,1)}, u32[]{:S(2)}, u32[]{:S(2)}) collective-permute-start(bf16[320,4480]{1,0:T(8,128)(2,1)} %shard_map.188), channel_id=1, source_target_pairs={{0,1},{1,0},{2,3},{3,2},{4,5},{5,4},{6,7},{7,6}} | collective-permute-start | bytes 8601608 | tf_op jit(solution)/shard_map/ppermute | solution.py:119
  85.6 144.9 %collective-permute-start.16 = (bf16[640,4480]{1,0:T(8,128)(2,1)}, bf16[640,4480]{1,0:T(8,128)(2,1)}, u32[]{:S(2)}, u32[]{:S(2)}) collective-permute-start(bf16[640,4480]{1,0:T(8,128)(2,1)} %shard_map.199), channel_id=1, source_target_pairs={{0,1},{1,0},{2,3},{3,2},{4,5},{5,4},{6,7},{7,6}} | collective-permute-start | bytes 17203208 | tf_op jit(solution)/shard_map/ppermute | solution.py:119
  88.9 20.2 %collective-permute-start.37 = (bf16[1120,1280]{1,0:T(8,128)(2,1)}, bf16[1120,1280]{1,0:T(8,128)(2,1)}, u32[]{:S(2)}, u32[]{:S(2)}) collective-permute-start(bf16[1120,1280]{1,0:T(8,128)(2,1)} %shard_map.216), channel_id=1, source_target_pairs={{0,1},{1,0},{2,3},{3,2},{4,5},{5,4},{6,7},{7,6}} | collective-permute-start | bytes 8601608 | tf_op jit(solution)/shard_map/ppermute | solution.py:119
  91.7 22.6 %collective-permute-start.39 = (bf16[1120,1280]{1,0:T(8,128)(2,1)}, bf16[1120,1280]{1,0:T(8,128)(2,1)}, u32[]{:S(2)}, u32[]{:S(2)}) collective-permute-start(bf16[1120,1280]{1,0:T(8,128)(2,1)} %shard_map.218), channel_id=1, source_target_pairs={{0,1},{1,0},{2,3},{3,2},{4,5},{5,4},{6,7},{7,6}} | collective-permute-start | bytes 8601608 | tf_op jit(solution)/shard_map/ppermute | solution.py:119
  97.1 65.3 %collective-permute-start.18 = (bf16[320,4480]{1,0:T(8,128)(2,1)}, bf16[320,4480]{1,0:T(8,128)(2,1)}, u32[]{:S(2)}, u32[]{:S(2)}) collective-permute-start(bf16[320,4480]{1,0:T(8,128)(2,1)} %shard_map.201), channel_id=1, source_target_pairs={{0,2},{2,0},{1,3},{3,1},{4,6},{6,4},{5,7},{7,5}} | collective-permute-start | bytes 8601608 | tf_op jit(solution)/shard_map/ppermute | solution.py:119
  103.8 120.1 %collective-permute-start.20 = (bf16[320,4480]{1,0:T(8,128)(2,1)}, bf16[320,4480]{1,0:T(8,128)(2,1)}, u32[]{:S(2)}, u32[]{:S(2)}) collective-permute-start(bf16[320,4480]{1,0:T(8,128)(2,1)} %shard_map.203), channel_id=1, source_target_pairs={{0,2},{2,0},{1,3},{3,1},{4,6},{6,4},{5,7},{7,5}} | collective-permute-start | bytes 8601608 | tf_op jit(solution)/shard_map/ppermute | solution.py:119
  109.2 335.6 %collective-permute-start = (bf16[640,4480]{1,0:T(8,128)(2,1)}, bf16[640,4480]{1,0:T(8,128)(2,1)}, u32[]{:S(2)}, u32[]{:S(2)}) collective-permute-start(bf16[640,4480]{1,0:T(8,128)(2,1)} %shard_map.187), channel_id=1, source_target_pairs={{0,1},{1,0},{2,3},{3,2},{4,5},{5,4},{6,7},{7,6}} | collective-permute-start | bytes 17203208 | tf_op jit(solution)/shard_map/ppermute | solution.py:119
  114.3 331.0 %collective-permute-start.36 = (bf16[2240,1280]{1,0:T(8,128)(2,1)}, bf16[2240,1280]{1,0:T(8,128)(2,1)}, u32[]{:S(2)}, u32[]{:S(2)}) collective-permute-start(bf16[2240,1280]{1,0:T(8,128)(2,1)} %shard_map.215), channel_id=1, source_target_pairs={{0,1},{1,0},{2,3},{3,2},{4,5},{5,4},{6,7},{7,6}} | collective-permute-start | bytes 17203208 | tf_op jit(solution)/shard_map/ppermute | solution.py:119
  162.5 122.9 %collective-permute-start.2 = (bf16[320,4480]{1,0:T(8,128)(2,1)}, bf16[320,4480]{1,0:T(8,128)(2,1)}, u32[]{:S(2)}, u32[]{:S(2)}) collective-permute-start(bf16[320,4480]{1,0:T(8,128)(2,1)} %shard_map.189), channel_id=1, source_target_pairs={{0,2},{2,0},{1,3},{3,1},{4,6},{6,4},{5,7},{7,5}} | collective-permute-start | bytes 8601608 | tf_op jit(solution)/shard_map/ppermute | solution.py:119
  223.9 122.9 %collective-permute-start.38 = (bf16[1120,1280]{1,0:T(8,128)(2,1)}, bf16[1120,1280]{1,0:T(8,128)(2,1)}, u32[]{:S(2)}, u32[]{:S(2)}) collective-permute-start(bf16[1120,1280]{1,0:T(8,128)(2,1)} %shard_map.217), channel_id=1, source_target_pairs={{0,2},{2,0},{1,3},{3,1},{4,6},{6,4},{5,7},{7,5}} | collective-permute-start | bytes 8601608 | tf_op jit(solution)/shard_map/ppermute | solution.py:119
  230.6 177.7 %collective-permute-start.40 = (bf16[1120,1280]{1,0:T(8,128)(2,1)}, bf16[1120,1280]{1,0:T(8,128)(2,1)}, u32[]{:S(2)}, u32[]{:S(2)}) collective-permute-start(bf16[1120,1280]{1,0:T(8,128)(2,1)} %shard_map.219), channel_id=1, source_target_pairs={{0,2},{2,0},{1,3},{3,1},{4,6},{6,4},{5,7},{7,5}} | collective-permute-start | bytes 8601608 | tf_op jit(solution)/shard_map/ppermute | solution.py:119
  285.4 159.9 %collective-permute-start.29 = (bf16[160,4480]{1,0:T(8,128)(2,1)}, bf16[160,4480]{1,0:T(8,128)(2,1)}, u32[]{:S(2)}, u32[]{:S(2)}) collective-permute-start(bf16[160,4480]{1,0:T(8,128)(2,1)} %get-tuple-element.72), channel_id=1, source_target_pairs={{0,2},{2,0},{1,3},{3,1},{4,6},{6,4},{5,7},{7,5}} | collective-permute-start | bytes 4300808 | tf_op jit(solution)/shard_map/ppermute | solution.py:119
  346.8 97.3 %collective-permute-start.21 = (bf16[32,4480]{1,0:T(8,128)(2,1)}, bf16[32,4480]{1,0:T(8,128)(2,1)S(1)}, u32[]{:S(2)}, u32[]{:S(2)}) collective-permute-start(bf16[32,4480]{1,0:T(8,128)(2,1)} %get-tuple-element.69), channel_id=1, source_target_pairs={{0,2},{2,0},{1,3},{3,1},{4,6},{6,4},{5,7},{7,5}} | collective-permute-start | bytes 860168 | tf_op jit(solution)/shard_map/ppermute | solution.py:119
  408.2 37.6 %collective-permute-start.35 = (bf16[32,4480]{1,0:T(8,128)(2,1)}, bf16[32,4480]{1,0:T(8,128)(2,1)S(1)}, u32[]{:S(2)}, u32[]{:S(2)}) collective-permute-start(bf16[32,4480]{1,0:T(8,128)(2,1)} %get-tuple-element.69), channel_id=1, source_target_pairs={{0,1},{1,0},{2,3},{3,2},{4,5},{5,4},{6,7},{7,6}} | collective-permute-start | bytes 860168 | tf_op jit(solution)/shard_map/ppermute | solution.py:119
  444.1 3.5 collective-permute-start.22
  444.8 57.9 %collective-permute-start.30 = (bf16[160,4480]{1,0:T(8,128)(2,1)}, bf16[160,4480]{1,0:T(8,128)(2,1)}, u32[]{:S(2)}, u32[]{:S(2)}) collective-permute-start(bf16[160,4480]{1,0:T(8,128)(2,1)} %get-tuple-element.72), channel_id=1, source_target_pairs={{0,1},{1,0},{2,3},{3,2},{4,5},{5,4},{6,7},{7,6}} | collective-permute-start | bytes 4300808 | tf_op jit(solution)/shard_map/ppermute | solution.py:119
  445.3 57.7 %collective-permute-start.31 = (bf16[160,4480]{1,0:T(8,128)(2,1)}, bf16[160,4480]{1,0:T(8,128)(2,1)}, u32[]{:S(2)}, u32[]{:S(2)}) collective-permute-start(bf16[160,4480]{1,0:T(8,128)(2,1)} %collective-permute-done.29.refs_0_), channel_id=1, source_target_pairs={{0,1},{1,0},{2,3},{3,2},{4,5},{5,4},{6,7},{7,6}} | collective-permute-start | bytes 4300808 | tf_op jit(solution)/shard_map/ppermute | solution.py:119
  445.3 6.0 collective-permute-start.24
  445.8 16.2 %collective-permute-start.23 = (bf16[64,4480]{1,0:T(8,128)(2,1)}, bf16[64,4480]{1,0:T(8,128)(2,1)}, u32[]{:S(2)}, u32[]{:S(2)}) collective-permute-start(bf16[64,4480]{1,0:T(8,128)(2,1)} %get-tuple-element.70), channel_id=1, source_target_pairs={{0,2},{2,0},{1,3},{3,1},{4,6},{6,4},{5,7},{7,5}} | collective-permute-start | bytes 1720328 | tf_op jit(solution)/shard_map/ppermute | solution.py:119
  448.3 25.1 %collective-permute-start.26 = (bf16[64,4480]{1,0:T(8,128)(2,1)}, bf16[64,4480]{1,0:T(8,128)(2,1)}, u32[]{:S(2)}, u32[]{:S(2)}) collective-permute-start(bf16[64,4480]{1,0:T(8,128)(2,1)} %get-tuple-element.71), channel_id=1, source_target_pairs={{0,2},{2,0},{1,3},{3,1},{4,6},{6,4},{5,7},{7,5}} | collective-permute-start | bytes 1720328 | tf_op jit(solution)/shard_map/ppermute | solution.py:119
  451.3 49.3 %collective-permute-start.27 = (bf16[64,4480]{1,0:T(8,128)(2,1)}, bf16[64,4480]{1,0:T(8,128)(2,1)}, u32[]{:S(2)}, u32[]{:S(2)}) collective-permute-start(bf16[64,4480]{1,0:T(8,128)(2,1)} %get-tuple-element.71), channel_id=1, source_target_pairs={{0,1},{1,0},{2,3},{3,2},{4,5},{5,4},{6,7},{7,6}} | collective-permute-start | bytes 1720328 | tf_op jit(solution)/shard_map/ppermute | solution.py:119
  462.0 39.0 %collective-permute-start.25 = (bf16[64,4480]{1,0:T(8,128)(2,1)}, bf16[64,4480]{1,0:T(8,128)(2,1)}, u32[]{:S(2)}, u32[]{:S(2)}) collective-permute-start(bf16[64,4480]{1,0:T(8,128)(2,1)} %collective-permute-done.23.refs_0_), channel_id=1, source_target_pairs={{0,1},{1,0},{2,3},{3,2},{4,5},{5,4},{6,7},{7,6}} | collective-permute-start | bytes 1720328 | tf_op jit(solution)/shard_map/ppermute | solution.py:119
  473.3 29.3 %collective-permute-start.28 = (bf16[64,4480]{1,0:T(8,128)(2,1)}, bf16[64,4480]{1,0:T(8,128)(2,1)}, u32[]{:S(2)}, u32[]{:S(2)}) collective-permute-start(bf16[64,4480]{1,0:T(8,128)(2,1)} %collective-permute-done.26.refs_0_), channel_id=1, source_target_pairs={{0,1},{1,0},{2,3},{3,2},{4,5},{5,4},{6,7},{7,6}} | collective-permute-start | bytes 1720328 | tf_op jit(solution)/shard_map/ppermute | solution.py:119
  500.6 35.9 %collective-permute-start.42 = (bf16[1120,1280]{1,0:T(8,128)(2,1)}, bf16[1120,1280]{1,0:T(8,128)(2,1)}, u32[]{:S(2)}, u32[]{:S(2)}) collective-permute-start(bf16[1120,1280]{1,0:T(8,128)(2,1)} %get-tuple-element.78), channel_id=1, source_target_pairs={{0,1},{1,0},{2,3},{3,2},{4,5},{5,4},{6,7},{7,6}} | collective-permute-start | bytes 8601608 | tf_op jit(solution)/shard_map/ppermute | solution.py:119
  500.9 65.3 %collective-permute-start.41 = (bf16[1120,1280]{1,0:T(8,128)(2,1)}, bf16[1120,1280]{1,0:T(8,128)(2,1)}, u32[]{:S(2)}, u32[]{:S(2)}) collective-permute-start(bf16[1120,1280]{1,0:T(8,128)(2,1)} %get-tuple-element.78), channel_id=1, source_target_pairs={{0,2},{2,0},{1,3},{3,1},{4,6},{6,4},{5,7},{7,5}} | collective-permute-start | bytes 8601608 | tf_op jit(solution)/shard_map/ppermute | solution.py:119
  502.7 65.3 %collective-permute-start.45 = (bf16[1120,1280]{1,0:T(8,128)(2,1)}, bf16[1120,1280]{1,0:T(8,128)(2,1)}, u32[]{:S(2)}, u32[]{:S(2)}) collective-permute-start(bf16[1120,1280]{1,0:T(8,128)(2,1)} %get-tuple-element.79), channel_id=1, source_target_pairs={{0,1},{1,0},{2,3},{3,2},{4,5},{5,4},{6,7},{7,6}} | collective-permute-start | bytes 8601608 | tf_op jit(solution)/shard_map/ppermute | solution.py:119
  502.7 125.0 %collective-permute-start.44 = (bf16[1120,1280]{1,0:T(8,128)(2,1)}, bf16[1120,1280]{1,0:T(8,128)(2,1)}, u32[]{:S(2)}, u32[]{:S(2)}) collective-permute-start(bf16[1120,1280]{1,0:T(8,128)(2,1)} %get-tuple-element.79), channel_id=1, source_target_pairs={{0,2},{2,0},{1,3},{3,1},{4,6},{6,4},{5,7},{7,5}} | collective-permute-start | bytes 8601608 | tf_op jit(solution)/shard_map/ppermute | solution.py:119
  503.0 186.1 %collective-permute-start.32 = (bf16[320,4480]{1,0:T(8,128)(2,1)}, bf16[320,4480]{1,0:T(8,128)(2,1)}, u32[]{:S(2)}, u32[]{:S(2)}) collective-permute-start(bf16[320,4480]{1,0:T(8,128)(2,1)} %get-tuple-element.73), channel_id=1, source_target_pairs={{0,2},{2,0},{1,3},{3,1},{4,6},{6,4},{5,7},{7,5}} | collective-permute-start | bytes 8601608 | tf_op jit(solution)/shard_map/ppermute | solution.py:119
  536.5 214.1 %collective-permute-start.10 = (bf16[320,4480]{1,0:T(8,128)(2,1)}, bf16[320,4480]{1,0:T(8,128)(2,1)}, u32[]{:S(2)}, u32[]{:S(2)}) collective-permute-start(bf16[320,4480]{1,0:T(8,128)(2,1)} %get-tuple-element.54), channel_id=1, source_target_pairs={{0,2},{2,0},{1,3},{3,1},{4,6},{6,4},{5,7},{7,5}} | collective-permute-start | bytes 8601608 | tf_op jit(solution)/shard_map/ppermute | solution.py:119
  566.3 245.0 %collective-permute-start.13 = (bf16[320,4480]{1,0:T(8,128)(2,1)}, bf16[320,4480]{1,0:T(8,128)(2,1)}, u32[]{:S(2)}, u32[]{:S(2)}) collective-permute-start(bf16[320,4480]{1,0:T(8,128)(2,1)} %get-tuple-element.55), channel_id=1, source_target_pairs={{0,2},{2,0},{1,3},{3,1},{4,6},{6,4},{5,7},{7,5}} | collective-permute-start | bytes 8601608 | tf_op jit(solution)/shard_map/ppermute | solution.py:119
  568.0 243.3 %collective-permute-start.33 = (bf16[320,4480]{1,0:T(8,128)(2,1)}, bf16[320,4480]{1,0:T(8,128)(2,1)}, u32[]{:S(2)}, u32[]{:S(2)}) collective-permute-start(bf16[320,4480]{1,0:T(8,128)(2,1)} %get-tuple-element.73), channel_id=1, source_target_pairs={{0,1},{1,0},{2,3},{3,2},{4,5},{5,4},{6,7},{7,6}} | collective-permute-start | bytes 8601608 | tf_op jit(solution)/shard_map/ppermute | solution.py:119
  627.7 184.1 %collective-permute-start.46 = (bf16[1120,1280]{1,0:T(8,128)(2,1)}, bf16[1120,1280]{1,0:T(8,128)(2,1)}, u32[]{:S(2)}, u32[]{:S(2)}) collective-permute-start(bf16[1120,1280]{1,0:T(8,128)(2,1)} %collective-permute-done.44.refs_0_), channel_id=1, source_target_pairs={{0,1},{1,0},{2,3},{3,2},{4,5},{5,4},{6,7},{7,6}} | collective-permute-start | bytes 8601608 | tf_op jit(solution)/shard_map/ppermute | solution.py:119
  689.1 122.7 %collective-permute-start.34 = (bf16[320,4480]{1,0:T(8,128)(2,1)}, bf16[320,4480]{1,0:T(8,128)(2,1)}, u32[]{:S(2)}, u32[]{:S(2)}) collective-permute-start(bf16[320,4480]{1,0:T(8,128)(2,1)} %collective-permute-done.32.refs_0_), channel_id=1, source_target_pairs={{0,1},{1,0},{2,3},{3,2},{4,5},{5,4},{6,7},{7,6}} | collective-permute-start | bytes 8601608 | tf_op jit(solution)/shard_map/ppermute | solution.py:119
  750.6 86.8 %collective-permute-start.43 = (bf16[1120,1280]{1,0:T(8,128)(2,1)}, bf16[1120,1280]{1,0:T(8,128)(2,1)}, u32[]{:S(2)}, u32[]{:S(2)}) collective-permute-start(bf16[1120,1280]{1,0:T(8,128)(2,1)} %collective-permute-done.41.refs_0_), channel_id=1, source_target_pairs={{0,1},{1,0},{2,3},{3,2},{4,5},{5,4},{6,7},{7,6}} | collective-permute-start | bytes 8601608 | tf_op jit(solution)/shard_map/ppermute | solution.py:119
  811.3 32.6 %collective-permute-start.14 = (bf16[320,4480]{1,0:T(8,128)(2,1)}, bf16[320,4480]{1,0:T(8,128)(2,1)}, u32[]{:S(2)}, u32[]{:S(2)}) collective-permute-start(bf16[320,4480]{1,0:T(8,128)(2,1)} %get-tuple-element.55), channel_id=1, source_target_pairs={{0,1},{1,0},{2,3},{3,2},{4,5},{5,4},{6,7},{7,6}} | collective-permute-start | bytes 8601608 | tf_op jit(solution)/shard_map/ppermute | solution.py:119
  811.3 32.6 %collective-permute-start.15 = (bf16[320,4480]{1,0:T(8,128)(2,1)}, bf16[320,4480]{1,0:T(8,128)(2,1)}, u32[]{:S(2)}, u32[]{:S(2)}) collective-permute-start(bf16[320,4480]{1,0:T(8,128)(2,1)} %collective-permute-done.13.refs_0_), channel_id=1, source_target_pairs={{0,1},{1,0},{2,3},{3,2},{4,5},{5,4},{6,7},{7,6}} | collective-permute-start | bytes 8601608 | tf_op jit(solution)/shard_map/ppermute | solution.py:119
  811.8 38.7 %collective-permute-start.11 = (bf16[320,4480]{1,0:T(8,128)(2,1)}, bf16[320,4480]{1,0:T(8,128)(2,1)}, u32[]{:S(2)}, u32[]{:S(2)}) collective-permute-start(bf16[320,4480]{1,0:T(8,128)(2,1)} %get-tuple-element.54), channel_id=1, source_target_pairs={{0,1},{1,0},{2,3},{3,2},{4,5},{5,4},{6,7},{7,6}} | collective-permute-start | bytes 8601608 | tf_op jit(solution)/shard_map/ppermute | solution.py:119
  811.8 38.7 %collective-permute-start.12 = (bf16[320,4480]{1,0:T(8,128)(2,1)}, bf16[320,4480]{1,0:T(8,128)(2,1)}, u32[]{:S(2)}, u32[]{:S(2)}) collective-permute-start(bf16[320,4480]{1,0:T(8,128)(2,1)} %collective-permute-done.10.refs_0_), channel_id=1, source_target_pairs={{0,1},{1,0},{2,3},{3,2},{4,5},{5,4},{6,7},{7,6}} | collective-permute-start | bytes 8601608 | tf_op jit(solution)/shard_map/ppermute | solution.py:119
  826.5 2.4 copy-start.1
  (4 other events, 4.1 us)

commit v7 on v6

--- a/solution.py
+++ b/solution.py
@@ -10,6 +10,7 @@
 
 FAR = [(0, 2), (2, 0), (1, 3), (3, 1)]
 MATE = [(0, 1), (1, 0), (2, 3), (3, 2)]
+FAR_MATE = [(0, 3), (3, 0), (1, 2), (2, 1)]
 UNITS = 20
 
 SUMS = [
@@ -36,11 +37,12 @@
 ]
 EARLY = 2
 LAST = len(NEWS) - 1
+RIGHT = 896
 
 FULL = 67043328
 SPARE = {"cutf_2": 2 << 20, "sum_1": 4 << 20}
 SPARE |= {name: 600 << 10 for name in ("cutf_3", "sum_2", "cutf_4")}
-SPARE |= {f"place_{LAST - 1}": 320 << 10, "place_last": 1 << 20}
+SPARE |= {f"place_{LAST - 1}": 640 << 10, "place_last": 1 << 20}
 
 ANY = pl.BlockSpec(memory_space=pltpu.HBM)
 WHOLE = pl.BlockSpec(memory_space=pltpu.VMEM)
@@ -212,7 +214,7 @@
             mode = {"pipeline_mode": pl.Buffered(1)} if n == b == UNITS else {}
 
             def body(t, r, wt, mm, vv, *refs):
-                o, full, mo, vo = refs[-4:]
+                o, full, mo, vo, *parts = refs[len(ins) - 5 :]
                 first = 0
                 for f in refs[: len(far_sums)]:
                     at = pl.ds(first, f.shape[0])
@@ -221,6 +223,8 @@
                     new, mo[0, at], vo[0, at] = adamw(wt[0, at].astype(jnp.float32), mm[0, at], vv[0, at], g)
                     o[at] = new
                     full[0, at] = new
+                    for part, start in zip(parts, (0, cols[w] - RIGHT)):
+                        part[at] = new[:, start : start + part.shape[1]]
                     first += f.shape[0]
 
             moment = pl.BlockSpec((1, b * rows[w], cols[w]), lambda i: (layer, u0 // b + i, 0), **mode)
@@ -235,11 +239,16 @@
                 ins += [new_w[w], new_m[w], new_v[w]]
                 specs += [ANY] * 3
             outs = [shape(w, n), *(jax.ShapeDtypeStruct(a.shape, a.dtype) for a in (weights[w], m[w], v[w]))]
-            new, new_w[w], new_m[w], new_v[w] = run(f"adam_{k}", body, (n // b,), ins, specs, outs, [out, mine, moment, moment], aliases)
+            out_specs = [out, mine, moment, moment]
+            if k == LAST:
+                for wide in (cols[w] - RIGHT, RIGHT):
+                    outs.append(jax.ShapeDtypeStruct((n * rows[w], wide), jnp.bfloat16))
+                    out_specs.append(pl.BlockSpec((b * rows[w], wide), lambda i: (i, 0)))
+            new, new_w[w], new_m[w], new_v[w], *parts = run(f"adam_{k}", body, (n // b,), ins, specs, outs, out_specs, aliases)
             if k < LAST:
                 return send(new, FAR), send(new, MATE)
             place(k, "place_own", [send(new, MATE)], [mate_of])
-            return new
+            return parts
 
         def place(k, name, pieces, owners):
             w, layer, u0, n, _ = NEWS[k]
@@ -269,19 +278,23 @@
 
         def place_last(far, far_mate):
             w, layer, u0, n, _ = NEWS[LAST]
-
-            def body(far, far_mate, _, full, sem):
-                copies = [
-                    pltpu.make_async_copy(one, full.at[layer, at(w, of(me()) * UNITS + u0, n)], sem.at[j])
-                    for j, (one, of) in enumerate(((far, far_of), (far_mate, far_mate_of)))
-                ]
+            left = cols[w] - RIGHT
+
+            def body(*refs):
+                full, sem = refs[-2:]
+                copies = []
+                for j, of in enumerate((far_of, far_mate_of)):
+                    here = at(w, of(me()) * UNITS + u0, n)
+                    for i, columns in enumerate((pl.ds(0, left), pl.ds(left, RIGHT))):
+                        copies.append(pltpu.make_async_copy(refs[2 * j + i], full.at[layer, here, columns], sem.at[2 * j + i]))
                 for one in copies:
                     one.start()
                 for one in copies:
                     one.wait()
 
             like = jax.ShapeDtypeStruct(weights[w].shape, jnp.bfloat16)
-            (new_w[w],) = run("place_last", body, (), [far, far_mate, new_w[w]], [WHOLE, WHOLE, ANY], [like], [ANY], {2: 0}, [DMA((2,))])
+            ins, specs = [*far, *far_mate, new_w[w]], [WHOLE] * 4 + [ANY]
+            (new_w[w],) = run("place_last", body, (), ins, specs, [like], [ANY], {4: 0}, [DMA((4,))])
 
         first, piece, own = head()
         far_sum = [send(first, FAR)]
@@ -300,11 +313,12 @@
             out.append(update(k, mate_term[w], [f for f, of in zip(far_sum, SUMS) if of[:2] == (w, layer)]))
         for k in range(LAST):
             if k == LAST - 1:
-                last = send(out[LAST], FAR, pltpu.VMEM)
+                left, right = out[LAST]
+                far = [send(left, FAR, pltpu.VMEM), send(right, FAR, pltpu.VMEM)]
+                across = send(right, FAR_MATE, pltpu.VMEM)
             forward = send(out[k][0], MATE)
             place(k, f"place_{k}", [*out[k], forward], [far_of, mate_of, far_mate_of])
-        forward = send(last, MATE, pltpu.VMEM)
-        place_last(last, forward)
+        place_last(far, (send(far[0], MATE, pltpu.VMEM), across))
         return (*new_w, *new_m, *new_v)
 
     all_of, cut_of = P(None, None, None), P(None, "dp", None)

time: 858 us -> 843 us (0.983)
  waiting for transfers between devices: 615 us -> 600 us
    ppermute x47 -> x49, waiting for transfers between devices: 615 us -> 600 us  [send(): return in_space(lax.ppermute(x, 'dp', pairs), space)]
    ppermute x47 -> x49, starting transfers between devices: 30 us -> 30.5 us  [send(): return in_space(lax.ppermute(x, 'dp', pairs), space)]
  transfers between devices with their start and end apart: 47 -> 49, of which waited for: 16 -> 16; matrix products, arithmetic and copies ran while one was open for 0% -> 0% of each run, Pallas kernels for 23% -> 24%
where the time goes in v7:
time: 843 us; the launch traced here: 842 us
  waiting for transfers between devices  600 us (71%)
  Pallas kernels  208 us (25%)
  starting transfers between devices  30.5 us (4%)
    ppermute x49, waiting for transfers between devices, send(): return in_space(lax.ppermute(x, 'dp', pairs), space)  600 us
    pallas_call x37, Pallas kernels, run(): pl.pallas_call(body, out_shape=outs, grid=grid, in_specs=in_specs, out_sp...  202 us
    ppermute x49, starting transfers between devices, send(): return in_space(lax.ppermute(x, 'dp', pairs), space)  30.5 us
  transfers between devices with their start and end apart: 49, of which 16 were waited for; matrix products, arithmetic and copies ran while one was open for 0% of the time, Pallas kernels for 24%

profile of v7, /device:TPU:0, one launch (start us, length us, event | category | flops | bytes accessed | tf_op | source)
XLA Modules:
  0.0 842.2 jit_solution(1862356011398189023)
XLA Ops:
  0.6 2.8 shard_map.202
  4.3 2.7 shard_map.200
  11.8 6.1 head.1
  19.1 3.2 shard_map.192
  22.2 2.5 collective-permute-start.7
  25.6 25.4 %collective-permute-done.3.refs_0_ = bf16[32,4480]{1,0:T(8,128)(2,1)} collective-permute-done((bf16[32,4480]{1,0:T(8,128)(2,1)}, bf16[32,4480]{1,0:T(8,128)(2,1)}, u32[]{:S(2)}, u32[]{:S(2)}) %collective-permute-start.3) | collective-permute-done | bytes 286752 | tf_op jit(solution)/shard_map/ppermute | solution.py:121
  52.7 5.1 shard_map.199
  59.9 2.7 shard_map.188
  63.2 2.7 shard_map.218
  65.9 3.2 shard_map.194
  70.7 2.7 shard_map.216
  73.6 5.1 shard_map.187
  78.7 24.6 %collective-permute-done.9.refs_3_ = bf16[160,4480]{1,0:T(8,128)(2,1)} collective-permute-done((bf16[160,4480]{1,0:T(8,128)(2,1)}, bf16[160,4480]{1,0:T(8,128)(2,1)}, u32[]{:S(2)}, u32[]{:S(2)}) %collective-permute-start.9) | collective-permute-done | bytes 1433632 | tf_op jit(solution)/shard_map/ppermute | solution.py:121
  103.3 5.1 shard_map.215
  108.9 4.9 shard_map.203
  115.3 4.9 shard_map.201
  120.8 4.9 shard_map.189
  127.1 4.9 shard_map.219
  132.0 47.1 %collective-permute-done.20.refs_0_ = bf16[320,4480]{1,0:T(8,128)(2,1)} collective-permute-done((bf16[320,4480]{1,0:T(8,128)(2,1)}, bf16[320,4480]{1,0:T(8,128)(2,1)}, u32[]{:S(2)}, u32[]{:S(2)}) %collective-permute-start.20) | collective-permute-done | bytes 2867232 | tf_op jit(solution)/shard_map/ppermute | solution.py:121
  180.6 4.9 shard_map.217
  185.5 55.1 %collective-permute-done.18.refs_0_ = bf16[320,4480]{1,0:T(8,128)(2,1)} collective-permute-done((bf16[320,4480]{1,0:T(8,128)(2,1)}, bf16[320,4480]{1,0:T(8,128)(2,1)}, u32[]{:S(2)}, u32[]{:S(2)}) %collective-permute-start.18) | collective-permute-done | bytes 2867232 | tf_op jit(solution)/shard_map/ppermute | solution.py:121
  242.1 13.5 %shard_map.204 = (bf16[320,4480]{1,0:T(8,128)(2,1)}, bf16[2,1280,4480]{2,1,0:T(8,128)(2,1)}, f32[2,320,4480]{2,1,0:T(8,128)}, f32[2,320,4480]{2,1,0:T(8,128)}) custom-call(bf16[1,2,1280,4480]{3,2,1,0:T(8,128)(2,1)} %t.46, bf16[640,4480]{1,0:T(8,128)(2,1)} %collective-permute-done.16.r, bf16[2,1280,4480]{2,1,0:T(8,128)(2,1)} %wt.15, f32[2,320,4480]{2,1,0:T(8,128)} %mm.15, ...), custom_call_target="tpu_custom_call" | custom-call | flops 37273600 | bytes 37273600 | tf_op jit(solution)/shard_map/pallas_call | solution.py:108
  255.5 9.8 %shard_map.205 = (bf16[160,4480]{1,0:T(8,128)(2,1)}, bf16[2,1280,4480]{2,1,0:T(8,128)(2,1)}, f32[2,320,4480]{2,1,0:T(8,128)}, f32[2,320,4480]{2,1,0:T(8,128)}) custom-call(bf16[1,2,1280,4480]{3,2,1,0:T(8,128)(2,1)} %t.46, bf16[640,4480]{1,0:T(8,128)(2,1)} %collective-permute-done.16.r, ...), custom_call_target="tpu_custom_call", output_to_operand_aliasing={{1}: (6, {}), {2}: (7, {}), {3}: (8, {})} | custom-call | flops 35840000 | bytes 35840000 | tf_op jit(solution)/shard_map/pallas_call | solution.py:108
  265.9 4.0 shard_map.206
  269.8 4.0 shard_map.207
  273.8 3.1 shard_map.208
  276.9 25.1 %collective-permute-done.2.refs_0_ = bf16[320,4480]{1,0:T(8,128)(2,1)} collective-permute-done((bf16[320,4480]{1,0:T(8,128)(2,1)}, bf16[320,4480]{1,0:T(8,128)(2,1)}, u32[]{:S(2)}, u32[]{:S(2)}) %collective-permute-start.2) | collective-permute-done | bytes 2867232 | tf_op jit(solution)/shard_map/ppermute | solution.py:121
  303.5 60.0 %collective-permute-done.42.refs_0_ = bf16[1120,1280]{1,0:T(8,128)(2,1)} collective-permute-done((bf16[1120,1280]{1,0:T(8,128)(2,1)}, bf16[1120,1280]{1,0:T(8,128)(2,1)}, u32[]{:S(2)}, u32[]{:S(2)}) %collective-permute-start.42) | collective-permute-done | bytes 2867232 | tf_op jit(solution)/shard_map/ppermute | solution.py:121
  363.5 92.2 %collective-permute-done.31.refs_0_ = bf16[160,4480]{1,0:T(8,128)(2,1)} collective-permute-done((bf16[160,4480]{1,0:T(8,128)(2,1)}, bf16[160,4480]{1,0:T(8,128)(2,1)}, u32[]{:S(2)}, u32[]{:S(2)}) %collective-permute-start.31) | collective-permute-done | bytes 1433632 | tf_op jit(solution)/shard_map/ppermute | solution.py:121
  457.1 3.0 collective-permute-done.21.refs_0_
  461.7 10.7 %collective-permute-done.28.refs_0_ = bf16[64,4480]{1,0:T(8,128)(2,1)S(1)} collective-permute-done((bf16[64,4480]{1,0:T(8,128)(2,1)}, bf16[64,4480]{1,0:T(8,128)(2,1)S(1)}, u32[]{:S(2)}, u32[]{:S(2)}) %collective-permute-start.28) | collective-permute-done | bytes 573472 | tf_op jit(solution)/shard_map/ppermute | solution.py:121
  473.2 11.0 %collective-permute-done.25.refs_0_ = bf16[64,4480]{1,0:T(8,128)(2,1)} collective-permute-done((bf16[64,4480]{1,0:T(8,128)(2,1)}, bf16[64,4480]{1,0:T(8,128)(2,1)}, u32[]{:S(2)}, u32[]{:S(2)}) %collective-permute-start.25) | collective-permute-done | bytes 573472 | tf_op jit(solution)/shard_map/ppermute | solution.py:121
  486.7 17.8 %shard_map.195 = (bf16[320,4480]{1,0:T(8,128)(2,1)}, bf16[2,1280,4480]{2,1,0:T(8,128)(2,1)}, f32[2,320,4480]{2,1,0:T(8,128)}, f32[2,320,4480]{2,1,0:T(8,128)}) custom-call(bf16[1,2,1280,4480]{3,2,1,0:T(8,128)(2,1)} %t.36, bf16[640,4480]{1,0:T(8,128)(2,1)} %collective-permute-done.r, bf16[2,1280,4480]{2,1,0:T(8,128)(2,1)} %wt.10, f32[2,320,4480]{2,1,0:T(8,128)} %mm.10, ...), custom_call_target="tpu_custom_call" | custom-call | flops 37273600 | bytes 37273600 | tf_op jit(solution)/shard_map/pallas_call | solution.py:108
  505.6 13.5 %shard_map.196 = (bf16[320,4480]{1,0:T(8,128)(2,1)}, bf16[2,1280,4480]{2,1,0:T(8,128)(2,1)}, f32[2,320,4480]{2,1,0:T(8,128)}, f32[2,320,4480]{2,1,0:T(8,128)}) custom-call(bf16[1,2,1280,4480]{3,2,1,0:T(8,128)(2,1)} %t.36, bf16[640,4480]{1,0:T(8,128)(2,1)} %collective-permute-done.r, ...), custom_call_target="tpu_custom_call", output_to_operand_aliasing={{1}: (6, {}), {2}: (7, {}), {3}: (8, {})} | custom-call | flops 37273600 | bytes 37273600 | tf_op jit(solution)/shard_map/pallas_call | solution.py:108
  520.1 29.4 %collective-permute-done.34.refs_0_ = bf16[320,4480]{1,0:T(8,128)(2,1)} collective-permute-done((bf16[320,4480]{1,0:T(8,128)(2,1)}, bf16[320,4480]{1,0:T(8,128)(2,1)}, u32[]{:S(2)}, u32[]{:S(2)}) %collective-permute-start.34) | collective-permute-done | bytes 2867232 | tf_op jit(solution)/shard_map/ppermute | solution.py:121
  549.6 13.5 %shard_map.220 = (bf16[1120,1280]{1,0:T(8,128)(2,1)}, bf16[2,4480,1280]{2,1,0:T(8,128)(2,1)}, f32[2,1120,1280]{2,1,0:T(8,128)}, f32[2,1120,1280]{2,1,0:T(8,128)}) custom-call(bf16[1,2,4480,1280]{3,2,1,0:T(8,128)(2,1)} %t.53, bf16[2240,1280]{1,0:T(8,128)(2,1)} %collective-permute-done.38.r, bf16[2,4480,1280]{2,1,0:T(8,128)(2,1)} %wt.17, ...), custom_call_target="tpu_custom_call" | custom-call | flops 37273600 | bytes 37273600 | tf_op jit(solution)/shard_map/pallas_call | solution.py:108
  564.6 46.4 %collective-permute-done.13.refs_0_ = bf16[320,4480]{1,0:T(8,128)(2,1)} collective-permute-done((bf16[320,4480]{1,0:T(8,128)(2,1)}, bf16[320,4480]{1,0:T(8,128)(2,1)}, u32[]{:S(2)}, u32[]{:S(2)}) %collective-permute-start.13) | collective-permute-done | bytes 2867232 | tf_op jit(solution)/shard_map/ppermute | solution.py:121
  611.0 13.7 %shard_map.221 = (bf16[1120,1280]{1,0:T(8,128)(2,1)}, bf16[2,4480,1280]{2,1,0:T(8,128)(2,1)}, f32[2,1120,1280]{2,1,0:T(8,128)}, f32[2,1120,1280]{2,1,0:T(8,128)}) custom-call(bf16[1,2,4480,1280]{3,2,1,0:T(8,128)(2,1)} %t.53, bf16[2240,1280]{1,0:T(8,128)(2,1)} %collective-permute-done.38.r, ...), custom_call_target="tpu_custom_call", output_to_operand_aliasing={{1}: (6, {}), {2}: (7, {}), {3}: (8, {})} | custom-call | flops 37273600 | bytes 37273600 | tf_op jit(solution)/shard_map/pallas_call | solution.py:108
  626.2 46.2 %collective-permute-done.10.refs_0_ = bf16[320,4480]{1,0:T(8,128)(2,1)} collective-permute-done((bf16[320,4480]{1,0:T(8,128)(2,1)}, bf16[320,4480]{1,0:T(8,128)(2,1)}, u32[]{:S(2)}, u32[]{:S(2)}) %collective-permute-start.10) | collective-permute-done | bytes 2867232 | tf_op jit(solution)/shard_map/ppermute | solution.py:121
  673.0 60.9 %collective-permute-done.46.refs_0_ = bf16[1120,1280]{1,0:T(8,128)(2,1)} collective-permute-done((bf16[1120,1280]{1,0:T(8,128)(2,1)}, bf16[1120,1280]{1,0:T(8,128)(2,1)}, u32[]{:S(2)}, u32[]{:S(2)}) %collective-permute-start.46) | collective-permute-done | bytes 2867232 | tf_op jit(solution)/shard_map/ppermute | solution.py:121
  734.4 60.4 %collective-permute-done.43.refs_0_ = bf16[1120,1280]{1,0:T(8,128)(2,1)} collective-permute-done((bf16[1120,1280]{1,0:T(8,128)(2,1)}, bf16[1120,1280]{1,0:T(8,128)(2,1)}, u32[]{:S(2)}, u32[]{:S(2)}) %collective-permute-start.43) | collective-permute-done | bytes 2867232 | tf_op jit(solution)/shard_map/ppermute | solution.py:121
  798.9 6.5 shard_map.210.refs_3_
  805.5 3.6 shard_map.211.refs_3_
  809.1 2.4 shard_map.212.refs_3_
  813.9 6.5 shard_map.197.refs_3_
  820.4 6.5 shard_map.198
  827.0 6.6 shard_map.222.refs_3_
  833.6 6.6 shard_map.223
  (100 shorter events, 43.3 us)
Async XLA Ops:
  3.4 65.8 %collective-permute-start.19 = (bf16[320,4480]{1,0:T(8,128)(2,1)}, bf16[320,4480]{1,0:T(8,128)(2,1)}, u32[]{:S(2)}, u32[]{:S(2)}) collective-permute-start(bf16[320,4480]{1,0:T(8,128)(2,1)} %shard_map.202), channel_id=1, source_target_pairs={{0,1},{1,0},{2,3},{3,2},{4,5},{5,4},{6,7},{7,6}} | collective-permute-start | bytes 8601608 | tf_op jit(solution)/shard_map/ppermute | solution.py:121
  7.0 66.4 %collective-permute-start.17 = (bf16[320,4480]{1,0:T(8,128)(2,1)}, bf16[320,4480]{1,0:T(8,128)(2,1)}, u32[]{:S(2)}, u32[]{:S(2)}) collective-permute-start(bf16[320,4480]{1,0:T(8,128)(2,1)} %shard_map.200), channel_id=1, source_target_pairs={{0,1},{1,0},{2,3},{3,2},{4,5},{5,4},{6,7},{7,6}} | collective-permute-start | bytes 8601608 | tf_op jit(solution)/shard_map/ppermute | solution.py:121
  9.0 10.1 %collective-permute-start.6 = (bf16[96,4480]{1,0:T(8,128)(2,1)}, bf16[96,4480]{1,0:T(8,128)(2,1)}, u32[]{:S(2)}, u32[]{:S(2)}) collective-permute-start(bf16[96,4480]{1,0:T(8,128)(2,1)} %shard_map.191), channel_id=1, source_target_pairs={{0,1},{1,0},{2,3},{3,2},{4,5},{5,4},{6,7},{7,6}} | collective-permute-start | bytes 2580488 | tf_op jit(solution)/shard_map/ppermute | solution.py:121
  11.7 50.9 %collective-permute-start.8 = (bf16[160,4480]{1,0:T(8,128)(2,1)}, bf16[160,4480]{1,0:T(8,128)(2,1)}, u32[]{:S(2)}, u32[]{:S(2)}) collective-permute-start(bf16[160,4480]{1,0:T(8,128)(2,1)} %shard_map.193), channel_id=1, source_target_pairs={{0,1},{1,0},{2,3},{3,2},{4,5},{5,4},{6,7},{7,6}} | collective-permute-start | bytes 4300808 | tf_op jit(solution)/shard_map/ppermute | solution.py:121
  22.2 46.9 %collective-permute-start.7 = (bf16[96,4480]{1,0:T(8,128)(2,1)}, bf16[96,4480]{1,0:T(8,128)(2,1)}, u32[]{:S(2)}, u32[]{:S(2)}) collective-permute-start(bf16[96,4480]{1,0:T(8,128)(2,1)} %shard_map.192), channel_id=1, source_target_pairs={{0,2},{2,0},{1,3},{3,1},{4,6},{6,4},{5,7},{7,5}} | collective-permute-start | bytes 2580488 | tf_op jit(solution)/shard_map/ppermute | solution.py:121
  24.8 26.2 %collective-permute-start.3 = (bf16[32,4480]{1,0:T(8,128)(2,1)}, bf16[32,4480]{1,0:T(8,128)(2,1)}, u32[]{:S(2)}, u32[]{:S(2)}) collective-permute-start(bf16[32,4480]{1,0:T(8,128)(2,1)} %copy-done), channel_id=1, source_target_pairs={{0,2},{2,0},{1,3},{3,1},{4,6},{6,4},{5,7},{7,5}} | collective-permute-start | bytes 860168 | tf_op jit(solution)/shard_map/ppermute | solution.py:121
  51.0 8.9 %collective-permute-start.5 = (bf16[32,4480]{1,0:T(8,128)(2,1)}, bf16[32,4480]{1,0:T(8,128)(2,1)}, u32[]{:S(2)}, u32[]{:S(2)}) collective-permute-start(bf16[32,4480]{1,0:T(8,128)(2,1)} %shard_map.190), channel_id=1, source_target_pairs={{0,2},{2,0},{1,3},{3,1},{4,6},{6,4},{5,7},{7,5}} | collective-permute-start | bytes 860168 | tf_op jit(solution)/shard_map/ppermute | solution.py:121
  59.9 65.8 %collective-permute-start.16 = (bf16[640,4480]{1,0:T(8,128)(2,1)}, bf16[640,4480]{1,0:T(8,128)(2,1)}, u32[]{:S(2)}, u32[]{:S(2)}) collective-permute-start(bf16[640,4480]{1,0:T(8,128)(2,1)} %shard_map.199), channel_id=1, source_target_pairs={{0,1},{1,0},{2,3},{3,2},{4,5},{5,4},{6,7},{7,6}} | collective-permute-start | bytes 17203208 | tf_op jit(solution)/shard_map/ppermute | solution.py:121
  62.7 45.7 %collective-permute-start.1 = (bf16[320,4480]{1,0:T(8,128)(2,1)}, bf16[320,4480]{1,0:T(8,128)(2,1)}, u32[]{:S(2)}, u32[]{:S(2)}) collective-permute-start(bf16[320,4480]{1,0:T(8,128)(2,1)} %shard_map.188), channel_id=1, source_target_pairs={{0,1},{1,0},{2,3},{3,2},{4,5},{5,4},{6,7},{7,6}} | collective-permute-start | bytes 8601608 | tf_op jit(solution)/shard_map/ppermute | solution.py:121
  69.2 44.7 %collective-permute-start.41 = (bf16[1120,1280]{1,0:T(8,128)(2,1)}, bf16[1120,1280]{1,0:T(8,128)(2,1)}, u32[]{:S(2)}, u32[]{:S(2)}) collective-permute-start(bf16[1120,1280]{1,0:T(8,128)(2,1)} %shard_map.218), channel_id=1, source_target_pairs={{0,1},{1,0},{2,3},{3,2},{4,5},{5,4},{6,7},{7,6}} | collective-permute-start | bytes 8601608 | tf_op jit(solution)/shard_map/ppermute | solution.py:121
  69.2 34.1 %collective-permute-start.9 = (bf16[160,4480]{1,0:T(8,128)(2,1)}, bf16[160,4480]{1,0:T(8,128)(2,1)}, u32[]{:S(2)}, u32[]{:S(2)}) collective-permute-start(bf16[160,4480]{1,0:T(8,128)(2,1)} %shard_map.194), channel_id=1, source_target_pairs={{0,2},{2,0},{1,3},{3,1},{4,6},{6,4},{5,7},{7,5}} | collective-permute-start | bytes 4300808 | tf_op jit(solution)/shard_map/ppermute | solution.py:121
  73.4 46.8 %collective-permute-start.39 = (bf16[1120,1280]{1,0:T(8,128)(2,1)}, bf16[1120,1280]{1,0:T(8,128)(2,1)}, u32[]{:S(2)}, u32[]{:S(2)}) collective-permute-start(bf16[1120,1280]{1,0:T(8,128)(2,1)} %shard_map.216), channel_id=1, source_target_pairs={{0,1},{1,0},{2,3},{3,2},{4,5},{5,4},{6,7},{7,6}} | collective-permute-start | bytes 8601608 | tf_op jit(solution)/shard_map/ppermute | solution.py:121
  103.3 162.1 %collective-permute-start = (bf16[640,4480]{1,0:T(8,128)(2,1)}, bf16[640,4480]{1,0:T(8,128)(2,1)}, u32[]{:S(2)}, u32[]{:S(2)}) collective-permute-start(bf16[640,4480]{1,0:T(8,128)(2,1)} %shard_map.187), channel_id=1, source_target_pairs={{0,1},{1,0},{2,3},{3,2},{4,5},{5,4},{6,7},{7,6}} | collective-permute-start | bytes 17203208 | tf_op jit(solution)/shard_map/ppermute | solution.py:121
  108.4 193.6 %collective-permute-start.38 = (bf16[2240,1280]{1,0:T(8,128)(2,1)}, bf16[2240,1280]{1,0:T(8,128)(2,1)}, u32[]{:S(2)}, u32[]{:S(2)}) collective-permute-start(bf16[2240,1280]{1,0:T(8,128)(2,1)} %shard_map.215), channel_id=1, source_target_pairs={{0,1},{1,0},{2,3},{3,2},{4,5},{5,4},{6,7},{7,6}} | collective-permute-start | bytes 17203208 | tf_op jit(solution)/shard_map/ppermute | solution.py:121
  113.8 65.3 %collective-permute-start.20 = (bf16[320,4480]{1,0:T(8,128)(2,1)}, bf16[320,4480]{1,0:T(8,128)(2,1)}, u32[]{:S(2)}, u32[]{:S(2)}) collective-permute-start(bf16[320,4480]{1,0:T(8,128)(2,1)} %shard_map.203), channel_id=1, source_target_pairs={{0,2},{2,0},{1,3},{3,1},{4,6},{6,4},{5,7},{7,5}} | collective-permute-start | bytes 8601608 | tf_op jit(solution)/shard_map/ppermute | solution.py:121
  120.2 120.4 %collective-permute-start.18 = (bf16[320,4480]{1,0:T(8,128)(2,1)}, bf16[320,4480]{1,0:T(8,128)(2,1)}, u32[]{:S(2)}, u32[]{:S(2)}) collective-permute-start(bf16[320,4480]{1,0:T(8,128)(2,1)} %shard_map.201), channel_id=1, source_target_pairs={{0,2},{2,0},{1,3},{3,1},{4,6},{6,4},{5,7},{7,5}} | collective-permute-start | bytes 8601608 | tf_op jit(solution)/shard_map/ppermute | solution.py:121
  125.7 176.4 %collective-permute-start.2 = (bf16[320,4480]{1,0:T(8,128)(2,1)}, bf16[320,4480]{1,0:T(8,128)(2,1)}, u32[]{:S(2)}, u32[]{:S(2)}) collective-permute-start(bf16[320,4480]{1,0:T(8,128)(2,1)} %shard_map.189), channel_id=1, source_target_pairs={{0,2},{2,0},{1,3},{3,1},{4,6},{6,4},{5,7},{7,5}} | collective-permute-start | bytes 8601608 | tf_op jit(solution)/shard_map/ppermute | solution.py:121
  179.2 184.3 %collective-permute-start.42 = (bf16[1120,1280]{1,0:T(8,128)(2,1)}, bf16[1120,1280]{1,0:T(8,128)(2,1)}, u32[]{:S(2)}, u32[]{:S(2)}) collective-permute-start(bf16[1120,1280]{1,0:T(8,128)(2,1)} %shard_map.219), channel_id=1, source_target_pairs={{0,2},{2,0},{1,3},{3,1},{4,6},{6,4},{5,7},{7,5}} | collective-permute-start | bytes 8601608 | tf_op jit(solution)/shard_map/ppermute | solution.py:121
  240.6 215.1 %collective-permute-start.40 = (bf16[1120,1280]{1,0:T(8,128)(2,1)}, bf16[1120,1280]{1,0:T(8,128)(2,1)}, u32[]{:S(2)}, u32[]{:S(2)}) collective-permute-start(bf16[1120,1280]{1,0:T(8,128)(2,1)} %shard_map.217), channel_id=1, source_target_pairs={{0,2},{2,0},{1,3},{3,1},{4,6},{6,4},{5,7},{7,5}} | collective-permute-start | bytes 8601608 | tf_op jit(solution)/shard_map/ppermute | solution.py:121
  265.4 190.3 %collective-permute-start.31 = (bf16[160,4480]{1,0:T(8,128)(2,1)}, bf16[160,4480]{1,0:T(8,128)(2,1)}, u32[]{:S(2)}, u32[]{:S(2)}) collective-permute-start(bf16[160,4480]{1,0:T(8,128)(2,1)} %get-tuple-element.75), channel_id=1, source_target_pairs={{0,2},{2,0},{1,3},{3,1},{4,6},{6,4},{5,7},{7,5}} | collective-permute-start | bytes 4300808 | tf_op jit(solution)/shard_map/ppermute | solution.py:121
  302.0 158.1 %collective-permute-start.37 = (bf16[32,4480]{1,0:T(8,128)(2,1)}, bf16[32,4480]{1,0:T(8,128)(2,1)S(1)}, u32[]{:S(2)}, u32[]{:S(2)}) collective-permute-start(bf16[32,4480]{1,0:T(8,128)(2,1)} %get-tuple-element.77), channel_id=1, source_target_pairs={{0,1},{1,0},{2,3},{3,2},{4,5},{5,4},{6,7},{7,6}} | collective-permute-start | bytes 860168 | tf_op jit(solution)/shard_map/ppermute | solution.py:121
  302.1 158.1 %collective-permute-start.21 = (bf16[32,3584]{1,0:T(8,128)(2,1)}, bf16[32,3584]{1,0:T(8,128)(2,1)}, u32[]{:S(2)}, u32[]{:S(2)}) collective-permute-start(bf16[32,3584]{1,0:T(8,128)(2,1)} %get-tuple-element.71), channel_id=1, source_target_pairs={{0,2},{2,0},{1,3},{3,1},{4,6},{6,4},{5,7},{7,5}} | collective-permute-start | bytes 688136 | tf_op jit(solution)/shard_map/ppermute | solution.py:121
  363.5 155.6 %collective-permute-start.32 = (bf16[160,4480]{1,0:T(8,128)(2,1)}, bf16[160,4480]{1,0:T(8,128)(2,1)}, u32[]{:S(2)}, u32[]{:S(2)}) collective-permute-start(bf16[160,4480]{1,0:T(8,128)(2,1)} %get-tuple-element.75), channel_id=1, source_target_pairs={{0,1},{1,0},{2,3},{3,2},{4,5},{5,4},{6,7},{7,6}} | collective-permute-start | bytes 4300808 | tf_op jit(solution)/shard_map/ppermute | solution.py:121
  455.7 63.5 %collective-permute-start.33 = (bf16[160,4480]{1,0:T(8,128)(2,1)}, bf16[160,4480]{1,0:T(8,128)(2,1)}, u32[]{:S(2)}, u32[]{:S(2)}) collective-permute-start(bf16[160,4480]{1,0:T(8,128)(2,1)} %collective-permute-done.31.refs_0_), channel_id=1, source_target_pairs={{0,1},{1,0},{2,3},{3,2},{4,5},{5,4},{6,7},{7,6}} | collective-permute-start | bytes 4300808 | tf_op jit(solution)/shard_map/ppermute | solution.py:121
  455.7 16.7 %collective-permute-start.28 = (bf16[64,4480]{1,0:T(8,128)(2,1)}, bf16[64,4480]{1,0:T(8,128)(2,1)S(1)}, u32[]{:S(2)}, u32[]{:S(2)}) collective-permute-start(bf16[64,4480]{1,0:T(8,128)(2,1)} %get-tuple-element.74), channel_id=1, source_target_pairs={{0,2},{2,0},{1,3},{3,1},{4,6},{6,4},{5,7},{7,5}} | collective-permute-start | bytes 1720328 | tf_op jit(solution)/shard_map/ppermute | solution.py:121
  460.2 12.2 %collective-permute-start.29 = (bf16[64,4480]{1,0:T(8,128)(2,1)}, bf16[64,4480]{1,0:T(8,128)(2,1)S(1)}, u32[]{:S(2)}, u32[]{:S(2)}) collective-permute-start(bf16[64,4480]{1,0:T(8,128)(2,1)} %get-tuple-element.74), channel_id=1, source_target_pairs={{0,1},{1,0},{2,3},{3,2},{4,5},{5,4},{6,7},{7,6}} | collective-permute-start | bytes 1720328 | tf_op jit(solution)/shard_map/ppermute | solution.py:121
  460.2 24.0 %collective-permute-start.25 = (bf16[64,4480]{1,0:T(8,128)(2,1)}, bf16[64,4480]{1,0:T(8,128)(2,1)}, u32[]{:S(2)}, u32[]{:S(2)}) collective-permute-start(bf16[64,4480]{1,0:T(8,128)(2,1)} %get-tuple-element.73), channel_id=1, source_target_pairs={{0,2},{2,0},{1,3},{3,1},{4,6},{6,4},{5,7},{7,5}} | collective-permute-start | bytes 1720328 | tf_op jit(solution)/shard_map/ppermute | solution.py:121
  472.3 11.9 %collective-permute-start.26 = (bf16[64,4480]{1,0:T(8,128)(2,1)}, bf16[64,4480]{1,0:T(8,128)(2,1)S(1)}, u32[]{:S(2)}, u32[]{:S(2)}) collective-permute-start(bf16[64,4480]{1,0:T(8,128)(2,1)} %get-tuple-element.73), channel_id=1, source_target_pairs={{0,1},{1,0},{2,3},{3,2},{4,5},{5,4},{6,7},{7,6}} | collective-permute-start | bytes 1720328 | tf_op jit(solution)/shard_map/ppermute | solution.py:121
  473.2 12.5 %collective-permute-start.30 = (bf16[64,4480]{1,0:T(8,128)(2,1)S(1)}, bf16[64,4480]{1,0:T(8,128)(2,1)S(1)}, u32[]{:S(2)}, u32[]{:S(2)}) collective-permute-start(bf16[64,4480]{1,0:T(8,128)(2,1)S(1)} %collective-permute-done.28.refs_0_), channel_id=1, source_target_pairs={{0,1},{1,0},{2,3},{3,2},{4,5},{5,4},{6,7},{7,6}} | collective-permute-start | bytes 1720328 | tf_op jit(solution)/shard_map/ppermute | solution.py:121
  484.2 20.3 %collective-permute-start.27 = (bf16[64,4480]{1,0:T(8,128)(2,1)}, bf16[64,4480]{1,0:T(8,128)(2,1)}, u32[]{:S(2)}, u32[]{:S(2)}) collective-permute-start(bf16[64,4480]{1,0:T(8,128)(2,1)} %collective-permute-done.25.refs_0_), channel_id=1, source_target_pairs={{0,1},{1,0},{2,3},{3,2},{4,5},{5,4},{6,7},{7,6}} | collective-permute-start | bytes 1720328 | tf_op jit(solution)/shard_map/ppermute | solution.py:121
  484.2 65.3 %collective-permute-start.34 = (bf16[320,4480]{1,0:T(8,128)(2,1)}, bf16[320,4480]{1,0:T(8,128)(2,1)}, u32[]{:S(2)}, u32[]{:S(2)}) collective-permute-start(bf16[320,4480]{1,0:T(8,128)(2,1)} %get-tuple-element.76), channel_id=1, source_target_pairs={{0,2},{2,0},{1,3},{3,1},{4,6},{6,4},{5,7},{7,5}} | collective-permute-start | bytes 8601608 | tf_op jit(solution)/shard_map/ppermute | solution.py:121
  486.5 76.5 %collective-permute-start.35 = (bf16[320,4480]{1,0:T(8,128)(2,1)}, bf16[320,4480]{1,0:T(8,128)(2,1)}, u32[]{:S(2)}, u32[]{:S(2)}) collective-permute-start(bf16[320,4480]{1,0:T(8,128)(2,1)} %get-tuple-element.76), channel_id=1, source_target_pairs={{0,1},{1,0},{2,3},{3,2},{4,5},{5,4},{6,7},{7,6}} | collective-permute-start | bytes 8601608 | tf_op jit(solution)/shard_map/ppermute | solution.py:121
  504.5 106.5 %collective-permute-start.13 = (bf16[320,4480]{1,0:T(8,128)(2,1)}, bf16[320,4480]{1,0:T(8,128)(2,1)}, u32[]{:S(2)}, u32[]{:S(2)}) collective-permute-start(bf16[320,4480]{1,0:T(8,128)(2,1)} %get-tuple-element.57), channel_id=1, source_target_pairs={{0,2},{2,0},{1,3},{3,1},{4,6},{6,4},{5,7},{7,5}} | collective-permute-start | bytes 8601608 | tf_op jit(solution)/shard_map/ppermute | solution.py:121
  519.1 105.6 %collective-permute-start.14 = (bf16[320,4480]{1,0:T(8,128)(2,1)}, bf16[320,4480]{1,0:T(8,128)(2,1)}, u32[]{:S(2)}, u32[]{:S(2)}) collective-permute-start(bf16[320,4480]{1,0:T(8,128)(2,1)} %get-tuple-element.57), channel_id=1, source_target_pairs={{0,1},{1,0},{2,3},{3,2},{4,5},{5,4},{6,7},{7,6}} | collective-permute-start | bytes 8601608 | tf_op jit(solution)/shard_map/ppermute | solution.py:121
  519.2 153.3 %collective-permute-start.10 = (bf16[320,4480]{1,0:T(8,128)(2,1)}, bf16[320,4480]{1,0:T(8,128)(2,1)}, u32[]{:S(2)}, u32[]{:S(2)}) collective-permute-start(bf16[320,4480]{1,0:T(8,128)(2,1)} %get-tuple-element.56), channel_id=1, source_target_pairs={{0,2},{2,0},{1,3},{3,1},{4,6},{6,4},{5,7},{7,5}} | collective-permute-start | bytes 8601608 | tf_op jit(solution)/shard_map/ppermute | solution.py:121
  549.6 122.9 %collective-permute-start.11 = (bf16[320,4480]{1,0:T(8,128)(2,1)}, bf16[320,4480]{1,0:T(8,128)(2,1)}, u32[]{:S(2)}, u32[]{:S(2)}) collective-permute-start(bf16[320,4480]{1,0:T(8,128)(2,1)} %get-tuple-element.56), channel_id=1, source_target_pairs={{0,1},{1,0},{2,3},{3,2},{4,5},{5,4},{6,7},{7,6}} | collective-permute-start | bytes 8601608 | tf_op jit(solution)/shard_map/ppermute | solution.py:121
  563.1 170.8 %collective-permute-start.46 = (bf16[1120,1280]{1,0:T(8,128)(2,1)}, bf16[1120,1280]{1,0:T(8,128)(2,1)}, u32[]{:S(2)}, u32[]{:S(2)}) collective-permute-start(bf16[1120,1280]{1,0:T(8,128)(2,1)} %get-tuple-element.83), channel_id=1, source_target_pairs={{0,2},{2,0},{1,3},{3,1},{4,6},{6,4},{5,7},{7,5}} | collective-permute-start | bytes 8601608 | tf_op jit(solution)/shard_map/ppermute | solution.py:121
  611.0 122.9 %collective-permute-start.47 = (bf16[1120,1280]{1,0:T(8,128)(2,1)}, bf16[1120,1280]{1,0:T(8,128)(2,1)}, u32[]{:S(2)}, u32[]{:S(2)}) collective-permute-start(bf16[1120,1280]{1,0:T(8,128)(2,1)} %get-tuple-element.83), channel_id=1, source_target_pairs={{0,1},{1,0},{2,3},{3,2},{4,5},{5,4},{6,7},{7,6}} | collective-permute-start | bytes 8601608 | tf_op jit(solution)/shard_map/ppermute | solution.py:121
  624.8 170.1 %collective-permute-start.43 = (bf16[1120,1280]{1,0:T(8,128)(2,1)}, bf16[1120,1280]{1,0:T(8,128)(2,1)}, u32[]{:S(2)}, u32[]{:S(2)}) collective-permute-start(bf16[1120,1280]{1,0:T(8,128)(2,1)} %get-tuple-element.82), channel_id=1, source_target_pairs={{0,2},{2,0},{1,3},{3,1},{4,6},{6,4},{5,7},{7,5}} | collective-permute-start | bytes 8601608 | tf_op jit(solution)/shard_map/ppermute | solution.py:121
  672.4 122.4 %collective-permute-start.36 = (bf16[320,4480]{1,0:T(8,128)(2,1)}, bf16[320,4480]{1,0:T(8,128)(2,1)}, u32[]{:S(2)}, u32[]{:S(2)}) collective-permute-start(bf16[320,4480]{1,0:T(8,128)(2,1)} %collective-permute-done.34.refs_0_), channel_id=1, source_target_pairs={{0,1},{1,0},{2,3},{3,2},{4,5},{5,4},{6,7},{7,6}} | collective-permute-start | bytes 8601608 | tf_op jit(solution)/shard_map/ppermute | solution.py:121
  672.4 122.9 %collective-permute-start.15 = (bf16[320,4480]{1,0:T(8,128)(2,1)}, bf16[320,4480]{1,0:T(8,128)(2,1)}, u32[]{:S(2)}, u32[]{:S(2)}) collective-permute-start(bf16[320,4480]{1,0:T(8,128)(2,1)} %collective-permute-done.13.refs_0_), channel_id=1, source_target_pairs={{0,1},{1,0},{2,3},{3,2},{4,5},{5,4},{6,7},{7,6}} | collective-permute-start | bytes 8601608 | tf_op jit(solution)/shard_map/ppermute | solution.py:121
  733.9 61.5 %collective-permute-start.12 = (bf16[320,4480]{1,0:T(8,128)(2,1)}, bf16[320,4480]{1,0:T(8,128)(2,1)}, u32[]{:S(2)}, u32[]{:S(2)}) collective-permute-start(bf16[320,4480]{1,0:T(8,128)(2,1)} %collective-permute-done.10.refs_0_), channel_id=1, source_target_pairs={{0,1},{1,0},{2,3},{3,2},{4,5},{5,4},{6,7},{7,6}} | collective-permute-start | bytes 8601608 | tf_op jit(solution)/shard_map/ppermute | solution.py:121
  733.9 63.0 %collective-permute-start.48 = (bf16[1120,1280]{1,0:T(8,128)(2,1)}, bf16[1120,1280]{1,0:T(8,128)(2,1)}, u32[]{:S(2)}, u32[]{:S(2)}) collective-permute-start(bf16[1120,1280]{1,0:T(8,128)(2,1)} %collective-permute-done.46.refs_0_), channel_id=1, source_target_pairs={{0,1},{1,0},{2,3},{3,2},{4,5},{5,4},{6,7},{7,6}} | collective-permute-start | bytes 8601608 | tf_op jit(solution)/shard_map/ppermute | solution.py:121
  794.8 38.7 %collective-permute-start.44 = (bf16[1120,1280]{1,0:T(8,128)(2,1)}, bf16[1120,1280]{1,0:T(8,128)(2,1)}, u32[]{:S(2)}, u32[]{:S(2)}) collective-permute-start(bf16[1120,1280]{1,0:T(8,128)(2,1)} %get-tuple-element.82), channel_id=1, source_target_pairs={{0,1},{1,0},{2,3},{3,2},{4,5},{5,4},{6,7},{7,6}} | collective-permute-start | bytes 8601608 | tf_op jit(solution)/shard_map/ppermute | solution.py:121
  794.9 38.7 %collective-permute-start.45 = (bf16[1120,1280]{1,0:T(8,128)(2,1)}, bf16[1120,1280]{1,0:T(8,128)(2,1)}, u32[]{:S(2)}, u32[]{:S(2)}) collective-permute-start(bf16[1120,1280]{1,0:T(8,128)(2,1)} %collective-permute-done.43.refs_0_), channel_id=1, source_target_pairs={{0,1},{1,0},{2,3},{3,2},{4,5},{5,4},{6,7},{7,6}} | collective-permute-start | bytes 8601608 | tf_op jit(solution)/shard_map/ppermute | solution.py:121
  795.4 44.8 %collective-permute-start.23 = (bf16[32,3584]{1,0:T(8,128)(2,1)}, bf16[32,3584]{1,0:T(8,128)(2,1)}, u32[]{:S(2)}, u32[]{:S(2)}) collective-permute-start(bf16[32,3584]{1,0:T(8,128)(2,1)} %collective-permute-done.21.refs_0_), channel_id=1, source_target_pairs={{0,1},{1,0},{2,3},{3,2},{4,5},{5,4},{6,7},{7,6}} | collective-permute-start | bytes 688136 | tf_op jit(solution)/shard_map/ppermute | solution.py:121
  795.4 44.7 %collective-permute-start.22 = (bf16[32,896]{1,0:T(8,128)(2,1)}, bf16[32,896]{1,0:T(8,128)(2,1)}, u32[]{:S(2)}, u32[]{:S(2)}) collective-permute-start(bf16[32,896]{1,0:T(8,128)(2,1)} %get-tuple-element.72), channel_id=1, source_target_pairs={{0,2},{2,0},{1,3},{3,1},{4,6},{6,4},{5,7},{7,5}} | collective-permute-start | bytes 172040 | tf_op jit(solution)/shard_map/ppermute | solution.py:121
  796.9 43.3 %collective-permute-start.24 = (bf16[32,896]{1,0:T(8,128)(2,1)}, bf16[32,896]{1,0:T(8,128)(2,1)}, u32[]{:S(2)}, u32[]{:S(2)}) collective-permute-start(bf16[32,896]{1,0:T(8,128)(2,1)} %get-tuple-element.72), channel_id=1, source_target_pairs={{0,3},{3,0},{1,2},{2,1},{4,7},{7,4},{5,6},{6,5}} | collective-permute-start | bytes 172040 | tf_op jit(solution)/shard_map/ppermute | solution.py:121
  (7 other events, 24.1 us)

commit v8 on v7

--- a/solution.py
+++ b/solution.py
@@ -26,10 +26,10 @@
 ]
 NEWS = [
     (0, 0, 0, 20, 20),
-    (0, 1, 0, 20, 10),
-    (2, 0, 0, 20, 10),
-    (2, 1, 0, 20, 10),
-    (1, 0, 0, 20, 10),
+    (0, 1, 0, 20, 20),
+    (2, 0, 0, 20, 20),
+    (2, 1, 0, 20, 20),
+    (1, 0, 0, 20, 20),
     (1, 1, 0, 10, 10),
     (1, 1, 10, 4, 2),
     (1, 1, 14, 4, 2),
@@ -37,7 +37,7 @@
 ]
 EARLY = 2
 LAST = len(NEWS) - 1
-RIGHT = 896
+RIGHT = 1024
 
 FULL = 67043328
 SPARE = {"cutf_2": 2 << 20, "sum_1": 4 << 20}

time: 843 us -> 843 us (level)
  Pallas kernels: 208 us -> 226 us
  waiting for transfers between devices: 600 us -> 582 us
    ppermute x49, waiting for transfers between devices: 600 us -> 582 us  [send(): return in_space(lax.ppermute(x, 'dp', pairs), space)]
    pallas_call x37, Pallas kernels: 202 us -> 220 us  [run(): pl.pallas_call(body, out_shape=outs, grid=grid, in_specs=in_specs, out_sp...]
  transfers between devices with their start and end apart: 49 -> 49, of which waited for: 16 -> 16; matrix products, arithmetic and copies ran while one was open for 0% -> 0% of each run, Pallas kernels for 24% -> 26%
where the time goes in v8:
time: 843 us; the launch traced here: 842 us
  waiting for transfers between devices  582 us (69%)
  Pallas kernels  226 us (27%)
  starting transfers between devices  30.4 us (4%)
    ppermute x49, waiting for transfers between devices, send(): return in_space(lax.ppermute(x, 'dp', pairs), space)  582 us
    pallas_call x37, Pallas kernels, run(): pl.pallas_call(body, out_shape=outs, grid=grid, in_specs=in_specs, out_sp...  220 us
    ppermute x49, starting transfers between devices, send(): return in_space(lax.ppermute(x, 'dp', pairs), space)  30.4 us
  transfers between devices with their start and end apart: 49, of which 16 were waited for; matrix products, arithmetic and copies ran while one was open for 0% of the time, Pallas kernels for 26%

profile of v8, /device:TPU:0, one launch (start us, length us, event | category | flops | bytes accessed | tf_op | source)
XLA Modules:
  0.0 842.1 jit_solution(6353525175272826746)
XLA Ops:
  0.6 2.8 shard_map.202
  4.3 2.7 shard_map.200
  11.8 6.1 head.1
  19.1 3.2 shard_map.192
  22.2 2.5 collective-permute-start.7
  25.6 25.4 %collective-permute-done.3.refs_0_ = bf16[32,4480]{1,0:T(8,128)(2,1)} collective-permute-done((bf16[32,4480]{1,0:T(8,128)(2,1)}, bf16[32,4480]{1,0:T(8,128)(2,1)}, u32[]{:S(2)}, u32[]{:S(2)}) %collective-permute-start.3) | collective-permute-done | bytes 286752 | tf_op jit(solution)/shard_map/ppermute | solution.py:121
  52.7 5.1 shard_map.199
  59.9 2.7 shard_map.188
  63.2 2.7 shard_map.218
  65.9 3.2 shard_map.194
  70.7 2.7 shard_map.216
  73.6 5.1 shard_map.187
  78.7 24.6 %collective-permute-done.9.refs_3_ = bf16[160,4480]{1,0:T(8,128)(2,1)} collective-permute-done((bf16[160,4480]{1,0:T(8,128)(2,1)}, bf16[160,4480]{1,0:T(8,128)(2,1)}, u32[]{:S(2)}, u32[]{:S(2)}) %collective-permute-start.9) | collective-permute-done | bytes 1433632 | tf_op jit(solution)/shard_map/ppermute | solution.py:121
  103.3 5.1 shard_map.215
  108.9 4.9 shard_map.203
  115.3 4.9 shard_map.201
  120.8 4.9 shard_map.189
  127.1 4.9 shard_map.219
  132.0 47.1 %collective-permute-done.20.refs_0_ = bf16[320,4480]{1,0:T(8,128)(2,1)} collective-permute-done((bf16[320,4480]{1,0:T(8,128)(2,1)}, bf16[320,4480]{1,0:T(8,128)(2,1)}, u32[]{:S(2)}, u32[]{:S(2)}) %collective-permute-start.20) | collective-permute-done | bytes 2867232 | tf_op jit(solution)/shard_map/ppermute | solution.py:121
  180.6 4.9 shard_map.217
  185.5 55.1 %collective-permute-done.18.refs_0_ = bf16[320,4480]{1,0:T(8,128)(2,1)} collective-permute-done((bf16[320,4480]{1,0:T(8,128)(2,1)}, bf16[320,4480]{1,0:T(8,128)(2,1)}, u32[]{:S(2)}, u32[]{:S(2)}) %collective-permute-start.18) | collective-permute-done | bytes 2867232 | tf_op jit(solution)/shard_map/ppermute | solution.py:121
  242.1 17.8 %shard_map.204 = (bf16[320,4480]{1,0:T(8,128)(2,1)}, bf16[2,1280,4480]{2,1,0:T(8,128)(2,1)}, f32[2,320,4480]{2,1,0:T(8,128)}, f32[2,320,4480]{2,1,0:T(8,128)}) custom-call(bf16[1,2,1280,4480]{3,2,1,0:T(8,128)(2,1)} %t.46, bf16[640,4480]{1,0:T(8,128)(2,1)} %collective-permute-done.16.r, bf16[2,1280,4480]{2,1,0:T(8,128)(2,1)} %wt.15, f32[2,320,4480]{2,1,0:T(8,128)} %mm.15, ...), custom_call_target="tpu_custom_call" | custom-call | flops 37273600 | bytes 37273600 | tf_op jit(solution)/shard_map/pallas_call | solution.py:108
  259.9 9.8 %shard_map.205 = (bf16[160,4480]{1,0:T(8,128)(2,1)}, bf16[2,1280,4480]{2,1,0:T(8,128)(2,1)}, f32[2,320,4480]{2,1,0:T(8,128)}, f32[2,320,4480]{2,1,0:T(8,128)}) custom-call(bf16[1,2,1280,4480]{3,2,1,0:T(8,128)(2,1)} %t.46, bf16[640,4480]{1,0:T(8,128)(2,1)} %collective-permute-done.16.r, ...), custom_call_target="tpu_custom_call", output_to_operand_aliasing={{1}: (6, {}), {2}: (7, {}), {3}: (8, {})} | custom-call | flops 35840000 | bytes 35840000 | tf_op jit(solution)/shard_map/pallas_call | solution.py:108
  270.2 4.0 shard_map.206
  274.3 4.0 shard_map.207
  278.3 3.1 shard_map.208
  281.3 20.7 %collective-permute-done.2.refs_0_ = bf16[320,4480]{1,0:T(8,128)(2,1)} collective-permute-done((bf16[320,4480]{1,0:T(8,128)(2,1)}, bf16[320,4480]{1,0:T(8,128)(2,1)}, u32[]{:S(2)}, u32[]{:S(2)}) %collective-permute-start.2) | collective-permute-done | bytes 2867232 | tf_op jit(solution)/shard_map/ppermute | solution.py:121
  303.5 60.0 %collective-permute-done.42.refs_0_ = bf16[1120,1280]{1,0:T(8,128)(2,1)} collective-permute-done((bf16[1120,1280]{1,0:T(8,128)(2,1)}, bf16[1120,1280]{1,0:T(8,128)(2,1)}, u32[]{:S(2)}, u32[]{:S(2)}) %collective-permute-start.42) | collective-permute-done | bytes 2867232 | tf_op jit(solution)/shard_map/ppermute | solution.py:121
  363.5 92.2 %collective-permute-done.31.refs_0_ = bf16[160,4480]{1,0:T(8,128)(2,1)} collective-permute-done((bf16[160,4480]{1,0:T(8,128)(2,1)}, bf16[160,4480]{1,0:T(8,128)(2,1)}, u32[]{:S(2)}, u32[]{:S(2)}) %collective-permute-start.31) | collective-permute-done | bytes 1433632 | tf_op jit(solution)/shard_map/ppermute | solution.py:121
  457.1 2.7 collective-permute-done.21.refs_0_
  461.3 10.7 %collective-permute-done.28.refs_0_ = bf16[64,4480]{1,0:T(8,128)(2,1)S(1)} collective-permute-done((bf16[64,4480]{1,0:T(8,128)(2,1)}, bf16[64,4480]{1,0:T(8,128)(2,1)S(1)}, u32[]{:S(2)}, u32[]{:S(2)}) %collective-permute-start.28) | collective-permute-done | bytes 573472 | tf_op jit(solution)/shard_map/ppermute | solution.py:121
  472.8 11.2 %collective-permute-done.25.refs_0_ = bf16[64,4480]{1,0:T(8,128)(2,1)} collective-permute-done((bf16[64,4480]{1,0:T(8,128)(2,1)}, bf16[64,4480]{1,0:T(8,128)(2,1)}, u32[]{:S(2)}, u32[]{:S(2)}) %collective-permute-start.25) | collective-permute-done | bytes 573472 | tf_op jit(solution)/shard_map/ppermute | solution.py:121
  486.6 17.8 %shard_map.195 = (bf16[320,4480]{1,0:T(8,128)(2,1)}, bf16[2,1280,4480]{2,1,0:T(8,128)(2,1)}, f32[2,320,4480]{2,1,0:T(8,128)}, f32[2,320,4480]{2,1,0:T(8,128)}) custom-call(bf16[1,2,1280,4480]{3,2,1,0:T(8,128)(2,1)} %t.36, bf16[640,4480]{1,0:T(8,128)(2,1)} %collective-permute-done.r, bf16[2,1280,4480]{2,1,0:T(8,128)(2,1)} %wt.10, f32[2,320,4480]{2,1,0:T(8,128)} %mm.10, ...), custom_call_target="tpu_custom_call" | custom-call | flops 37273600 | bytes 37273600 | tf_op jit(solution)/shard_map/pallas_call | solution.py:108
  505.5 17.8 %shard_map.196 = (bf16[320,4480]{1,0:T(8,128)(2,1)}, bf16[2,1280,4480]{2,1,0:T(8,128)(2,1)}, f32[2,320,4480]{2,1,0:T(8,128)}, f32[2,320,4480]{2,1,0:T(8,128)}) custom-call(bf16[1,2,1280,4480]{3,2,1,0:T(8,128)(2,1)} %t.36, bf16[640,4480]{1,0:T(8,128)(2,1)} %collective-permute-done.r, ...), custom_call_target="tpu_custom_call", output_to_operand_aliasing={{1}: (6, {}), {2}: (7, {}), {3}: (8, {})} | custom-call | flops 37273600 | bytes 37273600 | tf_op jit(solution)/shard_map/pallas_call | solution.py:108
  524.3 25.1 %collective-permute-done.34.refs_0_ = bf16[320,4480]{1,0:T(8,128)(2,1)} collective-permute-done((bf16[320,4480]{1,0:T(8,128)(2,1)}, bf16[320,4480]{1,0:T(8,128)(2,1)}, u32[]{:S(2)}, u32[]{:S(2)}) %collective-permute-start.34) | collective-permute-done | bytes 2867232 | tf_op jit(solution)/shard_map/ppermute | solution.py:121
  549.4 18.0 %shard_map.220 = (bf16[1120,1280]{1,0:T(8,128)(2,1)}, bf16[2,4480,1280]{2,1,0:T(8,128)(2,1)}, f32[2,1120,1280]{2,1,0:T(8,128)}, f32[2,1120,1280]{2,1,0:T(8,128)}) custom-call(bf16[1,2,4480,1280]{3,2,1,0:T(8,128)(2,1)} %t.53, bf16[2240,1280]{1,0:T(8,128)(2,1)} %collective-permute-done.38.r, bf16[2,4480,1280]{2,1,0:T(8,128)(2,1)} %wt.17, ...), custom_call_target="tpu_custom_call" | custom-call | flops 37273600 | bytes 37273600 | tf_op jit(solution)/shard_map/pallas_call | solution.py:108
  568.8 42.0 %collective-permute-done.13.refs_0_ = bf16[320,4480]{1,0:T(8,128)(2,1)} collective-permute-done((bf16[320,4480]{1,0:T(8,128)(2,1)}, bf16[320,4480]{1,0:T(8,128)(2,1)}, u32[]{:S(2)}, u32[]{:S(2)}) %collective-permute-start.13) | collective-permute-done | bytes 2867232 | tf_op jit(solution)/shard_map/ppermute | solution.py:121
  610.8 17.8 %shard_map.221 = (bf16[1120,1280]{1,0:T(8,128)(2,1)}, bf16[2,4480,1280]{2,1,0:T(8,128)(2,1)}, f32[2,1120,1280]{2,1,0:T(8,128)}, f32[2,1120,1280]{2,1,0:T(8,128)}) custom-call(bf16[1,2,4480,1280]{3,2,1,0:T(8,128)(2,1)} %t.53, bf16[2240,1280]{1,0:T(8,128)(2,1)} %collective-permute-done.38.r, ...), custom_call_target="tpu_custom_call", output_to_operand_aliasing={{1}: (6, {}), {2}: (7, {}), {3}: (8, {})} | custom-call | flops 37273600 | bytes 37273600 | tf_op jit(solution)/shard_map/pallas_call | solution.py:108
  630.1 42.2 %collective-permute-done.10.refs_0_ = bf16[320,4480]{1,0:T(8,128)(2,1)} collective-permute-done((bf16[320,4480]{1,0:T(8,128)(2,1)}, bf16[320,4480]{1,0:T(8,128)(2,1)}, u32[]{:S(2)}, u32[]{:S(2)}) %collective-permute-start.10) | collective-permute-done | bytes 2867232 | tf_op jit(solution)/shard_map/ppermute | solution.py:121
  672.8 60.9 %collective-permute-done.46.refs_0_ = bf16[1120,1280]{1,0:T(8,128)(2,1)} collective-permute-done((bf16[1120,1280]{1,0:T(8,128)(2,1)}, bf16[1120,1280]{1,0:T(8,128)(2,1)}, u32[]{:S(2)}, u32[]{:S(2)}) %collective-permute-start.46) | collective-permute-done | bytes 2867232 | tf_op jit(solution)/shard_map/ppermute | solution.py:121
  734.2 60.4 %collective-permute-done.43.refs_0_ = bf16[1120,1280]{1,0:T(8,128)(2,1)} collective-permute-done((bf16[1120,1280]{1,0:T(8,128)(2,1)}, bf16[1120,1280]{1,0:T(8,128)(2,1)}, u32[]{:S(2)}, u32[]{:S(2)}) %collective-permute-start.43) | collective-permute-done | bytes 2867232 | tf_op jit(solution)/shard_map/ppermute | solution.py:121
  798.7 6.5 shard_map.210.refs_3_
  805.3 3.6 shard_map.211.refs_3_
  811.3 2.4 shard_map.213.refs_4_
  813.7 6.5 shard_map.197.refs_3_
  820.2 6.5 shard_map.198
  826.8 6.6 shard_map.222.refs_3_
  833.4 6.6 shard_map.223
  (100 shorter events, 43.3 us)
Async XLA Ops:
  3.4 65.8 %collective-permute-start.19 = (bf16[320,4480]{1,0:T(8,128)(2,1)}, bf16[320,4480]{1,0:T(8,128)(2,1)}, u32[]{:S(2)}, u32[]{:S(2)}) collective-permute-start(bf16[320,4480]{1,0:T(8,128)(2,1)} %shard_map.202), channel_id=1, source_target_pairs={{0,1},{1,0},{2,3},{3,2},{4,5},{5,4},{6,7},{7,6}} | collective-permute-start | bytes 8601608 | tf_op jit(solution)/shard_map/ppermute | solution.py:121
  7.0 66.4 %collective-permute-start.17 = (bf16[320,4480]{1,0:T(8,128)(2,1)}, bf16[320,4480]{1,0:T(8,128)(2,1)}, u32[]{:S(2)}, u32[]{:S(2)}) collective-permute-start(bf16[320,4480]{1,0:T(8,128)(2,1)} %shard_map.200), channel_id=1, source_target_pairs={{0,1},{1,0},{2,3},{3,2},{4,5},{5,4},{6,7},{7,6}} | collective-permute-start | bytes 8601608 | tf_op jit(solution)/shard_map/ppermute | solution.py:121
  9.0 10.1 %collective-permute-start.6 = (bf16[96,4480]{1,0:T(8,128)(2,1)}, bf16[96,4480]{1,0:T(8,128)(2,1)}, u32[]{:S(2)}, u32[]{:S(2)}) collective-permute-start(bf16[96,4480]{1,0:T(8,128)(2,1)} %shard_map.191), channel_id=1, source_target_pairs={{0,1},{1,0},{2,3},{3,2},{4,5},{5,4},{6,7},{7,6}} | collective-permute-start | bytes 2580488 | tf_op jit(solution)/shard_map/ppermute | solution.py:121
  11.7 50.9 %collective-permute-start.8 = (bf16[160,4480]{1,0:T(8,128)(2,1)}, bf16[160,4480]{1,0:T(8,128)(2,1)}, u32[]{:S(2)}, u32[]{:S(2)}) collective-permute-start(bf16[160,4480]{1,0:T(8,128)(2,1)} %shard_map.193), channel_id=1, source_target_pairs={{0,1},{1,0},{2,3},{3,2},{4,5},{5,4},{6,7},{7,6}} | collective-permute-start | bytes 4300808 | tf_op jit(solution)/shard_map/ppermute | solution.py:121
  22.2 46.9 %collective-permute-start.7 = (bf16[96,4480]{1,0:T(8,128)(2,1)}, bf16[96,4480]{1,0:T(8,128)(2,1)}, u32[]{:S(2)}, u32[]{:S(2)}) collective-permute-start(bf16[96,4480]{1,0:T(8,128)(2,1)} %shard_map.192), channel_id=1, source_target_pairs={{0,2},{2,0},{1,3},{3,1},{4,6},{6,4},{5,7},{7,5}} | collective-permute-start | bytes 2580488 | tf_op jit(solution)/shard_map/ppermute | solution.py:121
  24.8 26.2 %collective-permute-start.3 = (bf16[32,4480]{1,0:T(8,128)(2,1)}, bf16[32,4480]{1,0:T(8,128)(2,1)}, u32[]{:S(2)}, u32[]{:S(2)}) collective-permute-start(bf16[32,4480]{1,0:T(8,128)(2,1)} %copy-done), channel_id=1, source_target_pairs={{0,2},{2,0},{1,3},{3,1},{4,6},{6,4},{5,7},{7,5}} | collective-permute-start | bytes 860168 | tf_op jit(solution)/shard_map/ppermute | solution.py:121
  51.0 8.9 %collective-permute-start.5 = (bf16[32,4480]{1,0:T(8,128)(2,1)}, bf16[32,4480]{1,0:T(8,128)(2,1)}, u32[]{:S(2)}, u32[]{:S(2)}) collective-permute-start(bf16[32,4480]{1,0:T(8,128)(2,1)} %shard_map.190), channel_id=1, source_target_pairs={{0,2},{2,0},{1,3},{3,1},{4,6},{6,4},{5,7},{7,5}} | collective-permute-start | bytes 860168 | tf_op jit(solution)/shard_map/ppermute | solution.py:121
  59.9 65.8 %collective-permute-start.16 = (bf16[640,4480]{1,0:T(8,128)(2,1)}, bf16[640,4480]{1,0:T(8,128)(2,1)}, u32[]{:S(2)}, u32[]{:S(2)}) collective-permute-start(bf16[640,4480]{1,0:T(8,128)(2,1)} %shard_map.199), channel_id=1, source_target_pairs={{0,1},{1,0},{2,3},{3,2},{4,5},{5,4},{6,7},{7,6}} | collective-permute-start | bytes 17203208 | tf_op jit(solution)/shard_map/ppermute | solution.py:121
  62.7 45.7 %collective-permute-start.1 = (bf16[320,4480]{1,0:T(8,128)(2,1)}, bf16[320,4480]{1,0:T(8,128)(2,1)}, u32[]{:S(2)}, u32[]{:S(2)}) collective-permute-start(bf16[320,4480]{1,0:T(8,128)(2,1)} %shard_map.188), channel_id=1, source_target_pairs={{0,1},{1,0},{2,3},{3,2},{4,5},{5,4},{6,7},{7,6}} | collective-permute-start | bytes 8601608 | tf_op jit(solution)/shard_map/ppermute | solution.py:121
  69.2 44.7 %collective-permute-start.41 = (bf16[1120,1280]{1,0:T(8,128)(2,1)}, bf16[1120,1280]{1,0:T(8,128)(2,1)}, u32[]{:S(2)}, u32[]{:S(2)}) collective-permute-start(bf16[1120,1280]{1,0:T(8,128)(2,1)} %shard_map.218), channel_id=1, source_target_pairs={{0,1},{1,0},{2,3},{3,2},{4,5},{5,4},{6,7},{7,6}} | collective-permute-start | bytes 8601608 | tf_op jit(solution)/shard_map/ppermute | solution.py:121
  69.2 34.1 %collective-permute-start.9 = (bf16[160,4480]{1,0:T(8,128)(2,1)}, bf16[160,4480]{1,0:T(8,128)(2,1)}, u32[]{:S(2)}, u32[]{:S(2)}) collective-permute-start(bf16[160,4480]{1,0:T(8,128)(2,1)} %shard_map.194), channel_id=1, source_target_pairs={{0,2},{2,0},{1,3},{3,1},{4,6},{6,4},{5,7},{7,5}} | collective-permute-start | bytes 4300808 | tf_op jit(solution)/shard_map/ppermute | solution.py:121
  73.4 46.8 %collective-permute-start.39 = (bf16[1120,1280]{1,0:T(8,128)(2,1)}, bf16[1120,1280]{1,0:T(8,128)(2,1)}, u32[]{:S(2)}, u32[]{:S(2)}) collective-permute-start(bf16[1120,1280]{1,0:T(8,128)(2,1)} %shard_map.216), channel_id=1, source_target_pairs={{0,1},{1,0},{2,3},{3,2},{4,5},{5,4},{6,7},{7,6}} | collective-permute-start | bytes 8601608 | tf_op jit(solution)/shard_map/ppermute | solution.py:121
  103.3 166.4 %collective-permute-start = (bf16[640,4480]{1,0:T(8,128)(2,1)}, bf16[640,4480]{1,0:T(8,128)(2,1)}, u32[]{:S(2)}, u32[]{:S(2)}) collective-permute-start(bf16[640,4480]{1,0:T(8,128)(2,1)} %shard_map.187), channel_id=1, source_target_pairs={{0,1},{1,0},{2,3},{3,2},{4,5},{5,4},{6,7},{7,6}} | collective-permute-start | bytes 17203208 | tf_op jit(solution)/shard_map/ppermute | solution.py:121
  108.4 193.6 %collective-permute-start.38 = (bf16[2240,1280]{1,0:T(8,128)(2,1)}, bf16[2240,1280]{1,0:T(8,128)(2,1)}, u32[]{:S(2)}, u32[]{:S(2)}) collective-permute-start(bf16[2240,1280]{1,0:T(8,128)(2,1)} %shard_map.215), channel_id=1, source_target_pairs={{0,1},{1,0},{2,3},{3,2},{4,5},{5,4},{6,7},{7,6}} | collective-permute-start | bytes 17203208 | tf_op jit(solution)/shard_map/ppermute | solution.py:121
  113.8 65.3 %collective-permute-start.20 = (bf16[320,4480]{1,0:T(8,128)(2,1)}, bf16[320,4480]{1,0:T(8,128)(2,1)}, u32[]{:S(2)}, u32[]{:S(2)}) collective-permute-start(bf16[320,4480]{1,0:T(8,128)(2,1)} %shard_map.203), channel_id=1, source_target_pairs={{0,2},{2,0},{1,3},{3,1},{4,6},{6,4},{5,7},{7,5}} | collective-permute-start | bytes 8601608 | tf_op jit(solution)/shard_map/ppermute | solution.py:121
  120.2 120.4 %collective-permute-start.18 = (bf16[320,4480]{1,0:T(8,128)(2,1)}, bf16[320,4480]{1,0:T(8,128)(2,1)}, u32[]{:S(2)}, u32[]{:S(2)}) collective-permute-start(bf16[320,4480]{1,0:T(8,128)(2,1)} %shard_map.201), channel_id=1, source_target_pairs={{0,2},{2,0},{1,3},{3,1},{4,6},{6,4},{5,7},{7,5}} | collective-permute-start | bytes 8601608 | tf_op jit(solution)/shard_map/ppermute | solution.py:121
  125.7 176.4 %collective-permute-start.2 = (bf16[320,4480]{1,0:T(8,128)(2,1)}, bf16[320,4480]{1,0:T(8,128)(2,1)}, u32[]{:S(2)}, u32[]{:S(2)}) collective-permute-start(bf16[320,4480]{1,0:T(8,128)(2,1)} %shard_map.189), channel_id=1, source_target_pairs={{0,2},{2,0},{1,3},{3,1},{4,6},{6,4},{5,7},{7,5}} | collective-permute-start | bytes 8601608 | tf_op jit(solution)/shard_map/ppermute | solution.py:121
  179.2 184.3 %collective-permute-start.42 = (bf16[1120,1280]{1,0:T(8,128)(2,1)}, bf16[1120,1280]{1,0:T(8,128)(2,1)}, u32[]{:S(2)}, u32[]{:S(2)}) collective-permute-start(bf16[1120,1280]{1,0:T(8,128)(2,1)} %shard_map.219), channel_id=1, source_target_pairs={{0,2},{2,0},{1,3},{3,1},{4,6},{6,4},{5,7},{7,5}} | collective-permute-start | bytes 8601608 | tf_op jit(solution)/shard_map/ppermute | solution.py:121
  240.6 215.1 %collective-permute-start.40 = (bf16[1120,1280]{1,0:T(8,128)(2,1)}, bf16[1120,1280]{1,0:T(8,128)(2,1)}, u32[]{:S(2)}, u32[]{:S(2)}) collective-permute-start(bf16[1120,1280]{1,0:T(8,128)(2,1)} %shard_map.217), channel_id=1, source_target_pairs={{0,2},{2,0},{1,3},{3,1},{4,6},{6,4},{5,7},{7,5}} | collective-permute-start | bytes 8601608 | tf_op jit(solution)/shard_map/ppermute | solution.py:121
  269.7 185.9 %collective-permute-start.31 = (bf16[160,4480]{1,0:T(8,128)(2,1)}, bf16[160,4480]{1,0:T(8,128)(2,1)}, u32[]{:S(2)}, u32[]{:S(2)}) collective-permute-start(bf16[160,4480]{1,0:T(8,128)(2,1)} %get-tuple-element.75), channel_id=1, source_target_pairs={{0,2},{2,0},{1,3},{3,1},{4,6},{6,4},{5,7},{7,5}} | collective-permute-start | bytes 4300808 | tf_op jit(solution)/shard_map/ppermute | solution.py:121
  302.0 157.8 %collective-permute-start.37 = (bf16[32,4480]{1,0:T(8,128)(2,1)}, bf16[32,4480]{1,0:T(8,128)(2,1)S(1)}, u32[]{:S(2)}, u32[]{:S(2)}) collective-permute-start(bf16[32,4480]{1,0:T(8,128)(2,1)} %get-tuple-element.77), channel_id=1, source_target_pairs={{0,1},{1,0},{2,3},{3,2},{4,5},{5,4},{6,7},{7,6}} | collective-permute-start | bytes 860168 | tf_op jit(solution)/shard_map/ppermute | solution.py:121
  302.1 157.8 %collective-permute-start.21 = (bf16[32,3456]{1,0:T(8,128)(2,1)}, bf16[32,3456]{1,0:T(8,128)(2,1)}, u32[]{:S(2)}, u32[]{:S(2)}) collective-permute-start(bf16[32,3456]{1,0:T(8,128)(2,1)} %get-tuple-element.71), channel_id=1, source_target_pairs={{0,2},{2,0},{1,3},{3,1},{4,6},{6,4},{5,7},{7,5}} | collective-permute-start | bytes 663560 | tf_op jit(solution)/shard_map/ppermute | solution.py:121
  363.5 159.8 %collective-permute-start.32 = (bf16[160,4480]{1,0:T(8,128)(2,1)}, bf16[160,4480]{1,0:T(8,128)(2,1)}, u32[]{:S(2)}, u32[]{:S(2)}) collective-permute-start(bf16[160,4480]{1,0:T(8,128)(2,1)} %get-tuple-element.75), channel_id=1, source_target_pairs={{0,1},{1,0},{2,3},{3,2},{4,5},{5,4},{6,7},{7,6}} | collective-permute-start | bytes 4300808 | tf_op jit(solution)/shard_map/ppermute | solution.py:121
  455.7 67.7 %collective-permute-start.33 = (bf16[160,4480]{1,0:T(8,128)(2,1)}, bf16[160,4480]{1,0:T(8,128)(2,1)}, u32[]{:S(2)}, u32[]{:S(2)}) collective-permute-start(bf16[160,4480]{1,0:T(8,128)(2,1)} %collective-permute-done.31.refs_0_), channel_id=1, source_target_pairs={{0,1},{1,0},{2,3},{3,2},{4,5},{5,4},{6,7},{7,6}} | collective-permute-start | bytes 4300808 | tf_op jit(solution)/shard_map/ppermute | solution.py:121
  455.7 16.3 %collective-permute-start.28 = (bf16[64,4480]{1,0:T(8,128)(2,1)}, bf16[64,4480]{1,0:T(8,128)(2,1)S(1)}, u32[]{:S(2)}, u32[]{:S(2)}) collective-permute-start(bf16[64,4480]{1,0:T(8,128)(2,1)} %get-tuple-element.74), channel_id=1, source_target_pairs={{0,2},{2,0},{1,3},{3,1},{4,6},{6,4},{5,7},{7,5}} | collective-permute-start | bytes 1720328 | tf_op jit(solution)/shard_map/ppermute | solution.py:121
  459.8 12.2 %collective-permute-start.29 = (bf16[64,4480]{1,0:T(8,128)(2,1)}, bf16[64,4480]{1,0:T(8,128)(2,1)S(1)}, u32[]{:S(2)}, u32[]{:S(2)}) collective-permute-start(bf16[64,4480]{1,0:T(8,128)(2,1)} %get-tuple-element.74), channel_id=1, source_target_pairs={{0,1},{1,0},{2,3},{3,2},{4,5},{5,4},{6,7},{7,6}} | collective-permute-start | bytes 1720328 | tf_op jit(solution)/shard_map/ppermute | solution.py:121
  459.8 24.2 %collective-permute-start.25 = (bf16[64,4480]{1,0:T(8,128)(2,1)}, bf16[64,4480]{1,0:T(8,128)(2,1)}, u32[]{:S(2)}, u32[]{:S(2)}) collective-permute-start(bf16[64,4480]{1,0:T(8,128)(2,1)} %get-tuple-element.73), channel_id=1, source_target_pairs={{0,2},{2,0},{1,3},{3,1},{4,6},{6,4},{5,7},{7,5}} | collective-permute-start | bytes 1720328 | tf_op jit(solution)/shard_map/ppermute | solution.py:121
  472.0 12.0 %collective-permute-start.26 = (bf16[64,4480]{1,0:T(8,128)(2,1)}, bf16[64,4480]{1,0:T(8,128)(2,1)S(1)}, u32[]{:S(2)}, u32[]{:S(2)}) collective-permute-start(bf16[64,4480]{1,0:T(8,128)(2,1)} %get-tuple-element.73), channel_id=1, source_target_pairs={{0,1},{1,0},{2,3},{3,2},{4,5},{5,4},{6,7},{7,6}} | collective-permute-start | bytes 1720328 | tf_op jit(solution)/shard_map/ppermute | solution.py:121
  472.8 12.7 %collective-permute-start.30 = (bf16[64,4480]{1,0:T(8,128)(2,1)S(1)}, bf16[64,4480]{1,0:T(8,128)(2,1)S(1)}, u32[]{:S(2)}, u32[]{:S(2)}) collective-permute-start(bf16[64,4480]{1,0:T(8,128)(2,1)S(1)} %collective-permute-done.28.refs_0_), channel_id=1, source_target_pairs={{0,1},{1,0},{2,3},{3,2},{4,5},{5,4},{6,7},{7,6}} | collective-permute-start | bytes 1720328 | tf_op jit(solution)/shard_map/ppermute | solution.py:121
  484.0 20.3 %collective-permute-start.27 = (bf16[64,4480]{1,0:T(8,128)(2,1)}, bf16[64,4480]{1,0:T(8,128)(2,1)}, u32[]{:S(2)}, u32[]{:S(2)}) collective-permute-start(bf16[64,4480]{1,0:T(8,128)(2,1)} %collective-permute-done.25.refs_0_), channel_id=1, source_target_pairs={{0,1},{1,0},{2,3},{3,2},{4,5},{5,4},{6,7},{7,6}} | collective-permute-start | bytes 1720328 | tf_op jit(solution)/shard_map/ppermute | solution.py:121
  484.0 65.3 %collective-permute-start.34 = (bf16[320,4480]{1,0:T(8,128)(2,1)}, bf16[320,4480]{1,0:T(8,128)(2,1)}, u32[]{:S(2)}, u32[]{:S(2)}) collective-permute-start(bf16[320,4480]{1,0:T(8,128)(2,1)} %get-tuple-element.76), channel_id=1, source_target_pairs={{0,2},{2,0},{1,3},{3,1},{4,6},{6,4},{5,7},{7,5}} | collective-permute-start | bytes 8601608 | tf_op jit(solution)/shard_map/ppermute | solution.py:121
  486.4 81.0 %collective-permute-start.35 = (bf16[320,4480]{1,0:T(8,128)(2,1)}, bf16[320,4480]{1,0:T(8,128)(2,1)}, u32[]{:S(2)}, u32[]{:S(2)}) collective-permute-start(bf16[320,4480]{1,0:T(8,128)(2,1)} %get-tuple-element.76), channel_id=1, source_target_pairs={{0,1},{1,0},{2,3},{3,2},{4,5},{5,4},{6,7},{7,6}} | collective-permute-start | bytes 8601608 | tf_op jit(solution)/shard_map/ppermute | solution.py:121
  504.4 106.5 %collective-permute-start.13 = (bf16[320,4480]{1,0:T(8,128)(2,1)}, bf16[320,4480]{1,0:T(8,128)(2,1)}, u32[]{:S(2)}, u32[]{:S(2)}) collective-permute-start(bf16[320,4480]{1,0:T(8,128)(2,1)} %get-tuple-element.57), channel_id=1, source_target_pairs={{0,2},{2,0},{1,3},{3,1},{4,6},{6,4},{5,7},{7,5}} | collective-permute-start | bytes 8601608 | tf_op jit(solution)/shard_map/ppermute | solution.py:121
  523.3 105.3 %collective-permute-start.14 = (bf16[320,4480]{1,0:T(8,128)(2,1)}, bf16[320,4480]{1,0:T(8,128)(2,1)}, u32[]{:S(2)}, u32[]{:S(2)}) collective-permute-start(bf16[320,4480]{1,0:T(8,128)(2,1)} %get-tuple-element.57), channel_id=1, source_target_pairs={{0,1},{1,0},{2,3},{3,2},{4,5},{5,4},{6,7},{7,6}} | collective-permute-start | bytes 8601608 | tf_op jit(solution)/shard_map/ppermute | solution.py:121
  523.3 148.9 %collective-permute-start.10 = (bf16[320,4480]{1,0:T(8,128)(2,1)}, bf16[320,4480]{1,0:T(8,128)(2,1)}, u32[]{:S(2)}, u32[]{:S(2)}) collective-permute-start(bf16[320,4480]{1,0:T(8,128)(2,1)} %get-tuple-element.56), channel_id=1, source_target_pairs={{0,2},{2,0},{1,3},{3,1},{4,6},{6,4},{5,7},{7,5}} | collective-permute-start | bytes 8601608 | tf_op jit(solution)/shard_map/ppermute | solution.py:121
  549.4 122.9 %collective-permute-start.11 = (bf16[320,4480]{1,0:T(8,128)(2,1)}, bf16[320,4480]{1,0:T(8,128)(2,1)}, u32[]{:S(2)}, u32[]{:S(2)}) collective-permute-start(bf16[320,4480]{1,0:T(8,128)(2,1)} %get-tuple-element.56), channel_id=1, source_target_pairs={{0,1},{1,0},{2,3},{3,2},{4,5},{5,4},{6,7},{7,6}} | collective-permute-start | bytes 8601608 | tf_op jit(solution)/shard_map/ppermute | solution.py:121
  567.4 166.3 %collective-permute-start.46 = (bf16[1120,1280]{1,0:T(8,128)(2,1)}, bf16[1120,1280]{1,0:T(8,128)(2,1)}, u32[]{:S(2)}, u32[]{:S(2)}) collective-permute-start(bf16[1120,1280]{1,0:T(8,128)(2,1)} %get-tuple-element.83), channel_id=1, source_target_pairs={{0,2},{2,0},{1,3},{3,1},{4,6},{6,4},{5,7},{7,5}} | collective-permute-start | bytes 8601608 | tf_op jit(solution)/shard_map/ppermute | solution.py:121
  610.8 122.9 %collective-permute-start.47 = (bf16[1120,1280]{1,0:T(8,128)(2,1)}, bf16[1120,1280]{1,0:T(8,128)(2,1)}, u32[]{:S(2)}, u32[]{:S(2)}) collective-permute-start(bf16[1120,1280]{1,0:T(8,128)(2,1)} %get-tuple-element.83), channel_id=1, source_target_pairs={{0,1},{1,0},{2,3},{3,2},{4,5},{5,4},{6,7},{7,6}} | collective-permute-start | bytes 8601608 | tf_op jit(solution)/shard_map/ppermute | solution.py:121
  628.6 166.1 %collective-permute-start.43 = (bf16[1120,1280]{1,0:T(8,128)(2,1)}, bf16[1120,1280]{1,0:T(8,128)(2,1)}, u32[]{:S(2)}, u32[]{:S(2)}) collective-permute-start(bf16[1120,1280]{1,0:T(8,128)(2,1)} %get-tuple-element.82), channel_id=1, source_target_pairs={{0,2},{2,0},{1,3},{3,1},{4,6},{6,4},{5,7},{7,5}} | collective-permute-start | bytes 8601608 | tf_op jit(solution)/shard_map/ppermute | solution.py:121
  672.3 122.4 %collective-permute-start.36 = (bf16[320,4480]{1,0:T(8,128)(2,1)}, bf16[320,4480]{1,0:T(8,128)(2,1)}, u32[]{:S(2)}, u32[]{:S(2)}) collective-permute-start(bf16[320,4480]{1,0:T(8,128)(2,1)} %collective-permute-done.34.refs_0_), channel_id=1, source_target_pairs={{0,1},{1,0},{2,3},{3,2},{4,5},{5,4},{6,7},{7,6}} | collective-permute-start | bytes 8601608 | tf_op jit(solution)/shard_map/ppermute | solution.py:121
  672.3 122.9 %collective-permute-start.15 = (bf16[320,4480]{1,0:T(8,128)(2,1)}, bf16[320,4480]{1,0:T(8,128)(2,1)}, u32[]{:S(2)}, u32[]{:S(2)}) collective-permute-start(bf16[320,4480]{1,0:T(8,128)(2,1)} %collective-permute-done.13.refs_0_), channel_id=1, source_target_pairs={{0,1},{1,0},{2,3},{3,2},{4,5},{5,4},{6,7},{7,6}} | collective-permute-start | bytes 8601608 | tf_op jit(solution)/shard_map/ppermute | solution.py:121
  733.7 61.5 %collective-permute-start.12 = (bf16[320,4480]{1,0:T(8,128)(2,1)}, bf16[320,4480]{1,0:T(8,128)(2,1)}, u32[]{:S(2)}, u32[]{:S(2)}) collective-permute-start(bf16[320,4480]{1,0:T(8,128)(2,1)} %collective-permute-done.10.refs_0_), channel_id=1, source_target_pairs={{0,1},{1,0},{2,3},{3,2},{4,5},{5,4},{6,7},{7,6}} | collective-permute-start | bytes 8601608 | tf_op jit(solution)/shard_map/ppermute | solution.py:121
  733.7 63.0 %collective-permute-start.48 = (bf16[1120,1280]{1,0:T(8,128)(2,1)}, bf16[1120,1280]{1,0:T(8,128)(2,1)}, u32[]{:S(2)}, u32[]{:S(2)}) collective-permute-start(bf16[1120,1280]{1,0:T(8,128)(2,1)} %collective-permute-done.46.refs_0_), channel_id=1, source_target_pairs={{0,1},{1,0},{2,3},{3,2},{4,5},{5,4},{6,7},{7,6}} | collective-permute-start | bytes 8601608 | tf_op jit(solution)/shard_map/ppermute | solution.py:121
  794.7 38.7 %collective-permute-start.44 = (bf16[1120,1280]{1,0:T(8,128)(2,1)}, bf16[1120,1280]{1,0:T(8,128)(2,1)}, u32[]{:S(2)}, u32[]{:S(2)}) collective-permute-start(bf16[1120,1280]{1,0:T(8,128)(2,1)} %get-tuple-element.82), channel_id=1, source_target_pairs={{0,1},{1,0},{2,3},{3,2},{4,5},{5,4},{6,7},{7,6}} | collective-permute-start | bytes 8601608 | tf_op jit(solution)/shard_map/ppermute | solution.py:121
  794.7 38.7 %collective-permute-start.45 = (bf16[1120,1280]{1,0:T(8,128)(2,1)}, bf16[1120,1280]{1,0:T(8,128)(2,1)}, u32[]{:S(2)}, u32[]{:S(2)}) collective-permute-start(bf16[1120,1280]{1,0:T(8,128)(2,1)} %collective-permute-done.43.refs_0_), channel_id=1, source_target_pairs={{0,1},{1,0},{2,3},{3,2},{4,5},{5,4},{6,7},{7,6}} | collective-permute-start | bytes 8601608 | tf_op jit(solution)/shard_map/ppermute | solution.py:121
  795.2 44.8 %collective-permute-start.23 = (bf16[32,3456]{1,0:T(8,128)(2,1)}, bf16[32,3456]{1,0:T(8,128)(2,1)}, u32[]{:S(2)}, u32[]{:S(2)}) collective-permute-start(bf16[32,3456]{1,0:T(8,128)(2,1)} %collective-permute-done.21.refs_0_), channel_id=1, source_target_pairs={{0,1},{1,0},{2,3},{3,2},{4,5},{5,4},{6,7},{7,6}} | collective-permute-start | bytes 663560 | tf_op jit(solution)/shard_map/ppermute | solution.py:121
  795.2 44.7 %collective-permute-start.22 = (bf16[32,1024]{1,0:T(8,128)(2,1)}, bf16[32,1024]{1,0:T(8,128)(2,1)}, u32[]{:S(2)}, u32[]{:S(2)}) collective-permute-start(bf16[32,1024]{1,0:T(8,128)(2,1)} %get-tuple-element.72), channel_id=1, source_target_pairs={{0,2},{2,0},{1,3},{3,1},{4,6},{6,4},{5,7},{7,5}} | collective-permute-start | bytes 196616 | tf_op jit(solution)/shard_map/ppermute | solution.py:121
  796.7 43.3 %collective-permute-start.24 = (bf16[32,1024]{1,0:T(8,128)(2,1)}, bf16[32,1024]{1,0:T(8,128)(2,1)}, u32[]{:S(2)}, u32[]{:S(2)}) collective-permute-start(bf16[32,1024]{1,0:T(8,128)(2,1)} %get-tuple-element.72), channel_id=1, source_target_pairs={{0,3},{3,0},{1,2},{2,1},{4,7},{7,4},{5,6},{6,5}} | collective-permute-start | bytes 196616 | tf_op jit(solution)/shard_map/ppermute | solution.py:121
  (7 other events, 24.3 us)

commit v9 on v8

--- a/solution.py
+++ b/solution.py
@@ -42,7 +42,7 @@
 FULL = 67043328
 SPARE = {"cutf_2": 2 << 20, "sum_1": 4 << 20}
 SPARE |= {name: 600 << 10 for name in ("cutf_3", "sum_2", "cutf_4")}
-SPARE |= {f"place_{LAST - 1}": 640 << 10, "place_last": 1 << 20}
+SPARE |= {f"place_{LAST - 1}": 640 << 10, "place_left": 2 << 20, "place_last": 2 << 20}
 
 ANY = pl.BlockSpec(memory_space=pltpu.HBM)
 WHOLE = pl.BlockSpec(memory_space=pltpu.VMEM)
@@ -276,25 +276,26 @@
                 move_scratch(w, n // b * len(pieces), b),
             )
 
-        def place_last(far, far_mate):
+        def place_parts(name, parts):
             w, layer, u0, n, _ = NEWS[LAST]
             left = cols[w] - RIGHT
 
             def body(*refs):
                 full, sem = refs[-2:]
                 copies = []
-                for j, of in enumerate((far_of, far_mate_of)):
-                    here = at(w, of(me()) * UNITS + u0, n)
-                    for i, columns in enumerate((pl.ds(0, left), pl.ds(left, RIGHT))):
-                        copies.append(pltpu.make_async_copy(refs[2 * j + i], full.at[layer, here, columns], sem.at[2 * j + i]))
+                for j, (_, of, right) in enumerate(parts):
+                    columns = pl.ds(left, RIGHT) if right else pl.ds(0, left)
+                    to = full.at[layer, at(w, of(me()) * UNITS + u0, n), columns]
+                    copies.append(pltpu.make_async_copy(refs[j], to, sem.at[j]))
                 for one in copies:
                     one.start()
                 for one in copies:
                     one.wait()
 
             like = jax.ShapeDtypeStruct(weights[w].shape, jnp.bfloat16)
-            ins, specs = [*far, *far_mate, new_w[w]], [WHOLE] * 4 + [ANY]
-            (new_w[w],) = run("place_last", body, (), ins, specs, [like], [ANY], {4: 0}, [DMA((4,))])
+            count = len(parts)
+            ins, specs = [*(part for part, _, _ in parts), new_w[w]], [WHOLE] * count + [ANY]
+            (new_w[w],) = run(name, body, (), ins, specs, [like], [ANY], {count: 0}, [DMA((count,))])
 
         first, piece, own = head()
         far_sum = [send(first, FAR)]
@@ -318,7 +319,9 @@
                 across = send(right, FAR_MATE, pltpu.VMEM)
             forward = send(out[k][0], MATE)
             place(k, f"place_{k}", [*out[k], forward], [far_of, mate_of, far_mate_of])
-        place_last(far, (send(far[0], MATE, pltpu.VMEM), across))
+        forward = send(far[0], MATE, pltpu.VMEM)
+        place_parts("place_left", [(far[0], far_of, False)])
+        place_parts("place_last", [(far[1], far_of, True), (forward, far_mate_of, False), (across, far_mate_of, True)])
         return (*new_w, *new_m, *new_v)
 
     all_of, cut_of = P(None, None, None), P(None, "dp", None)

time: 843 us -> 844 us (level)
    pallas_call x37 -> x38, Pallas kernels: 220 us -> 221 us  [run(): pl.pallas_call(body, out_shape=outs, grid=grid, in_specs=in_specs, out_sp...]
where the time goes in v9:
time: 844 us
  waiting for transfers between devices  582 us (69%)
  Pallas kernels  227 us (27%)
  starting transfers between devices  30.4 us (4%)
    ppermute x49, waiting for transfers between devices, send(): return in_space(lax.ppermute(x, 'dp', pairs), space)  582 us
    pallas_call x38, Pallas kernels, run(): pl.pallas_call(body, out_shape=outs, grid=grid, in_specs=in_specs, out_sp...  221 us
    ppermute x49, starting transfers between devices, send(): return in_space(lax.ppermute(x, 'dp', pairs), space)  30.4 us
  transfers between devices with their start and end apart: 49, of which 16 were waited for; matrix products, arithmetic and copies ran while one was open for 0% of the time, Pallas kernels for 26%

profile of v9, /device:TPU:0, one launch (start us, length us, event | category | flops | bytes accessed | tf_op | source)
XLA Modules:
  0.0 843.5 jit_solution(6041608812126094760)
XLA Ops:
  0.6 2.8 shard_map.202
  4.3 2.7 shard_map.200
  11.8 6.1 head.1
  19.1 3.2 shard_map.192
  22.2 2.5 collective-permute-start.7
  25.6 25.4 %collective-permute-done.3.refs_0_ = bf16[32,4480]{1,0:T(8,128)(2,1)} collective-permute-done((bf16[32,4480]{1,0:T(8,128)(2,1)}, bf16[32,4480]{1,0:T(8,128)(2,1)}, u32[]{:S(2)}, u32[]{:S(2)}) %collective-permute-start.3) | collective-permute-done | bytes 286752 | tf_op jit(solution)/shard_map/ppermute | solution.py:121
  52.7 5.1 shard_map.199
  59.9 2.7 shard_map.188
  63.2 2.7 shard_map.219
  65.9 3.2 shard_map.194
  70.7 2.7 shard_map.217
  73.6 5.1 shard_map.187
  78.7 24.6 %collective-permute-done.9.refs_3_ = bf16[160,4480]{1,0:T(8,128)(2,1)} collective-permute-done((bf16[160,4480]{1,0:T(8,128)(2,1)}, bf16[160,4480]{1,0:T(8,128)(2,1)}, u32[]{:S(2)}, u32[]{:S(2)}) %collective-permute-start.9) | collective-permute-done | bytes 1433632 | tf_op jit(solution)/shard_map/ppermute | solution.py:121
  103.3 5.1 shard_map.216
  108.9 4.9 shard_map.203
  115.3 4.9 shard_map.201
  120.8 4.9 shard_map.189
  127.1 4.9 shard_map.220
  132.0 47.1 %collective-permute-done.20.refs_0_ = bf16[320,4480]{1,0:T(8,128)(2,1)} collective-permute-done((bf16[320,4480]{1,0:T(8,128)(2,1)}, bf16[320,4480]{1,0:T(8,128)(2,1)}, u32[]{:S(2)}, u32[]{:S(2)}) %collective-permute-start.20) | collective-permute-done | bytes 2867232 | tf_op jit(solution)/shard_map/ppermute | solution.py:121
  180.6 4.9 shard_map.218
  185.5 55.1 %collective-permute-done.18.refs_0_ = bf16[320,4480]{1,0:T(8,128)(2,1)} collective-permute-done((bf16[320,4480]{1,0:T(8,128)(2,1)}, bf16[320,4480]{1,0:T(8,128)(2,1)}, u32[]{:S(2)}, u32[]{:S(2)}) %collective-permute-start.18) | collective-permute-done | bytes 2867232 | tf_op jit(solution)/shard_map/ppermute | solution.py:121
  242.1 17.8 %shard_map.204 = (bf16[320,4480]{1,0:T(8,128)(2,1)}, bf16[2,1280,4480]{2,1,0:T(8,128)(2,1)}, f32[2,320,4480]{2,1,0:T(8,128)}, f32[2,320,4480]{2,1,0:T(8,128)}) custom-call(bf16[1,2,1280,4480]{3,2,1,0:T(8,128)(2,1)} %t.46, bf16[640,4480]{1,0:T(8,128)(2,1)} %collective-permute-done.16.r, bf16[2,1280,4480]{2,1,0:T(8,128)(2,1)} %wt.15, f32[2,320,4480]{2,1,0:T(8,128)} %mm.15, ...), custom_call_target="tpu_custom_call" | custom-call | flops 37273600 | bytes 37273600 | tf_op jit(solution)/shard_map/pallas_call | solution.py:108
  259.9 9.8 %shard_map.205 = (bf16[160,4480]{1,0:T(8,128)(2,1)}, bf16[2,1280,4480]{2,1,0:T(8,128)(2,1)}, f32[2,320,4480]{2,1,0:T(8,128)}, f32[2,320,4480]{2,1,0:T(8,128)}) custom-call(bf16[1,2,1280,4480]{3,2,1,0:T(8,128)(2,1)} %t.46, bf16[640,4480]{1,0:T(8,128)(2,1)} %collective-permute-done.16.r, ...), custom_call_target="tpu_custom_call", output_to_operand_aliasing={{1}: (6, {}), {2}: (7, {}), {3}: (8, {})} | custom-call | flops 35840000 | bytes 35840000 | tf_op jit(solution)/shard_map/pallas_call | solution.py:108
  270.2 4.0 shard_map.206
  274.3 4.0 shard_map.207
  278.3 3.1 shard_map.208
  281.3 20.7 %collective-permute-done.2.refs_0_ = bf16[320,4480]{1,0:T(8,128)(2,1)} collective-permute-done((bf16[320,4480]{1,0:T(8,128)(2,1)}, bf16[320,4480]{1,0:T(8,128)(2,1)}, u32[]{:S(2)}, u32[]{:S(2)}) %collective-permute-start.2) | collective-permute-done | bytes 2867232 | tf_op jit(solution)/shard_map/ppermute | solution.py:121
  303.5 60.0 %collective-permute-done.42.refs_0_ = bf16[1120,1280]{1,0:T(8,128)(2,1)} collective-permute-done((bf16[1120,1280]{1,0:T(8,128)(2,1)}, bf16[1120,1280]{1,0:T(8,128)(2,1)}, u32[]{:S(2)}, u32[]{:S(2)}) %collective-permute-start.42) | collective-permute-done | bytes 2867232 | tf_op jit(solution)/shard_map/ppermute | solution.py:121
  363.5 92.2 %collective-permute-done.31.refs_0_ = bf16[160,4480]{1,0:T(8,128)(2,1)} collective-permute-done((bf16[160,4480]{1,0:T(8,128)(2,1)}, bf16[160,4480]{1,0:T(8,128)(2,1)}, u32[]{:S(2)}, u32[]{:S(2)}) %collective-permute-start.31) | collective-permute-done | bytes 1433632 | tf_op jit(solution)/shard_map/ppermute | solution.py:121
  457.1 2.7 collective-permute-done.22.refs_0_
  461.3 10.7 %collective-permute-done.28.refs_0_ = bf16[64,4480]{1,0:T(8,128)(2,1)S(1)} collective-permute-done((bf16[64,4480]{1,0:T(8,128)(2,1)}, bf16[64,4480]{1,0:T(8,128)(2,1)S(1)}, u32[]{:S(2)}, u32[]{:S(2)}) %collective-permute-start.28) | collective-permute-done | bytes 573472 | tf_op jit(solution)/shard_map/ppermute | solution.py:121
  472.8 11.2 %collective-permute-done.25.refs_0_ = bf16[64,4480]{1,0:T(8,128)(2,1)} collective-permute-done((bf16[64,4480]{1,0:T(8,128)(2,1)}, bf16[64,4480]{1,0:T(8,128)(2,1)}, u32[]{:S(2)}, u32[]{:S(2)}) %collective-permute-start.25) | collective-permute-done | bytes 573472 | tf_op jit(solution)/shard_map/ppermute | solution.py:121
  486.6 17.8 %shard_map.195 = (bf16[320,4480]{1,0:T(8,128)(2,1)}, bf16[2,1280,4480]{2,1,0:T(8,128)(2,1)}, f32[2,320,4480]{2,1,0:T(8,128)}, f32[2,320,4480]{2,1,0:T(8,128)}) custom-call(bf16[1,2,1280,4480]{3,2,1,0:T(8,128)(2,1)} %t.36, bf16[640,4480]{1,0:T(8,128)(2,1)} %collective-permute-done.r, bf16[2,1280,4480]{2,1,0:T(8,128)(2,1)} %wt.10, f32[2,320,4480]{2,1,0:T(8,128)} %mm.10, ...), custom_call_target="tpu_custom_call" | custom-call | flops 37273600 | bytes 37273600 | tf_op jit(solution)/shard_map/pallas_call | solution.py:108
  505.5 17.8 %shard_map.196 = (bf16[320,4480]{1,0:T(8,128)(2,1)}, bf16[2,1280,4480]{2,1,0:T(8,128)(2,1)}, f32[2,320,4480]{2,1,0:T(8,128)}, f32[2,320,4480]{2,1,0:T(8,128)}) custom-call(bf16[1,2,1280,4480]{3,2,1,0:T(8,128)(2,1)} %t.36, bf16[640,4480]{1,0:T(8,128)(2,1)} %collective-permute-done.r, ...), custom_call_target="tpu_custom_call", output_to_operand_aliasing={{1}: (6, {}), {2}: (7, {}), {3}: (8, {})} | custom-call | flops 37273600 | bytes 37273600 | tf_op jit(solution)/shard_map/pallas_call | solution.py:108
  524.3 25.1 %collective-permute-done.34.refs_0_ = bf16[320,4480]{1,0:T(8,128)(2,1)} collective-permute-done((bf16[320,4480]{1,0:T(8,128)(2,1)}, bf16[320,4480]{1,0:T(8,128)(2,1)}, u32[]{:S(2)}, u32[]{:S(2)}) %collective-permute-start.34) | collective-permute-done | bytes 2867232 | tf_op jit(solution)/shard_map/ppermute | solution.py:121
  549.4 18.0 %shard_map.221 = (bf16[1120,1280]{1,0:T(8,128)(2,1)}, bf16[2,4480,1280]{2,1,0:T(8,128)(2,1)}, f32[2,1120,1280]{2,1,0:T(8,128)}, f32[2,1120,1280]{2,1,0:T(8,128)}) custom-call(bf16[1,2,4480,1280]{3,2,1,0:T(8,128)(2,1)} %t.53, bf16[2240,1280]{1,0:T(8,128)(2,1)} %collective-permute-done.38.r, bf16[2,4480,1280]{2,1,0:T(8,128)(2,1)} %wt.17, ...), custom_call_target="tpu_custom_call" | custom-call | flops 37273600 | bytes 37273600 | tf_op jit(solution)/shard_map/pallas_call | solution.py:108
  568.8 42.0 %collective-permute-done.13.refs_0_ = bf16[320,4480]{1,0:T(8,128)(2,1)} collective-permute-done((bf16[320,4480]{1,0:T(8,128)(2,1)}, bf16[320,4480]{1,0:T(8,128)(2,1)}, u32[]{:S(2)}, u32[]{:S(2)}) %collective-permute-start.13) | collective-permute-done | bytes 2867232 | tf_op jit(solution)/shard_map/ppermute | solution.py:121
  610.8 17.8 %shard_map.222 = (bf16[1120,1280]{1,0:T(8,128)(2,1)}, bf16[2,4480,1280]{2,1,0:T(8,128)(2,1)}, f32[2,1120,1280]{2,1,0:T(8,128)}, f32[2,1120,1280]{2,1,0:T(8,128)}) custom-call(bf16[1,2,4480,1280]{3,2,1,0:T(8,128)(2,1)} %t.53, bf16[2240,1280]{1,0:T(8,128)(2,1)} %collective-permute-done.38.r, ...), custom_call_target="tpu_custom_call", output_to_operand_aliasing={{1}: (6, {}), {2}: (7, {}), {3}: (8, {})} | custom-call | flops 37273600 | bytes 37273600 | tf_op jit(solution)/shard_map/pallas_call | solution.py:108
  630.1 42.2 %collective-permute-done.10.refs_0_ = bf16[320,4480]{1,0:T(8,128)(2,1)} collective-permute-done((bf16[320,4480]{1,0:T(8,128)(2,1)}, bf16[320,4480]{1,0:T(8,128)(2,1)}, u32[]{:S(2)}, u32[]{:S(2)}) %collective-permute-start.10) | collective-permute-done | bytes 2867232 | tf_op jit(solution)/shard_map/ppermute | solution.py:121
  672.8 60.9 %collective-permute-done.46.refs_0_ = bf16[1120,1280]{1,0:T(8,128)(2,1)} collective-permute-done((bf16[1120,1280]{1,0:T(8,128)(2,1)}, bf16[1120,1280]{1,0:T(8,128)(2,1)}, u32[]{:S(2)}, u32[]{:S(2)}) %collective-permute-start.46) | collective-permute-done | bytes 2867232 | tf_op jit(solution)/shard_map/ppermute | solution.py:121
  734.2 60.4 %collective-permute-done.43.refs_0_ = bf16[1120,1280]{1,0:T(8,128)(2,1)} collective-permute-done((bf16[1120,1280]{1,0:T(8,128)(2,1)}, bf16[1120,1280]{1,0:T(8,128)(2,1)}, u32[]{:S(2)}, u32[]{:S(2)}) %collective-permute-start.43) | collective-permute-done | bytes 2867232 | tf_op jit(solution)/shard_map/ppermute | solution.py:121
  798.7 6.5 shard_map.210.refs_3_
  805.3 3.6 shard_map.211.refs_3_
  811.3 2.4 shard_map.213.refs_1_
  815.3 6.5 shard_map.197.refs_3_
  821.9 6.5 shard_map.198
  828.4 6.6 shard_map.223.refs_3_
  835.0 6.6 shard_map.224
  (101 shorter events, 44.7 us)
Async XLA Ops:
  3.4 65.8 %collective-permute-start.19 = (bf16[320,4480]{1,0:T(8,128)(2,1)}, bf16[320,4480]{1,0:T(8,128)(2,1)}, u32[]{:S(2)}, u32[]{:S(2)}) collective-permute-start(bf16[320,4480]{1,0:T(8,128)(2,1)} %shard_map.202), channel_id=1, source_target_pairs={{0,1},{1,0},{2,3},{3,2},{4,5},{5,4},{6,7},{7,6}} | collective-permute-start | bytes 8601608 | tf_op jit(solution)/shard_map/ppermute | solution.py:121
  7.0 66.4 %collective-permute-start.17 = (bf16[320,4480]{1,0:T(8,128)(2,1)}, bf16[320,4480]{1,0:T(8,128)(2,1)}, u32[]{:S(2)}, u32[]{:S(2)}) collective-permute-start(bf16[320,4480]{1,0:T(8,128)(2,1)} %shard_map.200), channel_id=1, source_target_pairs={{0,1},{1,0},{2,3},{3,2},{4,5},{5,4},{6,7},{7,6}} | collective-permute-start | bytes 8601608 | tf_op jit(solution)/shard_map/ppermute | solution.py:121
  9.0 10.1 %collective-permute-start.6 = (bf16[96,4480]{1,0:T(8,128)(2,1)}, bf16[96,4480]{1,0:T(8,128)(2,1)}, u32[]{:S(2)}, u32[]{:S(2)}) collective-permute-start(bf16[96,4480]{1,0:T(8,128)(2,1)} %shard_map.191), channel_id=1, source_target_pairs={{0,1},{1,0},{2,3},{3,2},{4,5},{5,4},{6,7},{7,6}} | collective-permute-start | bytes 2580488 | tf_op jit(solution)/shard_map/ppermute | solution.py:121
  11.7 50.9 %collective-permute-start.8 = (bf16[160,4480]{1,0:T(8,128)(2,1)}, bf16[160,4480]{1,0:T(8,128)(2,1)}, u32[]{:S(2)}, u32[]{:S(2)}) collective-permute-start(bf16[160,4480]{1,0:T(8,128)(2,1)} %shard_map.193), channel_id=1, source_target_pairs={{0,1},{1,0},{2,3},{3,2},{4,5},{5,4},{6,7},{7,6}} | collective-permute-start | bytes 4300808 | tf_op jit(solution)/shard_map/ppermute | solution.py:121
  22.2 46.9 %collective-permute-start.7 = (bf16[96,4480]{1,0:T(8,128)(2,1)}, bf16[96,4480]{1,0:T(8,128)(2,1)}, u32[]{:S(2)}, u32[]{:S(2)}) collective-permute-start(bf16[96,4480]{1,0:T(8,128)(2,1)} %shard_map.192), channel_id=1, source_target_pairs={{0,2},{2,0},{1,3},{3,1},{4,6},{6,4},{5,7},{7,5}} | collective-permute-start | bytes 2580488 | tf_op jit(solution)/shard_map/ppermute | solution.py:121
  24.8 26.2 %collective-permute-start.3 = (bf16[32,4480]{1,0:T(8,128)(2,1)}, bf16[32,4480]{1,0:T(8,128)(2,1)}, u32[]{:S(2)}, u32[]{:S(2)}) collective-permute-start(bf16[32,4480]{1,0:T(8,128)(2,1)} %copy-done), channel_id=1, source_target_pairs={{0,2},{2,0},{1,3},{3,1},{4,6},{6,4},{5,7},{7,5}} | collective-permute-start | bytes 860168 | tf_op jit(solution)/shard_map/ppermute | solution.py:121
  51.0 8.9 %collective-permute-start.5 = (bf16[32,4480]{1,0:T(8,128)(2,1)}, bf16[32,4480]{1,0:T(8,128)(2,1)}, u32[]{:S(2)}, u32[]{:S(2)}) collective-permute-start(bf16[32,4480]{1,0:T(8,128)(2,1)} %shard_map.190), channel_id=1, source_target_pairs={{0,2},{2,0},{1,3},{3,1},{4,6},{6,4},{5,7},{7,5}} | collective-permute-start | bytes 860168 | tf_op jit(solution)/shard_map/ppermute | solution.py:121
  59.9 65.8 %collective-permute-start.16 = (bf16[640,4480]{1,0:T(8,128)(2,1)}, bf16[640,4480]{1,0:T(8,128)(2,1)}, u32[]{:S(2)}, u32[]{:S(2)}) collective-permute-start(bf16[640,4480]{1,0:T(8,128)(2,1)} %shard_map.199), channel_id=1, source_target_pairs={{0,1},{1,0},{2,3},{3,2},{4,5},{5,4},{6,7},{7,6}} | collective-permute-start | bytes 17203208 | tf_op jit(solution)/shard_map/ppermute | solution.py:121
  62.7 45.7 %collective-permute-start.1 = (bf16[320,4480]{1,0:T(8,128)(2,1)}, bf16[320,4480]{1,0:T(8,128)(2,1)}, u32[]{:S(2)}, u32[]{:S(2)}) collective-permute-start(bf16[320,4480]{1,0:T(8,128)(2,1)} %shard_map.188), channel_id=1, source_target_pairs={{0,1},{1,0},{2,3},{3,2},{4,5},{5,4},{6,7},{7,6}} | collective-permute-start | bytes 8601608 | tf_op jit(solution)/shard_map/ppermute | solution.py:121
  69.2 44.7 %collective-permute-start.41 = (bf16[1120,1280]{1,0:T(8,128)(2,1)}, bf16[1120,1280]{1,0:T(8,128)(2,1)}, u32[]{:S(2)}, u32[]{:S(2)}) collective-permute-start(bf16[1120,1280]{1,0:T(8,128)(2,1)} %shard_map.219), channel_id=1, source_target_pairs={{0,1},{1,0},{2,3},{3,2},{4,5},{5,4},{6,7},{7,6}} | collective-permute-start | bytes 8601608 | tf_op jit(solution)/shard_map/ppermute | solution.py:121
  69.2 34.1 %collective-permute-start.9 = (bf16[160,4480]{1,0:T(8,128)(2,1)}, bf16[160,4480]{1,0:T(8,128)(2,1)}, u32[]{:S(2)}, u32[]{:S(2)}) collective-permute-start(bf16[160,4480]{1,0:T(8,128)(2,1)} %shard_map.194), channel_id=1, source_target_pairs={{0,2},{2,0},{1,3},{3,1},{4,6},{6,4},{5,7},{7,5}} | collective-permute-start | bytes 4300808 | tf_op jit(solution)/shard_map/ppermute | solution.py:121
  73.4 46.8 %collective-permute-start.39 = (bf16[1120,1280]{1,0:T(8,128)(2,1)}, bf16[1120,1280]{1,0:T(8,128)(2,1)}, u32[]{:S(2)}, u32[]{:S(2)}) collective-permute-start(bf16[1120,1280]{1,0:T(8,128)(2,1)} %shard_map.217), channel_id=1, source_target_pairs={{0,1},{1,0},{2,3},{3,2},{4,5},{5,4},{6,7},{7,6}} | collective-permute-start | bytes 8601608 | tf_op jit(solution)/shard_map/ppermute | solution.py:121
  103.3 166.4 %collective-permute-start = (bf16[640,4480]{1,0:T(8,128)(2,1)}, bf16[640,4480]{1,0:T(8,128)(2,1)}, u32[]{:S(2)}, u32[]{:S(2)}) collective-permute-start(bf16[640,4480]{1,0:T(8,128)(2,1)} %shard_map.187), channel_id=1, source_target_pairs={{0,1},{1,0},{2,3},{3,2},{4,5},{5,4},{6,7},{7,6}} | collective-permute-start | bytes 17203208 | tf_op jit(solution)/shard_map/ppermute | solution.py:121
  108.4 193.6 %collective-permute-start.38 = (bf16[2240,1280]{1,0:T(8,128)(2,1)}, bf16[2240,1280]{1,0:T(8,128)(2,1)}, u32[]{:S(2)}, u32[]{:S(2)}) collective-permute-start(bf16[2240,1280]{1,0:T(8,128)(2,1)} %shard_map.216), channel_id=1, source_target_pairs={{0,1},{1,0},{2,3},{3,2},{4,5},{5,4},{6,7},{7,6}} | collective-permute-start | bytes 17203208 | tf_op jit(solution)/shard_map/ppermute | solution.py:121
  113.8 65.3 %collective-permute-start.20 = (bf16[320,4480]{1,0:T(8,128)(2,1)}, bf16[320,4480]{1,0:T(8,128)(2,1)}, u32[]{:S(2)}, u32[]{:S(2)}) collective-permute-start(bf16[320,4480]{1,0:T(8,128)(2,1)} %shard_map.203), channel_id=1, source_target_pairs={{0,2},{2,0},{1,3},{3,1},{4,6},{6,4},{5,7},{7,5}} | collective-permute-start | bytes 8601608 | tf_op jit(solution)/shard_map/ppermute | solution.py:121
  120.2 120.4 %collective-permute-start.18 = (bf16[320,4480]{1,0:T(8,128)(2,1)}, bf16[320,4480]{1,0:T(8,128)(2,1)}, u32[]{:S(2)}, u32[]{:S(2)}) collective-permute-start(bf16[320,4480]{1,0:T(8,128)(2,1)} %shard_map.201), channel_id=1, source_target_pairs={{0,2},{2,0},{1,3},{3,1},{4,6},{6,4},{5,7},{7,5}} | collective-permute-start | bytes 8601608 | tf_op jit(solution)/shard_map/ppermute | solution.py:121
  125.7 176.4 %collective-permute-start.2 = (bf16[320,4480]{1,0:T(8,128)(2,1)}, bf16[320,4480]{1,0:T(8,128)(2,1)}, u32[]{:S(2)}, u32[]{:S(2)}) collective-permute-start(bf16[320,4480]{1,0:T(8,128)(2,1)} %shard_map.189), channel_id=1, source_target_pairs={{0,2},{2,0},{1,3},{3,1},{4,6},{6,4},{5,7},{7,5}} | collective-permute-start | bytes 8601608 | tf_op jit(solution)/shard_map/ppermute | solution.py:121
  179.2 184.3 %collective-permute-start.42 = (bf16[1120,1280]{1,0:T(8,128)(2,1)}, bf16[1120,1280]{1,0:T(8,128)(2,1)}, u32[]{:S(2)}, u32[]{:S(2)}) collective-permute-start(bf16[1120,1280]{1,0:T(8,128)(2,1)} %shard_map.220), channel_id=1, source_target_pairs={{0,2},{2,0},{1,3},{3,1},{4,6},{6,4},{5,7},{7,5}} | collective-permute-start | bytes 8601608 | tf_op jit(solution)/shard_map/ppermute | solution.py:121
  240.6 215.1 %collective-permute-start.40 = (bf16[1120,1280]{1,0:T(8,128)(2,1)}, bf16[1120,1280]{1,0:T(8,128)(2,1)}, u32[]{:S(2)}, u32[]{:S(2)}) collective-permute-start(bf16[1120,1280]{1,0:T(8,128)(2,1)} %shard_map.218), channel_id=1, source_target_pairs={{0,2},{2,0},{1,3},{3,1},{4,6},{6,4},{5,7},{7,5}} | collective-permute-start | bytes 8601608 | tf_op jit(solution)/shard_map/ppermute | solution.py:121
  269.7 185.9 %collective-permute-start.31 = (bf16[160,4480]{1,0:T(8,128)(2,1)}, bf16[160,4480]{1,0:T(8,128)(2,1)}, u32[]{:S(2)}, u32[]{:S(2)}) collective-permute-start(bf16[160,4480]{1,0:T(8,128)(2,1)} %get-tuple-element.75), channel_id=1, source_target_pairs={{0,2},{2,0},{1,3},{3,1},{4,6},{6,4},{5,7},{7,5}} | collective-permute-start | bytes 4300808 | tf_op jit(solution)/shard_map/ppermute | solution.py:121
  302.0 157.8 %collective-permute-start.37 = (bf16[32,4480]{1,0:T(8,128)(2,1)}, bf16[32,4480]{1,0:T(8,128)(2,1)S(1)}, u32[]{:S(2)}, u32[]{:S(2)}) collective-permute-start(bf16[32,4480]{1,0:T(8,128)(2,1)} %get-tuple-element.77), channel_id=1, source_target_pairs={{0,1},{1,0},{2,3},{3,2},{4,5},{5,4},{6,7},{7,6}} | collective-permute-start | bytes 860168 | tf_op jit(solution)/shard_map/ppermute | solution.py:121
  302.1 157.8 %collective-permute-start.22 = (bf16[32,3456]{1,0:T(8,128)(2,1)}, bf16[32,3456]{1,0:T(8,128)(2,1)}, u32[]{:S(2)}, u32[]{:S(2)}) collective-permute-start(bf16[32,3456]{1,0:T(8,128)(2,1)} %get-tuple-element.72), channel_id=1, source_target_pairs={{0,2},{2,0},{1,3},{3,1},{4,6},{6,4},{5,7},{7,5}} | collective-permute-start | bytes 663560 | tf_op jit(solution)/shard_map/ppermute | solution.py:121
  363.5 159.8 %collective-permute-start.32 = (bf16[160,4480]{1,0:T(8,128)(2,1)}, bf16[160,4480]{1,0:T(8,128)(2,1)}, u32[]{:S(2)}, u32[]{:S(2)}) collective-permute-start(bf16[160,4480]{1,0:T(8,128)(2,1)} %get-tuple-element.75), channel_id=1, source_target_pairs={{0,1},{1,0},{2,3},{3,2},{4,5},{5,4},{6,7},{7,6}} | collective-permute-start | bytes 4300808 | tf_op jit(solution)/shard_map/ppermute | solution.py:121
  455.7 67.7 %collective-permute-start.33 = (bf16[160,4480]{1,0:T(8,128)(2,1)}, bf16[160,4480]{1,0:T(8,128)(2,1)}, u32[]{:S(2)}, u32[]{:S(2)}) collective-permute-start(bf16[160,4480]{1,0:T(8,128)(2,1)} %collective-permute-done.31.refs_0_), channel_id=1, source_target_pairs={{0,1},{1,0},{2,3},{3,2},{4,5},{5,4},{6,7},{7,6}} | collective-permute-start | bytes 4300808 | tf_op jit(solution)/shard_map/ppermute | solution.py:121
  455.7 16.3 %collective-permute-start.28 = (bf16[64,4480]{1,0:T(8,128)(2,1)}, bf16[64,4480]{1,0:T(8,128)(2,1)S(1)}, u32[]{:S(2)}, u32[]{:S(2)}) collective-permute-start(bf16[64,4480]{1,0:T(8,128)(2,1)} %get-tuple-element.74), channel_id=1, source_target_pairs={{0,2},{2,0},{1,3},{3,1},{4,6},{6,4},{5,7},{7,5}} | collective-permute-start | bytes 1720328 | tf_op jit(solution)/shard_map/ppermute | solution.py:121
  459.8 12.2 %collective-permute-start.29 = (bf16[64,4480]{1,0:T(8,128)(2,1)}, bf16[64,4480]{1,0:T(8,128)(2,1)S(1)}, u32[]{:S(2)}, u32[]{:S(2)}) collective-permute-start(bf16[64,4480]{1,0:T(8,128)(2,1)} %get-tuple-element.74), channel_id=1, source_target_pairs={{0,1},{1,0},{2,3},{3,2},{4,5},{5,4},{6,7},{7,6}} | collective-permute-start | bytes 1720328 | tf_op jit(solution)/shard_map/ppermute | solution.py:121
  459.8 24.2 %collective-permute-start.25 = (bf16[64,4480]{1,0:T(8,128)(2,1)}, bf16[64,4480]{1,0:T(8,128)(2,1)}, u32[]{:S(2)}, u32[]{:S(2)}) collective-permute-start(bf16[64,4480]{1,0:T(8,128)(2,1)} %get-tuple-element.73), channel_id=1, source_target_pairs={{0,2},{2,0},{1,3},{3,1},{4,6},{6,4},{5,7},{7,5}} | collective-permute-start | bytes 1720328 | tf_op jit(solution)/shard_map/ppermute | solution.py:121
  472.0 12.0 %collective-permute-start.26 = (bf16[64,4480]{1,0:T(8,128)(2,1)}, bf16[64,4480]{1,0:T(8,128)(2,1)S(1)}, u32[]{:S(2)}, u32[]{:S(2)}) collective-permute-start(bf16[64,4480]{1,0:T(8,128)(2,1)} %get-tuple-element.73), channel_id=1, source_target_pairs={{0,1},{1,0},{2,3},{3,2},{4,5},{5,4},{6,7},{7,6}} | collective-permute-start | bytes 1720328 | tf_op jit(solution)/shard_map/ppermute | solution.py:121
  472.8 12.7 %collective-permute-start.30 = (bf16[64,4480]{1,0:T(8,128)(2,1)S(1)}, bf16[64,4480]{1,0:T(8,128)(2,1)S(1)}, u32[]{:S(2)}, u32[]{:S(2)}) collective-permute-start(bf16[64,4480]{1,0:T(8,128)(2,1)S(1)} %collective-permute-done.28.refs_0_), channel_id=1, source_target_pairs={{0,1},{1,0},{2,3},{3,2},{4,5},{5,4},{6,7},{7,6}} | collective-permute-start | bytes 1720328 | tf_op jit(solution)/shard_map/ppermute | solution.py:121
  484.0 20.3 %collective-permute-start.27 = (bf16[64,4480]{1,0:T(8,128)(2,1)}, bf16[64,4480]{1,0:T(8,128)(2,1)}, u32[]{:S(2)}, u32[]{:S(2)}) collective-permute-start(bf16[64,4480]{1,0:T(8,128)(2,1)} %collective-permute-done.25.refs_0_), channel_id=1, source_target_pairs={{0,1},{1,0},{2,3},{3,2},{4,5},{5,4},{6,7},{7,6}} | collective-permute-start | bytes 1720328 | tf_op jit(solution)/shard_map/ppermute | solution.py:121
  484.0 65.3 %collective-permute-start.34 = (bf16[320,4480]{1,0:T(8,128)(2,1)}, bf16[320,4480]{1,0:T(8,128)(2,1)}, u32[]{:S(2)}, u32[]{:S(2)}) collective-permute-start(bf16[320,4480]{1,0:T(8,128)(2,1)} %get-tuple-element.76), channel_id=1, source_target_pairs={{0,2},{2,0},{1,3},{3,1},{4,6},{6,4},{5,7},{7,5}} | collective-permute-start | bytes 8601608 | tf_op jit(solution)/shard_map/ppermute | solution.py:121
  486.4 81.0 %collective-permute-start.35 = (bf16[320,4480]{1,0:T(8,128)(2,1)}, bf16[320,4480]{1,0:T(8,128)(2,1)}, u32[]{:S(2)}, u32[]{:S(2)}) collective-permute-start(bf16[320,4480]{1,0:T(8,128)(2,1)} %get-tuple-element.76), channel_id=1, source_target_pairs={{0,1},{1,0},{2,3},{3,2},{4,5},{5,4},{6,7},{7,6}} | collective-permute-start | bytes 8601608 | tf_op jit(solution)/shard_map/ppermute | solution.py:121
  504.4 106.5 %collective-permute-start.13 = (bf16[320,4480]{1,0:T(8,128)(2,1)}, bf16[320,4480]{1,0:T(8,128)(2,1)}, u32[]{:S(2)}, u32[]{:S(2)}) collective-permute-start(bf16[320,4480]{1,0:T(8,128)(2,1)} %get-tuple-element.57), channel_id=1, source_target_pairs={{0,2},{2,0},{1,3},{3,1},{4,6},{6,4},{5,7},{7,5}} | collective-permute-start | bytes 8601608 | tf_op jit(solution)/shard_map/ppermute | solution.py:121
  523.3 105.3 %collective-permute-start.14 = (bf16[320,4480]{1,0:T(8,128)(2,1)}, bf16[320,4480]{1,0:T(8,128)(2,1)}, u32[]{:S(2)}, u32[]{:S(2)}) collective-permute-start(bf16[320,4480]{1,0:T(8,128)(2,1)} %get-tuple-element.57), channel_id=1, source_target_pairs={{0,1},{1,0},{2,3},{3,2},{4,5},{5,4},{6,7},{7,6}} | collective-permute-start | bytes 8601608 | tf_op jit(solution)/shard_map/ppermute | solution.py:121
  523.3 148.9 %collective-permute-start.10 = (bf16[320,4480]{1,0:T(8,128)(2,1)}, bf16[320,4480]{1,0:T(8,128)(2,1)}, u32[]{:S(2)}, u32[]{:S(2)}) collective-permute-start(bf16[320,4480]{1,0:T(8,128)(2,1)} %get-tuple-element.56), channel_id=1, source_target_pairs={{0,2},{2,0},{1,3},{3,1},{4,6},{6,4},{5,7},{7,5}} | collective-permute-start | bytes 8601608 | tf_op jit(solution)/shard_map/ppermute | solution.py:121
  549.4 122.9 %collective-permute-start.11 = (bf16[320,4480]{1,0:T(8,128)(2,1)}, bf16[320,4480]{1,0:T(8,128)(2,1)}, u32[]{:S(2)}, u32[]{:S(2)}) collective-permute-start(bf16[320,4480]{1,0:T(8,128)(2,1)} %get-tuple-element.56), channel_id=1, source_target_pairs={{0,1},{1,0},{2,3},{3,2},{4,5},{5,4},{6,7},{7,6}} | collective-permute-start | bytes 8601608 | tf_op jit(solution)/shard_map/ppermute | solution.py:121
  567.4 166.3 %collective-permute-start.46 = (bf16[1120,1280]{1,0:T(8,128)(2,1)}, bf16[1120,1280]{1,0:T(8,128)(2,1)}, u32[]{:S(2)}, u32[]{:S(2)}) collective-permute-start(bf16[1120,1280]{1,0:T(8,128)(2,1)} %get-tuple-element.83), channel_id=1, source_target_pairs={{0,2},{2,0},{1,3},{3,1},{4,6},{6,4},{5,7},{7,5}} | collective-permute-start | bytes 8601608 | tf_op jit(solution)/shard_map/ppermute | solution.py:121
  610.8 122.9 %collective-permute-start.47 = (bf16[1120,1280]{1,0:T(8,128)(2,1)}, bf16[1120,1280]{1,0:T(8,128)(2,1)}, u32[]{:S(2)}, u32[]{:S(2)}) collective-permute-start(bf16[1120,1280]{1,0:T(8,128)(2,1)} %get-tuple-element.83), channel_id=1, source_target_pairs={{0,1},{1,0},{2,3},{3,2},{4,5},{5,4},{6,7},{7,6}} | collective-permute-start | bytes 8601608 | tf_op jit(solution)/shard_map/ppermute | solution.py:121
  628.6 166.1 %collective-permute-start.43 = (bf16[1120,1280]{1,0:T(8,128)(2,1)}, bf16[1120,1280]{1,0:T(8,128)(2,1)}, u32[]{:S(2)}, u32[]{:S(2)}) collective-permute-start(bf16[1120,1280]{1,0:T(8,128)(2,1)} %get-tuple-element.82), channel_id=1, source_target_pairs={{0,2},{2,0},{1,3},{3,1},{4,6},{6,4},{5,7},{7,5}} | collective-permute-start | bytes 8601608 | tf_op jit(solution)/shard_map/ppermute | solution.py:121
  672.3 122.4 %collective-permute-start.36 = (bf16[320,4480]{1,0:T(8,128)(2,1)}, bf16[320,4480]{1,0:T(8,128)(2,1)}, u32[]{:S(2)}, u32[]{:S(2)}) collective-permute-start(bf16[320,4480]{1,0:T(8,128)(2,1)} %collective-permute-done.34.refs_0_), channel_id=1, source_target_pairs={{0,1},{1,0},{2,3},{3,2},{4,5},{5,4},{6,7},{7,6}} | collective-permute-start | bytes 8601608 | tf_op jit(solution)/shard_map/ppermute | solution.py:121
  672.3 122.9 %collective-permute-start.15 = (bf16[320,4480]{1,0:T(8,128)(2,1)}, bf16[320,4480]{1,0:T(8,128)(2,1)}, u32[]{:S(2)}, u32[]{:S(2)}) collective-permute-start(bf16[320,4480]{1,0:T(8,128)(2,1)} %collective-permute-done.13.refs_0_), channel_id=1, source_target_pairs={{0,1},{1,0},{2,3},{3,2},{4,5},{5,4},{6,7},{7,6}} | collective-permute-start | bytes 8601608 | tf_op jit(solution)/shard_map/ppermute | solution.py:121
  733.7 61.5 %collective-permute-start.12 = (bf16[320,4480]{1,0:T(8,128)(2,1)}, bf16[320,4480]{1,0:T(8,128)(2,1)}, u32[]{:S(2)}, u32[]{:S(2)}) collective-permute-start(bf16[320,4480]{1,0:T(8,128)(2,1)} %collective-permute-done.10.refs_0_), channel_id=1, source_target_pairs={{0,1},{1,0},{2,3},{3,2},{4,5},{5,4},{6,7},{7,6}} | collective-permute-start | bytes 8601608 | tf_op jit(solution)/shard_map/ppermute | solution.py:121
  733.7 63.0 %collective-permute-start.48 = (bf16[1120,1280]{1,0:T(8,128)(2,1)}, bf16[1120,1280]{1,0:T(8,128)(2,1)}, u32[]{:S(2)}, u32[]{:S(2)}) collective-permute-start(bf16[1120,1280]{1,0:T(8,128)(2,1)} %collective-permute-done.46.refs_0_), channel_id=1, source_target_pairs={{0,1},{1,0},{2,3},{3,2},{4,5},{5,4},{6,7},{7,6}} | collective-permute-start | bytes 8601608 | tf_op jit(solution)/shard_map/ppermute | solution.py:121
  794.7 40.3 %collective-permute-start.44 = (bf16[1120,1280]{1,0:T(8,128)(2,1)}, bf16[1120,1280]{1,0:T(8,128)(2,1)}, u32[]{:S(2)}, u32[]{:S(2)}) collective-permute-start(bf16[1120,1280]{1,0:T(8,128)(2,1)} %get-tuple-element.82), channel_id=1, source_target_pairs={{0,1},{1,0},{2,3},{3,2},{4,5},{5,4},{6,7},{7,6}} | collective-permute-start | bytes 8601608 | tf_op jit(solution)/shard_map/ppermute | solution.py:121
  794.7 40.3 %collective-permute-start.45 = (bf16[1120,1280]{1,0:T(8,128)(2,1)}, bf16[1120,1280]{1,0:T(8,128)(2,1)}, u32[]{:S(2)}, u32[]{:S(2)}) collective-permute-start(bf16[1120,1280]{1,0:T(8,128)(2,1)} %collective-permute-done.43.refs_0_), channel_id=1, source_target_pairs={{0,1},{1,0},{2,3},{3,2},{4,5},{5,4},{6,7},{7,6}} | collective-permute-start | bytes 8601608 | tf_op jit(solution)/shard_map/ppermute | solution.py:121
  795.2 46.4 %collective-permute-start.23 = (bf16[32,3456]{1,0:T(8,128)(2,1)}, bf16[32,3456]{1,0:T(8,128)(2,1)}, u32[]{:S(2)}, u32[]{:S(2)}) collective-permute-start(bf16[32,3456]{1,0:T(8,128)(2,1)} %collective-permute-done.22.refs_0_), channel_id=1, source_target_pairs={{0,1},{1,0},{2,3},{3,2},{4,5},{5,4},{6,7},{7,6}} | collective-permute-start | bytes 663560 | tf_op jit(solution)/shard_map/ppermute | solution.py:121
  795.2 46.4 %collective-permute-start.21 = (bf16[32,1024]{1,0:T(8,128)(2,1)}, bf16[32,1024]{1,0:T(8,128)(2,1)}, u32[]{:S(2)}, u32[]{:S(2)}) collective-permute-start(bf16[32,1024]{1,0:T(8,128)(2,1)} %get-tuple-element.71), channel_id=1, source_target_pairs={{0,2},{2,0},{1,3},{3,1},{4,6},{6,4},{5,7},{7,5}} | collective-permute-start | bytes 196616 | tf_op jit(solution)/shard_map/ppermute | solution.py:121
  796.7 44.9 %collective-permute-start.24 = (bf16[32,1024]{1,0:T(8,128)(2,1)}, bf16[32,1024]{1,0:T(8,128)(2,1)}, u32[]{:S(2)}, u32[]{:S(2)}) collective-permute-start(bf16[32,1024]{1,0:T(8,128)(2,1)} %get-tuple-element.71), channel_id=1, source_target_pairs={{0,3},{3,0},{1,2},{2,1},{4,7},{7,4},{5,6},{6,5}} | collective-permute-start | bytes 196616 | tf_op jit(solution)/shard_map/ppermute | solution.py:121
  (7 other events, 24.3 us)
